TPU v7x, 128 devices: a whole 4x4x4 slice. The times are simulated.
128 devices in a mesh: dp: 16 (over z, x_lo, core), tensor: 8 (over x_hi, y).
Axes of the slice: x: 4 (x_hi: 2, x_lo: 2; x = x_hi * 2 + x_lo), y: 4, z: 4, core: 2. Of those that a mesh axis runs over, the one named last changes fastest.
Arguments:
- prompt_ids: int32 [16384], P(('dp', 'tensor')), may hold values from 0 to 128255
- prompt_lengths: int32 [32], replicated, may hold values from 1 to 512, as said below
- embed_table: bfloat16 [4096, 128256], P(('dp', 'tensor')), may hold values from -4 to 4
- norm_gain: float32 [4096], replicated, may hold values from 0.5 to 1.5
- w_query: bfloat16 [4096, 4096], P('dp', 'tensor'), may hold values from -3 to 3
- w_key: bfloat16 [4096, 1024], P('dp', 'tensor'), may hold values from -1 to 1
- w_value: bfloat16 [4096, 1024], P('dp', 'tensor'), may hold values from -0.09375 to 0.09375
- w_out: bfloat16 [4096, 4096], P('tensor', 'dp'), may hold values from -0.09375 to 0.09375
Outputs:
- hidden: bfloat16 [16384, 4096], P(('dp', 'tensor'))
- kv_cache: bfloat16 [128, 2, 512, 256], P(('dp', 'tensor'))
Inputs may be any that keep to these rules, and one draw needn't show every extreme that they name: `prompt_lengths`: each group's prompt has 1 to 512 live tokens, and some group's has 512.
All inputs are finite; a program needn't handle non-finite values.
Results may differ from a plain program's by a relative error of at most 0.0095.
Values may be sent and summed in bfloat16 or wider, within the bound.
No kernel may reach another device: no remote copies, remote signals or barrier semaphores. Data moves between devices by JAX's collectives and lax.ppermute only.
A program may use at most 192 MiB of HBM per device.

v0:
```python
import jax
import jax.numpy as jnp
from jax import lax
from jax.sharding import Mesh
from jax.sharding import PartitionSpec as P

HEADS = 32
KVH = 8
HD = 128
TPG = 4
TENSOR = ("tensor_0", "tensor_1")
DP_TENSOR = ("dp_0", "dp_1", "dp_2", "tensor_0", "tensor_1")
DP = ("dp_0", "dp_1", "dp_2")


norm_eps = 1e-05
rope_theta = 500000.0


def piece_ends(length, count):
    turn = length // count
    if turn >= 8:
        turn -= turn % 8
    return [turn * k for k in range(1, count)]


def stacked_from(shard, axes, sequence):
    pieces = shard[None]
    for k in sequence:
        pieces = lax.all_gather(pieces, axes[k], axis=0, tiled=True)
    block = [lax.axis_size(axes[k]) for k in reversed(sequence)]
    pieces = pieces.reshape(*block, *shard.shape)
    turned = sorted(range(len(sequence)), key=lambda place: sequence[len(sequence) - 1 - place])
    return pieces.transpose(*turned, *range(len(sequence), pieces.ndim)).reshape(-1, *shard.shape)


def laid_out(pieces, dim):
    shape = list(pieces.shape[1:])
    shape[dim] *= pieces.shape[0]
    return jnp.moveaxis(pieces, 0, dim).reshape(shape)


def gather_at_once(shard, axes, dim):
    split_at = max(range(max(1, shard.ndim - 1)), key=lambda d: shard.shape[d])
    count, outs = (len(axes), [])
    for first, slab in enumerate(
        jnp.split(shard, piece_ends(shard.shape[split_at], count), axis=split_at)
    ):
        if slab.size:
            sequence = [(first - k) % count for k in range(count)]
            outs.append(stacked_from(slab, axes, sequence))
    return laid_out(jnp.concatenate(outs, axis=split_at + 1), dim)


def swapped(block, axis, apart):
    count = lax.axis_size(axis)
    route = []
    for low in range(count):
        high = low | 1 << apart
        if high != low and high < count:
            route += [(low, high), (high, low)]
    return lax.ppermute(block, axis, route)


def rotate(heads_in, positions):
    half = heads_in.shape[-1] // 2
    freq = rope_theta ** (-2.0 * jnp.arange(half, dtype=jnp.float32) / heads_in.shape[-1])
    angle = positions.astype(jnp.float32)[:, None] * freq[None, :]
    cosine = jnp.cos(angle)[:, None, :]
    sine = jnp.sin(angle)[:, None, :]
    first = heads_in[..., :half]
    second = heads_in[..., half:]
    return jnp.concatenate(
        [first * cosine - second * sine, second * cosine + first * sine], axis=-1
    )


def attend(query_rot, key_rot, value_rows, length):
    row_count = query_rot.shape[0]
    block = min(512, row_count)
    positions = jnp.arange(row_count, dtype=jnp.int32)

    def one_block(offset):
        scores = jnp.einsum(
            "qhgd,khd->hgqk", query_rot, key_rot, preferred_element_type=jnp.float32
        ) / jnp.sqrt(jnp.float32(HD))
        query_pos = offset + jnp.arange(block, dtype=jnp.int32)
        allowed = (positions[None, :] <= query_pos[:, None]) & (positions[None, :] < length)
        scores = jnp.where(allowed, scores, -1e30)
        biggest = jnp.max(scores, axis=-1, keepdims=True)
        expd = jnp.exp(scores - biggest)
        weights = (expd / jnp.sum(expd, axis=-1, keepdims=True)).astype(jnp.bfloat16)
        result = jnp.einsum(
            "hgqk,khd->qhgd", weights, value_rows, preferred_element_type=jnp.float32
        )
        return result.astype(jnp.bfloat16)

    starts = jnp.arange(0, row_count, block, dtype=jnp.int32)
    outs = lax.map(one_block, starts)
    return outs.reshape(row_count, -1)


def ordered_pair(mine, theirs, bit_index):
    upper_half = lax.axis_index(TENSOR) >> bit_index & 1 == 1
    first_half = jnp.where(upper_half, theirs, mine)
    second_half = jnp.where(upper_half, mine, theirs)
    return jnp.concatenate([first_half, second_half], axis=0)


def collect_blocks(shard, swapper):
    stacked = shard[None]
    stacked = ordered_pair(stacked, swapper(stacked, 2), 2)
    return stacked


def rms_normed(tokens_in, norm_gain):
    wide_in = tokens_in.astype(jnp.float32)
    scale = lax.rsqrt(jnp.mean(wide_in * wide_in, axis=1, keepdims=True) + norm_eps)
    return (wide_in * scale * norm_gain[None, :]).astype(jnp.bfloat16)


def lookup_rows(embed_table, token_ids):
    columns = embed_table.shape[0]
    vocab_size = embed_table.shape[1]
    packing = max(1, 128 // columns)
    token_major = embed_table.T.reshape(vocab_size // packing, packing * columns)
    fetched = jnp.take(token_major, token_ids // packing, axis=0).reshape(
        token_ids.shape[0], packing, columns
    )
    slot_ids = jnp.arange(packing, dtype=jnp.int32)
    wanted = (token_ids % packing)[:, None] == slot_ids[None, :]
    chosen = jnp.where(wanted[:, :, None], fetched, jnp.zeros_like(fetched))
    return jnp.sum(chosen, axis=1, dtype=jnp.bfloat16)


def shards(prompt_ids, prompt_lengths, embed_table, norm_gain, w_query, w_key, w_value, w_out):
    quarter = prompt_ids.shape[0]
    row_count = quarter * TPG
    devices = lax.axis_size(DP_TENSOR)
    columns = embed_table.shape[0]
    model_width = columns * devices
    member = lax.axis_index(TENSOR) % TPG
    group_index = (
        lax.axis_index(DP) * (lax.axis_size(TENSOR) // TPG) + lax.axis_index(TENSOR) // TPG
    )
    length = lax.dynamic_slice_in_dim(prompt_lengths, group_index, 1, 0)[0]
    all_ids = gather_at_once(prompt_ids, DP_TENSOR, 0)
    picked = lookup_rows(embed_table, all_ids)
    group_count = devices // TPG
    outgoing = jnp.broadcast_to(
        picked.reshape(group_count, 1, row_count, columns), (group_count, TPG, row_count, columns)
    )
    arrived = lax.all_to_all(
        outgoing.reshape(devices, row_count, columns),
        DP_TENSOR,
        split_axis=0,
        concat_axis=2,
        tiled=True,
    )
    group_rows = arrived.reshape(row_count, model_width)
    normed = rms_normed(group_rows, norm_gain)
    own_rows = lax.dynamic_slice_in_dim(group_rows, member * quarter, quarter, 0)
    query_width = w_query.shape[1]
    key_width = w_key.shape[1]
    packed = jnp.concatenate([w_query, w_key, w_value], axis=1)
    stacked = collect_blocks(packed, lambda values, bit_index: swapped(values, TENSOR, bit_index))
    projected = jnp.einsum(
        "rd,kdc->rkc",
        normed,
        lax.all_gather(stacked, DP, axis=1, tiled=True),
        preferred_element_type=jnp.float32,
    )
    blocks = projected.shape[1]
    local_heads = blocks * query_width // HD
    local_kv = blocks * key_width // HD
    positions = jnp.arange(row_count, dtype=jnp.int32)
    query = projected[:, :, :query_width].reshape(row_count, local_heads, HD)
    key_raw = projected[:, :, query_width : query_width + key_width]
    value_raw = projected[:, :, query_width + key_width :]
    query_rot = rotate(query, positions).astype(jnp.bfloat16)
    key_rot = rotate(key_raw, positions).astype(jnp.bfloat16)
    value_rows = value_raw.astype(jnp.bfloat16)
    cache = jnp.stack(
        [key_rot.reshape(row_count, local_kv * HD), value_rows.reshape(row_count, local_kv * HD)],
        axis=0,
    )[None]
    attended = attend(
        query_rot.reshape(row_count, local_kv, HEADS // KVH, HD), key_rot, value_rows, length
    )
    attended = attended.reshape(row_count, blocks, query_width)
    out_blocks = collect_blocks(w_out, lambda values, bit_index: swapped(values, TENSOR, bit_index))
    partial_sum = jnp.einsum(
        "rkw,kwc->rc",
        attended,
        lax.all_gather(out_blocks, DP, axis=2, tiled=True),
        preferred_element_type=jnp.float32,
    )
    levels_in = TPG.bit_length() - 1
    running = partial_sum
    for bit_index in reversed(range(levels_in)):
        half_rows = running.shape[0] // 2
        upper_half = lax.axis_index(TENSOR) >> bit_index & 1 == 1
        kept = jnp.where(upper_half, running[half_rows:], running[:half_rows]).astype(jnp.bfloat16)
        given = jnp.where(upper_half, running[:half_rows], running[half_rows:]).astype(jnp.bfloat16)
        arrived_sum = swapped(given, TENSOR, bit_index)
        running = kept.astype(jnp.float32) + arrived_sum.astype(jnp.float32)
    hidden = (own_rows.astype(jnp.float32) + running).astype(jnp.bfloat16)
    return (hidden, cache)


def solution(mesh):
    split = Mesh(
        mesh.devices.reshape(4, 2, 2, 2, 4), ("dp_0", "dp_1", "dp_2", "tensor_0", "tensor_1")
    )
    placed = (
        P(DP_TENSOR),
        P(),
        P(DP_TENSOR, None),
        P(),
        P(DP, TENSOR),
        P(DP, TENSOR),
        P(DP, TENSOR),
        P(TENSOR, DP),
    )
    return jax.shard_map(
        shards,
        mesh=split,
        in_specs=placed,
        out_specs=(P(DP_TENSOR, None), P(DP_TENSOR, None, None, None)),
        check_vma=False,
    )
```

profile of v0, /device:TPU:6, one launch (start us, length us, event | category | flops | bytes accessed | tf_op | source)
XLA Modules:
  0.0 529.5 jit_solution(4063840537244072791)
XLA Ops:
  9.9 11.0 %collective-permute-done = bf16[1,256,768]{2,1,0:T(8,128)(2,1)S(1)} collective-permute-done((bf16[1,256,768]{2,1,0:T(8,128)(2,1)S(1)}, bf16[1,256,768]{2,1,0:T(8,128)(2,1)S(1)}, u32[]{:S(2)}, u32[]{:S(2)}) %collective-permute-start) | collective-permute-done | bytes 393248 | tf_op jit(solution)/shard_map/ppermute | solution.py:62
  30.0 9.8 %all-reduce = s32[96]{0:T(128)S(1)} all-reduce(s32[96]{0:T(128)S(1)} %get-tuple-element.44), channel_id=2, replica_groups=mesh['dp_0'=4,'dp_1'=2,'dp_2'=2,'tensor_0'=2,'tensor_1'=4] {'dp_0'}, use_global_device_ids=true, to_apply=%add | all-reduce | flops 96 | bytes 768
  39.9 11.4 %all-gather.5 = s32[4,4,24]{2,1,0:T(4,128)S(1)} all-gather(s32[1,4,24]{2,1,0:T(4,128)S(1)} %reshape.312), channel_id=1, replica_groups=mesh['dp_0'=4,'dp_1'=2,'dp_2'=2,'tensor_0'=2,'tensor_1'=4] {'tensor_1'}, dimensions={0}, use_global_device_ids=true | all-gather | bytes 1920 | tf_op jit(solution)/shard_map/all_gather | solution.py:30
  51.2 6.2 %all_gather.83 = s32[32,24]{1,0:T(8,128)S(1)} all-gather(s32[16,24]{1,0:T(8,128)S(1)} %bitcast.153), channel_id=1, replica_groups=mesh['dp_0'=4,'dp_1'=2,'dp_2'=2,'tensor_0'=2,'tensor_1'=4] {'tensor_0'}, dimensions={0}, use_global_device_ids=true | all-gather | bytes 4608 | tf_op jit(solution)/shard_map/all_gather | solution.py:30
  57.5 1.8 all-gather.6
  59.4 4.7 all-gather.7
  64.2 6.0 %all-reduce.3 = s32[48]{0:T(128)S(1)} all-reduce(s32[48]{0:T(128)S(1)} %get-tuple-element.43), channel_id=5, replica_groups=mesh['dp_0'=4,'dp_1'=2,'dp_2'=2,'tensor_0'=2,'tensor_1'=4] {'tensor_0'}, use_global_device_ids=true, to_apply=%add.3 | all-reduce | flops 48 | bytes 384
  70.3 1.8 all-gather.14
  72.1 4.5 all-gather.15
  76.6 12.0 %all_gather.99 = s32[32,24]{1,0:T(8,128)S(1)} all-gather(s32[8,24]{1,0:T(8,128)S(1)} %bitcast.156), channel_id=1, replica_groups=mesh['dp_0'=4,'dp_1'=2,'dp_2'=2,'tensor_0'=2,'tensor_1'=4] {'dp_0'}, dimensions={0}, use_global_device_ids=true | all-gather | bytes 3840 | tf_op jit(solution)/shard_map/all_gather | solution.py:30
  88.7 11.9 %all-gather.16 = s32[4,32,24]{1,2,0:T(8,128)S(1)} all-gather(s32[1,32,24]{1,2,0:T(8,128)S(1)} %copy.129), channel_id=1, replica_groups=mesh['dp_0'=4,'dp_1'=2,'dp_2'=2,'tensor_0'=2,'tensor_1'=4] {'tensor_1'}, dimensions={0}, use_global_device_ids=true | all-gather | bytes 15360 | tf_op jit(solution)/shard_map/all_gather | solution.py:30
  100.8 4.3 all-reduce.1
  105.1 7.6 %all-gather.8 = s32[4,2,24]{2,1,0:T(2,128)S(1)} all-gather(s32[1,2,24]{2,1,0:T(2,128)S(1)} %reshape.318), channel_id=1, replica_groups=mesh['dp_0'=4,'dp_1'=2,'dp_2'=2,'tensor_0'=2,'tensor_1'=4] {'dp_0'}, dimensions={0}, use_global_device_ids=true | all-gather | bytes 960 | tf_op jit(solution)/shard_map/all_gather | solution.py:30
  112.7 12.0 %all_gather.88 = s32[32,24]{1,0:T(8,128)S(1)} all-gather(s32[8,24]{1,0:T(8,128)S(1)} %bitcast.155), channel_id=1, replica_groups=mesh['dp_0'=4,'dp_1'=2,'dp_2'=2,'tensor_0'=2,'tensor_1'=4] {'tensor_1'}, dimensions={0}, use_global_device_ids=true | all-gather | bytes 3840 | tf_op jit(solution)/shard_map/all_gather | solution.py:30
  124.8 5.9 %all-gather.9 = s32[2,32,24]{1,2,0:T(8,128)S(1)} all-gather(s32[1,32,24]{1,2,0:T(8,128)S(1)} %copy.122), channel_id=1, replica_groups=mesh['dp_0'=4,'dp_1'=2,'dp_2'=2,'tensor_0'=2,'tensor_1'=4] {'tensor_0'}, dimensions={0}, use_global_device_ids=true | all-gather | bytes 9216 | tf_op jit(solution)/shard_map/all_gather | solution.py:30
  130.8 1.8 all-gather.10
  132.7 1.8 all-reduce.2
  134.6 4.2 all-gather.11
  138.9 10.4 %all-gather.12 = s32[4,4,24]{2,1,0:T(4,128)S(1)} all-gather(s32[1,4,24]{2,1,0:T(4,128)S(1)} %bitcast.159), channel_id=1, replica_groups=mesh['dp_0'=4,'dp_1'=2,'dp_2'=2,'tensor_0'=2,'tensor_1'=4] {'dp_0'}, dimensions={0}, use_global_device_ids=true | all-gather | bytes 1920 | tf_op jit(solution)/shard_map/all_gather | solution.py:30
  149.3 11.9 %all_gather.94 = s32[64,24]{1,0:T(8,128)S(1)} all-gather(s32[16,24]{1,0:T(8,128)S(1)} %bitcast.154), channel_id=1, replica_groups=mesh['dp_0'=4,'dp_1'=2,'dp_2'=2,'tensor_0'=2,'tensor_1'=4] {'tensor_1'}, dimensions={0}, use_global_device_ids=true | all-gather | bytes 7680 | tf_op jit(solution)/shard_map/all_gather | solution.py:30
  161.3 5.9 %all-gather.13 = s32[2,64,24]{1,2,0:T(8,128)S(1)} all-gather(s32[1,64,24]{1,2,0:T(8,128)S(1)} %copy.126), channel_id=1, replica_groups=mesh['dp_0'=4,'dp_1'=2,'dp_2'=2,'tensor_0'=2,'tensor_1'=4] {'tensor_0'}, dimensions={0}, use_global_device_ids=true | all-gather | bytes 18432 | tf_op jit(solution)/shard_map/all_gather | solution.py:30
  168.7 7.3 %all-reduce.4 = s32[128]{0:T(128)S(1)} all-reduce(s32[128]{0:T(128)S(1)} %slice_dynamic-update-slice_fusion), channel_id=6, replica_groups=mesh['dp_0'=4,'dp_1'=2,'dp_2'=2,'tensor_0'=2,'tensor_1'=4] {'tensor_1'}, use_global_device_ids=true, to_apply=%add.4 | all-reduce | flops 128 | bytes 1024
  176.1 5.9 %all-gather.17 = s32[2,4,32]{2,1,0:T(4,128)S(1)} all-gather(s32[1,4,32]{2,1,0:T(4,128)S(1)} %reshape.336), channel_id=1, replica_groups=mesh['dp_0'=4,'dp_1'=2,'dp_2'=2,'tensor_0'=2,'tensor_1'=4] {'tensor_0'}, dimensions={0}, use_global_device_ids=true | all-gather | bytes 1536 | tf_op jit(solution)/shard_map/all_gather | solution.py:30
  182.0 1.8 all_gather.103
  183.8 4.4 all_gather.104
  188.1 11.9 %all_gather.105 = s32[128,32]{1,0:T(8,128)S(1)} all-gather(s32[32,32]{1,0:T(8,128)S(1)} %all_gather.104), channel_id=1, replica_groups=mesh['dp_0'=4,'dp_1'=2,'dp_2'=2,'tensor_0'=2,'tensor_1'=4] {'dp_0'}, dimensions={0}, use_global_device_ids=true | all-gather | bytes 20480 | tf_op jit(solution)/shard_map/all_gather | solution.py:30
  201.4 24.9 %copy.132 = bf16[128256,32]{1,0:T(8,128)(2,1)} copy(bf16[128256,32]{0,1:T(8,128)(2,1)} %bitcast.131) | data formatting | bytes 16416768 | tf_op jit(solution)/shard_map/transpose | solution.py:126
  226.3 37.7 %reshape.279 = bf16[32064,128]{1,0:T(8,128)(2,1)} reshape(bf16[128256,32]{1,0:T(8,128)(2,1)} %copy.132) | data formatting | bytes 16416768 | tf_op jit(solution)/shard_map/reshape | solution.py:126
  264.0 59.3 %gather_fusion = bf16[16384,128]{1,0:T(8,128)(2,1)} fusion(bf16[32064,128]{1,0:T(8,128)(2,1)} %reshape.279, s32[16384]{0:T(1024)S(1)} %broadcast_clamp_fusion), kind=kCustom, calls=%fused_computation | custom fusion | bytes 8454144 | tf_op jit(solution)/shard_map/jit(_take)/gather | solution.py:127
  323.4 6.5 %copy.133 = bf16[16384,128]{0,1:T(8,128)(2,1)} copy(bf16[16384,128]{1,0:T(8,128)(2,1)} %gather_fusion) | data formatting | bytes 8388608 | tf_op jit(solution)/shard_map/jit(_take)/gather | solution.py:127
  330.0 4.5 select_reduce_fusion
  334.6 2.5 broadcast_in_dim.98
  337.1 7.0 %all-to-all-start = ((bf16[128,512,32]{1,2,0:T(8,128)(2,1)}), bf16[128,512,32]{1,2,0:T(8,128)(2,1)}, u32[]{:S(2)}, u32[]{:S(2)}) async-start(bf16[128,512,32]{1,2,0:T(8,128)(2,1)} %bitcast.128), calls=%async_computation | async-start | bytes 8388608 | tf_op jit(solution)/shard_map/all_to_all | solution.py:153
  348.5 46.7 %all-to-all-done = bf16[128,512,32]{1,2,0:T(8,128)(2,1)} async-done(((bf16[128,512,32]{1,2,0:T(8,128)(2,1)}), bf16[128,512,32]{1,2,0:T(8,128)(2,1)}, u32[]{:S(2)}, u32[]{:S(2)}) %all-to-all-start) | async-done | bytes 4194336 | tf_op jit(solution)/shard_map/all_to_all | solution.py:153
  395.2 3.1 multiply_reduce_fusion
  398.3 11.9 %fusion.3 = f32[512,2,768]{2,0,1:T(8,128)S(1)} fusion(bf16[2,4096,768]{2,1,0:T(8,128)(2,1)} %all-gather.21.cloned.1.call-done, bf16[512,4096]{0,1:T(8,128)(2,1)} %bitcast.36, f32[4096]{0:T(1024)S(1)} %copy-done.6, f32[512]{0:T(512)S(1)} %add_rsqrt_fusion), kind=kOutput, calls=%fused_computation.10 | convolution fusion | flops 6450839552 | bytes 19941376 | tf_op jit(solution)/shard_map/rd,kdc->rkc/dot_general | solution.py:167
  413.5 1.9 copy.139
  416.8 1.6 multiply_subtract_fusion
  419.9 5.7 %fusion.25 = (f32[2,4,512]{2,1,0:T(4,128)S(1)}, f32[2,4,512,512]{2,3,1,0:T(8,128)}) fusion(f32[2,512,512,4]{2,1,3,0:T(8,128)S(1)} %fusion.12, pred[512,512]{0,1:T(8,128)(4,1)S(1)} %copy-done.3), kind=kOutput, calls=%fused_computation.82 | output fusion | flops 12583423 | bytes 17055744 | tf_op jit(solution)/shard_map/while/body/eval_jaxpr/sub | solution.py:91
  425.6 4.4 fusion.11
  430.1 8.4 %convolution_bitcast_fusion = bf16[512,4096]{1,0:T(8,128)(2,1)S(1)} fusion(bf16[512,2,512]{0,2,1:T(8,128)(2,1)S(1)} %bitcast.160, bf16[2,512,4096]{2,1,0:T(8,128)(2,1)} %all-gather.23.cloned.1.call-done), kind=kOutput, calls=%fused_computation.7 | convolution fusion | flops 4294967296 | bytes 13631488 | tf_op jit(solution)/shard_map/rkw,kwc->rc/dot_general | solution.py:192
  438.6 1.9 copy-done
  442.3 47.9 %collective-permute-done.2 = bf16[256,4096]{1,0:T(8,128)(2,1)} collective-permute-done((bf16[256,4096]{1,0:T(8,128)(2,1)S(1)}, bf16[256,4096]{1,0:T(8,128)(2,1)}, u32[]{:S(2)}, u32[]{:S(2)}) %collective-permute-start.2) | collective-permute-done | bytes 2097184 | tf_op jit(solution)/shard_map/ppermute | solution.py:62
  490.1 3.9 convert_add_fusion
  500.5 1.9 maximum_bitcast_fusion
  502.4 2.0 copy.147
  504.4 15.4 %collective-permute-done.3 = bf16[128,4096]{1,0:T(8,128)(2,1)} collective-permute-done((bf16[128,4096]{1,0:T(8,128)(2,1)}, bf16[128,4096]{1,0:T(8,128)(2,1)}, u32[]{:S(2)}, u32[]{:S(2)}) %collective-permute-start.3) | collective-permute-done | bytes 1048608 | tf_op jit(solution)/shard_map/ppermute | solution.py:62
  519.8 2.8 add_convert_fusion
  (105 shorter events, 31.7 us)
Async XLA Ops:
  7.2 17.4 %copy-start.12 = (u32[128]{0:T(128)S(1)}, u32[128]{0:T(128)}, u32[]{:S(2)}) copy-start(u32[128]{0:T(128)} %constant.129) | copy-start | bytes 1540
  7.2 18.0 %copy-start.11 = (u32[128]{0:T(128)S(1)}, u32[128]{0:T(128)}, u32[]{:S(2)}) copy-start(u32[128]{0:T(128)} %constant.144) | copy-start | bytes 1540
  7.2 19.7 %copy-start.10 = (u32[128]{0:T(128)S(1)}, u32[128]{0:T(128)}, u32[]{:S(2)}) copy-start(u32[128]{0:T(128)} %constant.134) | copy-start | bytes 1540
  7.2 21.1 %copy-start.9 = (u32[128]{0:T(128)S(1)}, u32[128]{0:T(128)}, u32[]{:S(2)}) copy-start(u32[128]{0:T(128)} %constant.139) | copy-start | bytes 1540
  7.2 160.1 %copy-start.8 = (u32[128]{0:T(128)S(1)}, u32[128]{0:T(128)}, u32[]{:S(2)}) copy-start(u32[128]{0:T(128)} %constant.149) | copy-start | bytes 1540
  7.2 15.8 %copy-start.4 = (bf16[512,256]{1,0:T(8,128)(2,1)S(1)}, bf16[512,256]{1,0:T(8,128)(2,1)}, u32[]{:S(2)}) copy-start(bf16[512,256]{1,0:T(8,128)(2,1)} %param.15) | copy-start | bytes 786436
  7.2 22.2 %copy-start.5 = (s32[128]{0:T(128)S(1)}, s32[128]{0:T(128)}, u32[]{:S(2)}) copy-start(s32[128]{0:T(128)} %param.8) | copy-start | bytes 1540
  7.2 391.1 %all-gather.21.cloned.1.call-start = ((), (), s32[]{:S(2)}) async-start(), calls=%async_computation.1 | async-start | bytes 13369344 | tf_op jit(solution)/shard_map/all_gather | solution.py:170
  8.4 12.4 %collective-permute-start = (bf16[1,256,768]{2,1,0:T(8,128)(2,1)S(1)}, bf16[1,256,768]{2,1,0:T(8,128)(2,1)S(1)}, u32[]{:S(2)}, u32[]{:S(2)}) collective-permute-start(bf16[1,256,768]{2,1,0:T(8,128)(2,1)S(1)} %maximum_bitcast_fusion.1), channel_id=1, source_target_pairs={{0,4},{4,0},{1,5},{5,1},{2,6},{6,2},{3,7},{7,3},{8,12},{12,8},{9,1... | collective-permute-start | bytes 1179656 | tf_op jit(solution)/shard_map/ppermute | solution.py:62
  23.0 407.1 %all-gather.23.cloned.1.call-start = ((), (), s32[]{:S(2)}) async-start(), calls=%async_computation.2 | async-start | bytes 8912896 | tf_op jit(solution)/shard_map/all_gather | solution.py:195
  23.1 177.1 %collective-permute-start.1 = (bf16[1,512,256]{2,1,0:T(8,128)(2,1)S(1)}, bf16[1,512,256]{2,1,0:T(8,128)(2,1)S(1)}, u32[]{:S(2)}, u32[]{:S(2)}) collective-permute-start(bf16[1,512,256]{2,1,0:T(8,128)(2,1)S(1)} %bitcast.148), channel_id=1, source_target_pairs={{0,4},{4,0},{1,5},{5,1},{2,6},{6,2},{3,7},{7,3},{8,12},{12,8},{9,1... | collective-permute-start | bytes 786440 | tf_op jit(solution)/shard_map/ppermute | solution.py:62
  337.1 9.3 %copy-start.7 = (s32[32]{0:T(128)S(1)}, s32[32]{0:T(128)}, u32[]{:S(2)}) copy-start(s32[32]{0:T(128)} %param.9) | copy-start | bytes 388
  337.1 58.1 %all-to-all-start = ((bf16[128,512,32]{1,2,0:T(8,128)(2,1)}), bf16[128,512,32]{1,2,0:T(8,128)(2,1)}, u32[]{:S(2)}, u32[]{:S(2)}) async-start(bf16[128,512,32]{1,2,0:T(8,128)(2,1)} %bitcast.128), calls=%async_computation | async-start | bytes 8388608 | tf_op jit(solution)/shard_map/all_to_all | solution.py:153
  344.1 54.2 %copy-start.6 = (f32[4096]{0:T(1024)S(1)}, f32[4096]{0:T(1024)}, u32[]{:S(2)}) copy-start(f32[4096]{0:T(1024)} %param.11) | copy-start | bytes 49156
  410.3 1.6 copy-start.2
  418.6 1.4 copy-start.3
  438.5 1.9 copy-start
  440.7 49.4 %collective-permute-start.2 = (bf16[256,4096]{1,0:T(8,128)(2,1)S(1)}, bf16[256,4096]{1,0:T(8,128)(2,1)}, u32[]{:S(2)}, u32[]{:S(2)}) collective-permute-start(bf16[256,4096]{1,0:T(8,128)(2,1)S(1)} %select_convert_fusion), channel_id=1, source_target_pairs={{0,2},{2,0},{1,3},{3,1},{4,6},{6,4},{5,7},{7,5},{8,10},{10,8},{9,1... | collective-permute-start | bytes 6291464 | tf_op jit(solution)/shard_map/ppermute | solution.py:62
  495.1 24.7 %collective-permute-start.3 = (bf16[128,4096]{1,0:T(8,128)(2,1)}, bf16[128,4096]{1,0:T(8,128)(2,1)}, u32[]{:S(2)}, u32[]{:S(2)}) collective-permute-start(bf16[128,4096]{1,0:T(8,128)(2,1)} %select_convert_fusion.2), channel_id=1, source_target_pairs={{0,1},{1,0},{2,3},{3,2},{4,5},{5,4},{6,7},{7,6},{8,9},{9,8},{10,11... | collective-permute-start | bytes 3145736 | tf_op jit(solution)/shard_map/ppermute | solution.py:62
  497.7 22.1 %copy-start.1 = (bf16[128,4096]{1,0:T(8,128)(2,1)S(1)}, bf16[128,4096]{1,0:T(8,128)(2,1)}, u32[]{:S(2)}) copy-start(bf16[128,4096]{1,0:T(8,128)(2,1)} %copy.156) | copy-start | bytes 3145732
Sparse Core Ops, SparseCore 0:
  23.1 74.2 all-gather.20
  201.2 58.3 all-gather.22
where the time goes:
time: 532 us; the launch traced here: 529 us
  blocking collectives  167 us (31%)
  local copies, waits for them, and re-layouts  154 us (29%)
  waiting for transfers between devices  121 us (23%)
  other arithmetic  32.1 us (6%)
  matrix products  26.1 us (5%)
  between operations  17.6 us (3%)
  starting transfers between devices  11.6 us (2%)
    all_gather x20, blocking collectives, stacked_from(): pieces = lax.all_gather(pieces, axes[k], axis=0, tiled=True)  138 us
    ppermute x4, waiting for transfers between devices, swapped(): return lax.ppermute(block, axis, route)  74.2 us
    gather x2, local copies, waits for them, and re-layouts, lookup_rows(): jnp.take(token_major, token_ids // packing, axis=0)  65.8 us
    all_to_all x1, waiting for transfers between devices, shards(): lax.all_to_all(outgoing.reshape(devices, row_count, columns), DP_TENSOR,...  46.7 us
    reshape x1, local copies, waits for them, and re-layouts, lookup_rows(): embed_table.T.reshape(vocab_size // packing, packing * columns)  37.7 us
    unnamed x5, blocking collectives  29.3 us
    transpose x1, local copies, waits for them, and re-layouts, lookup_rows(): embed_table.T.reshape(vocab_size // packing, packing * columns)  24.9 us
    dot_general x1, matrix products, shards(): jnp.einsum('rd,kdc->rkc', normed, lax.all_gather(stacked, DP, axis=1, til...  11.9 us
  transfers between devices with their start and end apart: 7, of which 4 were waited for; matrix products, arithmetic and copies ran while one was open for 36% of the time, Pallas kernels for 0%

commit v1 on v0

v1 whole, which is shorter than its diff:
```python
import functools

import jax
import jax.numpy as jnp
from jax import lax
from jax.experimental import pallas as pl
from jax.experimental.pallas import tpu as pltpu
from jax.sharding import Mesh
from jax.sharding import PartitionSpec as P

HEADS = 32
KVH = 8
HD = 128
TPG = 4
TENSOR = ("tensor_0", "tensor_1")
DP_TENSOR = ("dp_0", "dp_1", "dp_2", "tensor_0", "tensor_1")
DP = ("dp_0", "dp_1", "dp_2")
RING = "tensor_1"
LANES = 128

norm_eps = 1e-05
rope_theta = 500000.0


def swapped(block, axis, apart):
    count = lax.axis_size(axis)
    route = []
    for low in range(count):
        high = low | 1 << apart
        if high != low and high < count:
            route += [(low, high), (high, low)]
    return lax.ppermute(block, axis, route)


def ordered_pair(mine, theirs, bit_index):
    upper_half = lax.axis_index(TENSOR) >> bit_index & 1 == 1
    first_half = jnp.where(upper_half, theirs, mine)
    second_half = jnp.where(upper_half, mine, theirs)
    return jnp.concatenate([first_half, second_half], axis=0)


def collect_blocks(shard):
    stacked = shard[None]
    return ordered_pair(stacked, swapped(stacked, TENSOR, 2), 2)


def lane_gather(block, lanes):
    dims = lax.GatherDimensionNumbers(
        offset_dims=(),
        collapsed_slice_dims=(1,),
        start_index_map=(1,),
        operand_batching_dims=(0,),
        start_indices_batching_dims=(0,),
    )
    return lax.gather(
        block,
        lanes[..., None],
        dims,
        slice_sizes=(1, 1),
        mode=lax.GatherScatterMode.PROMISE_IN_BOUNDS,
    )


def lookup_kernel(slots_ref, lanes_ref, table_ref, out_ref, tiles):
    columns = table_ref.shape[0]
    tile_count = tiles.shape[0] // 2
    lane = lax.broadcasted_iota(jnp.int32, (columns, LANES), 1).astype(jnp.int16)
    left = lane < jnp.int16(LANES // 2)
    unroll = next(u for u in (6, 4, 3, 2, 1) if tile_count % u == 0)

    def prepare(step, carry):
        for u in range(unroll):
            t = step * unroll + u
            tile = table_ref[:, pl.ds(pl.multiple_of(t * LANES, LANES), LANES)]
            tiles[t] = tile
            tiles[t + tile_count] = lane_gather(tile, lane ^ jnp.int16(LANES // 2))
        return carry

    lax.fori_loop(0, tile_count // unroll, prepare, 0)
    groups, copies, _, row_count = out_ref.shape
    per_group = row_count // LANES

    def one_block(block, carry):
        first = block * LANES
        wanted = jnp.broadcast_to(lanes_ref[pl.ds(block, 1), :], (columns, LANES)).astype(jnp.int16)
        picked = jnp.zeros((columns, LANES), jnp.bfloat16)
        for i in range(0, LANES, 2):
            pair = jnp.where(left, tiles[slots_ref[first + i]], tiles[slots_ref[first + i + 1]])
            picked = jnp.where(lane >= jnp.int16(i), lane_gather(pair, wanted), picked)
        group = lax.div(block, per_group)
        place = pl.multiple_of(lax.rem(block, per_group) * LANES, LANES)
        for copy in range(copies):
            out_ref[group, copy, :, pl.ds(place, LANES)] = picked
        return carry

    lax.fori_loop(0, groups * per_group, one_block, 0)


def lookup(embed_table, token_ids, group_count):
    columns, vocab_size = embed_table.shape
    tile_count = vocab_size // LANES
    count = token_ids.shape[0]
    odd = jnp.arange(count, dtype=jnp.int32) & 1
    lane = token_ids & (LANES - 1)
    half = LANES // 2
    slots = lax.shift_right_logical(token_ids, 7) + tile_count * (lax.shift_right_logical(lane, 6) ^ odd)
    lanes = ((lane & (half - 1)) | (odd * half)).reshape(count // LANES, LANES)
    return pl.pallas_call(
        lookup_kernel,
        out_shape=jax.ShapeDtypeStruct(
            (group_count, TPG, columns, count // group_count), jnp.bfloat16
        ),
        in_specs=[
            pl.BlockSpec(memory_space=pltpu.SMEM),
            pl.BlockSpec(memory_space=pltpu.VMEM),
            pl.BlockSpec(memory_space=pltpu.VMEM),
        ],
        out_specs=pl.BlockSpec(memory_space=pltpu.VMEM),
        scratch_shapes=[pltpu.VMEM((2 * tile_count, columns, LANES), jnp.bfloat16)],
        compiler_params=pltpu.CompilerParams(vmem_limit_bytes=40 * 2**20),
        cost_estimate=pl.CostEstimate(
            flops=30_000_000_000, bytes_accessed=embed_table.size * 2, transcendentals=0
        ),
    )(slots, lanes, embed_table)


def attention_kernel(length_ref, proj_ref, cos_ref, sin_ref, attended_ref, cache_ref):
    row_count = proj_ref.shape[0]
    q_heads = HEADS // KVH
    cosine = cos_ref[...]
    sine = sin_ref[...]

    def rotate(part):
        return (part * cosine + pltpu.roll(part, HD // 2, 1) * sine).astype(jnp.bfloat16)

    key_rot = rotate(proj_ref[:, q_heads * HD : (q_heads + 1) * HD])
    value = proj_ref[:, (q_heads + 1) * HD : (q_heads + 2) * HD].astype(jnp.bfloat16)
    cache_ref[0] = key_rot
    cache_ref[1] = value
    length = length_ref[0]
    block = min(256, row_count)
    root = jnp.float32(HD) ** 0.5
    for h in range(q_heads):
        query = rotate(proj_ref[:, h * HD : (h + 1) * HD])
        for start in range(0, row_count, block):
            keys = start + block
            scores = (
                lax.dot_general(
                    query[start : start + block],
                    key_rot[:keys],
                    (((1,), (1,)), ((), ())),
                    preferred_element_type=jnp.float32,
                )
                / root
            )
            q_pos = start + lax.broadcasted_iota(jnp.int32, (block, keys), 0)
            k_pos = lax.broadcasted_iota(jnp.int32, (block, keys), 1)
            scores = jnp.where((k_pos <= q_pos) & (k_pos < length), scores, -1e30)
            expd = jnp.exp(scores - jnp.max(scores, axis=-1, keepdims=True))
            weights = (expd / jnp.sum(expd, axis=-1, keepdims=True)).astype(jnp.bfloat16)
            attended_ref[start : start + block, h * HD : (h + 1) * HD] = jnp.dot(
                weights, value[:keys], preferred_element_type=jnp.float32
            ).astype(jnp.bfloat16)


def rotated_attention(projected, length, cosine, sine):
    row_count, blocks, width = projected.shape
    query_width = HEADS // KVH * HD
    flat = projected.reshape(row_count, blocks * width)
    attended, cache = pl.pallas_call(
        attention_kernel,
        grid=(blocks,),
        out_shape=(
            jax.ShapeDtypeStruct((row_count, blocks * query_width), jnp.bfloat16),
            jax.ShapeDtypeStruct((2, row_count, blocks * HD), jnp.bfloat16),
        ),
        in_specs=[
            pl.BlockSpec(memory_space=pltpu.SMEM),
            pl.BlockSpec((row_count, width), lambda k: (0, k)),
            pl.BlockSpec((row_count, HD), lambda k: (0, 0)),
            pl.BlockSpec((row_count, HD), lambda k: (0, 0)),
        ],
        out_specs=(
            pl.BlockSpec((row_count, query_width), lambda k: (0, k)),
            pl.BlockSpec((2, row_count, HD), lambda k: (0, 0, k)),
        ),
        compiler_params=pltpu.CompilerParams(vmem_limit_bytes=40 * 2**20),
        cost_estimate=pl.CostEstimate(
            flops=2_000_000_000, bytes_accessed=6_000_000, transcendentals=2_000_000
        ),
    )(length, flat, cosine, sine)
    return attended, cache


def rope_tables(row_count):
    half = HD // 2
    freq = rope_theta ** (-2.0 * jnp.arange(half, dtype=jnp.float32) / HD)
    angle = jnp.arange(row_count, dtype=jnp.int32).astype(jnp.float32)[:, None] * freq[None, :]
    cosine, sine = jnp.cos(angle), jnp.sin(angle)
    return jnp.concatenate([cosine, cosine], axis=1), jnp.concatenate([-sine, sine], axis=1)


def ring_reduced(attended, weight, quarter):
    place = lax.axis_index(RING)
    count = lax.axis_size(RING)
    half = weight.shape[1] // 2

    def part(turn, columns):
        rows = lax.dynamic_slice_in_dim(attended, (place + turn) % count * quarter, quarter, 0)
        return jnp.dot(rows, columns, preferred_element_type=jnp.float32)

    sums = []
    for way, columns in ((1, weight[:, :half]), (-1, weight[:, half:])):
        route = [(k, (k + way) % count) for k in range(count)]
        running = part(-way, columns)
        for step in range(1, count):
            running = lax.ppermute(running.astype(jnp.bfloat16), RING, route)
            running = running.astype(jnp.float32) + part(-way * (step + 1), columns)
        sums.append(running)
    return jnp.concatenate(sums, axis=1)


def shards(prompt_ids, prompt_lengths, embed_table, norm_gain, w_query, w_key, w_value, w_out):
    quarter = prompt_ids.shape[0]
    row_count = quarter * TPG
    devices = lax.axis_size(DP_TENSOR)
    columns = embed_table.shape[0]
    model_width = columns * devices
    group_count = devices // TPG
    member = lax.axis_index(TENSOR) % TPG
    group_index = (
        lax.axis_index(DP) * (lax.axis_size(TENSOR) // TPG) + lax.axis_index(TENSOR) // TPG
    )
    length = lax.dynamic_slice_in_dim(prompt_lengths, group_index, 1, 0)
    cosine, sine = rope_tables(row_count)

    packed = jnp.concatenate([w_query, w_key, w_value], axis=1)
    w_in = lax.all_gather(collect_blocks(packed), DP, axis=1, tiled=True)
    w_back = lax.all_gather(collect_blocks(w_out), DP, axis=2, tiled=True)

    all_ids = lax.all_to_all(
        jnp.broadcast_to(prompt_ids[None], (devices, quarter)),
        DP_TENSOR,
        split_axis=0,
        concat_axis=0,
        tiled=True,
    ).reshape(-1)
    outgoing = lookup(embed_table, all_ids, group_count)
    arrived = lax.all_to_all(
        outgoing.reshape(devices, columns, row_count),
        DP_TENSOR,
        split_axis=0,
        concat_axis=0,
        tiled=True,
    )
    tokens_t = arrived.reshape(model_width, row_count)
    wide = tokens_t.astype(jnp.float32)
    scale = lax.rsqrt(jnp.mean(wide * wide, axis=0, keepdims=True) + norm_eps)
    normed_t = (wide * scale * norm_gain[:, None]).astype(jnp.bfloat16)
    own_rows = lax.dynamic_slice_in_dim(tokens_t, member * quarter, quarter, 1).T

    projected = jnp.einsum("dr,kdc->rkc", normed_t, w_in, preferred_element_type=jnp.float32)
    attended, cache = rotated_attention(projected, length, cosine, sine)
    summed = ring_reduced(attended, w_back.reshape(-1, model_width), quarter)
    hidden = (own_rows.astype(jnp.float32) + summed).astype(jnp.bfloat16)
    return hidden, cache[None]


def solution(mesh):
    split = Mesh(
        mesh.devices.reshape(4, 2, 2, 2, 4), ("dp_0", "dp_1", "dp_2", "tensor_0", "tensor_1")
    )
    placed = (
        P(DP_TENSOR),
        P(),
        P(DP_TENSOR, None),
        P(),
        P(DP, TENSOR),
        P(DP, TENSOR),
        P(DP, TENSOR),
        P(TENSOR, DP),
    )
    return jax.shard_map(
        shards,
        mesh=split,
        in_specs=placed,
        out_specs=(P(DP_TENSOR, None), P(DP_TENSOR, None, None, None)),
        check_vma=False,
    )
```

time: 532 us -> 277 us (0.52)
  blocking collectives: 167 us -> 18.7 us
  local copies, waits for them, and re-layouts: 154 us -> 10.9 us
  Pallas kernels: 0 us -> 53.5 us
  other arithmetic: 32.1 us -> 12 us
  waiting for transfers between devices: 121 us -> 108 us
  matrix products: 26.1 us -> 36.1 us
  starting transfers between devices: 11.6 us -> 21.5 us
    all_gather x20 -> x0, blocking collectives: 138 us -> none  [stacked_from(): pieces = lax.all_gather(pieces, axes[k], axis=0, tiled=True)]
    gather x2 -> x0, local copies, waits for them, and re-layouts: 65.8 us -> none  [lookup_rows(): jnp.take(token_major, token_ids // packing, axis=0)]
    ppermute x4 -> x2, waiting for transfers between devices: 74.2 us -> 18.2 us  [swapped(): return lax.ppermute(block, axis, route)]
    pallas_call x0 -> x2, Pallas kernels: none -> 53.5 us  [the longest x1 44.5 us: lookup(): pl.pallas_call(lookup_kernel, out_shape=jax.ShapeDtypeStruct((group_count...]
    reshape x1 -> x0, local copies, waits for them, and re-layouts: 37.7 us -> none  [lookup_rows(): embed_table.T.reshape(vocab_size // packing, packing * columns)]
    unnamed x5 -> x0, blocking collectives: 29.3 us -> none
    transpose x5 -> x0, local copies, waits for them, and re-layouts: 25 us -> none  [the longest x1 24.9 us: lookup_rows(): embed_table.T.reshape(vocab_size // packing, packing * columns)]
    ppermute x0 -> x6, waiting for transfers between devices: none -> 22.9 us  [ring_reduced(): running = lax.ppermute(running.astype(jnp.bfloat16), RING, route)]
  transfers between devices with their start and end apart: 7 -> 11, of which waited for: 4 -> 7; matrix products, arithmetic and copies ran while one was open for 36% -> 15% of each run, Pallas kernels for 0% -> 19%
where the time goes in v1:
time: 277 us; the launch traced here: 275 us
  waiting for transfers between devices  108 us (39%)
  Pallas kernels  53.5 us (19%)
  matrix products  36.1 us (13%)
  starting transfers between devices  21.5 us (8%)
  blocking collectives  18.7 us (7%)
  between operations  14.3 us (5%)
  other arithmetic  12 us (4%)
  local copies, waits for them, and re-layouts  10.9 us (4%)
    all_to_all x1, waiting for transfers between devices, shards(): lax.all_to_all(outgoing.reshape(devices, columns, row_count), DP_TENSOR,...  49.9 us
    pallas_call x1, Pallas kernels, lookup(): pl.pallas_call(lookup_kernel, out_shape=jax.ShapeDtypeStruct((group_count...  44.5 us
    dot_general x8, matrix products, part(): return jnp.dot(rows, columns, preferred_element_type=jnp.float32)  25.2 us
    ppermute x6, waiting for transfers between devices, ring_reduced(): running = lax.ppermute(running.astype(jnp.bfloat16), RING, route)  22.9 us
    all_to_all x1, blocking collectives, shards(): lax.all_to_all(jnp.broadcast_to(prompt_ids[None], (devices, quarter)), DP...  18.7 us
    ppermute x2, waiting for transfers between devices, swapped(): return lax.ppermute(block, axis, route)  18.2 us
    all_gather x1, waiting for transfers between devices, shards(): w_back = lax.all_gather(collect_blocks(w_out), DP, axis=2, tiled=True)  16.6 us
    ppermute x6, starting transfers between devices, ring_reduced(): running = lax.ppermute(running.astype(jnp.bfloat16), RING, route)  11.8 us
  transfers between devices with their start and end apart: 11, of which 7 were waited for; matrix products, arithmetic and copies ran while one was open for 15% of the time, Pallas kernels for 19%

profile of v1, /device:TPU:6, one launch (start us, length us, event | category | flops | bytes accessed | tf_op | source)
XLA Modules:
  0.0 274.7 jit_solution(13404381630073624286)
XLA Ops:
  7.2 0.0 all-gather.3.cloned.1.call-start
  7.2 1.1 copy.17
  8.3 0.9 copy.18
  9.3 0.9 copy.19
  10.3 1.5 collective-permute-start
  11.8 11.0 %collective-permute-done = bf16[1,256,768]{1,2,0:T(8,128)(2,1)S(1)} collective-permute-done((bf16[1,256,768]{1,2,0:T(8,128)(2,1)S(1)}, bf16[1,256,768]{1,2,0:T(8,128)(2,1)S(1)}, u32[]{:S(2)}, u32[]{:S(2)}) %collective-permute-start) | collective-permute-done | bytes 393248 | tf_op jit(solution)/shard_map/ppermute | solution.py:32
  22.7 0.2 broadcast_select_fusion.1
  22.9 0.9 pad_maximum_fusion
  23.8 0.0 all-gather.3.cloned.1.call-update
  23.9 0.0 all-gather.5.cloned.1.call-start
  23.9 1.5 collective-permute-start.1
  25.4 7.3 %collective-permute-done.1 = bf16[1,512,256]{2,1,0:T(8,128)(2,1)S(1)} collective-permute-done((bf16[1,512,256]{2,1,0:T(8,128)(2,1)S(1)}, bf16[1,512,256]{2,1,0:T(8,128)(2,1)S(1)}, u32[]{:S(2)}, u32[]{:S(2)}) %collective-permute-start.1) | collective-permute-done | bytes 262176 | tf_op jit(solution)/shard_map/ppermute | solution.py:32
  32.7 0.9 pad_maximum_fusion.1
  33.7 18.7 %all_to_all.11 = s32[128,1,128]{2,1,0:T(1,128)S(1)} all-to-all(s32[128,1,128]{2,1,0:T(1,128)S(1)} %broadcast_in_dim.8), channel_id=1, replica_groups=mesh['dp_0'=4,'dp_1'=2,'dp_2'=2,'tensor_0'=2,'tensor_1'=4] {'dp_0','dp_1..., dimensions={0} | all-to-all | bytes 131072 | tf_op jit(solution)/shard_map/all_to_all | solution.py:241
  52.5 0.1 broadcast_shift-right-logical_fusion
  52.6 3.3 %copy-done.1 = bf16[32,128256]{1,0:T(8,128)(2,1)S(1)} copy-done((bf16[32,128256]{1,0:T(8,128)(2,1)S(1)}, bf16[32,128256]{1,0:T(8,128)(2,1)}, u32[]{:S(2)}) %copy-start.1) | copy-done | bytes 8208408
  55.9 44.5 %shard_map.95 = bf16[32,4,32,512]{3,2,1,0:T(8,128)(2,1)S(1)} custom-call(s32[16384]{0:T(1024)S(1)} %fusion.60.slots_ref, s32[128,128]{1,0:T(8,128)S(1)} %bitcast_or_fusion.lanes_ref, bf16[32,128256]{1,0:T(8,128)(2,1)S(1)} %copy-done.1), custom_call_target="tpu_custom_call" | custom-call | flops 30000001024 | bytes 8208384 | tf_op jit(solution)/shard_map/pallas_call | solution.py:108
  100.4 2.0 copy-done
  102.4 6.7 %all-to-all-start.1 = ((bf16[128,32,512]{2,1,0:T(8,128)(2,1)}), bf16[128,32,512]{2,1,0:T(8,128)(2,1)}, u32[]{:S(2)}, u32[]{:S(2)}) async-start(bf16[128,32,512]{2,1,0:T(8,128)(2,1)} %bitcast.31), calls=%async_computation.1 | async-start | bytes 8388608 | tf_op jit(solution)/shard_map/all_to_all | solution.py:249
  109.1 0.1 mul.125
  109.2 0.7 dynamic_slice.31.length_ref
  109.8 1.0 fusion.58
  110.9 0.2 pad_maximum_fusion.2
  111.1 49.9 %all-to-all-done.1 = bf16[128,32,512]{2,1,0:T(8,128)(2,1)} async-done(((bf16[128,32,512]{2,1,0:T(8,128)(2,1)}), bf16[128,32,512]{2,1,0:T(8,128)(2,1)}, u32[]{:S(2)}, u32[]{:S(2)}) %all-to-all-start.1) | async-done | bytes 4194336 | tf_op jit(solution)/shard_map/all_to_all | solution.py:249
  161.0 3.3 %fusion = f32[512]{0:T(512)S(1)} fusion(bf16[128,32,512]{2,1,0:T(8,128)(2,1)} %all-to-all-done.1), kind=kLoop, calls=%fused_computation.2 | loop fusion | flops 6290944 | bytes 4196352 | tf_op jit(solution)/shard_map/reduce_sum | solution.py:258
  164.2 4.1 %fusion.2 = bf16[128,32,512]{2,1,0:T(8,128)(2,1)} fusion(bf16[128,32,512]{2,1,0:T(8,128)(2,1)} %all-to-all-done.1, f32[128,32]{1,0:T(8,128)S(1)} %mul.125, f32[512]{0:T(512)S(1)} %add_rsqrt_fusion), kind=kLoop, calls=%fused_computation.4 | loop fusion | flops 8388608 | bytes 8407040 | tf_op jit(solution)/shard_map/convert_element_type | solution.py:259
  168.4 10.9 %fusion.69.proj_ref = f32[512,1536]{1,0:T(8,128)S(1)} fusion(bf16[4096,512]{1,0:T(8,128)(2,1)} %bitcast.32, bf16[1536,4096]{1,0:T(8,128)(2,1)} %bitcast.37), kind=kOutput, calls=%fused_computation.68 | convolution fusion | flops 6442450944 | bytes 19922944 | tf_op jit(solution)/shard_map/dr,kdc->rkc/dot_general | solution.py:262
  179.3 9.0 %shard_map.96 = (bf16[512,1024]{1,0:T(8,128)(2,1)S(1)}, bf16[2,512,256]{2,1,0:T(8,128)(2,1)}) custom-call(s32[1]{0:T(128)} %dynamic_slice.31.length_ref, f32[512,1536]{1,0:T(8,128)S(1)} %fusion.69.proj_ref, f32[512,128]{1,0:T(8,128)S(1)} %get-tuple-element.13.cos_ref, f32[512,128]{1,0:T(8,128)S(1)} %get-tuple-element.14.sin_ref), custom_call_target="tpu_custom_call" | custom-call | flops 2000000000 | bytes 6000000 | tf_op jit(solution)/shard_map/pallas_call | solution.py:170
  188.3 16.6 %all-gather.5.cloned.1.call-done = bf16[2,512,4096]{2,1,0:T(8,128)(2,1)} async-done(((bf16[2,512,256]{2,1,0:T(8,128)(2,1)}), bf16[2,512,4096]{2,1,0:T(8,128)(2,1)}) %all-gather.5.cloned.1.call-update) | async-done | bytes 8388624 | tf_op jit(solution)/shard_map/all_gather | solution.py:239
  204.9 2.9 %fusion.19 = bf16[128,2048]{1,0:T(8,128)(2,1)S(1)} fusion(bf16[1024,4096]{1,0:T(8,128)(2,1)} %bitcast.38, bf16[512,1024]{1,0:T(8,128)(2,1)S(1)} %get-tuple-element.4, s32[]{:T(128)S(6)} %select_n.105), kind=kOutput, calls=%fused_computation.21 | convolution fusion | flops 537133056 | bytes 4980740 | tf_op jit(solution)/shard_map/dot_general | solution.py:210
  207.8 3.6 %collective-permute-start.2 = (bf16[128,2048]{1,0:T(8,128)(2,1)S(1)}, bf16[128,2048]{1,0:T(8,128)(2,1)S(1)}, u32[]{:S(2)}, u32[]{:S(2)}) collective-permute-start(bf16[128,2048]{1,0:T(8,128)(2,1)S(1)} %fusion.19), channel_id=1, source_target_pairs={{0,1},{1,2},{2,3},{3,0},{4,5},{5,6},{6,7},{7,4},{8,9},{9,10},{10,1... | collective-permute-start | bytes 1572872 | tf_op jit(solution)/shard_map/ppermute | solution.py:217
  211.4 2.9 %fusion.22 = bf16[128,2048]{1,0:T(8,128)(2,1)S(1)} fusion(bf16[1024,4096]{1,0:T(8,128)(2,1)} %bitcast.39, bf16[512,1024]{1,0:T(8,128)(2,1)S(1)} %get-tuple-element.4, s32[]{:T(128)S(6)} %select_n.116), kind=kOutput, calls=%fused_computation.22 | convolution fusion | flops 537133056 | bytes 4980740 | tf_op jit(solution)/shard_map/dot_general | solution.py:210
  214.3 1.4 collective-permute-start.5
  215.7 9.3 %collective-permute-done.2 = bf16[128,2048]{1,0:T(8,128)(2,1)S(1)} collective-permute-done((bf16[128,2048]{1,0:T(8,128)(2,1)S(1)}, bf16[128,2048]{1,0:T(8,128)(2,1)S(1)}, u32[]{:S(2)}, u32[]{:S(2)}) %collective-permute-start.2) | collective-permute-done | bytes 524320 | tf_op jit(solution)/shard_map/ppermute | solution.py:217
  225.0 2.9 %add_convert_fusion.3 = bf16[128,2048]{1,0:T(8,128)(2,1)S(1)} fusion(bf16[128,2048]{1,0:T(8,128)(2,1)S(1)} %collective-permute-done.2, bf16[1024,4096]{1,0:T(8,128)(2,1)} %bitcast.40, bf16[512,1024]{1,0:T(8,128)(2,1)S(1)} %get-tuple-element.4, s32[]{:T(128)S(6)} %select_n.110), kind=kOutput, calls=%fused_computation.30 | convolution fusion | flops 537657344 | bytes 5505028 | tf_op jit(solution)/shard_map/dot_general | solution.py:210
  227.9 0.6 collective-permute-start.3
  228.5 3.0 %add_convert_fusion.1 = bf16[128,2048]{1,0:T(8,128)(2,1)S(1)} fusion(bf16[128,2048]{1,0:T(8,128)(2,1)} %collective-permute-done.5, bf16[1024,4096]{1,0:T(8,128)(2,1)} %bitcast.41, bf16[512,1024]{1,0:T(8,128)(2,1)S(1)} %get-tuple-element.4, s32[]{:T(128)S(6)} %select_n.118), kind=kOutput, calls=%fused_computation.27 | convolution fusion | flops 537657344 | bytes 5505028 | tf_op jit(solution)/shard_map/dot_general | solution.py:210
  231.5 3.0 %collective-permute-start.6 = (bf16[128,2048]{1,0:T(8,128)(2,1)S(1)}, bf16[128,2048]{1,0:T(8,128)(2,1)S(1)}, u32[]{:S(2)}, u32[]{:S(2)}) collective-permute-start(bf16[128,2048]{1,0:T(8,128)(2,1)S(1)} %add_convert_fusion.1), channel_id=1, source_target_pairs={{0,3},{1,0},{2,1},{3,2},{4,7},{5,4},{6,5},{7,6},{8,11},{9,8},{10,9... | collective-permute-start | bytes 1572872 | tf_op jit(solution)/shard_map/ppermute | solution.py:217
  234.5 8.2 %collective-permute-done.3 = bf16[128,2048]{1,0:T(8,128)(2,1)S(1)} collective-permute-done((bf16[128,2048]{1,0:T(8,128)(2,1)S(1)}, bf16[128,2048]{1,0:T(8,128)(2,1)S(1)}, u32[]{:S(2)}, u32[]{:S(2)}) %collective-permute-start.3) | collective-permute-done | bytes 524320 | tf_op jit(solution)/shard_map/ppermute | solution.py:217
  242.7 3.7 %add_convert_fusion.2 = bf16[128,2048]{1,0:T(8,128)(2,1)} fusion(bf16[128,2048]{1,0:T(8,128)(2,1)S(1)} %collective-permute-done.3, bf16[1024,4096]{1,0:T(8,128)(2,1)} %bitcast.42, bf16[512,1024]{1,0:T(8,128)(2,1)S(1)} %get-tuple-element.4, s32[]{:T(128)S(6)} %select_n.112), kind=kOutput, calls=%fused_computation.29 | convolution fusion | flops 537657344 | bytes 5505028 | tf_op jit(solution)/shard_map/dot_general | solution.py:210
  246.4 3.7 %add_convert_fusion = bf16[128,2048]{1,0:T(8,128)(2,1)} fusion(bf16[128,2048]{1,0:T(8,128)(2,1)S(1)} %collective-permute-done.6, bf16[1024,4096]{1,0:T(8,128)(2,1)} %bitcast.43, bf16[512,1024]{1,0:T(8,128)(2,1)S(1)} %get-tuple-element.4, s32[]{:T(128)S(6)} %select_n.120), kind=kOutput, calls=%fused_computation.26 | convolution fusion | flops 537657344 | bytes 5505028 | tf_op jit(solution)/shard_map/dot_general | solution.py:210
  250.1 3.2 %collective-permute-start.7 = (bf16[128,2048]{1,0:T(8,128)(2,1)}, bf16[128,2048]{1,0:T(8,128)(2,1)}, u32[]{:S(2)}, u32[]{:S(2)}) collective-permute-start(bf16[128,2048]{1,0:T(8,128)(2,1)} %add_convert_fusion), channel_id=1, source_target_pairs={{0,3},{1,0},{2,1},{3,2},{4,7},{5,4},{6,5},{7,6},{8,11},{9,8},{10,9... | collective-permute-start | bytes 1572872 | tf_op jit(solution)/shard_map/ppermute | solution.py:217
  253.4 1.3 constant_dynamic-slice_fusion
  254.7 0.5 copy.20
  255.2 5.4 %collective-permute-done.4 = bf16[128,2048]{1,0:T(8,128)(2,1)} collective-permute-done((bf16[128,2048]{1,0:T(8,128)(2,1)}, bf16[128,2048]{1,0:T(8,128)(2,1)}, u32[]{:S(2)}, u32[]{:S(2)}) %collective-permute-start.4) | collective-permute-done | bytes 524320 | tf_op jit(solution)/shard_map/ppermute | solution.py:217
  260.6 3.0 %convert_add_fusion.1 = f32[128,2048]{1,0:T(8,128)S(1)} fusion(bf16[128,2048]{1,0:T(8,128)(2,1)} %collective-permute-done.4, bf16[1024,4096]{1,0:T(8,128)(2,1)} %bitcast.44, bf16[512,1024]{1,0:T(8,128)(2,1)S(1)} %get-tuple-element.4, s32[]{:T(128)S(6)} %select_n.114), kind=kOutput, calls=%fused_computation.28 | convolution fusion | flops 537395200 | bytes 6029316 | tf_op jit(solution)/shard_map/dot_general | solution.py:210
  263.6 3.0 %convert_add_fusion = f32[128,2048]{1,0:T(8,128)S(1)} fusion(bf16[128,2048]{1,0:T(8,128)(2,1)} %collective-permute-done.7, bf16[1024,4096]{1,0:T(8,128)(2,1)} %bitcast.45, bf16[512,1024]{1,0:T(8,128)(2,1)S(1)} %get-tuple-element.4, s32[]{:T(128)S(6)} %select_n.122), kind=kOutput, calls=%fused_computation.25 | convolution fusion | flops 537395200 | bytes 6029316 | tf_op jit(solution)/shard_map/dot_general | solution.py:210
  266.7 1.2 fusion.25
  (24 shorter events, 0.2 us)
Async XLA Ops:
  7.2 16.7 %copy-start.2 = (bf16[512,256]{1,0:T(8,128)(2,1)S(1)}, bf16[512,256]{1,0:T(8,128)(2,1)}, u32[]{:S(2)}) copy-start(bf16[512,256]{1,0:T(8,128)(2,1)} %param.15) | copy-start | bytes 786436
  7.2 26.5 %copy-start.4 = (s32[128]{0:T(128)S(1)}, s32[128]{0:T(128)}, u32[]{:S(2)}) copy-start(s32[128]{0:T(128)} %param.8) | copy-start | bytes 1540
  7.2 161.2 %all-gather.3.cloned.1.call-start = ((), (), s32[]{:S(2)}) async-start(), calls=%async_computation.2 | async-start | bytes 13369344 | tf_op jit(solution)/shard_map/all_gather | solution.py:238
  10.3 12.4 %collective-permute-start = (bf16[1,256,768]{1,2,0:T(8,128)(2,1)S(1)}, bf16[1,256,768]{1,2,0:T(8,128)(2,1)S(1)}, u32[]{:S(2)}, u32[]{:S(2)}) collective-permute-start(bf16[1,256,768]{1,2,0:T(8,128)(2,1)S(1)} %maximum_bitcast_fusion), channel_id=1, source_target_pairs={{0,4},{4,0},{1,5},{5,1},{2,6},{6,2},{3,7},{7,3},{8,12},{12,8},{9,1... | collective-permute-start | bytes 1179656 | tf_op jit(solution)/shard_map/ppermute | solution.py:32
  23.9 181.0 %all-gather.5.cloned.1.call-start = ((), (), s32[]{:S(2)}) async-start(), calls=%async_computation.3 | async-start | bytes 8912896 | tf_op jit(solution)/shard_map/all_gather | solution.py:239
  23.9 8.8 %collective-permute-start.1 = (bf16[1,512,256]{2,1,0:T(8,128)(2,1)S(1)}, bf16[1,512,256]{2,1,0:T(8,128)(2,1)S(1)}, u32[]{:S(2)}, u32[]{:S(2)}) collective-permute-start(bf16[1,512,256]{2,1,0:T(8,128)(2,1)S(1)} %bitcast.36), channel_id=1, source_target_pairs={{0,4},{4,0},{1,5},{5,1},{2,6},{6,2},{3,7},{7,3},{8,12},{12,8},{9,1... | collective-permute-start | bytes 786440 | tf_op jit(solution)/shard_map/ppermute | solution.py:32
  52.5 3.3 %copy-start.1 = (bf16[32,128256]{1,0:T(8,128)(2,1)S(1)}, bf16[32,128256]{1,0:T(8,128)(2,1)}, u32[]{:S(2)}) copy-start(bf16[32,128256]{1,0:T(8,128)(2,1)} %table_ref.1) | copy-start | bytes 24625156
  100.4 2.0 copy-start
  102.4 6.7 %copy-start.3 = (f32[4096]{0:T(1024)S(1)}, f32[4096]{0:T(1024)}, u32[]{:S(2)}) copy-start(f32[4096]{0:T(1024)} %param.11) | copy-start | bytes 49156
  102.4 6.8 %copy-start.5 = (s32[32]{0:T(128)S(1)}, s32[32]{0:T(128)}, u32[]{:S(2)}) copy-start(s32[32]{0:T(128)} %param.9) | copy-start | bytes 388
  102.4 58.6 %all-to-all-start.1 = ((bf16[128,32,512]{2,1,0:T(8,128)(2,1)}), bf16[128,32,512]{2,1,0:T(8,128)(2,1)}, u32[]{:S(2)}, u32[]{:S(2)}) async-start(bf16[128,32,512]{2,1,0:T(8,128)(2,1)} %bitcast.31), calls=%async_computation.1 | async-start | bytes 8388608 | tf_op jit(solution)/shard_map/all_to_all | solution.py:249
  207.8 17.2 %collective-permute-start.2 = (bf16[128,2048]{1,0:T(8,128)(2,1)S(1)}, bf16[128,2048]{1,0:T(8,128)(2,1)S(1)}, u32[]{:S(2)}, u32[]{:S(2)}) collective-permute-start(bf16[128,2048]{1,0:T(8,128)(2,1)S(1)} %fusion.19), channel_id=1, source_target_pairs={{0,1},{1,2},{2,3},{3,0},{4,5},{5,6},{6,7},{7,4},{8,9},{9,10},{10,1... | collective-permute-start | bytes 1572872 | tf_op jit(solution)/shard_map/ppermute | solution.py:217
  214.3 14.2 %collective-permute-start.5 = (bf16[128,2048]{1,0:T(8,128)(2,1)S(1)}, bf16[128,2048]{1,0:T(8,128)(2,1)}, u32[]{:S(2)}, u32[]{:S(2)}) collective-permute-start(bf16[128,2048]{1,0:T(8,128)(2,1)S(1)} %fusion.22), channel_id=1, source_target_pairs={{0,3},{1,0},{2,1},{3,2},{4,7},{5,4},{6,5},{7,6},{8,11},{9,8},{10,9... | collective-permute-start | bytes 1572872 | tf_op jit(solution)/shard_map/ppermute | solution.py:217
  227.9 14.8 %collective-permute-start.3 = (bf16[128,2048]{1,0:T(8,128)(2,1)S(1)}, bf16[128,2048]{1,0:T(8,128)(2,1)S(1)}, u32[]{:S(2)}, u32[]{:S(2)}) collective-permute-start(bf16[128,2048]{1,0:T(8,128)(2,1)S(1)} %add_convert_fusion.3), channel_id=1, source_target_pairs={{0,1},{1,2},{2,3},{3,0},{4,5},{5,6},{6,7},{7,4},{8,9},{9,10},{10,1... | collective-permute-start | bytes 1572872 | tf_op jit(solution)/shard_map/ppermute | solution.py:217
  231.5 14.9 %collective-permute-start.6 = (bf16[128,2048]{1,0:T(8,128)(2,1)S(1)}, bf16[128,2048]{1,0:T(8,128)(2,1)S(1)}, u32[]{:S(2)}, u32[]{:S(2)}) collective-permute-start(bf16[128,2048]{1,0:T(8,128)(2,1)S(1)} %add_convert_fusion.1), channel_id=1, source_target_pairs={{0,3},{1,0},{2,1},{3,2},{4,7},{5,4},{6,5},{7,6},{8,11},{9,8},{10,9... | collective-permute-start | bytes 1572872 | tf_op jit(solution)/shard_map/ppermute | solution.py:217
  246.4 14.2 %collective-permute-start.4 = (bf16[128,2048]{1,0:T(8,128)(2,1)}, bf16[128,2048]{1,0:T(8,128)(2,1)}, u32[]{:S(2)}, u32[]{:S(2)}) collective-permute-start(bf16[128,2048]{1,0:T(8,128)(2,1)} %add_convert_fusion.2), channel_id=1, source_target_pairs={{0,1},{1,2},{2,3},{3,0},{4,5},{5,6},{6,7},{7,4},{8,9},{9,10},{10,1... | collective-permute-start | bytes 1572872 | tf_op jit(solution)/shard_map/ppermute | solution.py:217
  250.1 13.5 %collective-permute-start.7 = (bf16[128,2048]{1,0:T(8,128)(2,1)}, bf16[128,2048]{1,0:T(8,128)(2,1)}, u32[]{:S(2)}, u32[]{:S(2)}) collective-permute-start(bf16[128,2048]{1,0:T(8,128)(2,1)} %add_convert_fusion), channel_id=1, source_target_pairs={{0,3},{1,0},{2,1},{3,2},{4,7},{5,4},{6,5},{7,6},{8,11},{9,8},{10,9... | collective-permute-start | bytes 1572872 | tf_op jit(solution)/shard_map/ppermute | solution.py:217
Sparse Core Ops, SparseCore 0:
  24.0 81.0 all-gather.2
  106.7 98.1 all-gather.4

commit v2 on v1

v2 whole, which is shorter than its diff:
```python
import functools

import jax
import jax.numpy as jnp
from jax import lax
from jax.experimental import pallas as pl
from jax.experimental.pallas import tpu as pltpu
from jax.sharding import Mesh
from jax.sharding import PartitionSpec as P


HEADS = 32
KVH = 8
HD = 128
TPG = 4
TENSOR = ("tensor_0", "tensor_1")
DP_TENSOR = ("dp_0", "dp_1", "dp_2", "tensor_0", "tensor_1")
DP = ("dp_0", "dp_1", "dp_2")
RING = "tensor_1"
PLANE = ("dp_0", "dp_1", "dp_2", "tensor_0")
LANES = 128

norm_eps = 1e-05
rope_theta = 500000.0


def swapped(block, axis, apart):
    count = lax.axis_size(axis)
    route = []
    for low in range(count):
        high = low | 1 << apart
        if high != low and high < count:
            route += [(low, high), (high, low)]
    return lax.ppermute(block, axis, route)


def ordered_pair(mine, theirs, bit_index):
    upper_half = lax.axis_index(TENSOR) >> bit_index & 1 == 1
    first_half = jnp.where(upper_half, theirs, mine)
    second_half = jnp.where(upper_half, mine, theirs)
    return jnp.concatenate([first_half, second_half], axis=0)


def collect_blocks(shard, after):
    stacked = shard[None]
    theirs, _ = lax.optimization_barrier((swapped(stacked, TENSOR, 2), after))
    return ordered_pair(stacked, theirs, 2)


def lane_gather(block, lanes):
    dims = lax.GatherDimensionNumbers(
        offset_dims=(),
        collapsed_slice_dims=(1,),
        start_index_map=(1,),
        operand_batching_dims=(0,),
        start_indices_batching_dims=(0,),
    )
    return lax.gather(
        block,
        lanes[..., None],
        dims,
        slice_sizes=(1, 1),
        mode=lax.GatherScatterMode.PROMISE_IN_BOUNDS,
    )


def prepare_kernel(table_ref, tiles_ref):
    columns = table_ref.shape[0]
    tile_count = tiles_ref.shape[0] // 2
    lane = lax.broadcasted_iota(jnp.int32, (columns, LANES), 1).astype(jnp.int16)
    unroll = min(32, tile_count)

    def prepare(step, carry):
        first = jnp.minimum(step * unroll, tile_count - unroll)
        for u in range(unroll):
            t = first + u
            tile = table_ref[:, pl.ds(pl.multiple_of(t * LANES, LANES), LANES)]
            tiles_ref[t] = tile
            tiles_ref[t + tile_count] = lane_gather(tile, lane ^ jnp.int16(LANES // 2))
        return carry

    lax.fori_loop(0, -(-tile_count // unroll), prepare, 0)


def lookup_kernel(slots_ref, lanes_ref, tiles_ref, out_ref):
    groups, columns, row_count = out_ref.shape
    lane = lax.broadcasted_iota(jnp.int32, (columns, LANES), 1).astype(jnp.int16)
    left = lane < jnp.int16(LANES // 2)
    per_group = row_count // LANES
    together = 2

    def one_block(step, carry):
        for part in range(together):
            block = step * together + part
            first = block * LANES
            wanted = jnp.broadcast_to(lanes_ref[pl.ds(block, 1), :], (columns, LANES)).astype(
                jnp.int16
            )
            picked = jnp.zeros((columns, LANES), jnp.bfloat16)
            for i in range(0, LANES, 2):
                pair = jnp.where(
                    left, tiles_ref[slots_ref[first + i]], tiles_ref[slots_ref[first + i + 1]]
                )
                picked = jnp.where(lane >= jnp.int16(i), lane_gather(pair, wanted), picked)
            place = pl.multiple_of(lax.rem(block, per_group) * LANES, LANES)
            out_ref[lax.div(block, per_group), :, pl.ds(place, LANES)] = picked
        return carry

    lax.fori_loop(0, groups * per_group // together, one_block, 0)


def prepared(embed_table):
    columns, vocab_size = embed_table.shape
    return pl.pallas_call(
        prepare_kernel,
        out_shape=jax.ShapeDtypeStruct((2 * vocab_size // LANES, columns, LANES), jnp.bfloat16),
        in_specs=[pl.BlockSpec(memory_space=pltpu.VMEM)],
        out_specs=pl.BlockSpec(memory_space=pltpu.VMEM),
        compiler_params=pltpu.CompilerParams(vmem_limit_bytes=4 * 2**20),
        cost_estimate=pl.CostEstimate(
            flops=8_000_000_000, bytes_accessed=embed_table.size * 6, transcendentals=0
        ),
        name="prepare",
    )(embed_table)


def lookup(tiles, token_ids, group_count):
    tile_count, columns = tiles.shape[0] // 2, tiles.shape[1]
    count = token_ids.shape[0]
    odd = jnp.arange(count, dtype=jnp.int32) & 1
    lane = token_ids & (LANES - 1)
    half = LANES // 2
    slots = lax.shift_right_logical(token_ids, 7) + tile_count * (lax.shift_right_logical(lane, 6) ^ odd)
    lanes = ((lane & (half - 1)) | (odd * half)).reshape(count // LANES, LANES)
    return pl.pallas_call(
        lookup_kernel,
        out_shape=jax.ShapeDtypeStruct((group_count, columns, count // group_count), jnp.bfloat16),
        in_specs=[
            pl.BlockSpec(memory_space=pltpu.SMEM),
            pl.BlockSpec(memory_space=pltpu.VMEM),
            pl.BlockSpec(memory_space=pltpu.VMEM),
        ],
        out_specs=pl.BlockSpec(memory_space=pltpu.VMEM),
        compiler_params=pltpu.CompilerParams(vmem_limit_bytes=4 * 2**20),
        cost_estimate=pl.CostEstimate(
            flops=30_000_000_000, bytes_accessed=tiles.size * 2, transcendentals=0
        ),
        name="lookup",
    )(slots, lanes, tiles)


def transposed_product(rows_ref, weight_ref):
    weight = weight_ref[...]
    width = weight.shape[-1]
    return lax.dot_general(
        rows_ref[...],
        weight.reshape(-1, width),
        (((0,), (0,)), ((), ())),
        preferred_element_type=jnp.float32,
    )


def square_sum(rows_ref):
    wide = rows_ref[...].astype(jnp.float32)
    return jnp.sum(wide * wide, axis=0, keepdims=True)


def project_kernel(places_ref, *refs, parts, carried):
    rows, weights = refs[:parts], refs[parts : 2 * parts]
    total_ref, squares_ref = refs[-2:]
    total = sum(transposed_product(r, w) for r, w in zip(rows, weights))
    squares = sum(square_sum(r) for r in rows)
    if carried:
        total += refs[2 * parts][...]
        squares += refs[2 * parts + 1][...]
    total_ref[...] = total
    squares_ref[...] = squares


def weight_spec(weights, turn, share, which):
    dp_count, _, plane, _, columns, width = weights.shape
    return pl.BlockSpec(
        (dp_count // share, 1, plane, 1, columns, width),
        lambda b, places: (which, b, 0, places[turn], 0, 0),
    )


def project(places, weights, parts, carried=None):
    row_count = parts[0][0].shape[1]
    blocks, width = weights.shape[1], weights.shape[-1]
    in_specs = [pl.BlockSpec(rows.shape, lambda b, places: (0, 0)) for rows, *_ in parts]
    in_specs += [weight_spec(weights, *where) for _, *where in parts]
    total_spec = pl.BlockSpec((row_count, width), lambda b, places: (0, b))
    squares_spec = pl.BlockSpec((1, row_count), lambda b, places: (0, 0))
    operands = [rows for rows, *_ in parts] + [weights] * len(parts)
    if carried is not None:
        in_specs += [total_spec, squares_spec]
        operands += list(carried)
    depth = sum(rows.shape[0] for rows, *_ in parts)
    return pl.pallas_call(
        functools.partial(project_kernel, parts=len(parts), carried=carried is not None),
        grid_spec=pltpu.PrefetchScalarGridSpec(
            num_scalar_prefetch=1,
            grid=(blocks,),
            in_specs=in_specs,
            out_specs=(total_spec, squares_spec),
        ),
        out_shape=(
            jax.ShapeDtypeStruct((row_count, blocks * width), jnp.float32),
            jax.ShapeDtypeStruct((1, row_count), jnp.float32),
        ),
        compiler_params=pltpu.CompilerParams(vmem_limit_bytes=52 * 2**20),
        cost_estimate=pl.CostEstimate(
            flops=2 * row_count * depth * blocks * width,
            bytes_accessed=2 * depth * (blocks * width + row_count),
            transcendentals=0,
        ),
        name="project",
    )(places, *operands)


def attention_kernel(
    places_ref, length_ref, *refs, parts, model_width
):
    rows, weights = refs[:parts], refs[parts : 2 * parts]
    total_ref, squares_ref, cos_ref, sin_ref, attended_ref, cache_ref, proj_ref = refs[2 * parts :]
    row_count = cos_ref.shape[0]
    q_heads = HEADS // KVH
    proj_ref[...] = total_ref[...] + sum(transposed_product(r, w) for r, w in zip(rows, weights))
    squares = squares_ref[...] + sum(square_sum(r) for r in rows)
    scale = lax.rsqrt(squares / model_width + norm_eps)
    scale = jnp.transpose(jnp.broadcast_to(scale, (HD, row_count)))
    cosine = cos_ref[...] * scale
    sine = sin_ref[...] * scale

    def rotate(part):
        return (part * cosine + pltpu.roll(part, HD // 2, 1) * sine).astype(jnp.bfloat16)

    key_rot = rotate(proj_ref[:, q_heads * HD : (q_heads + 1) * HD])
    value = (proj_ref[:, (q_heads + 1) * HD : (q_heads + 2) * HD] * scale).astype(jnp.bfloat16)
    cache_ref[0] = key_rot
    cache_ref[1] = value
    length = length_ref[0]
    block = min(256, row_count)
    root = jnp.float32(HD) ** 0.5
    for h in range(q_heads):
        query = rotate(proj_ref[:, h * HD : (h + 1) * HD])
        for start in range(0, row_count, block):
            keys = start + block
            scores = (
                lax.dot_general(
                    query[start : start + block],
                    key_rot[:keys],
                    (((1,), (1,)), ((), ())),
                    preferred_element_type=jnp.float32,
                )
                / root
            )
            q_pos = start + lax.broadcasted_iota(jnp.int32, (block, keys), 0)
            k_pos = lax.broadcasted_iota(jnp.int32, (block, keys), 1)
            scores = jnp.where((k_pos <= q_pos) & (k_pos < length), scores, -1e30)
            expd = jnp.exp(scores - jnp.max(scores, axis=-1, keepdims=True))
            weights_now = (expd / jnp.sum(expd, axis=-1, keepdims=True)).astype(jnp.bfloat16)
            attended_ref[start : start + block, h * HD : (h + 1) * HD] = jnp.dot(
                weights_now, value[:keys], preferred_element_type=jnp.float32
            ).astype(jnp.bfloat16)


def attend(places, weights, parts, carried, length, cosine, sine, model_width):
    row_count = cosine.shape[0]
    blocks, width = weights.shape[1], weights.shape[-1]
    query_width = HEADS // KVH * HD
    in_specs = [pl.BlockSpec(memory_space=pltpu.SMEM)]
    in_specs += [pl.BlockSpec(rows.shape, lambda b, places: (0, 0)) for rows, *_ in parts]
    in_specs += [weight_spec(weights, *where) for _, *where in parts]
    in_specs += [
        pl.BlockSpec((row_count, width), lambda b, places: (0, b)),
        pl.BlockSpec((1, row_count), lambda b, places: (0, 0)),
        pl.BlockSpec((row_count, HD), lambda b, places: (0, 0)),
        pl.BlockSpec((row_count, HD), lambda b, places: (0, 0)),
    ]
    return pl.pallas_call(
        functools.partial(attention_kernel, parts=len(parts), model_width=model_width),
        grid_spec=pltpu.PrefetchScalarGridSpec(
            num_scalar_prefetch=1,
            grid=(blocks,),
            in_specs=in_specs,
            out_specs=(
                pl.BlockSpec((row_count, query_width), lambda b, places: (0, b)),
                pl.BlockSpec((2, row_count, HD), lambda b, places: (0, 0, b)),
            ),
            scratch_shapes=[pltpu.VMEM((row_count, width), jnp.float32)],
        ),
        out_shape=(
            jax.ShapeDtypeStruct((row_count, blocks * query_width), jnp.bfloat16),
            jax.ShapeDtypeStruct((2, row_count, blocks * HD), jnp.bfloat16),
        ),
        compiler_params=pltpu.CompilerParams(vmem_limit_bytes=52 * 2**20),
        cost_estimate=pl.CostEstimate(
            flops=4_000_000_000, bytes_accessed=9_000_000, transcendentals=2_000_000
        ),
        name="attend",
    )(
        places,
        length,
        *[rows for rows, *_ in parts],
        *[weights] * len(parts),
        *carried,
        cosine,
        sine,
    )


def rope_tables(row_count):
    half = HD // 2
    freq = rope_theta ** (-2.0 * jnp.arange(half, dtype=jnp.float32) / HD)
    angle = jnp.arange(row_count, dtype=jnp.int32).astype(jnp.float32)[:, None] * freq[None, :]
    cosine, sine = jnp.cos(angle), jnp.sin(angle)
    return jnp.concatenate([cosine, cosine], axis=1), jnp.concatenate([-sine, sine], axis=1)


def residual_kernel(places_ref, *refs, shares):
    rows_ref, ordered_ref = refs[-2:]
    plane, ring, columns, quarter = ordered_ref.shape
    at = 0
    for turn, share in enumerate(shares):
        count = plane // share
        for piece in range(share):
            ordered_ref[piece * count : (piece + 1) * count, places_ref[turn]] = refs[at][
                ...
            ].reshape(count, columns, quarter)
            at += 1
    width = ring * columns
    for p in range(plane):
        rows_ref[:, p * width : (p + 1) * width] = jnp.transpose(
            ordered_ref[p].reshape(width, quarter).astype(jnp.float32)
        ).astype(jnp.bfloat16)


def residual(places, pieces, columns, quarter):
    flat = [rows for turn in pieces for rows in turn]
    depth = sum(rows.shape[0] for rows in flat)
    ring = len(pieces)
    return pl.pallas_call(
        functools.partial(residual_kernel, shares=[len(turn) for turn in pieces]),
        grid_spec=pltpu.PrefetchScalarGridSpec(
            num_scalar_prefetch=1,
            grid=(1,),
            in_specs=[
                pl.BlockSpec((rows.shape[0], quarter), lambda i, places: (0, places[0]))
                for rows in flat
            ],
            out_specs=pl.BlockSpec((quarter, depth), lambda i, places: (0, 0)),
            scratch_shapes=[
                pltpu.VMEM((depth // (ring * columns), ring, columns, quarter), jnp.bfloat16)
            ],
        ),
        out_shape=jax.ShapeDtypeStruct((quarter, depth), jnp.bfloat16),
        compiler_params=pltpu.CompilerParams(vmem_limit_bytes=16 * 2**20),
        cost_estimate=pl.CostEstimate(
            flops=1_000_000_000, bytes_accessed=4 * depth * quarter, transcendentals=0
        ),
        name="residual",
    )(places, *flat)


def ring_route(way):
    count = lax.axis_size(RING)
    return [(k, (k + way) % count) for k in range(count)]


def ring_reduced(attended, weight, quarter):
    place = lax.axis_index(RING)
    count = lax.axis_size(RING)
    half = weight.shape[1] // 2
    sums = []
    for way, columns in ((1, weight[:, :half]), (-1, weight[:, half:])):
        product = lax.optimization_barrier(
            jnp.dot(attended, columns, preferred_element_type=jnp.float32).astype(jnp.bfloat16)
        )

        def part(turn):
            return lax.dynamic_slice_in_dim(product, (place + turn) % count * quarter, quarter, 0)

        running = part(-way)
        for step in range(1, count):
            running = lax.ppermute(running.astype(jnp.bfloat16), RING, ring_route(way))
            running = running.astype(jnp.float32) + part(-way * (step + 1)).astype(jnp.float32)
        sums.append(running)
    return jnp.concatenate(sums, axis=1)


def sublayer(prompt_ids, prompt_lengths, embed_table, norm_gain, w_query, w_key, w_value, w_out):
    quarter = prompt_ids.shape[0]
    row_count = quarter * TPG
    devices = lax.axis_size(DP_TENSOR)
    columns = embed_table.shape[0]
    model_width = columns * devices
    group_count = devices // TPG
    dp_count = lax.axis_size(DP)
    place = lax.axis_index(RING)
    ring = lax.axis_size(RING)
    group_index = lax.axis_index(DP) * lax.axis_size("tensor_0") + lax.axis_index("tensor_0")
    length = lax.dynamic_slice_in_dim(prompt_lengths, group_index, 1, 0)
    cosine, sine = rope_tables(row_count)

    depth = w_query.shape[0]
    gain = lax.dynamic_slice_in_dim(norm_gain, lax.axis_index(DP) * depth, depth, 0)
    packed = jnp.concatenate([w_query, w_key, w_value], axis=1).astype(jnp.float32)
    packed = (packed * gain[:, None]).astype(jnp.bfloat16)
    w_in = lax.all_gather(packed, PLANE, axis=0, tiled=True).reshape(
        dp_count, devices // ring // dp_count, devices // ring // dp_count, ring, columns, -1
    )

    all_ids = lax.all_to_all(
        jnp.broadcast_to(prompt_ids[None], (devices, quarter)),
        DP_TENSOR,
        split_axis=0,
        concat_axis=0,
        tiled=True,
    ).reshape(-1)
    tiles = prepared(embed_table)
    outgoing = lookup(tiles, all_ids, group_count)
    w_back = lax.all_gather(collect_blocks(w_out, outgoing), DP, axis=2, tiled=True)
    own = lax.all_to_all(outgoing, PLANE, split_axis=0, concat_axis=0, tiled=True).reshape(
        -1, row_count
    )
    half = own.shape[0] // 2
    low, high = own[:half], own[half:]
    low_before = lax.ppermute(low, RING, ring_route(1))
    high_after = lax.ppermute(high, RING, ring_route(-1))
    high_before = lax.ppermute(high, RING, ring_route(1))
    low_after = lax.ppermute(low, RING, ring_route(-1))
    low_across = lax.ppermute(low_before, RING, ring_route(1))
    high_across = lax.ppermute(high_after, RING, ring_route(-1))

    places = (place + jnp.arange(ring, dtype=jnp.int32)) % ring
    first = project(places, w_in, [(own, 0, 1, 0)])
    second = project(
        places,
        w_in,
        [
            (low_before, ring - 1, 2, 0),
            (high_before, ring - 1, 2, 1),
            (low_after, 1, 2, 0),
            (high_after, 1, 2, 1),
        ],
        first,
    )
    attended, cache = attend(
        places,
        w_in,
        [(low_across, 2, 2, 0), (high_across, 2, 2, 1)],
        second,
        length,
        cosine,
        sine,
        model_width,
    )

    pieces = [[own], [low_after, high_after], [low_across, high_across], [low_before, high_before]]
    pieces, _ = lax.optimization_barrier((pieces, attended))
    own_rows = residual(places, pieces, columns, quarter)

    summed = ring_reduced(attended, w_back.reshape(-1, model_width), quarter)
    hidden = (own_rows.astype(jnp.float32) + summed).astype(jnp.bfloat16)
    return hidden, cache[None]


def solution(mesh):
    split = Mesh(
        mesh.devices.reshape(4, 2, 2, 2, 4), ("dp_0", "dp_1", "dp_2", "tensor_0", "tensor_1")
    )
    placed = (
        P(DP_TENSOR),
        P(),
        P(DP_TENSOR, None),
        P(),
        P(DP, TENSOR),
        P(DP, TENSOR),
        P(DP, TENSOR),
        P(TENSOR, DP),
    )
    return jax.shard_map(
        sublayer,
        mesh=split,
        in_specs=placed,
        out_specs=(P(DP_TENSOR, None), P(DP_TENSOR, None, None, None)),
        check_vma=False,
    )
```

time: 277 us -> 258 us (0.931)
  waiting for transfers between devices: 108 us -> 78.3 us
  matrix products: 36.1 us -> 7.32 us
  local copies, waits for them, and re-layouts: 10.9 us -> 22.5 us
  starting transfers between devices: 21.5 us -> 32 us
  Pallas kernels: 53.5 us -> 61.4 us
  blocking collectives: 18.7 us -> 25.4 us
  other arithmetic: 12 us -> 15.1 us
    all_to_all x1, waiting for transfers between devices: 49.9 us -> 0.01 us  [sublayer(): lax.all_to_all(jnp.broadcast_to(prompt_ids[None], (devices, quarter)), DP...]
    dot_general x9 -> x2, matrix products: 36.1 us -> 7.32 us  [ring_reduced(): jnp.dot(attended, columns, preferred_element_type=jnp.float32)]
    pallas_call x1 -> x5, Pallas kernels: 8.97 us -> 34.3 us  [the longest x1 14.4 us: attend(): pl.pallas_call(functools.partial(attention_kernel, parts=len(parts), mode...]
    all_gather x2, waiting for transfers between devices: 16.6 us -> 41.9 us  [the longest x1 35.9 us: sublayer(): lax.all_gather(collect_blocks(w_out, outgoing), DP, axis=2, tiled=True)]
    ppermute x2 -> x1, waiting for transfers between devices: 18.2 us -> 0.01 us  [swapped(): return lax.ppermute(block, axis, route)]
    pallas_call x1, Pallas kernels: 44.5 us -> 27.1 us  [lookup(): pl.pallas_call(lookup_kernel, out_shape=jax.ShapeDtypeStruct((group_count...]
    ppermute x6 -> x12, waiting for transfers between devices: 22.9 us -> 36.4 us  [the longest x6 29.2 us: ring_reduced(): running = lax.ppermute(running.astype(jnp.bfloat16), RING, ring_route(way))]
    unnamed x16 -> x24, local copies, waits for them, and re-layouts: 8.85 us -> 17 us
  transfers between devices with their start and end apart: 11 -> 16, of which waited for: 7 -> 11; matrix products, arithmetic and copies ran while one was open for 15% -> 7% of each run, Pallas kernels for 19% -> 24%
where the time goes in v2:
time: 258 us; the launch traced here: 256 us
  waiting for transfers between devices  78.3 us (30%)
  Pallas kernels  61.4 us (24%)
  starting transfers between devices  32 us (12%)
  blocking collectives  25.4 us (10%)
  local copies, waits for them, and re-layouts  22.5 us (9%)
  other arithmetic  15.1 us (6%)
  between operations  14.3 us (6%)
  matrix products  7.32 us (3%)
    all_gather x1, waiting for transfers between devices, sublayer(): lax.all_gather(collect_blocks(w_out, outgoing), DP, axis=2, tiled=True)  35.9 us
    ppermute x6, waiting for transfers between devices, ring_reduced(): running = lax.ppermute(running.astype(jnp.bfloat16), RING, ring_route(way))  29.2 us
    pallas_call x1, Pallas kernels, lookup(): pl.pallas_call(lookup_kernel, out_shape=jax.ShapeDtypeStruct((group_count...  27.1 us
    all_to_all x1, blocking collectives, sublayer(): lax.all_to_all(outgoing, PLANE, split_axis=0, concat_axis=0, tiled=True)  25.4 us
    unnamed x24, local copies, waits for them, and re-layouts  17 us
    pallas_call x1, Pallas kernels, attend(): pl.pallas_call(functools.partial(attention_kernel, parts=len(parts), mode...  14.4 us
    pallas_call x2, Pallas kernels, project(): pl.pallas_call(functools.partial(project_kernel, parts=len(parts), carrie...  13.4 us
    all_to_all x1, starting transfers between devices, sublayer(): lax.all_to_all(jnp.broadcast_to(prompt_ids[None], (devices, quarter)), DP...  10.5 us
  transfers between devices with their start and end apart: 16, of which 11 were waited for; matrix products, arithmetic and copies ran while one was open for 7% of the time, Pallas kernels for 24%

profile of v2, /device:TPU:6, one launch (start us, length us, event | category | flops | bytes accessed | tf_op | source)
XLA Modules:
  0.0 256.3 jit_solution(16571289029670858049)
XLA Ops:
  7.2 0.8 dynamic_slice.31
  8.0 1.9 multiply_convert_fusion
  9.9 1.3 broadcast_in_dim.6
  11.2 10.5 %all-to-all-start = ((s32[128,1,128]{2,1,0:T(1,128)}), s32[128,1,128]{2,1,0:T(1,128)S(1)}, u32[]{:S(2)}, u32[]{:S(2)}) async-start(s32[128,1,128]{2,1,0:T(1,128)} %broadcast_in_dim.6), calls=%async_computation | async-start | bytes 131072 | tf_op jit(solution)/shard_map/all_to_all | solution.py:415
  21.8 1.5 collective-permute-start.6
  23.3 3.4 %copy-done.3 = bf16[32,128256]{1,0:T(8,128)(2,1)S(1)} copy-done((bf16[32,128256]{1,0:T(8,128)(2,1)S(1)}, bf16[32,128256]{1,0:T(8,128)(2,1)}, u32[]{:S(2)}) %copy-start.3) | copy-done | bytes 8208408
  26.7 4.5 %prepare.1.tiles_ref = bf16[2004,32,128]{2,1,0:T(8,128)(2,1)S(1)} custom-call(bf16[32,128256]{1,0:T(8,128)(2,1)S(1)} %copy-done.3), custom_call_target="tpu_custom_call" | custom-call | flops 8000000000 | bytes 24625152 | tf_op jit(solution)/shard_map/prepare/pallas_call | solution.py:114
  31.2 5.7 %copy-done.4 = bf16[2004,32,128]{2,1,0:T(8,128)(2,1)} copy-done((bf16[2004,32,128]{2,1,0:T(8,128)(2,1)}, bf16[2004,32,128]{2,1,0:T(8,128)(2,1)S(1)}, u32[]{:S(2)}) %copy-start.4) | copy-done | bytes 16416792
  37.0 5.9 %copy-done.5 = bf16[2004,32,128]{2,1,0:T(8,128)(2,1)S(1)} copy-done((bf16[2004,32,128]{2,1,0:T(8,128)(2,1)S(1)}, bf16[2004,32,128]{2,1,0:T(8,128)(2,1)}, u32[]{:S(2)}) %copy-start.5) | copy-done | bytes 16416792
  42.9 27.1 %lookup.1 = bf16[32,32,512]{2,1,0:T(8,128)(2,1)S(1)} custom-call(s32[16384]{0:T(1024)S(1)} %fusion.13.slots_ref, s32[128,128]{1,0:T(8,128)S(1)} %bitcast_or_fusion.lanes_ref, bf16[2004,32,128]{2,1,0:T(8,128)(2,1)S(1)} %copy-done.5), custom_call_target="tpu_custom_call" | custom-call | flops 30000001024 | bytes 16416768 | tf_op jit(solution)/shard_map/lookup/pallas_call | solution.py:135
  70.1 0.9 pad_maximum_fusion
  71.0 25.4 %all_to_all.11 = bf16[32,32,512]{2,1,0:T(8,128)(2,1)S(1)} all-to-all(bf16[32,32,512]{2,1,0:T(8,128)(2,1)S(1)} %lookup.1), channel_id=1, replica_groups=mesh['dp_0'=4,'dp_1'=2,'dp_2'=2,'tensor_0'=2,'tensor_1'=4] {'dp_0','dp_1..., dimensions={0} | all-to-all | bytes 2097152 | tf_op jit(solution)/shard_map/all_to_all | solution.py:425
  96.4 1.0 fusion.15
  97.4 1.6 collective-permute-start.2
  99.0 1.7 collective-permute-start.1
  100.7 0.7 dynamic_slice.30.length_ref
  101.7 2.9 %collective-permute-start = (bf16[512,512]{1,0:T(8,128)(2,1)}, bf16[512,512]{1,0:T(8,128)(2,1)S(1)}, u32[]{:S(2)}, u32[]{:S(2)}) collective-permute-start(bf16[512,512]{1,0:T(8,128)(2,1)} %bitcast.5), channel_id=1, source_target_pairs={{0,3},{1,0},{2,1},{3,2},{4,7},{5,4},{6,5},{7,6},{8,11},{9,8},{10,9... | collective-permute-start | bytes 1572872 | tf_op jit(solution)/shard_map/ppermute | solution.py:433
  104.6 1.0 fusion.11
  105.6 0.9 pad_maximum_fusion.1
  106.5 6.9 %collective-permute-done.2.refs_0_.refs_5_ = bf16[512,512]{1,0:T(8,128)(2,1)S(1)} collective-permute-done((bf16[512,512]{1,0:T(8,128)(2,1)}, bf16[512,512]{1,0:T(8,128)(2,1)S(1)}, u32[]{:S(2)}, u32[]{:S(2)}) %collective-permute-start.2) | collective-permute-done | bytes 524320 | tf_op jit(solution)/shard_map/ppermute | solution.py:430
  114.0 2.9 %collective-permute-start.4 = (bf16[512,512]{1,0:T(8,128)(2,1)S(1)}, bf16[512,512]{1,0:T(8,128)(2,1)}, u32[]{:S(2)}, u32[]{:S(2)}) collective-permute-start(bf16[512,512]{1,0:T(8,128)(2,1)S(1)} %collective-permute-done.1.refs_3_.refs_2_), channel_id=1, source_target_pairs={{0,3},{1,0},{2,1},{3,2},{4,7},{5,4},{6,5},{7,6},{8,11},{9,8},{10,9... | collective-permute-start | bytes 1572872 | tf_op jit(solution)/shard_map/ppermute | solution.py:435
  116.9 6.0 %all-gather.3.cloned.1.call-done = bf16[8192,768]{1,0:T(8,128)(2,1)} async-done(((bf16[256,768]{1,0:T(8,128)(2,1)}), bf16[8192,768]{1,0:T(8,128)(2,1)}) %all-gather.3.cloned.1.call-update) | async-done | bytes 12582928 | tf_op jit(solution)/shard_map/all_gather | solution.py:411
  123.0 5.3 %project.2 = (f32[512,1536]{1,0:T(8,128)}, f32[1,512]{1,0:T(1,128)S(1)}) custom-call(s32[4]{0:T(128)S(1)} %and_select_fusion.places_ref, bf16[1024,512]{1,0:T(8,128)(2,1)S(1)} %bitcast.21, bf16[16,2,2,4,32,768]{5,4,3,2,1,0:T(8,128)(2,1)} %bitcast.23), custom_call_target="tpu_custom_call" | custom-call | flops 1610612736 | bytes 4194304 | tf_op jit(solution)/shard_map/project/pallas_call | solution.py:200
  128.3 8.1 %project.3 = (f32[512,1536]{1,0:T(8,128)}, f32[1,512]{1,0:T(1,128)S(1)}) custom-call(s32[4]{0:T(128)S(1)} %and_select_fusion.places_ref, bf16[512,512]{1,0:T(8,128)(2,1)S(1)} %collective-permute-done.2.refs_0_.refs_5_, bf16[512,512]{1,0:T(8,128)(2,1)S(1)} %collective-permute-done.5.refs_1_.refs_6_, ...), custom_call_target="tpu_custom_call" | custom-call | flops 3221225472 | bytes 8388608 | tf_op jit(solution)/shard_map/project/pallas_call | solution.py:200
  136.5 14.4 %attend.1 = (bf16[512,1024]{1,0:T(8,128)(2,1)}, bf16[2,512,256]{2,1,0:T(8,128)(2,1)}) custom-call(s32[4]{0:T(128)S(1)} %and_select_fusion.places_ref, s32[1]{0:T(128)} %dynamic_slice.30.length_ref, bf16[512,512]{1,0:T(8,128)(2,1)} %collective-permute-done.3.refs_0_.refs_3_, bf16[512,512]{1,0:T(8,128)(2,1)} %collective-permute-done.4.refs_1_.refs_4_, ...), custom_call_target="tpu_custom_call" | custom-call | flops 4000000000 | bytes 9000000 | tf_op jit(solution)/shard_map/attend/pallas_call | solution.py:282
  150.9 35.9 %all-gather.5.cloned.1.call-done = bf16[2,512,4096]{2,1,0:T(8,128)(2,1)} async-done(((bf16[2,512,256]{2,1,0:T(8,128)(2,1)}), bf16[2,512,4096]{2,1,0:T(8,128)(2,1)}) %all-gather.5.cloned.1.call-update) | async-done | bytes 8388624 | tf_op jit(solution)/shard_map/all_gather | solution.py:424
  186.7 5.0 %fusion.7 = bf16[512,2048]{1,0:T(8,128)(2,1)S(1)} fusion(bf16[512,1024]{1,0:T(8,128)(2,1)} %get-tuple-element.20, bf16[1024,4096]{1,0:T(8,128)(2,1)} %bitcast.34), kind=kOutput, calls=%fused_computation.5 | convolution fusion | flops 2148532224 | bytes 7340032 | tf_op jit(solution)/shard_map/dot_general | solution.py:379
  191.7 0.9 constant_dynamic-slice_fusion
  193.3 2.7 %collective-permute-start.10 = (bf16[128,2048]{1,0:T(8,128)(2,1)}, bf16[128,2048]{1,0:T(8,128)(2,1)S(1)}, u32[]{:S(2)}, u32[]{:S(2)}) collective-permute-start(bf16[128,2048]{1,0:T(8,128)(2,1)} %constant_dynamic-slice_fusion), channel_id=1, source_target_pairs={{0,3},{1,0},{2,1},{3,2},{4,7},{5,4},{6,5},{7,6},{8,11},{9,8},{10,9... | collective-permute-start | bytes 1572872 | tf_op jit(solution)/shard_map/ppermute | solution.py:387
  196.0 2.3 fusion.4
  198.3 1.4 copy-done.6
  199.7 0.8 constant_dynamic-slice_fusion.1
  200.5 7.4 %collective-permute-done.10 = bf16[128,2048]{1,0:T(8,128)(2,1)S(1)} collective-permute-done((bf16[128,2048]{1,0:T(8,128)(2,1)}, bf16[128,2048]{1,0:T(8,128)(2,1)S(1)}, u32[]{:S(2)}, u32[]{:S(2)}) %collective-permute-start.10) | collective-permute-done | bytes 524320 | tf_op jit(solution)/shard_map/ppermute | solution.py:387
  207.9 2.0 add_convert_fusion.1
  209.8 3.6 %collective-permute-start.11 = (bf16[128,2048]{1,0:T(8,128)(2,1)}, bf16[128,2048]{1,0:T(8,128)(2,1)}, u32[]{:S(2)}, u32[]{:S(2)}) collective-permute-start(bf16[128,2048]{1,0:T(8,128)(2,1)} %add_convert_fusion.1), channel_id=1, source_target_pairs={{0,3},{1,0},{2,1},{3,2},{4,7},{5,4},{6,5},{7,6},{8,11},{9,8},{10,9... | collective-permute-start | bytes 1572872 | tf_op jit(solution)/shard_map/ppermute | solution.py:387
  213.4 2.4 collective-permute-done.7
  215.8 2.1 add_convert_fusion.3
  218.0 6.5 %collective-permute-done.11 = bf16[128,2048]{1,0:T(8,128)(2,1)} collective-permute-done((bf16[128,2048]{1,0:T(8,128)(2,1)}, bf16[128,2048]{1,0:T(8,128)(2,1)}, u32[]{:S(2)}, u32[]{:S(2)}) %collective-permute-start.11) | collective-permute-done | bytes 524320 | tf_op jit(solution)/shard_map/ppermute | solution.py:387
  224.5 1.3 add_convert_fusion
  225.8 3.8 %collective-permute-start.12 = (bf16[128,2048]{1,0:T(8,128)(2,1)S(1)}, bf16[128,2048]{1,0:T(8,128)(2,1)S(1)}, u32[]{:S(2)}, u32[]{:S(2)}) collective-permute-start(bf16[128,2048]{1,0:T(8,128)(2,1)S(1)} %add_convert_fusion), channel_id=1, source_target_pairs={{0,3},{1,0},{2,1},{3,2},{4,7},{5,4},{6,5},{7,6},{8,11},{9,8},{10,9... | collective-permute-start | bytes 1572872 | tf_op jit(solution)/shard_map/ppermute | solution.py:387
  229.6 2.9 %collective-permute-done.8 = bf16[128,2048]{1,0:T(8,128)(2,1)} collective-permute-done((bf16[128,2048]{1,0:T(8,128)(2,1)}, bf16[128,2048]{1,0:T(8,128)(2,1)}, u32[]{:S(2)}, u32[]{:S(2)}) %collective-permute-start.8) | collective-permute-done | bytes 524320 | tf_op jit(solution)/shard_map/ppermute | solution.py:387
  232.4 1.3 add_convert_fusion.2
  233.9 2.0 residual.1
  235.9 3.6 %collective-permute-done.12 = bf16[128,2048]{1,0:T(8,128)(2,1)S(1)} collective-permute-done((bf16[128,2048]{1,0:T(8,128)(2,1)S(1)}, bf16[128,2048]{1,0:T(8,128)(2,1)S(1)}, u32[]{:S(2)}, u32[]{:S(2)}) %collective-permute-start.12) | collective-permute-done | bytes 524320 | tf_op jit(solution)/shard_map/ppermute | solution.py:387
  239.5 1.2 convert_add_fusion
  240.6 6.5 %collective-permute-done.9 = bf16[128,2048]{1,0:T(8,128)(2,1)S(1)} collective-permute-done((bf16[128,2048]{1,0:T(8,128)(2,1)S(1)}, bf16[128,2048]{1,0:T(8,128)(2,1)S(1)}, u32[]{:S(2)}, u32[]{:S(2)}) %collective-permute-start.9) | collective-permute-done | bytes 524320 | tf_op jit(solution)/shard_map/ppermute | solution.py:387
  247.1 1.2 convert_add_fusion.1
  248.3 1.2 fusion.10
  (43 shorter events, 2.0 us)
Async XLA Ops:
  7.2 115.8 %all-gather.3.cloned.1.call-start = ((), (), s32[]{:S(2)}) async-start(), calls=%async_computation.2 | async-start | bytes 12976128 | tf_op jit(solution)/shard_map/all_gather | solution.py:411
  11.2 25.6 %all-to-all-start = ((s32[128,1,128]{2,1,0:T(1,128)}), s32[128,1,128]{2,1,0:T(1,128)S(1)}, u32[]{:S(2)}, u32[]{:S(2)}) async-start(s32[128,1,128]{2,1,0:T(1,128)} %broadcast_in_dim.6), calls=%async_computation | async-start | bytes 131072 | tf_op jit(solution)/shard_map/all_to_all | solution.py:415
  21.7 165.0 %all-gather.5.cloned.1.call-start = ((), (), s32[]{:S(2)}) async-start(), calls=%async_computation.3 | async-start | bytes 8912896 | tf_op jit(solution)/shard_map/all_gather | solution.py:424
  21.8 48.3 %collective-permute-start.6 = (bf16[1,512,256]{2,1,0:T(8,128)(2,1)}, bf16[1,512,256]{2,1,0:T(8,128)(2,1)S(1)}, u32[]{:S(2)}, u32[]{:S(2)}) collective-permute-start(bf16[1,512,256]{2,1,0:T(8,128)(2,1)} %bitcast.33), channel_id=1, source_target_pairs={{0,4},{4,0},{1,5},{5,1},{2,6},{6,2},{3,7},{7,3},{8,12},{12,8},{9,1... | collective-permute-start | bytes 786440 | tf_op jit(solution)/shard_map/ppermute | solution.py:34
  23.3 3.4 %copy-start.3 = (bf16[32,128256]{1,0:T(8,128)(2,1)S(1)}, bf16[32,128256]{1,0:T(8,128)(2,1)}, u32[]{:S(2)}) copy-start(bf16[32,128256]{1,0:T(8,128)(2,1)} %table_ref.1) | copy-start | bytes 24625156
  31.2 5.7 %copy-start.4 = (bf16[2004,32,128]{2,1,0:T(8,128)(2,1)}, bf16[2004,32,128]{2,1,0:T(8,128)(2,1)S(1)}, u32[]{:S(2)}) copy-start(bf16[2004,32,128]{2,1,0:T(8,128)(2,1)S(1)} %prepare.1.tiles_ref) | copy-start | bytes 49250308
  37.0 5.9 %copy-start.5 = (bf16[2004,32,128]{2,1,0:T(8,128)(2,1)S(1)}, bf16[2004,32,128]{2,1,0:T(8,128)(2,1)}, u32[]{:S(2)}) copy-start(bf16[2004,32,128]{2,1,0:T(8,128)(2,1)} %copy-done.4) | copy-start | bytes 49250308
  42.9 27.1 %copy-start.8 = (bf16[512,256]{1,0:T(8,128)(2,1)S(1)}, bf16[512,256]{1,0:T(8,128)(2,1)}, u32[]{:S(2)}) copy-start(bf16[512,256]{1,0:T(8,128)(2,1)} %param.15) | copy-start | bytes 786436
  71.0 29.7 %copy-start.11 = (s32[32]{0:T(128)S(1)}, s32[32]{0:T(128)}, u32[]{:S(2)}) copy-start(s32[32]{0:T(128)} %param.9) | copy-start | bytes 388
  97.4 16.0 %collective-permute-start.2 = (bf16[512,512]{1,0:T(8,128)(2,1)}, bf16[512,512]{1,0:T(8,128)(2,1)S(1)}, u32[]{:S(2)}, u32[]{:S(2)}) collective-permute-start(bf16[512,512]{1,0:T(8,128)(2,1)} %bitcast.5), channel_id=1, source_target_pairs={{0,1},{1,2},{2,3},{3,0},{4,5},{5,6},{6,7},{7,4},{8,9},{9,10},{10,1... | collective-permute-start | bytes 1572872 | tf_op jit(solution)/shard_map/ppermute | solution.py:430
  99.0 15.0 %collective-permute-start.1 = (bf16[512,512]{1,0:T(8,128)(2,1)}, bf16[512,512]{1,0:T(8,128)(2,1)S(1)}, u32[]{:S(2)}, u32[]{:S(2)}) collective-permute-start(bf16[512,512]{1,0:T(8,128)(2,1)} %bitcast.6), channel_id=1, source_target_pairs={{0,3},{1,0},{2,1},{3,2},{4,7},{5,4},{6,5},{7,6},{8,11},{9,8},{10,9... | collective-permute-start | bytes 1572872 | tf_op jit(solution)/shard_map/ppermute | solution.py:431
  101.4 26.9 %collective-permute-start.5 = (bf16[512,512]{1,0:T(8,128)(2,1)}, bf16[512,512]{1,0:T(8,128)(2,1)S(1)}, u32[]{:S(2)}, u32[]{:S(2)}) collective-permute-start(bf16[512,512]{1,0:T(8,128)(2,1)} %bitcast.6), channel_id=1, source_target_pairs={{0,1},{1,2},{2,3},{3,0},{4,5},{5,6},{6,7},{7,4},{8,9},{9,10},{10,1... | collective-permute-start | bytes 1572872 | tf_op jit(solution)/shard_map/ppermute | solution.py:432
  101.7 26.5 %collective-permute-start = (bf16[512,512]{1,0:T(8,128)(2,1)}, bf16[512,512]{1,0:T(8,128)(2,1)S(1)}, u32[]{:S(2)}, u32[]{:S(2)}) collective-permute-start(bf16[512,512]{1,0:T(8,128)(2,1)} %bitcast.5), channel_id=1, source_target_pairs={{0,3},{1,0},{2,1},{3,2},{4,7},{5,4},{6,5},{7,6},{8,11},{9,8},{10,9... | collective-permute-start | bytes 1572872 | tf_op jit(solution)/shard_map/ppermute | solution.py:433
  113.4 22.9 %collective-permute-start.3 = (bf16[512,512]{1,0:T(8,128)(2,1)S(1)}, bf16[512,512]{1,0:T(8,128)(2,1)}, u32[]{:S(2)}, u32[]{:S(2)}) collective-permute-start(bf16[512,512]{1,0:T(8,128)(2,1)S(1)} %collective-permute-done.2.refs_0_.refs_5_), channel_id=1, source_target_pairs={{0,1},{1,2},{2,3},{3,0},{4,5},{5,6},{6,7},{7,4},{8,9},{9,10},{10,1... | collective-permute-start | bytes 1572872 | tf_op jit(solution)/shard_map/ppermute | solution.py:434
  114.0 14.2 %copy-start = (bf16[512,512]{1,0:T(8,128)(2,1)}, bf16[512,512]{1,0:T(8,128)(2,1)S(1)}, u32[]{:S(2)}) copy-start(bf16[512,512]{1,0:T(8,128)(2,1)S(1)} %collective-permute-done.1.refs_3_.refs_2_) | copy-start | bytes 1572868
  114.0 22.4 %collective-permute-start.4 = (bf16[512,512]{1,0:T(8,128)(2,1)S(1)}, bf16[512,512]{1,0:T(8,128)(2,1)}, u32[]{:S(2)}, u32[]{:S(2)}) collective-permute-start(bf16[512,512]{1,0:T(8,128)(2,1)S(1)} %collective-permute-done.1.refs_3_.refs_2_), channel_id=1, source_target_pairs={{0,3},{1,0},{2,1},{3,2},{4,7},{5,4},{6,5},{7,6},{8,11},{9,8},{10,9... | collective-permute-start | bytes 1572872 | tf_op jit(solution)/shard_map/ppermute | solution.py:435
  128.3 8.2 %copy-start.2 = (f32[512,128]{1,0:T(8,128)S(1)}, f32[512,128]{1,0:T(8,128)}, u32[]{:S(2)}) copy-start(f32[512,128]{1,0:T(8,128)} %get-tuple-element.38.refs_7_) | copy-start | bytes 786436
  186.7 9.2 %copy-start.9 = (bf16[2,512,4096]{2,1,0:T(8,128)(2,1)S(1)}, bf16[2,512,4096]{2,1,0:T(8,128)(2,1)}, u32[]{:S(2)}) copy-start(bf16[2,512,4096]{2,1,0:T(8,128)(2,1)} %all-gather.5.cloned.1.call-done) | copy-start | bytes 25165828
  186.7 9.2 %copy-start.10 = (bf16[512,1024]{1,0:T(8,128)(2,1)S(1)}, bf16[512,1024]{1,0:T(8,128)(2,1)}, u32[]{:S(2)}) copy-start(bf16[512,1024]{1,0:T(8,128)(2,1)} %get-tuple-element.20) | copy-start | bytes 3145732
  191.7 1.5 copy-start.7
  193.3 14.6 %collective-permute-start.10 = (bf16[128,2048]{1,0:T(8,128)(2,1)}, bf16[128,2048]{1,0:T(8,128)(2,1)S(1)}, u32[]{:S(2)}, u32[]{:S(2)}) collective-permute-start(bf16[128,2048]{1,0:T(8,128)(2,1)} %constant_dynamic-slice_fusion), channel_id=1, source_target_pairs={{0,3},{1,0},{2,1},{3,2},{4,7},{5,4},{6,5},{7,6},{8,11},{9,8},{10,9... | collective-permute-start | bytes 1572872 | tf_op jit(solution)/shard_map/ppermute | solution.py:387
  198.3 1.4 copy-start.6
  200.5 15.3 %collective-permute-start.7 = (bf16[128,2048]{1,0:T(8,128)(2,1)}, bf16[128,2048]{1,0:T(8,128)(2,1)}, u32[]{:S(2)}, u32[]{:S(2)}) collective-permute-start(bf16[128,2048]{1,0:T(8,128)(2,1)} %constant_dynamic-slice_fusion.1), channel_id=1, source_target_pairs={{0,1},{1,2},{2,3},{3,0},{4,5},{5,6},{6,7},{7,4},{8,9},{9,10},{10,1... | collective-permute-start | bytes 1572872 | tf_op jit(solution)/shard_map/ppermute | solution.py:387
  209.8 24.0 %copy-start.1 = (bf16[512,512]{1,0:T(8,128)(2,1)S(1)}, bf16[512,512]{1,0:T(8,128)(2,1)}, u32[]{:S(2)}) copy-start(bf16[512,512]{1,0:T(8,128)(2,1)} %copy-done) | copy-start | bytes 1572868
  209.8 14.6 %collective-permute-start.11 = (bf16[128,2048]{1,0:T(8,128)(2,1)}, bf16[128,2048]{1,0:T(8,128)(2,1)}, u32[]{:S(2)}, u32[]{:S(2)}) collective-permute-start(bf16[128,2048]{1,0:T(8,128)(2,1)} %add_convert_fusion.1), channel_id=1, source_target_pairs={{0,3},{1,0},{2,1},{3,2},{4,7},{5,4},{6,5},{7,6},{8,11},{9,8},{10,9... | collective-permute-start | bytes 1572872 | tf_op jit(solution)/shard_map/ppermute | solution.py:387
  218.0 14.5 %collective-permute-start.8 = (bf16[128,2048]{1,0:T(8,128)(2,1)}, bf16[128,2048]{1,0:T(8,128)(2,1)}, u32[]{:S(2)}, u32[]{:S(2)}) collective-permute-start(bf16[128,2048]{1,0:T(8,128)(2,1)} %add_convert_fusion.3), channel_id=1, source_target_pairs={{0,1},{1,2},{2,3},{3,0},{4,5},{5,6},{6,7},{7,4},{8,9},{9,10},{10,1... | collective-permute-start | bytes 1572872 | tf_op jit(solution)/shard_map/ppermute | solution.py:387
  225.8 13.6 %collective-permute-start.12 = (bf16[128,2048]{1,0:T(8,128)(2,1)S(1)}, bf16[128,2048]{1,0:T(8,128)(2,1)S(1)}, u32[]{:S(2)}, u32[]{:S(2)}) collective-permute-start(bf16[128,2048]{1,0:T(8,128)(2,1)S(1)} %add_convert_fusion), channel_id=1, source_target_pairs={{0,3},{1,0},{2,1},{3,2},{4,7},{5,4},{6,5},{7,6},{8,11},{9,8},{10,9... | collective-permute-start | bytes 1572872 | tf_op jit(solution)/shard_map/ppermute | solution.py:387
  233.8 13.4 %collective-permute-start.9 = (bf16[128,2048]{1,0:T(8,128)(2,1)S(1)}, bf16[128,2048]{1,0:T(8,128)(2,1)S(1)}, u32[]{:S(2)}, u32[]{:S(2)}) collective-permute-start(bf16[128,2048]{1,0:T(8,128)(2,1)S(1)} %add_convert_fusion.2), channel_id=1, source_target_pairs={{0,1},{1,2},{2,3},{3,0},{4,5},{5,6},{6,7},{7,4},{8,9},{9,10},{10,1... | collective-permute-start | bytes 1572872 | tf_op jit(solution)/shard_map/ppermute | solution.py:387
Sparse Core Ops, SparseCore 0:
  10.0 112.8 all-gather.2
  124.6 62.1 all-gather.4

commit v3 on v2

--- a/solution.py
+++ b/solution.py
@@ -41,9 +41,9 @@
     return jnp.concatenate([first_half, second_half], axis=0)
 
 
-def collect_blocks(shard, after):
+def collect_blocks(shard):
     stacked = shard[None]
-    theirs, _ = lax.optimization_barrier((swapped(stacked, TENSOR, 2), after))
+    theirs = swapped(stacked, TENSOR, 2)
     return ordered_pair(stacked, theirs, 2)
 
 
@@ -64,28 +64,36 @@
     )
 
 
-def prepare_kernel(table_ref, tiles_ref):
-    columns = table_ref.shape[0]
-    tile_count = tiles_ref.shape[0] // 2
-    lane = lax.broadcasted_iota(jnp.int32, (columns, LANES), 1).astype(jnp.int16)
-    unroll = min(32, tile_count)
-
-    def prepare(step, carry):
-        first = jnp.minimum(step * unroll, tile_count - unroll)
-        for u in range(unroll):
-            t = first + u
-            tile = table_ref[:, pl.ds(pl.multiple_of(t * LANES, LANES), LANES)]
-            tiles_ref[t] = tile
-            tiles_ref[t + tile_count] = lane_gather(tile, lane ^ jnp.int16(LANES // 2))
-        return carry
-
-    lax.fori_loop(0, -(-tile_count // unroll), prepare, 0)
-
-
-def lookup_kernel(slots_ref, lanes_ref, tiles_ref, out_ref):
+def lookup_kernel(slots_ref, lanes_ref, table_ref, out_ref, table, tiles, arrived):
     groups, columns, row_count = out_ref.shape
+    tile_count = tiles.shape[0] // 2
+    slabs = arrived.shape[0]
+    slab = tile_count // slabs
     lane = lax.broadcasted_iota(jnp.int32, (columns, LANES), 1).astype(jnp.int16)
     left = lane < jnp.int16(LANES // 2)
+    unroll = min(32, slab)
+
+    def incoming(k):
+        part = pl.ds(k * slab * LANES, slab * LANES)
+        return pltpu.make_async_copy(table_ref.at[:, part], table.at[:, part], arrived.at[k])
+
+    for k in range(slabs):
+        incoming(k).start()
+
+    for k in range(slabs):
+        incoming(k).wait()
+
+        def prepare(step, carry, k=k):
+            first = k * slab + jnp.minimum(step * unroll, slab - unroll)
+            for u in range(unroll):
+                t = first + u
+                tile = table[:, pl.ds(pl.multiple_of(t * LANES, LANES), LANES)]
+                tiles[t] = tile
+                tiles[t + tile_count] = lane_gather(tile, lane ^ jnp.int16(LANES // 2))
+            return carry
+
+        lax.fori_loop(0, -(-slab // unroll), prepare, 0)
+
     per_group = row_count // LANES
     together = 2
 
@@ -99,7 +107,7 @@
             picked = jnp.zeros((columns, LANES), jnp.bfloat16)
             for i in range(0, LANES, 2):
                 pair = jnp.where(
-                    left, tiles_ref[slots_ref[first + i]], tiles_ref[slots_ref[first + i + 1]]
+                    left, tiles[slots_ref[first + i]], tiles[slots_ref[first + i + 1]]
                 )
                 picked = jnp.where(lane >= jnp.int16(i), lane_gather(pair, wanted), picked)
             place = pl.multiple_of(lax.rem(block, per_group) * LANES, LANES)
@@ -109,28 +117,16 @@
     lax.fori_loop(0, groups * per_group // together, one_block, 0)
 
 
-def prepared(embed_table):
+def lookup(embed_table, token_ids, group_count):
     columns, vocab_size = embed_table.shape
-    return pl.pallas_call(
-        prepare_kernel,
-        out_shape=jax.ShapeDtypeStruct((2 * vocab_size // LANES, columns, LANES), jnp.bfloat16),
-        in_specs=[pl.BlockSpec(memory_space=pltpu.VMEM)],
-        out_specs=pl.BlockSpec(memory_space=pltpu.VMEM),
-        compiler_params=pltpu.CompilerParams(vmem_limit_bytes=4 * 2**20),
-        cost_estimate=pl.CostEstimate(
-            flops=8_000_000_000, bytes_accessed=embed_table.size * 6, transcendentals=0
-        ),
-        name="prepare",
-    )(embed_table)
-
-
-def lookup(tiles, token_ids, group_count):
-    tile_count, columns = tiles.shape[0] // 2, tiles.shape[1]
+    tile_count = vocab_size // LANES
+    slabs = next(k for k in (6, 4, 3, 2, 1) if tile_count % k == 0)
     count = token_ids.shape[0]
+    half = LANES // 2
     odd = jnp.arange(count, dtype=jnp.int32) & 1
     lane = token_ids & (LANES - 1)
-    half = LANES // 2
-    slots = lax.shift_right_logical(token_ids, 7) + tile_count * (lax.shift_right_logical(lane, 6) ^ odd)
+    swapped_half = lax.shift_right_logical(lane, 6) ^ odd
+    slots = lax.shift_right_logical(token_ids, 7) + tile_count * swapped_half
     lanes = ((lane & (half - 1)) | (odd * half)).reshape(count // LANES, LANES)
     return pl.pallas_call(
         lookup_kernel,
@@ -138,15 +134,20 @@
         in_specs=[
             pl.BlockSpec(memory_space=pltpu.SMEM),
             pl.BlockSpec(memory_space=pltpu.VMEM),
-            pl.BlockSpec(memory_space=pltpu.VMEM),
+            pl.BlockSpec(memory_space=pltpu.HBM),
         ],
         out_specs=pl.BlockSpec(memory_space=pltpu.VMEM),
-        compiler_params=pltpu.CompilerParams(vmem_limit_bytes=4 * 2**20),
+        scratch_shapes=[
+            pltpu.VMEM((columns, vocab_size), jnp.bfloat16),
+            pltpu.VMEM((2 * tile_count, columns, LANES), jnp.bfloat16),
+            pltpu.SemaphoreType.DMA((slabs,)),
+        ],
+        compiler_params=pltpu.CompilerParams(vmem_limit_bytes=60 * 2**20),
         cost_estimate=pl.CostEstimate(
-            flops=30_000_000_000, bytes_accessed=tiles.size * 2, transcendentals=0
+            flops=30_000_000_000, bytes_accessed=embed_table.size * 2, transcendentals=0
         ),
         name="lookup",
-    )(slots, lanes, tiles)
+    )(slots, lanes, embed_table)
 
 
 def transposed_product(rows_ref, weight_ref):
@@ -178,16 +179,16 @@
 
 
 def weight_spec(weights, turn, share, which):
-    dp_count, _, plane, _, columns, width = weights.shape
+    _, plane, _, columns, width = weights.shape
     return pl.BlockSpec(
-        (dp_count // share, 1, plane, 1, columns, width),
-        lambda b, places: (which, b, 0, places[turn], 0, 0),
+        (1, plane // share, 1, columns, width),
+        lambda b, places: (b, which, places[turn], 0, 0),
     )
 
 
 def project(places, weights, parts, carried=None):
     row_count = parts[0][0].shape[1]
-    blocks, width = weights.shape[1], weights.shape[-1]
+    blocks, width = weights.shape[0], weights.shape[-1]
     in_specs = [pl.BlockSpec(rows.shape, lambda b, places: (0, 0)) for rows, *_ in parts]
     in_specs += [weight_spec(weights, *where) for _, *where in parts]
     total_spec = pl.BlockSpec((row_count, width), lambda b, places: (0, b))
@@ -268,7 +269,7 @@
 
 def attend(places, weights, parts, carried, length, cosine, sine, model_width):
     row_count = cosine.shape[0]
-    blocks, width = weights.shape[1], weights.shape[-1]
+    blocks, width = weights.shape[0], weights.shape[-1]
     query_width = HEADS // KVH * HD
     in_specs = [pl.BlockSpec(memory_space=pltpu.SMEM)]
     in_specs += [pl.BlockSpec(rows.shape, lambda b, places: (0, 0)) for rows, *_ in parts]
@@ -369,25 +370,107 @@
     return [(k, (k + way) % count) for k in range(count)]
 
 
-def ring_reduced(attended, weight, quarter):
+def product_kernel(places_ref, rows_ref, *refs, ring):
+    out_ref = refs[-1]
+    width = refs[0].shape[-1]
+    for k, weight_ref in enumerate(refs[:-1]):
+        _, halves, depth, _ = weight_ref.shape
+        total = None
+        for half in range(halves):
+            block = places_ref[ring] ^ half
+            rows = rows_ref[:, pl.ds(pl.multiple_of(block * depth, depth), depth)]
+            term = jnp.dot(rows, weight_ref[0, half], preferred_element_type=jnp.float32)
+            total = term if total is None else total + term
+        out_ref[:, k * width : (k + 1) * width] = total.astype(out_ref.dtype)
+
+
+def product(places, rows, weights):
+    sides, halves, depth, width = weights[0].shape
+    row_count = rows.shape[0]
+    wide = len(weights) * width
+    return pl.pallas_call(
+        functools.partial(product_kernel, ring=places.shape[0] - 3),
+        grid_spec=pltpu.PrefetchScalarGridSpec(
+            num_scalar_prefetch=1,
+            grid=(sides,),
+            in_specs=[pl.BlockSpec(rows.shape, lambda j, places: (0, 0))]
+            + [pl.BlockSpec((1, halves, depth, width), lambda j, places: (j, 0, 0, 0))]
+            * len(weights),
+            out_specs=pl.BlockSpec((row_count, wide), lambda j, places: (0, j)),
+        ),
+        out_shape=jax.ShapeDtypeStruct((row_count, sides * wide), jnp.bfloat16),
+        compiler_params=pltpu.CompilerParams(vmem_limit_bytes=16 * 2**20),
+        cost_estimate=pl.CostEstimate(
+            flops=2 * row_count * halves * depth * wide * sides,
+            bytes_accessed=2 * (rows.size + halves * depth * wide * sides),
+            transcendentals=0,
+        ),
+        name="product",
+    )(places, rows, *weights)
+
+
+def finish_kernel(where_ref, rows_ref, *refs, width):
+    hidden_ref = refs[-1]
+    chunks = (len(refs) - 1) // 4
+    layers = refs[0].shape[1] // width // 2
+    for chunk in range(chunks):
+        for core in range(2):
+            at = 2 * (2 * chunk + core)
+            for j in range(2 * layers):
+                z = lax.rem(where_ref[0] + chunks * layers - chunk * layers - j % layers, chunks * layers)
+                column = (z * 2 + (where_ref[1] ^ (j // layers))) * 2 + (where_ref[2] ^ core)
+                here = slice(j * width, (j + 1) * width)
+                there = pl.ds(pl.multiple_of(column * width, width), width)
+                total = refs[at][:, here].astype(jnp.float32) + refs[at + 1][:, here].astype(
+                    jnp.float32
+                )
+                hidden_ref[:, there] = (
+                    rows_ref[:, there].astype(jnp.float32) + total
+                ).astype(jnp.bfloat16)
+
+
+def finish(where, rows, sums, width):
+    return pl.pallas_call(
+        functools.partial(finish_kernel, width=width),
+        out_shape=jax.ShapeDtypeStruct(rows.shape, jnp.bfloat16),
+        in_specs=[pl.BlockSpec(memory_space=pltpu.SMEM)]
+        + [pl.BlockSpec(memory_space=pltpu.VMEM)] * (1 + len(sums)),
+        out_specs=pl.BlockSpec(memory_space=pltpu.VMEM),
+        compiler_params=pltpu.CompilerParams(vmem_limit_bytes=16 * 2**20),
+        cost_estimate=pl.CostEstimate(
+            flops=4 * rows.size, bytes_accessed=8 * rows.size, transcendentals=0
+        ),
+        name="finish",
+    )(where, rows, *sums)
+
+
+CHUNKS = 2
+
+
+def ring_sums(places, attended, weights, quarter):
     place = lax.axis_index(RING)
     count = lax.axis_size(RING)
-    half = weight.shape[1] // 2
+    each = len(weights[0]) // CHUNKS
     sums = []
-    for way, columns in ((1, weight[:, :half]), (-1, weight[:, half:])):
-        product = lax.optimization_barrier(
-            jnp.dot(attended, columns, preferred_element_type=jnp.float32).astype(jnp.bfloat16)
-        )
-
-        def part(turn):
-            return lax.dynamic_slice_in_dim(product, (place + turn) % count * quarter, quarter, 0)
-
-        running = part(-way)
-        for step in range(1, count):
-            running = lax.ppermute(running.astype(jnp.bfloat16), RING, ring_route(way))
-            running = running.astype(jnp.float32) + part(-way * (step + 1)).astype(jnp.float32)
-        sums.append(running)
-    return jnp.concatenate(sums, axis=1)
+    for chunk in range(CHUNKS):
+        for side, way in enumerate((1, -1)):
+            partial_sums = product(
+                places, attended, weights[side][chunk * each : (chunk + 1) * each]
+            )
+
+            def part(turn):
+                start = (place + turn) % count * quarter
+                return lax.dynamic_slice_in_dim(partial_sums, start, quarter, 0)
+
+            running = part(-way)
+            for step in range(1, count):
+                running = lax.ppermute(running, RING, ring_route(way))
+                mine = part(-way * (step + 1))
+                if step + 1 < count:
+                    running = running.astype(jnp.float32) + mine.astype(jnp.float32)
+                    running = running.astype(jnp.bfloat16)
+            sums += [running, mine]
+    return sums
 
 
 def sublayer(prompt_ids, prompt_lengths, embed_table, norm_gain, w_query, w_key, w_value, w_out):
@@ -397,7 +480,6 @@
     columns = embed_table.shape[0]
     model_width = columns * devices
     group_count = devices // TPG
-    dp_count = lax.axis_size(DP)
     place = lax.axis_index(RING)
     ring = lax.axis_size(RING)
     group_index = lax.axis_index(DP) * lax.axis_size("tensor_0") + lax.axis_index("tensor_0")
@@ -408,10 +490,8 @@
     gain = lax.dynamic_slice_in_dim(norm_gain, lax.axis_index(DP) * depth, depth, 0)
     packed = jnp.concatenate([w_query, w_key, w_value], axis=1).astype(jnp.float32)
     packed = (packed * gain[:, None]).astype(jnp.bfloat16)
-    w_in = lax.all_gather(packed, PLANE, axis=0, tiled=True).reshape(
-        dp_count, devices // ring // dp_count, devices // ring // dp_count, ring, columns, -1
-    )
-
+    w_in = lax.all_gather(collect_blocks(packed), DP, axis=1, tiled=True)
+    w_in = w_in.reshape(w_in.shape[0], -1, ring, columns, w_in.shape[-1])
     all_ids = lax.all_to_all(
         jnp.broadcast_to(prompt_ids[None], (devices, quarter)),
         DP_TENSOR,
@@ -419,11 +499,32 @@
         concat_axis=0,
         tiled=True,
     ).reshape(-1)
-    tiles = prepared(embed_table)
-    outgoing = lookup(tiles, all_ids, group_count)
-    w_back = lax.all_gather(collect_blocks(w_out, outgoing), DP, axis=2, tiled=True)
+    pieces_x = [w_out]
+    for axes, route in (
+        ("tensor_0", [(0, 1), (1, 0)]),
+        ("dp_1", [(0, 1), (1, 0)]),
+        (("dp_1", "tensor_0"), [(0, 3), (1, 2), (2, 1), (3, 0)]),
+    ):
+        pieces_x.append(lax.ppermute(w_out, axes, route))
+    outgoing = lookup(embed_table, all_ids, group_count)
     own = lax.all_to_all(outgoing, PLANE, split_axis=0, concat_axis=0, tiled=True).reshape(
         -1, row_count
+    )
+    pieces_x, _ = lax.optimization_barrier((pieces_x, outgoing))
+    w_mine = [jnp.stack(pieces_x).reshape(2, 2, *w_out.shape)]
+    layers = lax.axis_size("dp_0")
+    for k in range(1, layers):
+        route = [(z, (z + k) % layers) for z in range(layers)]
+        w_mine.append(lax.ppermute(w_mine[0], "dp_0", route))
+    w_other = []
+    for k in range(layers):
+        w_other.append(lax.ppermute(w_mine[k], "dp_2", [(0, 1), (1, 0)]))
+
+    places = jnp.concatenate(
+        [
+            (place + jnp.arange(ring, dtype=jnp.int32)) % ring,
+            jnp.stack([lax.axis_index(name) for name in ("tensor_0", "dp_1", "dp_2")]),
+        ]
     )
     half = own.shape[0] // 2
     low, high = own[:half], own[half:]
@@ -434,7 +535,6 @@
     low_across = lax.ppermute(low_before, RING, ring_route(1))
     high_across = lax.ppermute(high_after, RING, ring_route(-1))
 
-    places = (place + jnp.arange(ring, dtype=jnp.int32)) % ring
     first = project(places, w_in, [(own, 0, 1, 0)])
     second = project(
         places,
@@ -462,8 +562,9 @@
     pieces, _ = lax.optimization_barrier((pieces, attended))
     own_rows = residual(places, pieces, columns, quarter)
 
-    summed = ring_reduced(attended, w_back.reshape(-1, model_width), quarter)
-    hidden = (own_rows.astype(jnp.float32) + summed).astype(jnp.bfloat16)
+    sums = ring_sums(places, attended, (w_mine, w_other), quarter)
+    where = jnp.stack([lax.axis_index(name) for name in DP])
+    hidden = finish(where, own_rows, sums, w_out.shape[1])
     return hidden, cache[None]
 
 

time: 258 us -> 276 us (1.070)
  waiting for transfers between devices: 78.3 us -> 104 us
  Pallas kernels: 61.4 us -> 79.4 us
  local copies, waits for them, and re-layouts: 22.5 us -> 4.55 us
  starting transfers between devices: 32 us -> 45.4 us
  matrix products: 7.32 us -> 0 us
  other arithmetic: 15.1 us -> 8.32 us
  blocking collectives: 25.4 us -> 18.7 us
    ppermute x6 -> x22, waiting for transfers between devices: 29.2 us -> 82 us  [the longest x3 38.5 us: sublayer(): w_mine.append(lax.ppermute(w_mine[0], 'dp_0', route))]
    all_gather x2 -> x1, waiting for transfers between devices: 41.9 us -> 0.01 us  [sublayer(): w_in = lax.all_gather(collect_blocks(packed), DP, axis=1, tiled=True)]
    ppermute x6 -> x22, starting transfers between devices: 10.1 us -> 27.3 us  [the longest x12 18.5 us: ring_sums(): running = lax.ppermute(running, RING, ring_route(way))]
    unnamed x24 -> x12, local copies, waits for them, and re-layouts: 17 us -> 1.24 us
    ppermute x1, waiting for transfers between devices: 0.01 us -> 11 us  [swapped(): return lax.ppermute(block, axis, route)]
    ppermute x1, waiting for transfers between devices: 0.01 us -> 9.42 us  [sublayer(): low_across = lax.ppermute(low_before, RING, ring_route(1))]
    pallas_call x1 -> x5, Pallas kernels: 4.48 us -> 13.7 us  [the longest x4 11.7 us: product(): pl.pallas_call(functools.partial(product_kernel, ring=places.shape[0] - 3...]
    pallas_call x1, Pallas kernels: 27.1 us -> 35.6 us  [lookup(): pl.pallas_call(lookup_kernel, out_shape=jax.ShapeDtypeStruct((group_count...]
  transfers between devices with their start and end apart: 16 -> 31, of which waited for: 11 -> 12; matrix products, arithmetic and copies ran while one was open for 7% -> 3% of each run, Pallas kernels for 24% -> 28%
where the time goes in v3:
time: 276 us; the launch traced here: 274 us
  waiting for transfers between devices  104 us (38%)
  Pallas kernels  79.4 us (29%)
  starting transfers between devices  45.4 us (16%)
  blocking collectives  18.7 us (7%)
  between operations  14.4 us (5%)
  other arithmetic  8.32 us (3%)
  local copies, waits for them, and re-layouts  4.55 us (2%)
    ppermute x3, waiting for transfers between devices, sublayer(): w_mine.append(lax.ppermute(w_mine[0], 'dp_0', route))  38.5 us
    pallas_call x1, Pallas kernels, lookup(): pl.pallas_call(lookup_kernel, out_shape=jax.ShapeDtypeStruct((group_count...  35.6 us
    ppermute x3, waiting for transfers between devices, sublayer(): pieces_x.append(lax.ppermute(w_out, axes, route))  28.3 us
    all_to_all x1, blocking collectives, sublayer(): lax.all_to_all(jnp.broadcast_to(prompt_ids[None], (devices, quarter)), DP...  18.7 us
    ppermute x12, starting transfers between devices, ring_sums(): running = lax.ppermute(running, RING, ring_route(way))  18.5 us
    ppermute x12, waiting for transfers between devices, ring_sums(): running = lax.ppermute(running, RING, ring_route(way))  15.3 us
    pallas_call x1, Pallas kernels, attend(): pl.pallas_call(functools.partial(attention_kernel, parts=len(parts), mode...  14.3 us
    pallas_call x2, Pallas kernels, project(): pl.pallas_call(functools.partial(project_kernel, parts=len(parts), carrie...  13.6 us
  transfers between devices with their start and end apart: 31, of which 12 were waited for; matrix products, arithmetic and copies ran while one was open for 3% of the time, Pallas kernels for 28%

profile of v3, /device:TPU:6, one launch (start us, length us, event | category | flops | bytes accessed | tf_op | source)
XLA Modules:
  0.0 274.4 jit_solution(6481643360518009321)
XLA Ops:
  7.2 0.8 dynamic_slice.55
  8.0 1.2 multiply_convert_fusion
  9.2 1.5 collective-permute-start.6
  10.6 11.0 %collective-permute-done.6 = bf16[1,256,768]{2,1,0:T(8,128)(2,1)S(1)} collective-permute-done((bf16[1,256,768]{2,1,0:T(8,128)(2,1)S(1)}, bf16[1,256,768]{2,1,0:T(8,128)(2,1)S(1)}, u32[]{:S(2)}, u32[]{:S(2)}) %collective-permute-start.6) | collective-permute-done | bytes 393248 | tf_op jit(solution)/shard_map/ppermute | solution.py:34
  21.6 1.0 pad_maximum_fusion.1
  23.3 18.7 %all_to_all.11 = s32[128,1,128]{2,1,0:T(1,128)S(1)} all-to-all(s32[128,1,128]{2,1,0:T(1,128)S(1)} %broadcast_in_dim.4), channel_id=1, replica_groups=mesh['dp_0'=4,'dp_1'=2,'dp_2'=2,'tensor_0'=2,'tensor_1'=4] {'dp_0','dp_1..., dimensions={0} | all-to-all | bytes 131072 | tf_op jit(solution)/shard_map/all_to_all | solution.py:495
  43.4 35.6 %lookup.1 = bf16[32,32,512]{2,1,0:T(8,128)(2,1)} custom-call(s32[16384]{0:T(1024)} %fusion.2.slots_ref, s32[128,128]{1,0:T(8,128)} %bitcast_or_fusion.lanes_ref, bf16[32,128256]{1,0:T(8,128)(2,1)} %table_ref.1), custom_call_target="tpu_custom_call" | custom-call | flops 30000001024 | bytes 8208384 | tf_op jit(solution)/shard_map/lookup/pallas_call | solution.py:131
  79.0 5.8 %all-to-all-start.1 = ((bf16[32,32,512]{2,1,0:T(8,128)(2,1)}), bf16[32,32,512]{2,1,0:T(8,128)(2,1)S(1)}, u32[]{:S(2)}, u32[]{:S(2)}) async-start(bf16[32,32,512]{2,1,0:T(8,128)(2,1)} %lookup.1), calls=%async_computation.1 | async-start | bytes 2097152 | tf_op jit(solution)/shard_map/all_to_all | solution.py:510
  84.8 1.5 collective-permute-start.7
  86.3 2.6 collective-permute-start.9
  89.0 23.4 %collective-permute-done.7 = bf16[512,256]{1,0:T(8,128)(2,1)S(1)} collective-permute-done((bf16[512,256]{1,0:T(8,128)(2,1)S(1)}, bf16[512,256]{1,0:T(8,128)(2,1)S(1)}, u32[]{:S(2)}, u32[]{:S(2)}) %collective-permute-start.7) | collective-permute-done | bytes 262176 | tf_op jit(solution)/shard_map/ppermute | solution.py:508
  112.4 4.9 %collective-permute-done.8 = bf16[512,256]{1,0:T(8,128)(2,1)S(1)} collective-permute-done((bf16[512,256]{1,0:T(8,128)(2,1)S(1)}, bf16[512,256]{1,0:T(8,128)(2,1)S(1)}, u32[]{:S(2)}, u32[]{:S(2)}) %collective-permute-start.8) | collective-permute-done | bytes 262176 | tf_op jit(solution)/shard_map/ppermute | solution.py:508
  117.5 3.3 %collective-permute-start.20 = (bf16[2,2,512,256]{3,2,1,0:T(8,128)(2,1)S(1)}, bf16[2,2,512,256]{3,2,1,0:T(8,128)(2,1)}, u32[]{:S(2)}, u32[]{:S(2)}) collective-permute-start(bf16[2,2,512,256]{3,2,1,0:T(8,128)(2,1)S(1)} %bitcast.30), channel_id=1, source_target_pairs={{0,96},{32,0},{64,32},{96,64},{1,97},{33,1},{65,33},{97,65},{2,98}... | collective-permute-start | bytes 3145736 | tf_op jit(solution)/shard_map/ppermute | solution.py:518
  120.8 0.8 collective-permute-start.10
  121.5 1.1 fusion.4
  122.6 1.5 collective-permute-start.2
  124.1 1.7 collective-permute-start.1
  125.9 19.3 %collective-permute-done.19.refs_0_ = bf16[2,2,512,256]{3,2,1,0:T(8,128)(2,1)} collective-permute-done((bf16[2,2,512,256]{3,2,1,0:T(8,128)(2,1)S(1)}, bf16[2,2,512,256]{3,2,1,0:T(8,128)(2,1)}, u32[]{:S(2)}, u32[]{:S(2)}) %collective-permute-start.19) | collective-permute-done | bytes 1048608 | tf_op jit(solution)/shard_map/ppermute | solution.py:518
  145.1 2.8 %collective-permute-start = (bf16[512,512]{1,0:T(8,128)(2,1)}, bf16[512,512]{1,0:T(8,128)(2,1)}, u32[]{:S(2)}, u32[]{:S(2)}) collective-permute-start(bf16[512,512]{1,0:T(8,128)(2,1)} %bitcast.9), channel_id=1, source_target_pairs={{0,3},{1,0},{2,1},{3,2},{4,7},{5,4},{6,5},{7,6},{8,11},{9,8},{10,9... | collective-permute-start | bytes 1572872 | tf_op jit(solution)/shard_map/ppermute | solution.py:534
  147.9 19.2 %collective-permute-done.20.refs_1_ = bf16[2,2,512,256]{3,2,1,0:T(8,128)(2,1)} collective-permute-done((bf16[2,2,512,256]{3,2,1,0:T(8,128)(2,1)S(1)}, bf16[2,2,512,256]{3,2,1,0:T(8,128)(2,1)}, u32[]{:S(2)}, u32[]{:S(2)}) %collective-permute-start.20) | collective-permute-done | bytes 1048608 | tf_op jit(solution)/shard_map/ppermute | solution.py:518
  167.2 1.5 collective-permute-start.5
  168.7 1.5 collective-permute-start.3
  170.2 1.8 fusion
  172.6 2.1 pad_maximum_fusion.2
  175.2 1.8 collective-permute-start.4
  177.1 5.2 %project.2 = (f32[512,1536]{1,0:T(8,128)}, f32[1,512]{1,0:T(1,128)S(1)}) custom-call(s32[7]{0:T(128)S(1)} %pad_add_fusion.1.places_ref, bf16[1024,512]{1,0:T(8,128)(2,1)S(1)} %bitcast.27, bf16[2,32,4,32,768]{4,3,2,1,0:T(8,128)(2,1)} %bitcast.34), custom_call_target="tpu_custom_call" | custom-call | flops 1610612736 | bytes 4194304 | tf_op jit(solution)/shard_map/project/pallas_call | solution.py:201
  182.4 1.1 collective-permute-done.5.refs_1_.refs_6_
  183.5 9.4 %collective-permute-done.3.refs_0_.refs_3_ = bf16[512,512]{1,0:T(8,128)(2,1)} collective-permute-done((bf16[512,512]{1,0:T(8,128)(2,1)S(1)}, bf16[512,512]{1,0:T(8,128)(2,1)}, u32[]{:S(2)}, u32[]{:S(2)}) %collective-permute-start.3) | collective-permute-done | bytes 524320 | tf_op jit(solution)/shard_map/ppermute | solution.py:535
  192.9 8.4 %project.3 = (f32[512,1536]{1,0:T(8,128)}, f32[1,512]{1,0:T(1,128)S(1)}) custom-call(s32[7]{0:T(128)S(1)} %pad_add_fusion.1.places_ref, bf16[512,512]{1,0:T(8,128)(2,1)S(1)} %collective-permute-done.2.refs_0_.refs_5_, bf16[512,512]{1,0:T(8,128)(2,1)} %collective-permute-done.5.refs_1_.refs_6_, bf16[512,512]{1,0:T(8,128)(2,1)} %collective-permute-done.refs_2_.refs_1_, ...), custom_call_target="tpu_custom_call" | custom-call | flops 3221225472 | bytes 8388608 | tf_op jit(solution)/shard_map/project/pallas_call | solution.py:201
  201.3 14.3 %attend.1 = (bf16[512,1024]{1,0:T(8,128)(2,1)}, bf16[2,512,256]{2,1,0:T(8,128)(2,1)}) custom-call(s32[7]{0:T(128)S(1)} %pad_add_fusion.1.places_ref, s32[1]{0:T(128)} %dynamic_slice.54.length_ref, bf16[512,512]{1,0:T(8,128)(2,1)} %collective-permute-done.3.refs_0_.refs_3_, bf16[512,512]{1,0:T(8,128)(2,1)} %collective-permute-done.4.refs_1_.refs_4_, ...), custom_call_target="tpu_custom_call" | custom-call | flops 4000000000 | bytes 9000000 | tf_op jit(solution)/shard_map/attend/pallas_call | solution.py:283
  215.7 1.2 copy-done
  216.9 3.3 %product.7 = bf16[512,1024]{1,0:T(8,128)(2,1)S(1)} custom-call(s32[7]{0:T(128)S(1)} %pad_add_fusion.1.places_ref, bf16[512,1024]{1,0:T(8,128)(2,1)S(1)} %copy-done, bf16[2,2,512,256]{3,2,1,0:T(8,128)(2,1)} %collective-permute-done.24.refs_0_, bf16[2,2,512,256]{3,2,1,0:T(8,128)(2,1)} %collective-permute-done.25.refs_1_), custom_call_target="tpu_custom_call" | custom-call | flops 1073741824 | bytes 3145728 | tf_op jit(solution)/shard_map/product/pallas_call | solution.py:391
  220.2 1.6 collective-permute-start.26
  221.9 3.3 %product.6 = bf16[512,1024]{1,0:T(8,128)(2,1)S(1)} custom-call(s32[7]{0:T(128)S(1)} %pad_add_fusion.1.places_ref, bf16[512,1024]{1,0:T(8,128)(2,1)S(1)} %copy-done, bf16[2,2,512,256]{3,2,1,0:T(8,128)(2,1)} %collective-permute-done.19.refs_0_, bf16[2,2,512,256]{3,2,1,0:T(8,128)(2,1)} %collective-permute-done.20.refs_1_), custom_call_target="tpu_custom_call" | custom-call | flops 1073741824 | bytes 3145728 | tf_op jit(solution)/shard_map/product/pallas_call | solution.py:391
  225.7 2.1 product.5
  227.9 2.8 %collective-permute-start.16 = (bf16[128,1024]{1,0:T(8,128)(2,1)S(1)}, bf16[128,1024]{1,0:T(8,128)(2,1)S(1)}, u32[]{:S(2)}, u32[]{:S(2)}) collective-permute-start(bf16[128,1024]{1,0:T(8,128)(2,1)S(1)} %get-tuple-element.41), channel_id=1, source_target_pairs={{0,3},{1,0},{2,1},{3,2},{4,7},{5,4},{6,5},{7,6},{8,11},{9,8},{10,9... | collective-permute-start | bytes 786440 | tf_op jit(solution)/shard_map/ppermute | solution.py:467
  230.7 3.1 %product.4 = bf16[512,1024]{1,0:T(8,128)(2,1)S(1)} custom-call(s32[7]{0:T(128)S(1)} %pad_add_fusion.1.places_ref, bf16[512,1024]{1,0:T(8,128)(2,1)S(1)} %copy-done, bf16[2,2,512,256]{3,2,1,0:T(8,128)(2,1)S(1)} %bitcast.33, bf16[2,2,512,256]{3,2,1,0:T(8,128)(2,1)} %collective-permute-done.10.refs_1_), custom_call_target="tpu_custom_call" | custom-call | flops 1073741824 | bytes 3145728 | tf_op jit(solution)/shard_map/product/pallas_call | solution.py:391
  234.0 3.3 %collective-permute-start.27 = (bf16[128,1024]{1,0:T(8,128)(2,1)S(1)}, bf16[128,1024]{1,0:T(8,128)(2,1)S(1)}, u32[]{:S(2)}, u32[]{:S(2)}) collective-permute-start(bf16[128,1024]{1,0:T(8,128)(2,1)S(1)} %add_convert_fusion.1), channel_id=1, source_target_pairs={{0,3},{1,0},{2,1},{3,2},{4,7},{5,4},{6,5},{7,6},{8,11},{9,8},{10,9... | collective-permute-start | bytes 786440 | tf_op jit(solution)/shard_map/ppermute | solution.py:467
  237.6 3.3 %collective-permute-start.17 = (bf16[128,1024]{1,0:T(8,128)(2,1)S(1)}, bf16[128,1024]{1,0:T(8,128)(2,1)S(1)}, u32[]{:S(2)}, u32[]{:S(2)}) collective-permute-start(bf16[128,1024]{1,0:T(8,128)(2,1)S(1)} %add_convert_fusion.5), channel_id=1, source_target_pairs={{0,3},{1,0},{2,1},{3,2},{4,7},{5,4},{6,5},{7,6},{8,11},{9,8},{10,9... | collective-permute-start | bytes 786440 | tf_op jit(solution)/shard_map/ppermute | solution.py:467
  240.9 3.5 %collective-permute-done.11 = bf16[128,1024]{1,0:T(8,128)(2,1)S(1)} collective-permute-done((bf16[128,1024]{1,0:T(8,128)(2,1)S(1)}, bf16[128,1024]{1,0:T(8,128)(2,1)S(1)}, u32[]{:S(2)}, u32[]{:S(2)}) %collective-permute-start.11) | collective-permute-done | bytes 262176 | tf_op jit(solution)/shard_map/ppermute | solution.py:467
  244.6 3.3 %collective-permute-start.28 = (bf16[128,1024]{1,0:T(8,128)(2,1)S(1)}, bf16[128,1024]{1,0:T(8,128)(2,1)S(1)}, u32[]{:S(2)}, u32[]{:S(2)}) collective-permute-start(bf16[128,1024]{1,0:T(8,128)(2,1)S(1)} %add_convert_fusion), channel_id=1, source_target_pairs={{0,3},{1,0},{2,1},{3,2},{4,7},{5,4},{6,5},{7,6},{8,11},{9,8},{10,9... | collective-permute-start | bytes 786440 | tf_op jit(solution)/shard_map/ppermute | solution.py:467
  247.9 2.1 collective-permute-done.22
  250.2 3.3 %collective-permute-start.18 = (bf16[128,1024]{1,0:T(8,128)(2,1)S(1)}, bf16[128,1024]{1,0:T(8,128)(2,1)S(1)}, u32[]{:S(2)}, u32[]{:S(2)}) collective-permute-start(bf16[128,1024]{1,0:T(8,128)(2,1)S(1)} %add_convert_fusion.4), channel_id=1, source_target_pairs={{0,3},{1,0},{2,1},{3,2},{4,7},{5,4},{6,5},{7,6},{8,11},{9,8},{10,9... | collective-permute-start | bytes 786440 | tf_op jit(solution)/shard_map/ppermute | solution.py:467
  253.5 2.1 collective-permute-done.12
  255.8 2.1 residual.1.rows_ref
  257.9 3.3 %collective-permute-done.23.refs_4_ = bf16[128,1024]{1,0:T(8,128)(2,1)S(1)} collective-permute-done((bf16[128,1024]{1,0:T(8,128)(2,1)S(1)}, bf16[128,1024]{1,0:T(8,128)(2,1)S(1)}, u32[]{:S(2)}, u32[]{:S(2)}) %collective-permute-start.23) | collective-permute-done | bytes 262176 | tf_op jit(solution)/shard_map/ppermute | solution.py:467
  261.2 4.3 %collective-permute-done.13.refs_0_ = bf16[128,1024]{1,0:T(8,128)(2,1)S(1)} collective-permute-done((bf16[128,1024]{1,0:T(8,128)(2,1)S(1)}, bf16[128,1024]{1,0:T(8,128)(2,1)S(1)}, u32[]{:S(2)}, u32[]{:S(2)}) %collective-permute-start.13) | collective-permute-done | bytes 262176 | tf_op jit(solution)/shard_map/ppermute | solution.py:467
  265.5 2.0 finish.1
  (68 shorter events, 5.4 us)
Async XLA Ops:
  7.2 170.0 %all-gather.2.cloned.1.call-start = ((), (), s32[]{:S(2)}) async-start(), calls=%async_computation.2 | async-start | bytes 13369344 | tf_op jit(solution)/shard_map/all_gather | solution.py:493
  9.2 12.4 %collective-permute-start.6 = (bf16[1,256,768]{2,1,0:T(8,128)(2,1)S(1)}, bf16[1,256,768]{2,1,0:T(8,128)(2,1)S(1)}, u32[]{:S(2)}, u32[]{:S(2)}) collective-permute-start(bf16[1,256,768]{2,1,0:T(8,128)(2,1)S(1)} %multiply_convert_fusion), channel_id=1, source_target_pairs={{0,4},{4,0},{1,5},{5,1},{2,6},{6,2},{3,7},{7,3},{8,12},{12,8},{9,1... | collective-permute-start | bytes 1179656 | tf_op jit(solution)/shard_map/ppermute | solution.py:34
  43.4 41.4 %copy-start.4 = (bf16[512,256]{1,0:T(8,128)(2,1)S(1)}, bf16[512,256]{1,0:T(8,128)(2,1)}, u32[]{:S(2)}) copy-start(bf16[512,256]{1,0:T(8,128)(2,1)} %param.15) | copy-start | bytes 786436
  43.4 128.6 %copy-start.5 = (s32[32]{0:T(128)S(1)}, s32[32]{0:T(128)}, u32[]{:S(2)}) copy-start(s32[32]{0:T(128)} %param.9) | copy-start | bytes 388
  79.0 42.5 %all-to-all-start.1 = ((bf16[32,32,512]{2,1,0:T(8,128)(2,1)}), bf16[32,32,512]{2,1,0:T(8,128)(2,1)S(1)}, u32[]{:S(2)}, u32[]{:S(2)}) async-start(bf16[32,32,512]{2,1,0:T(8,128)(2,1)} %lookup.1), calls=%async_computation.1 | async-start | bytes 2097152 | tf_op jit(solution)/shard_map/all_to_all | solution.py:510
  84.8 27.6 %collective-permute-start.7 = (bf16[512,256]{1,0:T(8,128)(2,1)S(1)}, bf16[512,256]{1,0:T(8,128)(2,1)S(1)}, u32[]{:S(2)}, u32[]{:S(2)}) collective-permute-start(bf16[512,256]{1,0:T(8,128)(2,1)S(1)} %copy-done.4), channel_id=1, source_target_pairs={{0,4},{4,0},{1,5},{5,1},{2,6},{6,2},{3,7},{7,3},{8,12},{12,8},{9,1... | collective-permute-start | bytes 786440 | tf_op jit(solution)/shard_map/ppermute | solution.py:508
  86.3 30.9 %collective-permute-start.8 = (bf16[512,256]{1,0:T(8,128)(2,1)S(1)}, bf16[512,256]{1,0:T(8,128)(2,1)S(1)}, u32[]{:S(2)}, u32[]{:S(2)}) collective-permute-start(bf16[512,256]{1,0:T(8,128)(2,1)S(1)} %copy-done.4), channel_id=1, source_target_pairs={{0,16},{16,0},{1,17},{17,1},{2,18},{18,2},{3,19},{19,3},{4,20},{20... | collective-permute-start | bytes 786440 | tf_op jit(solution)/shard_map/ppermute | solution.py:508
  86.3 30.9 %collective-permute-start.9 = (bf16[512,256]{1,0:T(8,128)(2,1)S(1)}, bf16[512,256]{1,0:T(8,128)(2,1)S(1)}, u32[]{:S(2)}, u32[]{:S(2)}) collective-permute-start(bf16[512,256]{1,0:T(8,128)(2,1)S(1)} %copy-done.4), channel_id=1, source_target_pairs={{0,20},{4,16},{16,4},{20,0},{1,21},{5,17},{17,5},{21,1},{2,22},{6,... | collective-permute-start | bytes 786440 | tf_op jit(solution)/shard_map/ppermute | solution.py:508
  117.4 27.8 %collective-permute-start.19 = (bf16[2,2,512,256]{3,2,1,0:T(8,128)(2,1)S(1)}, bf16[2,2,512,256]{3,2,1,0:T(8,128)(2,1)}, u32[]{:S(2)}, u32[]{:S(2)}) collective-permute-start(bf16[2,2,512,256]{3,2,1,0:T(8,128)(2,1)S(1)} %bitcast.29), channel_id=1, source_target_pairs={{0,64},{32,96},{64,0},{96,32},{1,65},{33,97},{65,1},{97,33},{2,66}... | collective-permute-start | bytes 3145736 | tf_op jit(solution)/shard_map/ppermute | solution.py:518
  117.5 49.7 %collective-permute-start.20 = (bf16[2,2,512,256]{3,2,1,0:T(8,128)(2,1)S(1)}, bf16[2,2,512,256]{3,2,1,0:T(8,128)(2,1)}, u32[]{:S(2)}, u32[]{:S(2)}) collective-permute-start(bf16[2,2,512,256]{3,2,1,0:T(8,128)(2,1)S(1)} %bitcast.30), channel_id=1, source_target_pairs={{0,96},{32,0},{64,32},{96,64},{1,97},{33,1},{65,33},{97,65},{2,98}... | collective-permute-start | bytes 3145736 | tf_op jit(solution)/shard_map/ppermute | solution.py:518
  120.8 54.0 %collective-permute-start.10 = (bf16[2,2,512,256]{3,2,1,0:T(8,128)(2,1)S(1)}, bf16[2,2,512,256]{3,2,1,0:T(8,128)(2,1)}, u32[]{:S(2)}, u32[]{:S(2)}) collective-permute-start(bf16[2,2,512,256]{3,2,1,0:T(8,128)(2,1)S(1)} %bitcast.31), channel_id=1, source_target_pairs={{0,32},{32,64},{64,96},{96,0},{1,33},{33,65},{65,97},{97,1},{2,34}... | collective-permute-start | bytes 3145736 | tf_op jit(solution)/shard_map/ppermute | solution.py:518
  122.6 46.1 %collective-permute-start.2 = (bf16[512,512]{1,0:T(8,128)(2,1)}, bf16[512,512]{1,0:T(8,128)(2,1)S(1)}, u32[]{:S(2)}, u32[]{:S(2)}) collective-permute-start(bf16[512,512]{1,0:T(8,128)(2,1)} %bitcast.9), channel_id=1, source_target_pairs={{0,1},{1,2},{2,3},{3,0},{4,5},{5,6},{6,7},{7,4},{8,9},{9,10},{10,1... | collective-permute-start | bytes 1572872 | tf_op jit(solution)/shard_map/ppermute | solution.py:531
  124.1 50.6 %collective-permute-start.1 = (bf16[512,512]{1,0:T(8,128)(2,1)}, bf16[512,512]{1,0:T(8,128)(2,1)S(1)}, u32[]{:S(2)}, u32[]{:S(2)}) collective-permute-start(bf16[512,512]{1,0:T(8,128)(2,1)} %bitcast.10), channel_id=1, source_target_pairs={{0,3},{1,0},{2,1},{3,2},{4,7},{5,4},{6,5},{7,6},{8,11},{9,8},{10,9... | collective-permute-start | bytes 1572872 | tf_op jit(solution)/shard_map/ppermute | solution.py:532
  145.1 30.1 %collective-permute-start = (bf16[512,512]{1,0:T(8,128)(2,1)}, bf16[512,512]{1,0:T(8,128)(2,1)}, u32[]{:S(2)}, u32[]{:S(2)}) collective-permute-start(bf16[512,512]{1,0:T(8,128)(2,1)} %bitcast.9), channel_id=1, source_target_pairs={{0,3},{1,0},{2,1},{3,2},{4,7},{5,4},{6,5},{7,6},{8,11},{9,8},{10,9... | collective-permute-start | bytes 1572872 | tf_op jit(solution)/shard_map/ppermute | solution.py:534
  167.2 16.3 %collective-permute-start.5 = (bf16[512,512]{1,0:T(8,128)(2,1)}, bf16[512,512]{1,0:T(8,128)(2,1)}, u32[]{:S(2)}, u32[]{:S(2)}) collective-permute-start(bf16[512,512]{1,0:T(8,128)(2,1)} %bitcast.10), channel_id=1, source_target_pairs={{0,1},{1,2},{2,3},{3,0},{4,5},{5,6},{6,7},{7,4},{8,9},{9,10},{10,1... | collective-permute-start | bytes 1572872 | tf_op jit(solution)/shard_map/ppermute | solution.py:533
  168.7 24.2 %collective-permute-start.3 = (bf16[512,512]{1,0:T(8,128)(2,1)S(1)}, bf16[512,512]{1,0:T(8,128)(2,1)}, u32[]{:S(2)}, u32[]{:S(2)}) collective-permute-start(bf16[512,512]{1,0:T(8,128)(2,1)S(1)} %collective-permute-done.2.refs_0_.refs_5_), channel_id=1, source_target_pairs={{0,1},{1,2},{2,3},{3,0},{4,5},{5,6},{6,7},{7,4},{8,9},{9,10},{10,1... | collective-permute-start | bytes 1572872 | tf_op jit(solution)/shard_map/ppermute | solution.py:535
  174.7 41.0 %collective-permute-start.24 = (bf16[2,2,512,256]{3,2,1,0:T(8,128)(2,1)}, bf16[2,2,512,256]{3,2,1,0:T(8,128)(2,1)}, u32[]{:S(2)}, u32[]{:S(2)}) collective-permute-start(bf16[2,2,512,256]{3,2,1,0:T(8,128)(2,1)} %collective-permute-done.19.refs_0_), channel_id=1, source_target_pairs={{0,8},{8,0},{1,9},{9,1},{2,10},{10,2},{3,11},{11,3},{4,12},{12,4},... | collective-permute-start | bytes 3145736 | tf_op jit(solution)/shard_map/ppermute | solution.py:521
  174.7 18.2 %copy-start.1 = (bf16[512,512]{1,0:T(8,128)(2,1)}, bf16[512,512]{1,0:T(8,128)(2,1)S(1)}, u32[]{:S(2)}) copy-start(bf16[512,512]{1,0:T(8,128)(2,1)S(1)} %collective-permute-done.1.refs_3_.refs_2_) | copy-start | bytes 1572868
  174.7 40.9 %collective-permute-start.25 = (bf16[2,2,512,256]{3,2,1,0:T(8,128)(2,1)}, bf16[2,2,512,256]{3,2,1,0:T(8,128)(2,1)}, u32[]{:S(2)}, u32[]{:S(2)}) collective-permute-start(bf16[2,2,512,256]{3,2,1,0:T(8,128)(2,1)} %collective-permute-done.20.refs_1_), channel_id=1, source_target_pairs={{0,8},{8,0},{1,9},{9,1},{2,10},{10,2},{3,11},{11,3},{4,12},{12,4},... | collective-permute-start | bytes 3145736 | tf_op jit(solution)/shard_map/ppermute | solution.py:521
  175.2 26.1 %collective-permute-start.4 = (bf16[512,512]{1,0:T(8,128)(2,1)S(1)}, bf16[512,512]{1,0:T(8,128)(2,1)}, u32[]{:S(2)}, u32[]{:S(2)}) collective-permute-start(bf16[512,512]{1,0:T(8,128)(2,1)S(1)} %collective-permute-done.1.refs_3_.refs_2_), channel_id=1, source_target_pairs={{0,3},{1,0},{2,1},{3,2},{4,7},{5,4},{6,5},{7,6},{8,11},{9,8},{10,9... | collective-permute-start | bytes 1572872 | tf_op jit(solution)/shard_map/ppermute | solution.py:536
  183.5 42.2 %collective-permute-start.14 = (bf16[2,2,512,256]{3,2,1,0:T(8,128)(2,1)S(1)}, bf16[2,2,512,256]{3,2,1,0:T(8,128)(2,1)S(1)}, u32[]{:S(2)}, u32[]{:S(2)}) collective-permute-start(bf16[2,2,512,256]{3,2,1,0:T(8,128)(2,1)S(1)} %bitcast.32), channel_id=1, source_target_pairs={{0,8},{8,0},{1,9},{9,1},{2,10},{10,2},{3,11},{11,3},{4,12},{12,4},... | collective-permute-start | bytes 3145736 | tf_op jit(solution)/shard_map/ppermute | solution.py:521
  192.9 32.8 %collective-permute-start.15 = (bf16[2,2,512,256]{3,2,1,0:T(8,128)(2,1)}, bf16[2,2,512,256]{3,2,1,0:T(8,128)(2,1)S(1)}, u32[]{:S(2)}, u32[]{:S(2)}) collective-permute-start(bf16[2,2,512,256]{3,2,1,0:T(8,128)(2,1)} %collective-permute-done.10.refs_1_), channel_id=1, source_target_pairs={{0,8},{8,0},{1,9},{9,1},{2,10},{10,2},{3,11},{11,3},{4,12},{12,4},... | collective-permute-start | bytes 3145736 | tf_op jit(solution)/shard_map/ppermute | solution.py:521
  192.9 8.4 %copy-start.3 = (f32[512,128]{1,0:T(8,128)S(1)}, f32[512,128]{1,0:T(8,128)}, u32[]{:S(2)}) copy-start(f32[512,128]{1,0:T(8,128)} %get-tuple-element.52.refs_7_) | copy-start | bytes 786436
  215.7 1.2 copy-start
  220.2 13.7 %collective-permute-start.26 = (bf16[128,1024]{1,0:T(8,128)(2,1)S(1)}, bf16[128,1024]{1,0:T(8,128)(2,1)S(1)}, u32[]{:S(2)}, u32[]{:S(2)}) collective-permute-start(bf16[128,1024]{1,0:T(8,128)(2,1)S(1)} %get-tuple-element.37), channel_id=1, source_target_pairs={{0,3},{1,0},{2,1},{3,2},{4,7},{5,4},{6,5},{7,6},{8,11},{9,8},{10,9... | collective-permute-start | bytes 786440 | tf_op jit(solution)/shard_map/ppermute | solution.py:467
  225.2 30.6 %copy-start.2 = (bf16[512,512]{1,0:T(8,128)(2,1)S(1)}, bf16[512,512]{1,0:T(8,128)(2,1)}, u32[]{:S(2)}) copy-start(bf16[512,512]{1,0:T(8,128)(2,1)} %copy-done.1) | copy-start | bytes 1572868
  225.2 12.1 %collective-permute-start.21 = (bf16[128,1024]{1,0:T(8,128)(2,1)S(1)}, bf16[128,1024]{1,0:T(8,128)(2,1)S(1)}, u32[]{:S(2)}, u32[]{:S(2)}) collective-permute-start(bf16[128,1024]{1,0:T(8,128)(2,1)S(1)} %get-tuple-element.39), channel_id=1, source_target_pairs={{0,1},{1,2},{2,3},{3,0},{4,5},{5,6},{6,7},{7,4},{8,9},{9,10},{10,1... | collective-permute-start | bytes 786440 | tf_op jit(solution)/shard_map/ppermute | solution.py:467
  227.9 9.6 %collective-permute-start.16 = (bf16[128,1024]{1,0:T(8,128)(2,1)S(1)}, bf16[128,1024]{1,0:T(8,128)(2,1)S(1)}, u32[]{:S(2)}, u32[]{:S(2)}) collective-permute-start(bf16[128,1024]{1,0:T(8,128)(2,1)S(1)} %get-tuple-element.41), channel_id=1, source_target_pairs={{0,3},{1,0},{2,1},{3,2},{4,7},{5,4},{6,5},{7,6},{8,11},{9,8},{10,9... | collective-permute-start | bytes 786440 | tf_op jit(solution)/shard_map/ppermute | solution.py:467
  233.9 10.5 %collective-permute-start.11 = (bf16[128,1024]{1,0:T(8,128)(2,1)S(1)}, bf16[128,1024]{1,0:T(8,128)(2,1)S(1)}, u32[]{:S(2)}, u32[]{:S(2)}) collective-permute-start(bf16[128,1024]{1,0:T(8,128)(2,1)S(1)} %get-tuple-element.43), channel_id=1, source_target_pairs={{0,1},{1,2},{2,3},{3,0},{4,5},{5,6},{6,7},{7,4},{8,9},{9,10},{10,1... | collective-permute-start | bytes 786440 | tf_op jit(solution)/shard_map/ppermute | solution.py:467
  234.0 10.4 %collective-permute-start.27 = (bf16[128,1024]{1,0:T(8,128)(2,1)S(1)}, bf16[128,1024]{1,0:T(8,128)(2,1)S(1)}, u32[]{:S(2)}, u32[]{:S(2)}) collective-permute-start(bf16[128,1024]{1,0:T(8,128)(2,1)S(1)} %add_convert_fusion.1), channel_id=1, source_target_pairs={{0,3},{1,0},{2,1},{3,2},{4,7},{5,4},{6,5},{7,6},{8,11},{9,8},{10,9... | collective-permute-start | bytes 786440 | tf_op jit(solution)/shard_map/ppermute | solution.py:467
  237.4 12.5 %collective-permute-start.22 = (bf16[128,1024]{1,0:T(8,128)(2,1)S(1)}, bf16[128,1024]{1,0:T(8,128)(2,1)S(1)}, u32[]{:S(2)}, u32[]{:S(2)}) collective-permute-start(bf16[128,1024]{1,0:T(8,128)(2,1)S(1)} %add_convert_fusion.3), channel_id=1, source_target_pairs={{0,1},{1,2},{2,3},{3,0},{4,5},{5,6},{6,7},{7,4},{8,9},{9,10},{10,1... | collective-permute-start | bytes 786440 | tf_op jit(solution)/shard_map/ppermute | solution.py:467
  237.6 12.5 %collective-permute-start.17 = (bf16[128,1024]{1,0:T(8,128)(2,1)S(1)}, bf16[128,1024]{1,0:T(8,128)(2,1)S(1)}, u32[]{:S(2)}, u32[]{:S(2)}) collective-permute-start(bf16[128,1024]{1,0:T(8,128)(2,1)S(1)} %add_convert_fusion.5), channel_id=1, source_target_pairs={{0,3},{1,0},{2,1},{3,2},{4,7},{5,4},{6,5},{7,6},{8,11},{9,8},{10,9... | collective-permute-start | bytes 786440 | tf_op jit(solution)/shard_map/ppermute | solution.py:467
  244.4 11.2 %collective-permute-start.12 = (bf16[128,1024]{1,0:T(8,128)(2,1)S(1)}, bf16[128,1024]{1,0:T(8,128)(2,1)S(1)}, u32[]{:S(2)}, u32[]{:S(2)}) collective-permute-start(bf16[128,1024]{1,0:T(8,128)(2,1)S(1)} %add_convert_fusion.7), channel_id=1, source_target_pairs={{0,1},{1,2},{2,3},{3,0},{4,5},{5,6},{6,7},{7,4},{8,9},{9,10},{10,1... | collective-permute-start | bytes 786440 | tf_op jit(solution)/shard_map/ppermute | solution.py:467
  244.6 13.3 %collective-permute-start.28 = (bf16[128,1024]{1,0:T(8,128)(2,1)S(1)}, bf16[128,1024]{1,0:T(8,128)(2,1)S(1)}, u32[]{:S(2)}, u32[]{:S(2)}) collective-permute-start(bf16[128,1024]{1,0:T(8,128)(2,1)S(1)} %add_convert_fusion), channel_id=1, source_target_pairs={{0,3},{1,0},{2,1},{3,2},{4,7},{5,4},{6,5},{7,6},{8,11},{9,8},{10,9... | collective-permute-start | bytes 786440 | tf_op jit(solution)/shard_map/ppermute | solution.py:467
  250.0 11.2 %collective-permute-start.23 = (bf16[128,1024]{1,0:T(8,128)(2,1)S(1)}, bf16[128,1024]{1,0:T(8,128)(2,1)S(1)}, u32[]{:S(2)}, u32[]{:S(2)}) collective-permute-start(bf16[128,1024]{1,0:T(8,128)(2,1)S(1)} %add_convert_fusion.2), channel_id=1, source_target_pairs={{0,1},{1,2},{2,3},{3,0},{4,5},{5,6},{6,7},{7,4},{8,9},{9,10},{10,1... | collective-permute-start | bytes 786440 | tf_op jit(solution)/shard_map/ppermute | solution.py:467
  250.2 11.0 %collective-permute-start.18 = (bf16[128,1024]{1,0:T(8,128)(2,1)S(1)}, bf16[128,1024]{1,0:T(8,128)(2,1)S(1)}, u32[]{:S(2)}, u32[]{:S(2)}) collective-permute-start(bf16[128,1024]{1,0:T(8,128)(2,1)S(1)} %add_convert_fusion.4), channel_id=1, source_target_pairs={{0,3},{1,0},{2,1},{3,2},{4,7},{5,4},{6,5},{7,6},{8,11},{9,8},{10,9... | collective-permute-start | bytes 786440 | tf_op jit(solution)/shard_map/ppermute | solution.py:467
  255.6 9.9 %collective-permute-start.13 = (bf16[128,1024]{1,0:T(8,128)(2,1)S(1)}, bf16[128,1024]{1,0:T(8,128)(2,1)S(1)}, u32[]{:S(2)}, u32[]{:S(2)}) collective-permute-start(bf16[128,1024]{1,0:T(8,128)(2,1)S(1)} %add_convert_fusion.6), channel_id=1, source_target_pairs={{0,1},{1,2},{2,3},{3,0},{4,5},{5,6},{6,7},{7,4},{8,9},{9,10},{10,1... | collective-permute-start | bytes 786440 | tf_op jit(solution)/shard_map/ppermute | solution.py:467
Sparse Core Ops, SparseCore 0:
  22.7 85.9 all-gather.1

commit v4 on v3

--- a/solution.py
+++ b/solution.py
@@ -242,28 +242,26 @@
     cache_ref[0] = key_rot
     cache_ref[1] = value
     length = length_ref[0]
-    block = min(256, row_count)
-    root = jnp.float32(HD) ** 0.5
+    block = min(128, row_count)
+    power = 1.4426950408889634 / HD**0.5
     for h in range(q_heads):
         query = rotate(proj_ref[:, h * HD : (h + 1) * HD])
         for start in range(0, row_count, block):
             keys = start + block
-            scores = (
-                lax.dot_general(
-                    query[start : start + block],
-                    key_rot[:keys],
-                    (((1,), (1,)), ((), ())),
-                    preferred_element_type=jnp.float32,
-                )
-                / root
+            scores = lax.dot_general(
+                query[start : start + block],
+                key_rot[:keys],
+                (((1,), (1,)), ((), ())),
+                preferred_element_type=jnp.float32,
             )
-            q_pos = start + lax.broadcasted_iota(jnp.int32, (block, keys), 0)
+            q_pos = start + lax.broadcasted_iota(jnp.int32, (block, 1), 0)
             k_pos = lax.broadcasted_iota(jnp.int32, (block, keys), 1)
-            scores = jnp.where((k_pos <= q_pos) & (k_pos < length), scores, -1e30)
-            expd = jnp.exp(scores - jnp.max(scores, axis=-1, keepdims=True))
-            weights_now = (expd / jnp.sum(expd, axis=-1, keepdims=True)).astype(jnp.bfloat16)
+            scores = jnp.where(k_pos < jnp.minimum(q_pos + 1, length), scores, -1e30)
+            biggest = jnp.max(scores, axis=-1, keepdims=True)
+            expd = jnp.exp2((scores - biggest) * power)
+            weights_now = expd * (1.0 / jnp.sum(expd, axis=-1, keepdims=True))
             attended_ref[start : start + block, h * HD : (h + 1) * HD] = jnp.dot(
-                weights_now, value[:keys], preferred_element_type=jnp.float32
+                weights_now.astype(jnp.bfloat16), value[:keys], preferred_element_type=jnp.float32
             ).astype(jnp.bfloat16)
 
 
@@ -370,55 +368,70 @@
     return [(k, (k + way) % count) for k in range(count)]
 
 
-def product_kernel(places_ref, rows_ref, *refs, ring):
-    out_ref = refs[-1]
-    width = refs[0].shape[-1]
-    for k, weight_ref in enumerate(refs[:-1]):
-        _, halves, depth, _ = weight_ref.shape
+def product_kernel(xh_ref, rows_ref, *refs, pieces, outs):
+    held, arrived = refs[-2:]
+    out_refs = refs[-2 - outs : -2]
+    _, halves, depth, width = held.shape
+
+    def incoming(k):
+        array, index = pieces[k]
+        return pltpu.make_async_copy(refs[array].at[index], held.at[k], arrived.at[k])
+
+    for k in range(len(pieces)):
+        incoming(k).start()
+    each = len(pieces) // outs
+    for k in range(len(pieces)):
+        incoming(k).wait()
         total = None
         for half in range(halves):
-            block = places_ref[ring] ^ half
+            block = xh_ref[0] ^ half
             rows = rows_ref[:, pl.ds(pl.multiple_of(block * depth, depth), depth)]
-            term = jnp.dot(rows, weight_ref[0, half], preferred_element_type=jnp.float32)
+            term = jnp.dot(rows, held[k, half], preferred_element_type=jnp.float32)
             total = term if total is None else total + term
-        out_ref[:, k * width : (k + 1) * width] = total.astype(out_ref.dtype)
-
-
-def product(places, rows, weights):
-    sides, halves, depth, width = weights[0].shape
+        here = slice(k % each * width, (k % each + 1) * width)
+        out_refs[k // each][:, here] = total.astype(jnp.bfloat16)
+
+
+def product(xh, rows, weights, pieces, outs):
+    _, halves, depth, width = weights[0].shape
     row_count = rows.shape[0]
-    wide = len(weights) * width
+    count = len(pieces)
     return pl.pallas_call(
-        functools.partial(product_kernel, ring=places.shape[0] - 3),
-        grid_spec=pltpu.PrefetchScalarGridSpec(
-            num_scalar_prefetch=1,
-            grid=(sides,),
-            in_specs=[pl.BlockSpec(rows.shape, lambda j, places: (0, 0))]
-            + [pl.BlockSpec((1, halves, depth, width), lambda j, places: (j, 0, 0, 0))]
-            * len(weights),
-            out_specs=pl.BlockSpec((row_count, wide), lambda j, places: (0, j)),
-        ),
-        out_shape=jax.ShapeDtypeStruct((row_count, sides * wide), jnp.bfloat16),
-        compiler_params=pltpu.CompilerParams(vmem_limit_bytes=16 * 2**20),
+        functools.partial(product_kernel, pieces=pieces, outs=outs),
+        in_specs=[pl.BlockSpec(memory_space=pltpu.SMEM), pl.BlockSpec(memory_space=pltpu.VMEM)]
+        + [pl.BlockSpec(memory_space=pltpu.HBM)] * len(weights),
+        out_specs=tuple([pl.BlockSpec(memory_space=pltpu.VMEM)] * outs),
+        out_shape=tuple(
+            [jax.ShapeDtypeStruct((row_count, count // outs * width), jnp.bfloat16)] * outs
+        ),
+        scratch_shapes=[
+            pltpu.VMEM((count, halves, depth, width), jnp.bfloat16),
+            pltpu.SemaphoreType.DMA((count,)),
+        ],
+        compiler_params=pltpu.CompilerParams(vmem_limit_bytes=60 * 2**20),
         cost_estimate=pl.CostEstimate(
-            flops=2 * row_count * halves * depth * wide * sides,
-            bytes_accessed=2 * (rows.size + halves * depth * wide * sides),
+            flops=2 * row_count * halves * depth * width * count,
+            bytes_accessed=2 * (rows.size + halves * depth * width * count),
             transcendentals=0,
         ),
         name="product",
-    )(places, rows, *weights)
+    )(xh, rows, *weights)
+
+
+LAYERS = (0, 1, 3, 2)
 
 
 def finish_kernel(where_ref, rows_ref, *refs, width):
     hidden_ref = refs[-1]
     chunks = (len(refs) - 1) // 4
-    layers = refs[0].shape[1] // width // 2
-    for chunk in range(chunks):
-        for core in range(2):
-            at = 2 * (2 * chunk + core)
-            for j in range(2 * layers):
-                z = lax.rem(where_ref[0] + chunks * layers - chunk * layers - j % layers, chunks * layers)
-                column = (z * 2 + (where_ref[1] ^ (j // layers))) * 2 + (where_ref[2] ^ core)
+    each = refs[0].shape[1] // width
+    for core in range(2):
+        for chunk in range(chunks):
+            at = 2 * (chunks * core + chunk)
+            for j in range(each):
+                layer, side = divmod(chunk * each + j, 2)
+                z = lax.rem(where_ref[0] + len(LAYERS) - LAYERS[layer], len(LAYERS))
+                column = (z * 2 + (where_ref[1] ^ side)) * 2 + (where_ref[2] ^ core)
                 here = slice(j * width, (j + 1) * width)
                 there = pl.ds(pl.multiple_of(column * width, width), width)
                 total = refs[at][:, here].astype(jnp.float32) + refs[at + 1][:, here].astype(
@@ -447,16 +460,16 @@
 CHUNKS = 2
 
 
-def ring_sums(places, attended, weights, quarter):
+def ring_sums(attended, weights, quarter):
     place = lax.axis_index(RING)
     count = lax.axis_size(RING)
-    each = len(weights[0]) // CHUNKS
+    pieces = [(LAYERS.index(z), (side,)) for z in LAYERS[:3] for side in range(2)]
+    pieces += [(3, (0,)), (4, (0,))]
+    xh = lax.axis_index("tensor_0")[None]
     sums = []
-    for chunk in range(CHUNKS):
-        for side, way in enumerate((1, -1)):
-            partial_sums = product(
-                places, attended, weights[side][chunk * each : (chunk + 1) * each]
-            )
+    for side, way in enumerate((1, -1)):
+        chunks = product(xh, attended, weights[side], pieces, CHUNKS)
+        for partial_sums in chunks:
 
             def part(turn):
                 start = (place + turn) % count * quarter
@@ -513,19 +526,18 @@
     pieces_x, _ = lax.optimization_barrier((pieces_x, outgoing))
     w_mine = [jnp.stack(pieces_x).reshape(2, 2, *w_out.shape)]
     layers = lax.axis_size("dp_0")
-    for k in range(1, layers):
-        route = [(z, (z + k) % layers) for z in range(layers)]
+    ahead = [(z, (z + 1) % layers) for z in range(layers)]
+    back = [(z, (z - 1) % layers) for z in range(layers)]
+    for route in (ahead, back):
         w_mine.append(lax.ppermute(w_mine[0], "dp_0", route))
+    first_side, last_side = w_mine[1][:1], w_mine[2][1:]
+    w_mine.append(lax.ppermute(first_side, "dp_0", ahead))
+    w_mine.append(lax.ppermute(last_side, "dp_0", back))
     w_other = []
-    for k in range(layers):
+    for k in range(len(w_mine)):
         w_other.append(lax.ppermute(w_mine[k], "dp_2", [(0, 1), (1, 0)]))
 
-    places = jnp.concatenate(
-        [
-            (place + jnp.arange(ring, dtype=jnp.int32)) % ring,
-            jnp.stack([lax.axis_index(name) for name in ("tensor_0", "dp_1", "dp_2")]),
-        ]
-    )
+    places = (place + jnp.arange(ring, dtype=jnp.int32)) % ring
     half = own.shape[0] // 2
     low, high = own[:half], own[half:]
     low_before = lax.ppermute(low, RING, ring_route(1))
@@ -562,7 +574,7 @@
     pieces, _ = lax.optimization_barrier((pieces, attended))
     own_rows = residual(places, pieces, columns, quarter)
 
-    sums = ring_sums(places, attended, (w_mine, w_other), quarter)
+    sums = ring_sums(attended, (w_mine, w_other), quarter)
     where = jnp.stack([lax.axis_index(name) for name in DP])
     hidden = finish(where, own_rows, sums, w_out.shape[1])
     return hidden, cache[None]

time: 276 us -> 271 us (0.982)
  waiting for transfers between devices: 104 us -> 76.5 us
  Pallas kernels: 79.4 us -> 88.1 us
  local copies, waits for them, and re-layouts: 4.55 us -> 12.7 us
  other arithmetic: 8.32 us -> 14.9 us
    ppermute x3 -> x2, waiting for transfers between devices: 38.5 us -> 16.5 us  [sublayer(): w_mine.append(lax.ppermute(w_mine[0], 'dp_0', route))]
    ppermute x1, waiting for transfers between devices: 9.42 us -> 0.66 us  [sublayer(): low_across = lax.ppermute(low_before, RING, ring_route(1))]
    convert_element_type x8, other arithmetic: 0.56 us -> 8.29 us  [ring_sums(): running = running.astype(jnp.bfloat16)]
    pallas_call x4 -> x2, Pallas kernels: 11.7 us -> 17.7 us  [product(): pl.pallas_call(functools.partial(product_kernel, pieces=pieces, outs=outs...]
    dynamic_slice x4, local copies, waits for them, and re-layouts: 0.18 us -> 4.96 us  [part(): return lax.dynamic_slice_in_dim(partial_sums, start, quarter, 0)]
    ppermute x12, starting transfers between devices: 18.5 us -> 14.3 us  [ring_sums(): running = lax.ppermute(running, RING, ring_route(way))]
    slice x0 -> x2, local copies, waits for them, and re-layouts: none -> 3.79 us  [sublayer(): first_side, last_side = (w_mine[1][:1], w_mine[2][1:])]
    ppermute x0 -> x2, starting transfers between devices: none -> 3.24 us  [the longest x1 3.23 us: sublayer(): w_mine.append(lax.ppermute(last_side, 'dp_0', back))]
  transfers between devices with their start and end apart: 31 -> 33, of which waited for: 12 -> 13; matrix products, arithmetic and copies ran while one was open for 3% -> 8% of each run, Pallas kernels for 28% -> 29%
where the time goes in v4:
time: 271 us; the launch traced here: 269 us
  Pallas kernels  88.1 us (33%)
  waiting for transfers between devices  76.5 us (28%)
  starting transfers between devices  43.6 us (16%)
  blocking collectives  18.7 us (7%)
  other arithmetic  14.9 us (5%)
  between operations  14.3 us (5%)
  local copies, waits for them, and re-layouts  12.7 us (5%)
    pallas_call x1, Pallas kernels, lookup(): pl.pallas_call(lookup_kernel, out_shape=jax.ShapeDtypeStruct((group_count...  35.6 us
    ppermute x3, waiting for transfers between devices, sublayer(): pieces_x.append(lax.ppermute(w_out, axes, route))  28.3 us
    all_to_all x1, blocking collectives, sublayer(): lax.all_to_all(jnp.broadcast_to(prompt_ids[None], (devices, quarter)), DP...  18.7 us
    pallas_call x2, Pallas kernels, product(): pl.pallas_call(functools.partial(product_kernel, pieces=pieces, outs=outs...  17.7 us
    pallas_call x1, Pallas kernels, attend(): pl.pallas_call(functools.partial(attention_kernel, parts=len(parts), mode...  17.3 us
    ppermute x2, waiting for transfers between devices, sublayer(): w_mine.append(lax.ppermute(w_mine[0], 'dp_0', route))  16.5 us
    ppermute x12, waiting for transfers between devices, ring_sums(): running = lax.ppermute(running, RING, ring_route(way))  14.5 us
    ppermute x12, starting transfers between devices, ring_sums(): running = lax.ppermute(running, RING, ring_route(way))  14.3 us
  transfers between devices with their start and end apart: 33, of which 13 were waited for; matrix products, arithmetic and copies ran while one was open for 8% of the time, Pallas kernels for 29%

profile of v4, /device:TPU:6, one launch (start us, length us, event | category | flops | bytes accessed | tf_op | source)
XLA Modules:
  0.0 268.8 jit_solution(7329463177888984871)
XLA Ops:
  8.0 1.2 multiply_convert_fusion
  9.2 1.5 collective-permute-start.6
  10.6 11.0 %collective-permute-done.6 = bf16[1,256,768]{2,1,0:T(8,128)(2,1)S(1)} collective-permute-done((bf16[1,256,768]{2,1,0:T(8,128)(2,1)S(1)}, bf16[1,256,768]{2,1,0:T(8,128)(2,1)S(1)}, u32[]{:S(2)}, u32[]{:S(2)}) %collective-permute-start.6) | collective-permute-done | bytes 393248 | tf_op jit(solution)/shard_map/ppermute | solution.py:34
  23.3 18.7 %all_to_all.11 = s32[128,1,128]{2,1,0:T(1,128)S(1)} all-to-all(s32[128,1,128]{2,1,0:T(1,128)S(1)} %broadcast_in_dim.6), channel_id=1, replica_groups=mesh['dp_0'=4,'dp_1'=2,'dp_2'=2,'tensor_0'=2,'tensor_1'=4] {'dp_0','dp_1..., dimensions={0} | all-to-all | bytes 131072 | tf_op jit(solution)/shard_map/all_to_all | solution.py:508
  43.4 35.6 %lookup.1 = bf16[32,32,512]{2,1,0:T(8,128)(2,1)} custom-call(s32[16384]{0:T(1024)} %fusion.2.slots_ref, s32[128,128]{1,0:T(8,128)} %bitcast_or_fusion.lanes_ref, bf16[32,128256]{1,0:T(8,128)(2,1)} %table_ref.1), custom_call_target="tpu_custom_call" | custom-call | flops 30000001024 | bytes 8208384 | tf_op jit(solution)/shard_map/lookup/pallas_call | solution.py:131
  79.0 5.8 %all-to-all-start.1 = ((bf16[32,32,512]{2,1,0:T(8,128)(2,1)}), bf16[32,32,512]{2,1,0:T(8,128)(2,1)S(1)}, u32[]{:S(2)}, u32[]{:S(2)}) async-start(bf16[32,32,512]{2,1,0:T(8,128)(2,1)} %lookup.1), calls=%async_computation.1 | async-start | bytes 2097152 | tf_op jit(solution)/shard_map/all_to_all | solution.py:523
  84.8 1.5 collective-permute-start.7
  86.4 2.6 collective-permute-start.9
  89.0 23.4 %collective-permute-done.7 = bf16[512,256]{1,0:T(8,128)(2,1)S(1)} collective-permute-done((bf16[512,256]{1,0:T(8,128)(2,1)S(1)}, bf16[512,256]{1,0:T(8,128)(2,1)S(1)}, u32[]{:S(2)}, u32[]{:S(2)}) %collective-permute-start.7) | collective-permute-done | bytes 262176 | tf_op jit(solution)/shard_map/ppermute | solution.py:521
  112.4 4.9 %collective-permute-done.8 = bf16[512,256]{1,0:T(8,128)(2,1)S(1)} collective-permute-done((bf16[512,256]{1,0:T(8,128)(2,1)S(1)}, bf16[512,256]{1,0:T(8,128)(2,1)S(1)}, u32[]{:S(2)}, u32[]{:S(2)}) %collective-permute-start.8) | collective-permute-done | bytes 262176 | tf_op jit(solution)/shard_map/ppermute | solution.py:521
  117.2 1.1 pad_maximum_fusion
  118.3 3.2 %collective-permute-start.11 = (bf16[2,2,512,256]{3,2,1,0:T(8,128)(2,1)}, bf16[2,2,512,256]{3,2,1,0:T(8,128)(2,1)}, u32[]{:S(2)}, u32[]{:S(2)}) collective-permute-start(bf16[2,2,512,256]{3,2,1,0:T(8,128)(2,1)} %bitcast.19.refs_0_), channel_id=1, source_target_pairs={{0,96},{32,0},{64,32},{96,64},{1,97},{33,1},{65,33},{97,65},{2,98}... | collective-permute-start | bytes 3145736 | tf_op jit(solution)/shard_map/ppermute | solution.py:532
  121.6 1.1 fusion.4
  122.7 2.8 %collective-permute-start.1 = (bf16[512,512]{1,0:T(8,128)(2,1)}, bf16[512,512]{1,0:T(8,128)(2,1)S(1)}, u32[]{:S(2)}, u32[]{:S(2)}) collective-permute-start(bf16[512,512]{1,0:T(8,128)(2,1)} %bitcast.9), channel_id=1, source_target_pairs={{0,3},{1,0},{2,1},{3,2},{4,7},{5,4},{6,5},{7,6},{8,11},{9,8},{10,9... | collective-permute-start | bytes 1572872 | tf_op jit(solution)/shard_map/ppermute | solution.py:544
  125.5 3.2 %collective-permute-start = (bf16[512,512]{1,0:T(8,128)(2,1)}, bf16[512,512]{1,0:T(8,128)(2,1)S(1)}, u32[]{:S(2)}, u32[]{:S(2)}) collective-permute-start(bf16[512,512]{1,0:T(8,128)(2,1)} %bitcast.8), channel_id=1, source_target_pairs={{0,3},{1,0},{2,1},{3,2},{4,7},{5,4},{6,5},{7,6},{8,11},{9,8},{10,9... | collective-permute-start | bytes 1572872 | tf_op jit(solution)/shard_map/ppermute | solution.py:546
  128.7 16.5 %collective-permute-done.10.refs_1_ = bf16[2,2,512,256]{3,2,1,0:T(8,128)(2,1)} collective-permute-done((bf16[2,2,512,256]{3,2,1,0:T(8,128)(2,1)}, bf16[2,2,512,256]{3,2,1,0:T(8,128)(2,1)}, u32[]{:S(2)}, u32[]{:S(2)}) %collective-permute-start.10) | collective-permute-done | bytes 1048608 | tf_op jit(solution)/shard_map/ppermute | solution.py:532
  145.2 1.5 collective-permute-start.5
  146.7 1.9 slice.26
  148.6 1.9 slice.27
  150.5 3.2 %collective-permute-start.13 = (bf16[1,2,512,256]{3,2,1,0:T(8,128)(2,1)}, bf16[1,2,512,256]{3,2,1,0:T(8,128)(2,1)}, u32[]{:S(2)}, u32[]{:S(2)}) collective-permute-start(bf16[1,2,512,256]{3,2,1,0:T(8,128)(2,1)} %slice.27), channel_id=1, source_target_pairs={{0,96},{32,0},{64,32},{96,64},{1,97},{33,1},{65,33},{97,65},{2,98}... | collective-permute-start | bytes 1572872 | tf_op jit(solution)/shard_map/ppermute | solution.py:535
  154.3 1.6 collective-permute-start.3
  155.9 1.7 collective-permute-start.4
  158.6 2.7 %collective-permute-done.5.refs_1_.refs_6_ = bf16[512,512]{1,0:T(8,128)(2,1)S(1)} collective-permute-done((bf16[512,512]{1,0:T(8,128)(2,1)}, bf16[512,512]{1,0:T(8,128)(2,1)S(1)}, u32[]{:S(2)}, u32[]{:S(2)}) %collective-permute-start.5) | collective-permute-done | bytes 524320 | tf_op jit(solution)/shard_map/ppermute | solution.py:545
  161.4 1.6 collective-permute-done.12.refs_3_
  163.0 1.2 collective-permute-done.13.refs_4_
  165.1 5.4 %project.2 = (f32[512,1536]{1,0:T(8,128)}, f32[1,512]{1,0:T(1,128)S(1)}) custom-call(s32[4]{0:T(128)S(1)} %and_select_fusion.places_ref, bf16[1024,512]{1,0:T(8,128)(2,1)S(1)} %bitcast.27, bf16[2,32,4,32,768]{4,3,2,1,0:T(8,128)(2,1)} %bitcast.29), custom_call_target="tpu_custom_call" | custom-call | flops 1610612736 | bytes 4194304 | tf_op jit(solution)/shard_map/project/pallas_call | solution.py:201
  171.7 8.1 %project.3 = (f32[512,1536]{1,0:T(8,128)}, f32[1,512]{1,0:T(1,128)S(1)}) custom-call(s32[4]{0:T(128)S(1)} %and_select_fusion.places_ref, bf16[512,512]{1,0:T(8,128)(2,1)S(1)} %collective-permute-done.2.refs_0_.refs_5_, bf16[512,512]{1,0:T(8,128)(2,1)S(1)} %collective-permute-done.5.refs_1_.refs_6_, ...), custom_call_target="tpu_custom_call" | custom-call | flops 3221225472 | bytes 8388608 | tf_op jit(solution)/shard_map/project/pallas_call | solution.py:201
  179.8 17.3 %attend.1 = (bf16[512,1024]{1,0:T(8,128)(2,1)}, bf16[2,512,256]{2,1,0:T(8,128)(2,1)}) custom-call(s32[4]{0:T(128)S(1)} %and_select_fusion.places_ref, s32[1]{0:T(128)} %dynamic_slice.54.length_ref, bf16[512,512]{1,0:T(8,128)(2,1)} %collective-permute-done.3.refs_0_.refs_3_, bf16[512,512]{1,0:T(8,128)(2,1)} %collective-permute-done.4.refs_1_.refs_4_, ...), custom_call_target="tpu_custom_call" | custom-call | flops 4000000000 | bytes 9000000 | tf_op jit(solution)/shard_map/attend/pallas_call | solution.py:281
  197.9 8.8 %product.3 = (bf16[512,1024]{1,0:T(8,128)(2,1)}, bf16[512,1024]{1,0:T(8,128)(2,1)}) custom-call(s32[1]{0:T(128)} %bitcast.14.xh_ref, bf16[512,1024]{1,0:T(8,128)(2,1)} %get-tuple-element.27.rows_ref, bf16[2,2,512,256]{3,2,1,0:T(8,128)(2,1)} %collective-permute-done.20.refs_0_, bf16[2,2,512,256]{3,2,1,0:T(8,128)(2,1)} %collective-permute-done.21.refs_1_, ...), custom_call_target="tpu_custom_call" | custom-call | flops 2147483648 | bytes 5242880 | tf_op jit(solution)/shard_map/product/pallas_call | solution.py:399
  206.7 1.8 constant_dynamic-slice_fusion
  208.5 1.5 collective-permute-start.28
  210.0 1.1 constant_dynamic-slice_fusion.2
  211.1 1.6 collective-permute-start.25
  212.7 8.8 %product.2 = (bf16[512,1024]{1,0:T(8,128)(2,1)}, bf16[512,1024]{1,0:T(8,128)(2,1)}) custom-call(s32[1]{0:T(128)} %bitcast.14.xh_ref, bf16[512,1024]{1,0:T(8,128)(2,1)} %get-tuple-element.27.rows_ref, bf16[2,2,512,256]{3,2,1,0:T(8,128)(2,1)} %bitcast.19.refs_0_, bf16[2,2,512,256]{3,2,1,0:T(8,128)(2,1)} %collective-permute-done.10.refs_1_, ...), custom_call_target="tpu_custom_call" | custom-call | flops 2147483648 | bytes 5242880 | tf_op jit(solution)/shard_map/product/pallas_call | solution.py:399
  221.6 1.1 constant_dynamic-slice_fusion.4
  225.0 1.1 add_convert_fusion.1
  226.1 2.8 %collective-permute-start.29 = (bf16[128,1024]{1,0:T(8,128)(2,1)S(1)}, bf16[128,1024]{1,0:T(8,128)(2,1)S(1)}, u32[]{:S(2)}, u32[]{:S(2)}) collective-permute-start(bf16[128,1024]{1,0:T(8,128)(2,1)S(1)} %add_convert_fusion.1), channel_id=1, source_target_pairs={{0,3},{1,0},{2,1},{3,2},{4,7},{5,4},{6,5},{7,6},{8,11},{9,8},{10,9... | collective-permute-start | bytes 786440 | tf_op jit(solution)/shard_map/ppermute | solution.py:480
  229.0 1.1 add_convert_fusion.3
  230.1 1.4 collective-permute-start.26
  231.5 1.6 collective-permute-done.17
  234.2 4.5 %collective-permute-done.14 = bf16[128,1024]{1,0:T(8,128)(2,1)S(1)} collective-permute-done((bf16[128,1024]{1,0:T(8,128)(2,1)S(1)}, bf16[128,1024]{1,0:T(8,128)(2,1)S(1)}, u32[]{:S(2)}, u32[]{:S(2)}) %collective-permute-start.14) | collective-permute-done | bytes 262176 | tf_op jit(solution)/shard_map/ppermute | solution.py:480
  240.9 3.3 %collective-permute-start.30 = (bf16[128,1024]{1,0:T(8,128)(2,1)S(1)}, bf16[128,1024]{1,0:T(8,128)(2,1)S(1)}, u32[]{:S(2)}, u32[]{:S(2)}) collective-permute-start(bf16[128,1024]{1,0:T(8,128)(2,1)S(1)} %add_convert_fusion), channel_id=1, source_target_pairs={{0,3},{1,0},{2,1},{3,2},{4,7},{5,4},{6,5},{7,6},{8,11},{9,8},{10,9... | collective-permute-start | bytes 786440 | tf_op jit(solution)/shard_map/ppermute | solution.py:480
  246.3 2.1 collective-permute-start.19
  248.3 1.8 collective-permute-done.15
  251.4 2.0 residual.1.rows_ref
  253.4 3.0 %collective-permute-done.19.refs_2_ = bf16[128,1024]{1,0:T(8,128)(2,1)S(1)} collective-permute-done((bf16[128,1024]{1,0:T(8,128)(2,1)S(1)}, bf16[128,1024]{1,0:T(8,128)(2,1)S(1)}, u32[]{:S(2)}, u32[]{:S(2)}) %collective-permute-start.19) | collective-permute-done | bytes 262176 | tf_op jit(solution)/shard_map/ppermute | solution.py:480
  256.4 3.5 %collective-permute-done.16.refs_0_ = bf16[128,1024]{1,0:T(8,128)(2,1)S(1)} collective-permute-done((bf16[128,1024]{1,0:T(8,128)(2,1)S(1)}, bf16[128,1024]{1,0:T(8,128)(2,1)S(1)}, u32[]{:S(2)}, u32[]{:S(2)}) %collective-permute-start.16) | collective-permute-done | bytes 262176 | tf_op jit(solution)/shard_map/ppermute | solution.py:480
  259.9 2.0 finish.1
  (71 shorter events, 17.3 us)
Async XLA Ops:
  7.2 157.9 %all-gather.2.cloned.1.call-start = ((), (), s32[]{:S(2)}) async-start(), calls=%async_computation.2 | async-start | bytes 13369344 | tf_op jit(solution)/shard_map/all_gather | solution.py:506
  9.2 12.4 %collective-permute-start.6 = (bf16[1,256,768]{2,1,0:T(8,128)(2,1)S(1)}, bf16[1,256,768]{2,1,0:T(8,128)(2,1)S(1)}, u32[]{:S(2)}, u32[]{:S(2)}) collective-permute-start(bf16[1,256,768]{2,1,0:T(8,128)(2,1)S(1)} %multiply_convert_fusion), channel_id=1, source_target_pairs={{0,4},{4,0},{1,5},{5,1},{2,6},{6,2},{3,7},{7,3},{8,12},{12,8},{9,1... | collective-permute-start | bytes 1179656 | tf_op jit(solution)/shard_map/ppermute | solution.py:34
  43.4 41.4 %copy-start.3 = (bf16[512,256]{1,0:T(8,128)(2,1)S(1)}, bf16[512,256]{1,0:T(8,128)(2,1)}, u32[]{:S(2)}) copy-start(bf16[512,256]{1,0:T(8,128)(2,1)} %param.15) | copy-start | bytes 786436
  79.0 74.7 %copy-start.5 = (s32[32]{0:T(128)S(1)}, s32[32]{0:T(128)}, u32[]{:S(2)}) copy-start(s32[32]{0:T(128)} %param.9) | copy-start | bytes 388
  79.0 42.5 %all-to-all-start.1 = ((bf16[32,32,512]{2,1,0:T(8,128)(2,1)}), bf16[32,32,512]{2,1,0:T(8,128)(2,1)S(1)}, u32[]{:S(2)}, u32[]{:S(2)}) async-start(bf16[32,32,512]{2,1,0:T(8,128)(2,1)} %lookup.1), calls=%async_computation.1 | async-start | bytes 2097152 | tf_op jit(solution)/shard_map/all_to_all | solution.py:523
  84.8 27.6 %collective-permute-start.7 = (bf16[512,256]{1,0:T(8,128)(2,1)S(1)}, bf16[512,256]{1,0:T(8,128)(2,1)S(1)}, u32[]{:S(2)}, u32[]{:S(2)}) collective-permute-start(bf16[512,256]{1,0:T(8,128)(2,1)S(1)} %copy-done.3), channel_id=1, source_target_pairs={{0,4},{4,0},{1,5},{5,1},{2,6},{6,2},{3,7},{7,3},{8,12},{12,8},{9,1... | collective-permute-start | bytes 786440 | tf_op jit(solution)/shard_map/ppermute | solution.py:521
  86.3 30.9 %collective-permute-start.8 = (bf16[512,256]{1,0:T(8,128)(2,1)S(1)}, bf16[512,256]{1,0:T(8,128)(2,1)S(1)}, u32[]{:S(2)}, u32[]{:S(2)}) collective-permute-start(bf16[512,256]{1,0:T(8,128)(2,1)S(1)} %copy-done.3), channel_id=1, source_target_pairs={{0,16},{16,0},{1,17},{17,1},{2,18},{18,2},{3,19},{19,3},{4,20},{20... | collective-permute-start | bytes 786440 | tf_op jit(solution)/shard_map/ppermute | solution.py:521
  86.4 30.9 %collective-permute-start.9 = (bf16[512,256]{1,0:T(8,128)(2,1)S(1)}, bf16[512,256]{1,0:T(8,128)(2,1)S(1)}, u32[]{:S(2)}, u32[]{:S(2)}) collective-permute-start(bf16[512,256]{1,0:T(8,128)(2,1)S(1)} %copy-done.3), channel_id=1, source_target_pairs={{0,20},{4,16},{16,4},{20,0},{1,21},{5,17},{17,5},{21,1},{2,22},{6,... | collective-permute-start | bytes 786440 | tf_op jit(solution)/shard_map/ppermute | solution.py:521
  118.3 26.8 %collective-permute-start.10 = (bf16[2,2,512,256]{3,2,1,0:T(8,128)(2,1)}, bf16[2,2,512,256]{3,2,1,0:T(8,128)(2,1)}, u32[]{:S(2)}, u32[]{:S(2)}) collective-permute-start(bf16[2,2,512,256]{3,2,1,0:T(8,128)(2,1)} %bitcast.19.refs_0_), channel_id=1, source_target_pairs={{0,32},{32,64},{64,96},{96,0},{1,33},{33,65},{65,97},{97,1},{2,34}... | collective-permute-start | bytes 3145736 | tf_op jit(solution)/shard_map/ppermute | solution.py:532
  118.3 30.2 %collective-permute-start.11 = (bf16[2,2,512,256]{3,2,1,0:T(8,128)(2,1)}, bf16[2,2,512,256]{3,2,1,0:T(8,128)(2,1)}, u32[]{:S(2)}, u32[]{:S(2)}) collective-permute-start(bf16[2,2,512,256]{3,2,1,0:T(8,128)(2,1)} %bitcast.19.refs_0_), channel_id=1, source_target_pairs={{0,96},{32,0},{64,32},{96,64},{1,97},{33,1},{65,33},{97,65},{2,98}... | collective-permute-start | bytes 3145736 | tf_op jit(solution)/shard_map/ppermute | solution.py:532
  122.7 27.8 %collective-permute-start.1 = (bf16[512,512]{1,0:T(8,128)(2,1)}, bf16[512,512]{1,0:T(8,128)(2,1)S(1)}, u32[]{:S(2)}, u32[]{:S(2)}) collective-permute-start(bf16[512,512]{1,0:T(8,128)(2,1)} %bitcast.9), channel_id=1, source_target_pairs={{0,3},{1,0},{2,1},{3,2},{4,7},{5,4},{6,5},{7,6},{8,11},{9,8},{10,9... | collective-permute-start | bytes 1572872 | tf_op jit(solution)/shard_map/ppermute | solution.py:544
  125.5 28.9 %collective-permute-start.2 = (bf16[512,512]{1,0:T(8,128)(2,1)}, bf16[512,512]{1,0:T(8,128)(2,1)S(1)}, u32[]{:S(2)}, u32[]{:S(2)}) collective-permute-start(bf16[512,512]{1,0:T(8,128)(2,1)} %bitcast.8), channel_id=1, source_target_pairs={{0,1},{1,2},{2,3},{3,0},{4,5},{5,6},{6,7},{7,4},{8,9},{9,10},{10,1... | collective-permute-start | bytes 1572872 | tf_op jit(solution)/shard_map/ppermute | solution.py:543
  125.5 30.4 %collective-permute-start = (bf16[512,512]{1,0:T(8,128)(2,1)}, bf16[512,512]{1,0:T(8,128)(2,1)S(1)}, u32[]{:S(2)}, u32[]{:S(2)}) collective-permute-start(bf16[512,512]{1,0:T(8,128)(2,1)} %bitcast.8), channel_id=1, source_target_pairs={{0,3},{1,0},{2,1},{3,2},{4,7},{5,4},{6,5},{7,6},{8,11},{9,8},{10,9... | collective-permute-start | bytes 1572872 | tf_op jit(solution)/shard_map/ppermute | solution.py:546
  145.2 16.2 %collective-permute-start.5 = (bf16[512,512]{1,0:T(8,128)(2,1)}, bf16[512,512]{1,0:T(8,128)(2,1)S(1)}, u32[]{:S(2)}, u32[]{:S(2)}) collective-permute-start(bf16[512,512]{1,0:T(8,128)(2,1)} %bitcast.9), channel_id=1, source_target_pairs={{0,1},{1,2},{2,3},{3,0},{4,5},{5,6},{6,7},{7,4},{8,9},{9,10},{10,1... | collective-permute-start | bytes 1572872 | tf_op jit(solution)/shard_map/ppermute | solution.py:545
  148.6 14.5 %collective-permute-start.12 = (bf16[1,2,512,256]{3,2,1,0:T(8,128)(2,1)}, bf16[1,2,512,256]{3,2,1,0:T(8,128)(2,1)}, u32[]{:S(2)}, u32[]{:S(2)}) collective-permute-start(bf16[1,2,512,256]{3,2,1,0:T(8,128)(2,1)} %slice.26), channel_id=1, source_target_pairs={{0,32},{32,64},{64,96},{96,0},{1,33},{33,65},{65,97},{97,1},{2,34}... | collective-permute-start | bytes 1572872 | tf_op jit(solution)/shard_map/ppermute | solution.py:534
  150.5 21.2 %copy-start = (bf16[512,512]{1,0:T(8,128)(2,1)}, bf16[512,512]{1,0:T(8,128)(2,1)S(1)}, u32[]{:S(2)}) copy-start(bf16[512,512]{1,0:T(8,128)(2,1)S(1)} %collective-permute-done.1.refs_3_.refs_2_) | copy-start | bytes 1572868
  150.5 13.7 %collective-permute-start.13 = (bf16[1,2,512,256]{3,2,1,0:T(8,128)(2,1)}, bf16[1,2,512,256]{3,2,1,0:T(8,128)(2,1)}, u32[]{:S(2)}, u32[]{:S(2)}) collective-permute-start(bf16[1,2,512,256]{3,2,1,0:T(8,128)(2,1)} %slice.27), channel_id=1, source_target_pairs={{0,96},{32,0},{64,32},{96,64},{1,97},{33,1},{65,33},{97,65},{2,98}... | collective-permute-start | bytes 1572872 | tf_op jit(solution)/shard_map/ppermute | solution.py:535
  154.3 16.8 %collective-permute-start.3 = (bf16[512,512]{1,0:T(8,128)(2,1)S(1)}, bf16[512,512]{1,0:T(8,128)(2,1)}, u32[]{:S(2)}, u32[]{:S(2)}) collective-permute-start(bf16[512,512]{1,0:T(8,128)(2,1)S(1)} %collective-permute-done.2.refs_0_.refs_5_), channel_id=1, source_target_pairs={{0,1},{1,2},{2,3},{3,0},{4,5},{5,6},{6,7},{7,4},{8,9},{9,10},{10,1... | collective-permute-start | bytes 1572872 | tf_op jit(solution)/shard_map/ppermute | solution.py:547
  155.9 15.3 %collective-permute-start.4 = (bf16[512,512]{1,0:T(8,128)(2,1)S(1)}, bf16[512,512]{1,0:T(8,128)(2,1)}, u32[]{:S(2)}, u32[]{:S(2)}) collective-permute-start(bf16[512,512]{1,0:T(8,128)(2,1)S(1)} %collective-permute-done.1.refs_3_.refs_2_), channel_id=1, source_target_pairs={{0,3},{1,0},{2,1},{3,2},{4,7},{5,4},{6,5},{7,6},{8,11},{9,8},{10,9... | collective-permute-start | bytes 1572872 | tf_op jit(solution)/shard_map/ppermute | solution.py:548
  161.4 35.7 %collective-permute-start.20 = (bf16[2,2,512,256]{3,2,1,0:T(8,128)(2,1)}, bf16[2,2,512,256]{3,2,1,0:T(8,128)(2,1)}, u32[]{:S(2)}, u32[]{:S(2)}) collective-permute-start(bf16[2,2,512,256]{3,2,1,0:T(8,128)(2,1)} %bitcast.19.refs_0_), channel_id=1, source_target_pairs={{0,8},{8,0},{1,9},{9,1},{2,10},{10,2},{3,11},{11,3},{4,12},{12,4},... | collective-permute-start | bytes 3145736 | tf_op jit(solution)/shard_map/ppermute | solution.py:538
  163.0 34.0 %collective-permute-start.21 = (bf16[2,2,512,256]{3,2,1,0:T(8,128)(2,1)}, bf16[2,2,512,256]{3,2,1,0:T(8,128)(2,1)}, u32[]{:S(2)}, u32[]{:S(2)}) collective-permute-start(bf16[2,2,512,256]{3,2,1,0:T(8,128)(2,1)} %collective-permute-done.10.refs_1_), channel_id=1, source_target_pairs={{0,8},{8,0},{1,9},{9,1},{2,10},{10,2},{3,11},{11,3},{4,12},{12,4},... | collective-permute-start | bytes 3145736 | tf_op jit(solution)/shard_map/ppermute | solution.py:538
  164.2 32.9 %collective-permute-start.22 = (bf16[2,2,512,256]{3,2,1,0:T(8,128)(2,1)}, bf16[2,2,512,256]{3,2,1,0:T(8,128)(2,1)}, u32[]{:S(2)}, u32[]{:S(2)}) collective-permute-start(bf16[2,2,512,256]{3,2,1,0:T(8,128)(2,1)} %collective-permute-done.11.refs_2_), channel_id=1, source_target_pairs={{0,8},{8,0},{1,9},{9,1},{2,10},{10,2},{3,11},{11,3},{4,12},{12,4},... | collective-permute-start | bytes 3145736 | tf_op jit(solution)/shard_map/ppermute | solution.py:538
  171.1 25.9 %collective-permute-start.23 = (bf16[1,2,512,256]{3,2,1,0:T(8,128)(2,1)}, bf16[1,2,512,256]{3,2,1,0:T(8,128)(2,1)S(1)}, u32[]{:S(2)}, u32[]{:S(2)}) collective-permute-start(bf16[1,2,512,256]{3,2,1,0:T(8,128)(2,1)} %collective-permute-done.12.refs_3_), channel_id=1, source_target_pairs={{0,8},{8,0},{1,9},{9,1},{2,10},{10,2},{3,11},{11,3},{4,12},{12,4},... | collective-permute-start | bytes 1572872 | tf_op jit(solution)/shard_map/ppermute | solution.py:538
  171.2 25.9 %collective-permute-start.24 = (bf16[1,2,512,256]{3,2,1,0:T(8,128)(2,1)}, bf16[1,2,512,256]{3,2,1,0:T(8,128)(2,1)}, u32[]{:S(2)}, u32[]{:S(2)}) collective-permute-start(bf16[1,2,512,256]{3,2,1,0:T(8,128)(2,1)} %collective-permute-done.13.refs_4_), channel_id=1, source_target_pairs={{0,8},{8,0},{1,9},{9,1},{2,10},{10,2},{3,11},{11,3},{4,12},{12,4},... | collective-permute-start | bytes 1572872 | tf_op jit(solution)/shard_map/ppermute | solution.py:538
  171.7 8.1 %copy-start.2 = (f32[512,128]{1,0:T(8,128)S(1)}, f32[512,128]{1,0:T(8,128)}, u32[]{:S(2)}) copy-start(f32[512,128]{1,0:T(8,128)} %get-tuple-element.60.refs_7_) | copy-start | bytes 786436
  197.1 0.8 copy-start.4
  208.5 16.6 %collective-permute-start.28 = (bf16[128,1024]{1,0:T(8,128)(2,1)}, bf16[128,1024]{1,0:T(8,128)(2,1)}, u32[]{:S(2)}, u32[]{:S(2)}) collective-permute-start(bf16[128,1024]{1,0:T(8,128)(2,1)} %get-tuple-element.45), channel_id=1, source_target_pairs={{0,3},{1,0},{2,1},{3,2},{4,7},{5,4},{6,5},{7,6},{8,11},{9,8},{10,9... | collective-permute-start | bytes 786440 | tf_op jit(solution)/shard_map/ppermute | solution.py:480
  211.1 40.3 %copy-start.1 = (bf16[512,512]{1,0:T(8,128)(2,1)S(1)}, bf16[512,512]{1,0:T(8,128)(2,1)}, u32[]{:S(2)}) copy-start(bf16[512,512]{1,0:T(8,128)(2,1)} %copy-done) | copy-start | bytes 1572868
  211.1 17.9 %collective-permute-start.25 = (bf16[128,1024]{1,0:T(8,128)(2,1)S(1)}, bf16[128,1024]{1,0:T(8,128)(2,1)}, u32[]{:S(2)}, u32[]{:S(2)}) collective-permute-start(bf16[128,1024]{1,0:T(8,128)(2,1)S(1)} %get-tuple-element.47), channel_id=1, source_target_pairs={{0,3},{1,0},{2,1},{3,2},{4,7},{5,4},{6,5},{7,6},{8,11},{9,8},{10,9... | collective-permute-start | bytes 786440 | tf_op jit(solution)/shard_map/ppermute | solution.py:480
  222.6 10.5 %collective-permute-start.17 = (bf16[128,1024]{1,0:T(8,128)(2,1)S(1)}, bf16[128,1024]{1,0:T(8,128)(2,1)S(1)}, u32[]{:S(2)}, u32[]{:S(2)}) collective-permute-start(bf16[128,1024]{1,0:T(8,128)(2,1)S(1)} %get-tuple-element.49), channel_id=1, source_target_pairs={{0,1},{1,2},{2,3},{3,0},{4,5},{5,6},{6,7},{7,4},{8,9},{9,10},{10,1... | collective-permute-start | bytes 786440 | tf_op jit(solution)/shard_map/ppermute | solution.py:480
  224.5 14.2 %collective-permute-start.14 = (bf16[128,1024]{1,0:T(8,128)(2,1)S(1)}, bf16[128,1024]{1,0:T(8,128)(2,1)S(1)}, u32[]{:S(2)}, u32[]{:S(2)}) collective-permute-start(bf16[128,1024]{1,0:T(8,128)(2,1)S(1)} %get-tuple-element.51), channel_id=1, source_target_pairs={{0,1},{1,2},{2,3},{3,0},{4,5},{5,6},{6,7},{7,4},{8,9},{9,10},{10,1... | collective-permute-start | bytes 786440 | tf_op jit(solution)/shard_map/ppermute | solution.py:480
  226.1 13.7 %collective-permute-start.29 = (bf16[128,1024]{1,0:T(8,128)(2,1)S(1)}, bf16[128,1024]{1,0:T(8,128)(2,1)S(1)}, u32[]{:S(2)}, u32[]{:S(2)}) collective-permute-start(bf16[128,1024]{1,0:T(8,128)(2,1)S(1)} %add_convert_fusion.1), channel_id=1, source_target_pairs={{0,3},{1,0},{2,1},{3,2},{4,7},{5,4},{6,5},{7,6},{8,11},{9,8},{10,9... | collective-permute-start | bytes 786440 | tf_op jit(solution)/shard_map/ppermute | solution.py:480
  230.1 14.1 %collective-permute-start.26 = (bf16[128,1024]{1,0:T(8,128)(2,1)S(1)}, bf16[128,1024]{1,0:T(8,128)(2,1)S(1)}, u32[]{:S(2)}, u32[]{:S(2)}) collective-permute-start(bf16[128,1024]{1,0:T(8,128)(2,1)S(1)} %add_convert_fusion.3), channel_id=1, source_target_pairs={{0,3},{1,0},{2,1},{3,2},{4,7},{5,4},{6,5},{7,6},{8,11},{9,8},{10,9... | collective-permute-start | bytes 786440 | tf_op jit(solution)/shard_map/ppermute | solution.py:480
  234.1 11.1 %collective-permute-start.18 = (bf16[128,1024]{1,0:T(8,128)(2,1)S(1)}, bf16[128,1024]{1,0:T(8,128)(2,1)S(1)}, u32[]{:S(2)}, u32[]{:S(2)}) collective-permute-start(bf16[128,1024]{1,0:T(8,128)(2,1)S(1)} %add_convert_fusion.5), channel_id=1, source_target_pairs={{0,1},{1,2},{2,3},{3,0},{4,5},{5,6},{6,7},{7,4},{8,9},{9,10},{10,1... | collective-permute-start | bytes 786440 | tf_op jit(solution)/shard_map/ppermute | solution.py:480
  239.7 10.5 %collective-permute-start.15 = (bf16[128,1024]{1,0:T(8,128)(2,1)S(1)}, bf16[128,1024]{1,0:T(8,128)(2,1)S(1)}, u32[]{:S(2)}, u32[]{:S(2)}) collective-permute-start(bf16[128,1024]{1,0:T(8,128)(2,1)S(1)} %add_convert_fusion.7), channel_id=1, source_target_pairs={{0,1},{1,2},{2,3},{3,0},{4,5},{5,6},{6,7},{7,4},{8,9},{9,10},{10,1... | collective-permute-start | bytes 786440 | tf_op jit(solution)/shard_map/ppermute | solution.py:480
  240.9 12.5 %collective-permute-start.30 = (bf16[128,1024]{1,0:T(8,128)(2,1)S(1)}, bf16[128,1024]{1,0:T(8,128)(2,1)S(1)}, u32[]{:S(2)}, u32[]{:S(2)}) collective-permute-start(bf16[128,1024]{1,0:T(8,128)(2,1)S(1)} %add_convert_fusion), channel_id=1, source_target_pairs={{0,3},{1,0},{2,1},{3,2},{4,7},{5,4},{6,5},{7,6},{8,11},{9,8},{10,9... | collective-permute-start | bytes 786440 | tf_op jit(solution)/shard_map/ppermute | solution.py:480
  245.2 8.3 %collective-permute-start.27 = (bf16[128,1024]{1,0:T(8,128)(2,1)S(1)}, bf16[128,1024]{1,0:T(8,128)(2,1)S(1)}, u32[]{:S(2)}, u32[]{:S(2)}) collective-permute-start(bf16[128,1024]{1,0:T(8,128)(2,1)S(1)} %add_convert_fusion.2), channel_id=1, source_target_pairs={{0,3},{1,0},{2,1},{3,2},{4,7},{5,4},{6,5},{7,6},{8,11},{9,8},{10,9... | collective-permute-start | bytes 786440 | tf_op jit(solution)/shard_map/ppermute | solution.py:480
  246.3 10.1 %collective-permute-start.19 = (bf16[128,1024]{1,0:T(8,128)(2,1)S(1)}, bf16[128,1024]{1,0:T(8,128)(2,1)S(1)}, u32[]{:S(2)}, u32[]{:S(2)}) collective-permute-start(bf16[128,1024]{1,0:T(8,128)(2,1)S(1)} %add_convert_fusion.4), channel_id=1, source_target_pairs={{0,1},{1,2},{2,3},{3,0},{4,5},{5,6},{6,7},{7,4},{8,9},{9,10},{10,1... | collective-permute-start | bytes 786440 | tf_op jit(solution)/shard_map/ppermute | solution.py:480
  251.2 8.7 %collective-permute-start.16 = (bf16[128,1024]{1,0:T(8,128)(2,1)S(1)}, bf16[128,1024]{1,0:T(8,128)(2,1)S(1)}, u32[]{:S(2)}, u32[]{:S(2)}) collective-permute-start(bf16[128,1024]{1,0:T(8,128)(2,1)S(1)} %add_convert_fusion.6), channel_id=1, source_target_pairs={{0,1},{1,2},{2,3},{3,0},{4,5},{5,6},{6,7},{7,4},{8,9},{9,10},{10,1... | collective-permute-start | bytes 786440 | tf_op jit(solution)/shard_map/ppermute | solution.py:480
Sparse Core Ops, SparseCore 0:
  22.7 85.9 all-gather.1

commit v5 on v4

--- a/solution.py
+++ b/solution.py
@@ -71,7 +71,7 @@
     slab = tile_count // slabs
     lane = lax.broadcasted_iota(jnp.int32, (columns, LANES), 1).astype(jnp.int16)
     left = lane < jnp.int16(LANES // 2)
-    unroll = min(32, slab)
+    unroll = min(56, slab)
 
     def incoming(k):
         part = pl.ds(k * slab * LANES, slab * LANES)
@@ -242,26 +242,29 @@
     cache_ref[0] = key_rot
     cache_ref[1] = value
     length = length_ref[0]
-    block = min(128, row_count)
+    block = min(256, row_count)
     power = 1.4426950408889634 / HD**0.5
     for h in range(q_heads):
         query = rotate(proj_ref[:, h * HD : (h + 1) * HD])
         for start in range(0, row_count, block):
             keys = start + block
             scores = lax.dot_general(
+                key_rot[:keys],
                 query[start : start + block],
-                key_rot[:keys],
                 (((1,), (1,)), ((), ())),
                 preferred_element_type=jnp.float32,
             )
-            q_pos = start + lax.broadcasted_iota(jnp.int32, (block, 1), 0)
-            k_pos = lax.broadcasted_iota(jnp.int32, (block, keys), 1)
+            q_pos = start + lax.broadcasted_iota(jnp.int32, (1, block), 1)
+            k_pos = lax.broadcasted_iota(jnp.int32, (keys, block), 0)
             scores = jnp.where(k_pos < jnp.minimum(q_pos + 1, length), scores, -1e30)
-            biggest = jnp.max(scores, axis=-1, keepdims=True)
+            biggest = jnp.max(scores, axis=0, keepdims=True)
             expd = jnp.exp2((scores - biggest) * power)
-            weights_now = expd * (1.0 / jnp.sum(expd, axis=-1, keepdims=True))
-            attended_ref[start : start + block, h * HD : (h + 1) * HD] = jnp.dot(
-                weights_now.astype(jnp.bfloat16), value[:keys], preferred_element_type=jnp.float32
+            weights_now = expd * (1.0 / jnp.sum(expd, axis=0, keepdims=True))
+            attended_ref[start : start + block, h * HD : (h + 1) * HD] = lax.dot_general(
+                weights_now.astype(jnp.bfloat16),
+                value[:keys],
+                (((0,), (0,)), ((), ())),
+                preferred_element_type=jnp.float32,
             ).astype(jnp.bfloat16)
 
 
@@ -368,45 +371,60 @@
     return [(k, (k + way) % count) for k in range(count)]
 
 
-def product_kernel(xh_ref, rows_ref, *refs, pieces, outs):
-    held, arrived = refs[-2:]
-    out_refs = refs[-2 - outs : -2]
-    _, halves, depth, width = held.shape
-
-    def incoming(k):
+def product_kernel(where_ref, rows_ref, *refs, pieces, turns, chunks):
+    turned, held, arrived = refs[-3:]
+    out_refs = refs[-3 - len(turns) * chunks : -3]
+    quarter = out_refs[0].shape[0]
+    ring = rows_ref.shape[0] // quarter
+    _, halves, depth, width = refs[0].shape
+
+    def incoming(k, half):
         array, index = pieces[k]
-        return pltpu.make_async_copy(refs[array].at[index], held.at[k], arrived.at[k])
-
-    for k in range(len(pieces)):
-        incoming(k).start()
-    each = len(pieces) // outs
-    for k in range(len(pieces)):
-        incoming(k).wait()
-        total = None
-        for half in range(halves):
-            block = xh_ref[0] ^ half
-            rows = rows_ref[:, pl.ds(pl.multiple_of(block * depth, depth), depth)]
-            term = jnp.dot(rows, held[k, half], preferred_element_type=jnp.float32)
-            total = term if total is None else total + term
-        here = slice(k % each * width, (k % each + 1) * width)
-        out_refs[k // each][:, here] = total.astype(jnp.bfloat16)
-
-
-def product(xh, rows, weights, pieces, outs):
+        block = where_ref[1] ^ half
+        return pltpu.make_async_copy(
+            refs[array].at[index, half],
+            held.at[pl.ds(pl.multiple_of(block * depth, depth), depth), pl.ds(k * width, width)],
+            arrived.at[k, half],
+        )
+
+    copies = [(k, half) for k in range(len(pieces)) for half in range(halves)]
+    for copy in copies:
+        incoming(*copy).start()
+    for at, turn in enumerate(turns):
+        block = lax.rem(where_ref[0] + ring + turn, ring)
+        turned[at * quarter : (at + 1) * quarter] = rows_ref[
+            pl.ds(pl.multiple_of(block * quarter, quarter), quarter)
+        ]
+    each = len(pieces) // chunks
+    for chunk in range(chunks):
+        for copy in copies[chunk * each * halves : (chunk + 1) * each * halves]:
+            incoming(*copy).wait()
+        total = jnp.dot(
+            turned[...],
+            held[:, chunk * each * width : (chunk + 1) * each * width],
+            preferred_element_type=jnp.float32,
+        ).astype(jnp.bfloat16)
+        for at in range(len(turns)):
+            out_refs[chunk * len(turns) + at][...] = total[at * quarter : (at + 1) * quarter]
+
+
+def product(where, rows, weights, pieces, turns, chunks):
     _, halves, depth, width = weights[0].shape
     row_count = rows.shape[0]
     count = len(pieces)
     return pl.pallas_call(
-        functools.partial(product_kernel, pieces=pieces, outs=outs),
+        functools.partial(product_kernel, pieces=pieces, turns=turns, chunks=chunks),
         in_specs=[pl.BlockSpec(memory_space=pltpu.SMEM), pl.BlockSpec(memory_space=pltpu.VMEM)]
         + [pl.BlockSpec(memory_space=pltpu.HBM)] * len(weights),
-        out_specs=tuple([pl.BlockSpec(memory_space=pltpu.VMEM)] * outs),
+        out_specs=tuple([pl.BlockSpec(memory_space=pltpu.VMEM)] * (len(turns) * chunks)),
         out_shape=tuple(
-            [jax.ShapeDtypeStruct((row_count, count // outs * width), jnp.bfloat16)] * outs
+            [jax.ShapeDtypeStruct((row_count // len(turns), count // chunks * width), jnp.bfloat16)]
+            * (len(turns) * chunks)
         ),
         scratch_shapes=[
-            pltpu.VMEM((count, halves, depth, width), jnp.bfloat16),
-            pltpu.SemaphoreType.DMA((count,)),
+            pltpu.VMEM(rows.shape, jnp.bfloat16),
+            pltpu.VMEM((halves * depth, count * width), jnp.bfloat16),
+            pltpu.SemaphoreType.DMA((count, halves)),
         ],
         compiler_params=pltpu.CompilerParams(vmem_limit_bytes=60 * 2**20),
         cost_estimate=pl.CostEstimate(
@@ -415,7 +433,7 @@
             transcendentals=0,
         ),
         name="product",
-    )(xh, rows, *weights)
+    )(where, rows, *weights)
 
 
 LAYERS = (0, 1, 3, 2)
@@ -460,29 +478,23 @@
 CHUNKS = 2
 
 
-def ring_sums(attended, weights, quarter):
-    place = lax.axis_index(RING)
+def ring_sums(attended, weights):
     count = lax.axis_size(RING)
-    pieces = [(LAYERS.index(z), (side,)) for z in LAYERS[:3] for side in range(2)]
-    pieces += [(3, (0,)), (4, (0,))]
-    xh = lax.axis_index("tensor_0")[None]
+    pieces = [(LAYERS.index(z), side) for z in LAYERS[:3] for side in range(2)]
+    pieces += [(3, 0), (4, 0)]
+    where = jnp.stack([lax.axis_index(RING), lax.axis_index("tensor_0")])
     sums = []
     for side, way in enumerate((1, -1)):
-        chunks = product(xh, attended, weights[side], pieces, CHUNKS)
-        for partial_sums in chunks:
-
-            def part(turn):
-                start = (place + turn) % count * quarter
-                return lax.dynamic_slice_in_dim(partial_sums, start, quarter, 0)
-
-            running = part(-way)
+        turns = [-way * (step + 1) for step in range(count)]
+        parts = product(where, attended, weights[side], pieces, turns, CHUNKS)
+        for chunk in range(CHUNKS):
+            running, *mine = parts[chunk * count : (chunk + 1) * count]
             for step in range(1, count):
                 running = lax.ppermute(running, RING, ring_route(way))
-                mine = part(-way * (step + 1))
                 if step + 1 < count:
-                    running = running.astype(jnp.float32) + mine.astype(jnp.float32)
+                    running = running.astype(jnp.float32) + mine[step - 1].astype(jnp.float32)
                     running = running.astype(jnp.bfloat16)
-            sums += [running, mine]
+            sums += [running, mine[-1]]
     return sums
 
 
@@ -530,13 +542,6 @@
     back = [(z, (z - 1) % layers) for z in range(layers)]
     for route in (ahead, back):
         w_mine.append(lax.ppermute(w_mine[0], "dp_0", route))
-    first_side, last_side = w_mine[1][:1], w_mine[2][1:]
-    w_mine.append(lax.ppermute(first_side, "dp_0", ahead))
-    w_mine.append(lax.ppermute(last_side, "dp_0", back))
-    w_other = []
-    for k in range(len(w_mine)):
-        w_other.append(lax.ppermute(w_mine[k], "dp_2", [(0, 1), (1, 0)]))
-
     places = (place + jnp.arange(ring, dtype=jnp.int32)) % ring
     half = own.shape[0] // 2
     low, high = own[:half], own[half:]
@@ -559,6 +564,13 @@
         ],
         first,
     )
+    z_sides, _ = lax.optimization_barrier((w_mine[1:], second))
+    first_side, last_side = z_sides[0][:1], z_sides[1][1:]
+    w_mine.append(lax.ppermute(first_side, "dp_0", ahead))
+    w_mine.append(lax.ppermute(last_side, "dp_0", back))
+    w_other = []
+    for k in range(len(w_mine)):
+        w_other.append(lax.ppermute(w_mine[k], "dp_2", [(0, 1), (1, 0)]))
     attended, cache = attend(
         places,
         w_in,
@@ -574,7 +586,7 @@
     pieces, _ = lax.optimization_barrier((pieces, attended))
     own_rows = residual(places, pieces, columns, quarter)
 
-    sums = ring_sums(attended, (w_mine, w_other), quarter)
+    sums = ring_sums(attended, (w_mine, w_other))
     where = jnp.stack([lax.axis_index(name) for name in DP])
     hidden = finish(where, own_rows, sums, w_out.shape[1])
     return hidden, cache[None]

time: 271 us -> 252 us (0.930)
  Pallas kernels: 88.1 us -> 76 us
  waiting for transfers between devices: 76.5 us -> 68.2 us
  starting transfers between devices: 43.6 us -> 49.6 us
  local copies, waits for them, and re-layouts: 12.7 us -> 6.92 us
    ppermute x3, waiting for transfers between devices: 28.3 us -> 7.77 us  [sublayer(): pieces_x.append(lax.ppermute(w_out, axes, route))]
    all_to_all x1, waiting for transfers between devices: 0.01 us -> 17.7 us  [sublayer(): lax.all_to_all(outgoing, PLANE, split_axis=0, concat_axis=0, tiled=True)]
    ppermute x2, waiting for transfers between devices: 16.5 us -> 0.01 us  [sublayer(): w_mine.append(lax.ppermute(w_mine[0], 'dp_0', route))]
    ppermute x1, waiting for transfers between devices: 2.75 us -> 10.9 us  [sublayer(): high_before = lax.ppermute(high, RING, ring_route(1))]
    ppermute x12, starting transfers between devices: 14.3 us -> 22.4 us  [ring_sums(): running = lax.ppermute(running, RING, ring_route(way))]
    pallas_call x1, Pallas kernels: 17.3 us -> 11.3 us  [attend(): pl.pallas_call(functools.partial(attention_kernel, parts=len(parts), mode...]
    pallas_call x2, Pallas kernels: 17.7 us -> 12.6 us  [product(): pl.pallas_call(functools.partial(product_kernel, pieces=pieces, turns=tur...]
    dynamic_slice x4 -> x0, local copies, waits for them, and re-layouts: 4.96 us -> none  [part(): return lax.dynamic_slice_in_dim(partial_sums, start, quarter, 0)]
  transfers between devices with their start and end apart: 33 -> 33, of which waited for: 13 -> 13; matrix products, arithmetic and copies ran while one was open for 8% -> 8% of each run, Pallas kernels for 29% -> 30%
where the time goes in v5:
time: 252 us; the launch traced here: 250 us
  Pallas kernels  76 us (30%)
  waiting for transfers between devices  68.2 us (27%)
  starting transfers between devices  49.6 us (20%)
  blocking collectives  18.7 us (7%)
  other arithmetic  16.7 us (7%)
  between operations  14.3 us (6%)
  local copies, waits for them, and re-layouts  6.92 us (3%)
    pallas_call x1, Pallas kernels, lookup(): pl.pallas_call(lookup_kernel, out_shape=jax.ShapeDtypeStruct((group_count...  34.7 us
    ppermute x12, starting transfers between devices, ring_sums(): running = lax.ppermute(running, RING, ring_route(way))  22.4 us
    all_to_all x1, blocking collectives, sublayer(): lax.all_to_all(jnp.broadcast_to(prompt_ids[None], (devices, quarter)), DP...  18.7 us
    all_to_all x1, waiting for transfers between devices, sublayer(): lax.all_to_all(outgoing, PLANE, split_axis=0, concat_axis=0, tiled=True)  17.7 us
    ppermute x12, waiting for transfers between devices, ring_sums(): running = lax.ppermute(running, RING, ring_route(way))  15.2 us
    pallas_call x2, Pallas kernels, project(): pl.pallas_call(functools.partial(project_kernel, parts=len(parts), carrie...  13.3 us
    pallas_call x2, Pallas kernels, product(): pl.pallas_call(functools.partial(product_kernel, pieces=pieces, turns=tur...  12.6 us
    pallas_call x1, Pallas kernels, attend(): pl.pallas_call(functools.partial(attention_kernel, parts=len(parts), mode...  11.3 us
  transfers between devices with their start and end apart: 33, of which 13 were waited for; matrix products, arithmetic and copies ran while one was open for 8% of the time, Pallas kernels for 30%

profile of v5, /device:TPU:6, one launch (start us, length us, event | category | flops | bytes accessed | tf_op | source)
XLA Modules:
  0.0 250.4 jit_solution(7084852579028342588)
XLA Ops:
  8.0 1.2 multiply_convert_fusion
  9.2 1.5 collective-permute-start.6
  10.6 11.0 %collective-permute-done.6 = bf16[1,256,768]{2,1,0:T(8,128)(2,1)S(1)} collective-permute-done((bf16[1,256,768]{2,1,0:T(8,128)(2,1)S(1)}, bf16[1,256,768]{2,1,0:T(8,128)(2,1)S(1)}, u32[]{:S(2)}, u32[]{:S(2)}) %collective-permute-start.6) | collective-permute-done | bytes 393248 | tf_op jit(solution)/shard_map/ppermute | solution.py:34
  23.3 18.7 %all_to_all.11 = s32[128,1,128]{2,1,0:T(1,128)S(1)} all-to-all(s32[128,1,128]{2,1,0:T(1,128)S(1)} %broadcast_in_dim.4), channel_id=1, replica_groups=mesh['dp_0'=4,'dp_1'=2,'dp_2'=2,'tensor_0'=2,'tensor_1'=4] {'dp_0','dp_1..., dimensions={0} | all-to-all | bytes 131072 | tf_op jit(solution)/shard_map/all_to_all | solution.py:520
  43.4 34.7 %lookup.1 = bf16[32,32,512]{2,1,0:T(8,128)(2,1)} custom-call(s32[16384]{0:T(1024)} %fusion.2.slots_ref, s32[128,128]{1,0:T(8,128)} %bitcast_or_fusion.lanes_ref, bf16[32,128256]{1,0:T(8,128)(2,1)} %table_ref.1), custom_call_target="tpu_custom_call" | custom-call | flops 30000001024 | bytes 8208384 | tf_op jit(solution)/shard_map/lookup/pallas_call | solution.py:131
  78.1 5.8 %all-to-all-start.1 = ((bf16[32,32,512]{2,1,0:T(8,128)(2,1)}), bf16[32,32,512]{2,1,0:T(8,128)(2,1)S(1)}, u32[]{:S(2)}, u32[]{:S(2)}) async-start(bf16[32,32,512]{2,1,0:T(8,128)(2,1)} %lookup.1), calls=%async_computation.1 | async-start | bytes 2097152 | tf_op jit(solution)/shard_map/all_to_all | solution.py:535
  83.9 1.5 collective-permute-start.7
  85.4 2.6 %collective-permute-start.9 = (bf16[512,256]{1,0:T(8,128)(2,1)S(1)}, bf16[512,256]{1,0:T(8,128)(2,1)S(1)}, u32[]{:S(2)}, u32[]{:S(2)}) collective-permute-start(bf16[512,256]{1,0:T(8,128)(2,1)S(1)} %copy-done.7), channel_id=1, source_target_pairs={{0,20},{4,16},{16,4},{20,0},{1,21},{5,17},{17,5},{21,1},{2,22},{6,... | collective-permute-start | bytes 786440 | tf_op jit(solution)/shard_map/ppermute | solution.py:533
  88.1 17.7 %all-to-all-done.1 = bf16[32,32,512]{2,1,0:T(8,128)(2,1)S(1)} async-done(((bf16[32,32,512]{2,1,0:T(8,128)(2,1)}), bf16[32,32,512]{2,1,0:T(8,128)(2,1)S(1)}, u32[]{:S(2)}, u32[]{:S(2)}) %all-to-all-start.1) | async-done | bytes 1048608 | tf_op jit(solution)/shard_map/all_to_all | solution.py:535
  106.8 2.7 %collective-permute-start = (bf16[512,512]{1,0:T(8,128)(2,1)}, bf16[512,512]{1,0:T(8,128)(2,1)S(1)}, u32[]{:S(2)}, u32[]{:S(2)}) collective-permute-start(bf16[512,512]{1,0:T(8,128)(2,1)} %bitcast.8), channel_id=1, source_target_pairs={{0,3},{1,0},{2,1},{3,2},{4,7},{5,4},{6,5},{7,6},{8,11},{9,8},{10,9... | collective-permute-start | bytes 1572872 | tf_op jit(solution)/shard_map/ppermute | solution.py:551
  109.5 2.9 %collective-permute-done.7 = bf16[512,256]{1,0:T(8,128)(2,1)S(1)} collective-permute-done((bf16[512,256]{1,0:T(8,128)(2,1)S(1)}, bf16[512,256]{1,0:T(8,128)(2,1)S(1)}, u32[]{:S(2)}, u32[]{:S(2)}) %collective-permute-start.7) | collective-permute-done | bytes 262176 | tf_op jit(solution)/shard_map/ppermute | solution.py:533
  112.3 4.9 %collective-permute-done.8 = bf16[512,256]{1,0:T(8,128)(2,1)S(1)} collective-permute-done((bf16[512,256]{1,0:T(8,128)(2,1)S(1)}, bf16[512,256]{1,0:T(8,128)(2,1)S(1)}, u32[]{:S(2)}, u32[]{:S(2)}) %collective-permute-start.8) | collective-permute-done | bytes 262176 | tf_op jit(solution)/shard_map/ppermute | solution.py:533
  117.2 1.1 pad_maximum_fusion
  118.3 3.2 %collective-permute-start.11 = (bf16[2,2,512,256]{3,2,1,0:T(8,128)(2,1)}, bf16[2,2,512,256]{3,2,1,0:T(8,128)(2,1)}, u32[]{:S(2)}, u32[]{:S(2)}) collective-permute-start(bf16[2,2,512,256]{3,2,1,0:T(8,128)(2,1)} %bitcast.20.refs_0_), channel_id=1, source_target_pairs={{0,96},{32,0},{64,32},{96,64},{1,97},{33,1},{65,33},{97,65},{2,98}... | collective-permute-start | bytes 3145736 | tf_op jit(solution)/shard_map/ppermute | solution.py:544
  121.6 1.5 collective-permute-start.2
  123.1 1.7 collective-permute-start.1
  125.1 1.8 fusion
  127.0 5.2 %project.2 = (f32[512,1536]{1,0:T(8,128)}, f32[1,512]{1,0:T(1,128)S(1)}) custom-call(s32[4]{0:T(128)S(1)} %and_select_fusion.places_ref, bf16[1024,512]{1,0:T(8,128)(2,1)S(1)} %bitcast.28, bf16[2,32,4,32,768]{4,3,2,1,0:T(8,128)(2,1)} %bitcast.30), custom_call_target="tpu_custom_call" | custom-call | flops 1610612736 | bytes 4194304 | tf_op jit(solution)/shard_map/project/pallas_call | solution.py:201
  132.2 4.4 %collective-permute-done.1.refs_3_.refs_2_ = bf16[512,512]{1,0:T(8,128)(2,1)S(1)} collective-permute-done((bf16[512,512]{1,0:T(8,128)(2,1)}, bf16[512,512]{1,0:T(8,128)(2,1)S(1)}, u32[]{:S(2)}, u32[]{:S(2)}) %collective-permute-start.1) | collective-permute-done | bytes 524320 | tf_op jit(solution)/shard_map/ppermute | solution.py:549
  136.5 1.3 collective-permute-done.2.refs_0_.refs_5_
  138.1 10.9 %collective-permute-done.5.refs_1_.refs_6_ = bf16[512,512]{1,0:T(8,128)(2,1)S(1)} collective-permute-done((bf16[512,512]{1,0:T(8,128)(2,1)}, bf16[512,512]{1,0:T(8,128)(2,1)S(1)}, u32[]{:S(2)}, u32[]{:S(2)}) %collective-permute-start.5) | collective-permute-done | bytes 524320 | tf_op jit(solution)/shard_map/ppermute | solution.py:550
  149.0 1.6 collective-permute-start.4
  150.6 8.1 %project.3 = (f32[512,1536]{1,0:T(8,128)}, f32[1,512]{1,0:T(1,128)S(1)}) custom-call(s32[4]{0:T(128)S(1)} %and_select_fusion.places_ref, bf16[512,512]{1,0:T(8,128)(2,1)S(1)} %collective-permute-done.2.refs_0_.refs_5_, bf16[512,512]{1,0:T(8,128)(2,1)S(1)} %collective-permute-done.5.refs_1_.refs_6_, ...), custom_call_target="tpu_custom_call" | custom-call | flops 3221225472 | bytes 8388608 | tf_op jit(solution)/shard_map/project/pallas_call | solution.py:201
  158.7 1.9 slice.22
  160.7 1.9 slice.23
  162.6 3.2 %collective-permute-start.13 = (bf16[1,2,512,256]{3,2,1,0:T(8,128)(2,1)}, bf16[1,2,512,256]{3,2,1,0:T(8,128)(2,1)}, u32[]{:S(2)}, u32[]{:S(2)}) collective-permute-start(bf16[1,2,512,256]{3,2,1,0:T(8,128)(2,1)} %slice.23), channel_id=1, source_target_pairs={{0,96},{32,0},{64,32},{96,64},{1,97},{33,1},{65,33},{97,65},{2,98}... | collective-permute-start | bytes 1572872 | tf_op jit(solution)/shard_map/ppermute | solution.py:570
  167.1 1.3 pad_maximum_fusion.2
  169.0 11.3 %attend.1 = (bf16[512,1024]{1,0:T(8,128)(2,1)}, bf16[2,512,256]{2,1,0:T(8,128)(2,1)}) custom-call(s32[4]{0:T(128)S(1)} %and_select_fusion.places_ref, s32[1]{0:T(128)} %dynamic_slice.6.length_ref, bf16[512,512]{1,0:T(8,128)(2,1)} %collective-permute-done.3.refs_0_.refs_3_, bf16[512,512]{1,0:T(8,128)(2,1)} %collective-permute-done.4.refs_1_.refs_4_, ...), custom_call_target="tpu_custom_call" | custom-call | flops 4000000000 | bytes 9000000 | tf_op jit(solution)/shard_map/attend/pallas_call | solution.py:284
  180.8 6.3 %product.2 = (bf16[128,1024]{1,0:T(8,128)(2,1)}, bf16[128,1024]{1,0:T(8,128)(2,1)}, bf16[128,1024]{1,0:T(8,128)(2,1)}, bf16[128,1024]{1,0:T(8,128)(2,1)}, bf16[1...) custom-call(s32[2]{0:T(128)} %pad_add_fusion.1.where_ref, ...), custom_call_target="tpu_custom_call" | custom-call | flops 2147483648 | bytes 5242880 | tf_op jit(solution)/shard_map/product/pallas_call | solution.py:415
  187.7 9.3 %collective-permute-done.14 = bf16[128,1024]{1,0:T(8,128)(2,1)S(1)} collective-permute-done((bf16[128,1024]{1,0:T(8,128)(2,1)}, bf16[128,1024]{1,0:T(8,128)(2,1)S(1)}, u32[]{:S(2)}, u32[]{:S(2)}) %collective-permute-start.14) | collective-permute-done | bytes 262176 | tf_op jit(solution)/shard_map/ppermute | solution.py:493
  197.0 1.7 add_convert_fusion.7
  198.8 6.3 %product.3 = (bf16[128,1024]{1,0:T(8,128)(2,1)}, bf16[128,1024]{1,0:T(8,128)(2,1)}, bf16[128,1024]{1,0:T(8,128)(2,1)}, bf16[128,1024]{1,0:T(8,128)(2,1)}, bf16[1...) custom-call(s32[2]{0:T(128)} %pad_add_fusion.1.where_ref, ...), custom_call_target="tpu_custom_call" | custom-call | flops 2147483648 | bytes 5242880 | tf_op jit(solution)/shard_map/product/pallas_call | solution.py:415
  205.2 3.3 %collective-permute-start.25 = (bf16[128,1024]{1,0:T(8,128)(2,1)}, bf16[128,1024]{1,0:T(8,128)(2,1)S(1)}, u32[]{:S(2)}, u32[]{:S(2)}) collective-permute-start(bf16[128,1024]{1,0:T(8,128)(2,1)} %get-tuple-element.63), channel_id=1, source_target_pairs={{0,3},{1,0},{2,1},{3,2},{4,7},{5,4},{6,5},{7,6},{8,11},{9,8},{10,9... | collective-permute-start | bytes 786440 | tf_op jit(solution)/shard_map/ppermute | solution.py:493
  208.5 1.1 add_convert_fusion.5
  209.6 3.2 %collective-permute-start.28 = (bf16[128,1024]{1,0:T(8,128)(2,1)}, bf16[128,1024]{1,0:T(8,128)(2,1)S(1)}, u32[]{:S(2)}, u32[]{:S(2)}) collective-permute-start(bf16[128,1024]{1,0:T(8,128)(2,1)} %get-tuple-element.67), channel_id=1, source_target_pairs={{0,3},{1,0},{2,1},{3,2},{4,7},{5,4},{6,5},{7,6},{8,11},{9,8},{10,9... | collective-permute-start | bytes 786440 | tf_op jit(solution)/shard_map/ppermute | solution.py:493
  212.9 1.1 add_convert_fusion.6
  214.1 1.2 collective-permute-done.25
  215.2 1.0 add_convert_fusion.3
  216.3 3.7 %collective-permute-start.26 = (bf16[128,1024]{1,0:T(8,128)(2,1)S(1)}, bf16[128,1024]{1,0:T(8,128)(2,1)S(1)}, u32[]{:S(2)}, u32[]{:S(2)}) collective-permute-start(bf16[128,1024]{1,0:T(8,128)(2,1)S(1)} %add_convert_fusion.3), channel_id=1, source_target_pairs={{0,3},{1,0},{2,1},{3,2},{4,7},{5,4},{6,5},{7,6},{8,11},{9,8},{10,9... | collective-permute-start | bytes 786440 | tf_op jit(solution)/shard_map/ppermute | solution.py:493
  220.9 1.0 add_convert_fusion.1
  221.9 3.9 %collective-permute-start.29 = (bf16[128,1024]{1,0:T(8,128)(2,1)S(1)}, bf16[128,1024]{1,0:T(8,128)(2,1)S(1)}, u32[]{:S(2)}, u32[]{:S(2)}) collective-permute-start(bf16[128,1024]{1,0:T(8,128)(2,1)S(1)} %add_convert_fusion.1), channel_id=1, source_target_pairs={{0,3},{1,0},{2,1},{3,2},{4,7},{5,4},{6,5},{7,6},{8,11},{9,8},{10,9... | collective-permute-start | bytes 786440 | tf_op jit(solution)/shard_map/ppermute | solution.py:493
  226.6 1.0 add_convert_fusion.2
  227.7 3.8 %collective-permute-start.27 = (bf16[128,1024]{1,0:T(8,128)(2,1)S(1)}, bf16[128,1024]{1,0:T(8,128)(2,1)S(1)}, u32[]{:S(2)}, u32[]{:S(2)}) collective-permute-start(bf16[128,1024]{1,0:T(8,128)(2,1)S(1)} %add_convert_fusion.2), channel_id=1, source_target_pairs={{0,3},{1,0},{2,1},{3,2},{4,7},{5,4},{6,5},{7,6},{8,11},{9,8},{10,9... | collective-permute-start | bytes 786440 | tf_op jit(solution)/shard_map/ppermute | solution.py:493
  232.5 1.0 add_convert_fusion
  233.5 3.8 %collective-permute-start.30 = (bf16[128,1024]{1,0:T(8,128)(2,1)S(1)}, bf16[128,1024]{1,0:T(8,128)(2,1)S(1)}, u32[]{:S(2)}, u32[]{:S(2)}) collective-permute-start(bf16[128,1024]{1,0:T(8,128)(2,1)S(1)} %add_convert_fusion), channel_id=1, source_target_pairs={{0,3},{1,0},{2,1},{3,2},{4,7},{5,4},{6,5},{7,6},{8,11},{9,8},{10,9... | collective-permute-start | bytes 786440 | tf_op jit(solution)/shard_map/ppermute | solution.py:493
  237.4 2.0 residual.1.rows_ref
  239.4 2.0 collective-permute-done.30.refs_6_
  241.5 2.0 finish.1
  (74 shorter events, 11.6 us)
Async XLA Ops:
  7.2 119.8 %all-gather.2.cloned.1.call-start = ((), (), s32[]{:S(2)}) async-start(), calls=%async_computation.2 | async-start | bytes 13369344 | tf_op jit(solution)/shard_map/all_gather | solution.py:518
  9.2 12.4 %collective-permute-start.6 = (bf16[1,256,768]{2,1,0:T(8,128)(2,1)S(1)}, bf16[1,256,768]{2,1,0:T(8,128)(2,1)S(1)}, u32[]{:S(2)}, u32[]{:S(2)}) collective-permute-start(bf16[1,256,768]{2,1,0:T(8,128)(2,1)S(1)} %multiply_convert_fusion), channel_id=1, source_target_pairs={{0,4},{4,0},{1,5},{5,1},{2,6},{6,2},{3,7},{7,3},{8,12},{12,8},{9,1... | collective-permute-start | bytes 1179656 | tf_op jit(solution)/shard_map/ppermute | solution.py:34
  43.4 40.5 %copy-start.7 = (bf16[512,256]{1,0:T(8,128)(2,1)S(1)}, bf16[512,256]{1,0:T(8,128)(2,1)}, u32[]{:S(2)}) copy-start(bf16[512,256]{1,0:T(8,128)(2,1)} %param.15) | copy-start | bytes 786436
  78.1 27.6 %all-to-all-start.1 = ((bf16[32,32,512]{2,1,0:T(8,128)(2,1)}), bf16[32,32,512]{2,1,0:T(8,128)(2,1)S(1)}, u32[]{:S(2)}, u32[]{:S(2)}) async-start(bf16[32,32,512]{2,1,0:T(8,128)(2,1)} %lookup.1), calls=%async_computation.1 | async-start | bytes 2097152 | tf_op jit(solution)/shard_map/all_to_all | solution.py:535
  83.9 28.5 %collective-permute-start.7 = (bf16[512,256]{1,0:T(8,128)(2,1)S(1)}, bf16[512,256]{1,0:T(8,128)(2,1)S(1)}, u32[]{:S(2)}, u32[]{:S(2)}) collective-permute-start(bf16[512,256]{1,0:T(8,128)(2,1)S(1)} %copy-done.7), channel_id=1, source_target_pairs={{0,4},{4,0},{1,5},{5,1},{2,6},{6,2},{3,7},{7,3},{8,12},{12,8},{9,1... | collective-permute-start | bytes 786440 | tf_op jit(solution)/shard_map/ppermute | solution.py:533
  85.4 31.8 %collective-permute-start.8 = (bf16[512,256]{1,0:T(8,128)(2,1)S(1)}, bf16[512,256]{1,0:T(8,128)(2,1)S(1)}, u32[]{:S(2)}, u32[]{:S(2)}) collective-permute-start(bf16[512,256]{1,0:T(8,128)(2,1)S(1)} %copy-done.7), channel_id=1, source_target_pairs={{0,16},{16,0},{1,17},{17,1},{2,18},{18,2},{3,19},{19,3},{4,20},{20... | collective-permute-start | bytes 786440 | tf_op jit(solution)/shard_map/ppermute | solution.py:533
  85.4 31.8 %collective-permute-start.9 = (bf16[512,256]{1,0:T(8,128)(2,1)S(1)}, bf16[512,256]{1,0:T(8,128)(2,1)S(1)}, u32[]{:S(2)}, u32[]{:S(2)}) collective-permute-start(bf16[512,256]{1,0:T(8,128)(2,1)S(1)} %copy-done.7), channel_id=1, source_target_pairs={{0,20},{4,16},{16,4},{20,0},{1,21},{5,17},{17,5},{21,1},{2,22},{6,... | collective-permute-start | bytes 786440 | tf_op jit(solution)/shard_map/ppermute | solution.py:533
  106.8 18.1 %collective-permute-start = (bf16[512,512]{1,0:T(8,128)(2,1)}, bf16[512,512]{1,0:T(8,128)(2,1)S(1)}, u32[]{:S(2)}, u32[]{:S(2)}) collective-permute-start(bf16[512,512]{1,0:T(8,128)(2,1)} %bitcast.8), channel_id=1, source_target_pairs={{0,3},{1,0},{2,1},{3,2},{4,7},{5,4},{6,5},{7,6},{8,11},{9,8},{10,9... | collective-permute-start | bytes 1572872 | tf_op jit(solution)/shard_map/ppermute | solution.py:551
  118.3 40.4 %collective-permute-start.10 = (bf16[2,2,512,256]{3,2,1,0:T(8,128)(2,1)}, bf16[2,2,512,256]{3,2,1,0:T(8,128)(2,1)}, u32[]{:S(2)}, u32[]{:S(2)}) collective-permute-start(bf16[2,2,512,256]{3,2,1,0:T(8,128)(2,1)} %bitcast.20.refs_0_), channel_id=1, source_target_pairs={{0,32},{32,64},{64,96},{96,0},{1,33},{33,65},{65,97},{97,1},{2,34}... | collective-permute-start | bytes 3145736 | tf_op jit(solution)/shard_map/ppermute | solution.py:544
  118.3 40.4 %collective-permute-start.11 = (bf16[2,2,512,256]{3,2,1,0:T(8,128)(2,1)}, bf16[2,2,512,256]{3,2,1,0:T(8,128)(2,1)}, u32[]{:S(2)}, u32[]{:S(2)}) collective-permute-start(bf16[2,2,512,256]{3,2,1,0:T(8,128)(2,1)} %bitcast.20.refs_0_), channel_id=1, source_target_pairs={{0,96},{32,0},{64,32},{96,64},{1,97},{33,1},{65,33},{97,65},{2,98}... | collective-permute-start | bytes 3145736 | tf_op jit(solution)/shard_map/ppermute | solution.py:544
  121.6 16.2 %collective-permute-start.2 = (bf16[512,512]{1,0:T(8,128)(2,1)}, bf16[512,512]{1,0:T(8,128)(2,1)S(1)}, u32[]{:S(2)}, u32[]{:S(2)}) collective-permute-start(bf16[512,512]{1,0:T(8,128)(2,1)} %bitcast.8), channel_id=1, source_target_pairs={{0,1},{1,2},{2,3},{3,0},{4,5},{5,6},{6,7},{7,4},{8,9},{9,10},{10,1... | collective-permute-start | bytes 1572872 | tf_op jit(solution)/shard_map/ppermute | solution.py:548
  123.1 13.4 %collective-permute-start.1 = (bf16[512,512]{1,0:T(8,128)(2,1)}, bf16[512,512]{1,0:T(8,128)(2,1)S(1)}, u32[]{:S(2)}, u32[]{:S(2)}) collective-permute-start(bf16[512,512]{1,0:T(8,128)(2,1)} %bitcast.9), channel_id=1, source_target_pairs={{0,3},{1,0},{2,1},{3,2},{4,7},{5,4},{6,5},{7,6},{8,11},{9,8},{10,9... | collective-permute-start | bytes 1572872 | tf_op jit(solution)/shard_map/ppermute | solution.py:549
  124.8 24.2 %collective-permute-start.5 = (bf16[512,512]{1,0:T(8,128)(2,1)}, bf16[512,512]{1,0:T(8,128)(2,1)S(1)}, u32[]{:S(2)}, u32[]{:S(2)}) collective-permute-start(bf16[512,512]{1,0:T(8,128)(2,1)} %bitcast.9), channel_id=1, source_target_pairs={{0,1},{1,2},{2,3},{3,0},{4,5},{5,6},{6,7},{7,4},{8,9},{9,10},{10,1... | collective-permute-start | bytes 1572872 | tf_op jit(solution)/shard_map/ppermute | solution.py:550
  136.5 14.1 %copy-start = (bf16[512,512]{1,0:T(8,128)(2,1)}, bf16[512,512]{1,0:T(8,128)(2,1)S(1)}, u32[]{:S(2)}) copy-start(bf16[512,512]{1,0:T(8,128)(2,1)S(1)} %collective-permute-done.1.refs_3_.refs_2_) | copy-start | bytes 1572868
  136.5 50.6 %collective-permute-start.20 = (bf16[2,2,512,256]{3,2,1,0:T(8,128)(2,1)}, bf16[2,2,512,256]{3,2,1,0:T(8,128)(2,1)}, u32[]{:S(2)}, u32[]{:S(2)}) collective-permute-start(bf16[2,2,512,256]{3,2,1,0:T(8,128)(2,1)} %bitcast.20.refs_0_), channel_id=1, source_target_pairs={{0,8},{8,0},{1,9},{9,1},{2,10},{10,2},{3,11},{11,3},{4,12},{12,4},... | collective-permute-start | bytes 3145736 | tf_op jit(solution)/shard_map/ppermute | solution.py:573
  137.8 30.6 %collective-permute-start.3 = (bf16[512,512]{1,0:T(8,128)(2,1)S(1)}, bf16[512,512]{1,0:T(8,128)(2,1)}, u32[]{:S(2)}, u32[]{:S(2)}) collective-permute-start(bf16[512,512]{1,0:T(8,128)(2,1)S(1)} %collective-permute-done.2.refs_0_.refs_5_), channel_id=1, source_target_pairs={{0,1},{1,2},{2,3},{3,0},{4,5},{5,6},{6,7},{7,4},{8,9},{9,10},{10,1... | collective-permute-start | bytes 1572872 | tf_op jit(solution)/shard_map/ppermute | solution.py:552
  149.0 19.4 %collective-permute-start.4 = (bf16[512,512]{1,0:T(8,128)(2,1)S(1)}, bf16[512,512]{1,0:T(8,128)(2,1)}, u32[]{:S(2)}, u32[]{:S(2)}) collective-permute-start(bf16[512,512]{1,0:T(8,128)(2,1)S(1)} %collective-permute-done.1.refs_3_.refs_2_), channel_id=1, source_target_pairs={{0,3},{1,0},{2,1},{3,2},{4,7},{5,4},{6,5},{7,6},{8,11},{9,8},{10,9... | collective-permute-start | bytes 1572872 | tf_op jit(solution)/shard_map/ppermute | solution.py:553
  150.6 15.8 %copy-start.8 = (s32[32]{0:T(128)S(1)}, s32[32]{0:T(128)}, u32[]{:S(2)}) copy-start(s32[32]{0:T(128)} %param.9) | copy-start | bytes 388
  160.7 19.6 %collective-permute-start.12 = (bf16[1,2,512,256]{3,2,1,0:T(8,128)(2,1)}, bf16[1,2,512,256]{3,2,1,0:T(8,128)(2,1)}, u32[]{:S(2)}, u32[]{:S(2)}) collective-permute-start(bf16[1,2,512,256]{3,2,1,0:T(8,128)(2,1)} %slice.22), channel_id=1, source_target_pairs={{0,32},{32,64},{64,96},{96,0},{1,33},{33,65},{65,97},{97,1},{2,34}... | collective-permute-start | bytes 1572872 | tf_op jit(solution)/shard_map/ppermute | solution.py:569
  162.6 17.9 %collective-permute-start.13 = (bf16[1,2,512,256]{3,2,1,0:T(8,128)(2,1)}, bf16[1,2,512,256]{3,2,1,0:T(8,128)(2,1)}, u32[]{:S(2)}, u32[]{:S(2)}) collective-permute-start(bf16[1,2,512,256]{3,2,1,0:T(8,128)(2,1)} %slice.23), channel_id=1, source_target_pairs={{0,96},{32,0},{64,32},{96,64},{1,97},{33,1},{65,33},{97,65},{2,98}... | collective-permute-start | bytes 1572872 | tf_op jit(solution)/shard_map/ppermute | solution.py:570
  168.4 30.3 %collective-permute-start.21 = (bf16[2,2,512,256]{3,2,1,0:T(8,128)(2,1)}, bf16[2,2,512,256]{3,2,1,0:T(8,128)(2,1)}, u32[]{:S(2)}, u32[]{:S(2)}) collective-permute-start(bf16[2,2,512,256]{3,2,1,0:T(8,128)(2,1)} %collective-permute-done.10.refs_1_), channel_id=1, source_target_pairs={{0,8},{8,0},{1,9},{9,1},{2,10},{10,2},{3,11},{11,3},{4,12},{12,4},... | collective-permute-start | bytes 3145736 | tf_op jit(solution)/shard_map/ppermute | solution.py:573
  168.5 30.3 %collective-permute-start.22 = (bf16[2,2,512,256]{3,2,1,0:T(8,128)(2,1)}, bf16[2,2,512,256]{3,2,1,0:T(8,128)(2,1)}, u32[]{:S(2)}, u32[]{:S(2)}) collective-permute-start(bf16[2,2,512,256]{3,2,1,0:T(8,128)(2,1)} %collective-permute-done.11.refs_2_), channel_id=1, source_target_pairs={{0,8},{8,0},{1,9},{9,1},{2,10},{10,2},{3,11},{11,3},{4,12},{12,4},... | collective-permute-start | bytes 3145736 | tf_op jit(solution)/shard_map/ppermute | solution.py:573
  180.2 18.5 %collective-permute-start.23 = (bf16[1,2,512,256]{3,2,1,0:T(8,128)(2,1)}, bf16[1,2,512,256]{3,2,1,0:T(8,128)(2,1)}, u32[]{:S(2)}, u32[]{:S(2)}) collective-permute-start(bf16[1,2,512,256]{3,2,1,0:T(8,128)(2,1)} %collective-permute-done.12.refs_3_), channel_id=1, source_target_pairs={{0,8},{8,0},{1,9},{9,1},{2,10},{10,2},{3,11},{11,3},{4,12},{12,4},... | collective-permute-start | bytes 1572872 | tf_op jit(solution)/shard_map/ppermute | solution.py:573
  180.4 18.4 %collective-permute-start.24 = (bf16[1,2,512,256]{3,2,1,0:T(8,128)(2,1)}, bf16[1,2,512,256]{3,2,1,0:T(8,128)(2,1)}, u32[]{:S(2)}, u32[]{:S(2)}) collective-permute-start(bf16[1,2,512,256]{3,2,1,0:T(8,128)(2,1)} %collective-permute-done.13.refs_4_), channel_id=1, source_target_pairs={{0,8},{8,0},{1,9},{9,1},{2,10},{10,2},{3,11},{11,3},{4,12},{12,4},... | collective-permute-start | bytes 1572872 | tf_op jit(solution)/shard_map/ppermute | solution.py:573
  187.1 38.6 %copy-start.6 = (bf16[128,1024]{1,0:T(8,128)(2,1)S(1)}, bf16[128,1024]{1,0:T(8,128)(2,1)}, u32[]{:S(2)}) copy-start(bf16[128,1024]{1,0:T(8,128)(2,1)} %get-tuple-element.61) | copy-start | bytes 786436
  187.2 50.2 %copy-start.1 = (bf16[512,512]{1,0:T(8,128)(2,1)S(1)}, bf16[512,512]{1,0:T(8,128)(2,1)}, u32[]{:S(2)}) copy-start(bf16[512,512]{1,0:T(8,128)(2,1)} %copy-done) | copy-start | bytes 1572868
  187.2 9.8 %collective-permute-start.14 = (bf16[128,1024]{1,0:T(8,128)(2,1)}, bf16[128,1024]{1,0:T(8,128)(2,1)S(1)}, u32[]{:S(2)}, u32[]{:S(2)}) collective-permute-start(bf16[128,1024]{1,0:T(8,128)(2,1)} %get-tuple-element.55), channel_id=1, source_target_pairs={{0,1},{1,2},{2,3},{3,0},{4,5},{5,6},{6,7},{7,4},{8,9},{9,10},{10,1... | collective-permute-start | bytes 786440 | tf_op jit(solution)/shard_map/ppermute | solution.py:493
  197.0 11.5 %collective-permute-start.17 = (bf16[128,1024]{1,0:T(8,128)(2,1)}, bf16[128,1024]{1,0:T(8,128)(2,1)}, u32[]{:S(2)}, u32[]{:S(2)}) collective-permute-start(bf16[128,1024]{1,0:T(8,128)(2,1)} %get-tuple-element.59), channel_id=1, source_target_pairs={{0,1},{1,2},{2,3},{3,0},{4,5},{5,6},{6,7},{7,4},{8,9},{9,10},{10,1... | collective-permute-start | bytes 786440 | tf_op jit(solution)/shard_map/ppermute | solution.py:493
  198.7 42.8 %copy-start.2 = (bf16[128,1024]{1,0:T(8,128)(2,1)S(1)}, bf16[128,1024]{1,0:T(8,128)(2,1)}, u32[]{:S(2)}) copy-start(bf16[128,1024]{1,0:T(8,128)(2,1)} %get-tuple-element.58.refs_1_) | copy-start | bytes 786436
  198.7 42.8 %copy-start.3 = (bf16[128,1024]{1,0:T(8,128)(2,1)S(1)}, bf16[128,1024]{1,0:T(8,128)(2,1)}, u32[]{:S(2)}) copy-start(bf16[128,1024]{1,0:T(8,128)(2,1)} %get-tuple-element.62.refs_3_) | copy-start | bytes 786436
  198.7 14.2 %collective-permute-start.15 = (bf16[128,1024]{1,0:T(8,128)(2,1)}, bf16[128,1024]{1,0:T(8,128)(2,1)}, u32[]{:S(2)}, u32[]{:S(2)}) collective-permute-start(bf16[128,1024]{1,0:T(8,128)(2,1)} %add_convert_fusion.7), channel_id=1, source_target_pairs={{0,1},{1,2},{2,3},{3,0},{4,5},{5,6},{6,7},{7,4},{8,9},{9,10},{10,1... | collective-permute-start | bytes 786440 | tf_op jit(solution)/shard_map/ppermute | solution.py:493
  205.1 36.3 %copy-start.4 = (bf16[128,1024]{1,0:T(8,128)(2,1)S(1)}, bf16[128,1024]{1,0:T(8,128)(2,1)}, u32[]{:S(2)}) copy-start(bf16[128,1024]{1,0:T(8,128)(2,1)} %get-tuple-element.66.refs_5_) | copy-start | bytes 786436
  205.2 36.3 %copy-start.5 = (bf16[128,1024]{1,0:T(8,128)(2,1)S(1)}, bf16[128,1024]{1,0:T(8,128)(2,1)}, u32[]{:S(2)}) copy-start(bf16[128,1024]{1,0:T(8,128)(2,1)} %get-tuple-element.70.refs_7_) | copy-start | bytes 786436
  205.2 10.1 %collective-permute-start.25 = (bf16[128,1024]{1,0:T(8,128)(2,1)}, bf16[128,1024]{1,0:T(8,128)(2,1)S(1)}, u32[]{:S(2)}, u32[]{:S(2)}) collective-permute-start(bf16[128,1024]{1,0:T(8,128)(2,1)} %get-tuple-element.63), channel_id=1, source_target_pairs={{0,3},{1,0},{2,1},{3,2},{4,7},{5,4},{6,5},{7,6},{8,11},{9,8},{10,9... | collective-permute-start | bytes 786440 | tf_op jit(solution)/shard_map/ppermute | solution.py:493
  209.6 16.2 %collective-permute-start.18 = (bf16[128,1024]{1,0:T(8,128)(2,1)S(1)}, bf16[128,1024]{1,0:T(8,128)(2,1)S(1)}, u32[]{:S(2)}, u32[]{:S(2)}) collective-permute-start(bf16[128,1024]{1,0:T(8,128)(2,1)S(1)} %add_convert_fusion.5), channel_id=1, source_target_pairs={{0,1},{1,2},{2,3},{3,0},{4,5},{5,6},{6,7},{7,4},{8,9},{9,10},{10,1... | collective-permute-start | bytes 786440 | tf_op jit(solution)/shard_map/ppermute | solution.py:493
  209.6 11.2 %collective-permute-start.28 = (bf16[128,1024]{1,0:T(8,128)(2,1)}, bf16[128,1024]{1,0:T(8,128)(2,1)S(1)}, u32[]{:S(2)}, u32[]{:S(2)}) collective-permute-start(bf16[128,1024]{1,0:T(8,128)(2,1)} %get-tuple-element.67), channel_id=1, source_target_pairs={{0,3},{1,0},{2,1},{3,2},{4,7},{5,4},{6,5},{7,6},{8,11},{9,8},{10,9... | collective-permute-start | bytes 786440 | tf_op jit(solution)/shard_map/ppermute | solution.py:493
  214.0 25.4 %collective-permute-start.16 = (bf16[128,1024]{1,0:T(8,128)(2,1)S(1)}, bf16[128,1024]{1,0:T(8,128)(2,1)S(1)}, u32[]{:S(2)}, u32[]{:S(2)}) collective-permute-start(bf16[128,1024]{1,0:T(8,128)(2,1)S(1)} %add_convert_fusion.6), channel_id=1, source_target_pairs={{0,1},{1,2},{2,3},{3,0},{4,5},{5,6},{6,7},{7,4},{8,9},{9,10},{10,1... | collective-permute-start | bytes 786440 | tf_op jit(solution)/shard_map/ppermute | solution.py:493
  216.3 10.4 %collective-permute-start.26 = (bf16[128,1024]{1,0:T(8,128)(2,1)S(1)}, bf16[128,1024]{1,0:T(8,128)(2,1)S(1)}, u32[]{:S(2)}, u32[]{:S(2)}) collective-permute-start(bf16[128,1024]{1,0:T(8,128)(2,1)S(1)} %add_convert_fusion.3), channel_id=1, source_target_pairs={{0,3},{1,0},{2,1},{3,2},{4,7},{5,4},{6,5},{7,6},{8,11},{9,8},{10,9... | collective-permute-start | bytes 786440 | tf_op jit(solution)/shard_map/ppermute | solution.py:493
  221.9 10.6 %collective-permute-start.29 = (bf16[128,1024]{1,0:T(8,128)(2,1)S(1)}, bf16[128,1024]{1,0:T(8,128)(2,1)S(1)}, u32[]{:S(2)}, u32[]{:S(2)}) collective-permute-start(bf16[128,1024]{1,0:T(8,128)(2,1)S(1)} %add_convert_fusion.1), channel_id=1, source_target_pairs={{0,3},{1,0},{2,1},{3,2},{4,7},{5,4},{6,5},{7,6},{8,11},{9,8},{10,9... | collective-permute-start | bytes 786440 | tf_op jit(solution)/shard_map/ppermute | solution.py:493
  225.9 13.5 %collective-permute-start.19 = (bf16[128,1024]{1,0:T(8,128)(2,1)S(1)}, bf16[128,1024]{1,0:T(8,128)(2,1)S(1)}, u32[]{:S(2)}, u32[]{:S(2)}) collective-permute-start(bf16[128,1024]{1,0:T(8,128)(2,1)S(1)} %add_convert_fusion.4), channel_id=1, source_target_pairs={{0,1},{1,2},{2,3},{3,0},{4,5},{5,6},{6,7},{7,4},{8,9},{9,10},{10,1... | collective-permute-start | bytes 786440 | tf_op jit(solution)/shard_map/ppermute | solution.py:493
  227.7 11.7 %collective-permute-start.27 = (bf16[128,1024]{1,0:T(8,128)(2,1)S(1)}, bf16[128,1024]{1,0:T(8,128)(2,1)S(1)}, u32[]{:S(2)}, u32[]{:S(2)}) collective-permute-start(bf16[128,1024]{1,0:T(8,128)(2,1)S(1)} %add_convert_fusion.2), channel_id=1, source_target_pairs={{0,3},{1,0},{2,1},{3,2},{4,7},{5,4},{6,5},{7,6},{8,11},{9,8},{10,9... | collective-permute-start | bytes 786440 | tf_op jit(solution)/shard_map/ppermute | solution.py:493
  233.5 7.9 %collective-permute-start.30 = (bf16[128,1024]{1,0:T(8,128)(2,1)S(1)}, bf16[128,1024]{1,0:T(8,128)(2,1)S(1)}, u32[]{:S(2)}, u32[]{:S(2)}) collective-permute-start(bf16[128,1024]{1,0:T(8,128)(2,1)S(1)} %add_convert_fusion), channel_id=1, source_target_pairs={{0,3},{1,0},{2,1},{3,2},{4,7},{5,4},{6,5},{7,6},{8,11},{9,8},{10,9... | collective-permute-start | bytes 786440 | tf_op jit(solution)/shard_map/ppermute | solution.py:493
Sparse Core Ops, SparseCore 0:
  22.7 85.9 all-gather.1

commit v6 on v5

--- a/solution.py
+++ b/solution.py
@@ -64,7 +64,7 @@
     )
 
 
-def lookup_kernel(slots_ref, lanes_ref, table_ref, out_ref, table, tiles, arrived):
+def lookup_kernel(slots_ref, lanes_ref, table_ref, out_ref, table, tiles, arrived, *, cores):
     groups, columns, row_count = out_ref.shape
     tile_count = tiles.shape[0] // 2
     slabs = arrived.shape[0]
@@ -95,6 +95,7 @@
         lax.fori_loop(0, -(-slab // unroll), prepare, 0)
 
     per_group = row_count // LANES
+    tensor_size = lax.axis_size(TENSOR)
     together = 2
 
     def one_block(step, carry):
@@ -110,8 +111,11 @@
                     left, tiles[slots_ref[first + i]], tiles[slots_ref[first + i + 1]]
                 )
                 picked = jnp.where(lane >= jnp.int16(i), lane_gather(pair, wanted), picked)
-            place = pl.multiple_of(lax.rem(block, per_group) * LANES, LANES)
-            out_ref[lax.div(block, per_group), :, pl.ds(place, LANES)] = picked
+            span = cores * tensor_size
+            within = lax.rem(block, span)
+            device = block - within + lax.rem(within, cores) * tensor_size + lax.div(within, cores)
+            place = pl.multiple_of(lax.rem(device, per_group) * LANES, LANES)
+            out_ref[lax.div(device, per_group), :, pl.ds(place, LANES)] = picked
         return carry
 
     lax.fori_loop(0, groups * per_group // together, one_block, 0)
@@ -129,7 +133,7 @@
     slots = lax.shift_right_logical(token_ids, 7) + tile_count * swapped_half
     lanes = ((lane & (half - 1)) | (odd * half)).reshape(count // LANES, LANES)
     return pl.pallas_call(
-        lookup_kernel,
+        functools.partial(lookup_kernel, cores=lax.axis_size("dp_2")),
         out_shape=jax.ShapeDtypeStruct((group_count, columns, count // group_count), jnp.bfloat16),
         in_specs=[
             pl.BlockSpec(memory_space=pltpu.SMEM),
@@ -480,8 +484,7 @@
 
 def ring_sums(attended, weights):
     count = lax.axis_size(RING)
-    pieces = [(LAYERS.index(z), side) for z in LAYERS[:3] for side in range(2)]
-    pieces += [(3, 0), (4, 0)]
+    pieces = [(k, side) for k in range(len(LAYERS)) for side in range(2)]
     where = jnp.stack([lax.axis_index(RING), lax.axis_index("tensor_0")])
     sums = []
     for side, way in enumerate((1, -1)):
@@ -517,13 +520,17 @@
     packed = (packed * gain[:, None]).astype(jnp.bfloat16)
     w_in = lax.all_gather(collect_blocks(packed), DP, axis=1, tiled=True)
     w_in = w_in.reshape(w_in.shape[0], -1, ring, columns, w_in.shape[-1])
+    cores = lax.axis_size("dp_2")
+    chip_ids = lax.all_gather(prompt_ids, "dp_2")
+    others = ("dp_0", "dp_1", "tensor_0", "tensor_1")
     all_ids = lax.all_to_all(
-        jnp.broadcast_to(prompt_ids[None], (devices, quarter)),
-        DP_TENSOR,
+        jnp.broadcast_to(chip_ids[None], (devices // cores, cores, quarter)),
+        others,
         split_axis=0,
         concat_axis=0,
         tiled=True,
-    ).reshape(-1)
+    )
+    all_ids = all_ids.reshape(-1)
     pieces_x = [w_out]
     for axes, route in (
         ("tensor_0", [(0, 1), (1, 0)]),
@@ -538,10 +545,13 @@
     pieces_x, _ = lax.optimization_barrier((pieces_x, outgoing))
     w_mine = [jnp.stack(pieces_x).reshape(2, 2, *w_out.shape)]
     layers = lax.axis_size("dp_0")
-    ahead = [(z, (z + 1) % layers) for z in range(layers)]
-    back = [(z, (z - 1) % layers) for z in range(layers)]
-    for route in (ahead, back):
+    for k in LAYERS[1:]:
+        route = [(z, (z + k) % layers) for z in range(layers)]
         w_mine.append(lax.ppermute(w_mine[0], "dp_0", route))
+    w_other = []
+    for k in range(layers):
+        w_other.append(lax.ppermute(w_mine[k], "dp_2", [(0, 1), (1, 0)]))
+
     places = (place + jnp.arange(ring, dtype=jnp.int32)) % ring
     half = own.shape[0] // 2
     low, high = own[:half], own[half:]
@@ -564,13 +574,6 @@
         ],
         first,
     )
-    z_sides, _ = lax.optimization_barrier((w_mine[1:], second))
-    first_side, last_side = z_sides[0][:1], z_sides[1][1:]
-    w_mine.append(lax.ppermute(first_side, "dp_0", ahead))
-    w_mine.append(lax.ppermute(last_side, "dp_0", back))
-    w_other = []
-    for k in range(len(w_mine)):
-        w_other.append(lax.ppermute(w_mine[k], "dp_2", [(0, 1), (1, 0)]))
     attended, cache = attend(
         places,
         w_in,

time: 252 us -> 279 us (1.11)
  the two profiles are of different devices: /device:TPU:6 before, /device:TPU:96 now
where the time goes in v6:
time: 279 us
  waiting for transfers between devices  111 us (40%)
  Pallas kernels  75.9 us (27%)
  starting transfers between devices  39.7 us (14%)
  blocking collectives  19.8 us (7%)
  other arithmetic  14.6 us (5%)
  between operations  14.3 us (5%)
  local copies, waits for them, and re-layouts  3.45 us (1%)
    ppermute x3, waiting for transfers between devices, sublayer(): w_mine.append(lax.ppermute(w_mine[0], 'dp_0', route))  39 us
    pallas_call x1, Pallas kernels, lookup(): pl.pallas_call(functools.partial(lookup_kernel, cores=lax.axis_size('dp_2...  34.5 us
    ppermute x3, waiting for transfers between devices, sublayer(): pieces_x.append(lax.ppermute(w_out, axes, route))  28.6 us
    all_to_all x1, blocking collectives, sublayer(): lax.all_to_all(jnp.broadcast_to(chip_ids[None], (devices // cores, cores,...  17.9 us
    ppermute x12, waiting for transfers between devices, ring_sums(): running = lax.ppermute(running, RING, ring_route(way))  14.8 us
    pallas_call x2, Pallas kernels, project(): pl.pallas_call(functools.partial(project_kernel, parts=len(parts), carrie...  13.5 us
    ppermute x12, starting transfers between devices, ring_sums(): running = lax.ppermute(running, RING, ring_route(way))  13.2 us
    pallas_call x2, Pallas kernels, product(): pl.pallas_call(functools.partial(product_kernel, pieces=pieces, turns=tur...  12.6 us
  transfers between devices with their start and end apart: 31, of which 13 were waited for; matrix products, arithmetic and copies ran while one was open for 5% of the time, Pallas kernels for 24%

profile of v6, /device:TPU:96, one launch (start us, length us, event | category | flops | bytes accessed | tf_op | source)
XLA Modules:
  0.0 278.8 jit_solution(9445391890649477452)
XLA Ops:
  8.0 1.2 multiply_convert_fusion
  9.2 3.1 %collective-permute-start.6 = (bf16[1,256,768]{2,1,0:T(8,128)(2,1)S(1)}, bf16[1,256,768]{2,1,0:T(8,128)(2,1)S(1)}, u32[]{:S(2)}, u32[]{:S(2)}) collective-permute-start(bf16[1,256,768]{2,1,0:T(8,128)(2,1)S(1)} %multiply_convert_fusion), channel_id=1, source_target_pairs={{0,4},{4,0},{1,5},{5,1},{2,6},{6,2},{3,7},{7,3},{8,12},{12,8},{9,1... | collective-permute-start | bytes 1179656 | tf_op jit(solution)/shard_map/ppermute | solution.py:34
  12.3 9.3 %collective-permute-done.6 = bf16[1,256,768]{2,1,0:T(8,128)(2,1)S(1)} collective-permute-done((bf16[1,256,768]{2,1,0:T(8,128)(2,1)S(1)}, bf16[1,256,768]{2,1,0:T(8,128)(2,1)S(1)}, u32[]{:S(2)}, u32[]{:S(2)}) %collective-permute-start.6) | collective-permute-done | bytes 393248 | tf_op jit(solution)/shard_map/ppermute | solution.py:34
  22.6 1.9 all-gather.1
  24.6 17.9 %all_to_all.10 = s32[64,2,128]{2,1,0:T(2,128)S(1)} all-to-all(s32[64,2,128]{2,1,0:T(2,128)S(1)} %broadcast_in_dim.4), channel_id=1, replica_groups=mesh['dp_0'=4,'dp_1'=2,'dp_2'=2,'tensor_0'=2,'tensor_1'=4] {'dp_0','dp_1..., dimensions={0} | all-to-all | bytes 131072 | tf_op jit(solution)/shard_map/all_to_all | solution.py:526
  43.8 34.5 %lookup.1 = bf16[32,32,512]{2,1,0:T(8,128)(2,1)} custom-call(s32[16384]{0:T(1024)} %multiply_add_fusion.slots_ref, s32[128,128]{1,0:T(8,128)} %multiply_or_fusion.lanes_ref, bf16[32,128256]{1,0:T(8,128)(2,1)} %table_ref.1), custom_call_target="tpu_custom_call" | custom-call | flops 30000001024 | bytes 8208384 | tf_op jit(solution)/shard_map/lookup/pallas_call | solution.py:135
  78.3 6.0 %all-to-all-start.1 = ((bf16[32,32,512]{2,1,0:T(8,128)(2,1)}), bf16[32,32,512]{2,1,0:T(8,128)(2,1)S(1)}, u32[]{:S(2)}, u32[]{:S(2)}) async-start(bf16[32,32,512]{2,1,0:T(8,128)(2,1)} %lookup.1), calls=%async_computation.1 | async-start | bytes 2097152 | tf_op jit(solution)/shard_map/all_to_all | solution.py:542
  84.4 3.1 %collective-permute-start.7 = (bf16[512,256]{1,0:T(8,128)(2,1)S(1)}, bf16[512,256]{1,0:T(8,128)(2,1)S(1)}, u32[]{:S(2)}, u32[]{:S(2)}) collective-permute-start(bf16[512,256]{1,0:T(8,128)(2,1)S(1)} %copy-done.8), channel_id=1, source_target_pairs={{0,4},{4,0},{1,5},{5,1},{2,6},{6,2},{3,7},{7,3},{8,12},{12,8},{9,1... | collective-permute-start | bytes 786440 | tf_op jit(solution)/shard_map/ppermute | solution.py:540
  88.6 24.7 %collective-permute-done.7 = bf16[512,256]{1,0:T(8,128)(2,1)S(1)} collective-permute-done((bf16[512,256]{1,0:T(8,128)(2,1)S(1)}, bf16[512,256]{1,0:T(8,128)(2,1)S(1)}, u32[]{:S(2)}, u32[]{:S(2)}) %collective-permute-start.7) | collective-permute-done | bytes 262176 | tf_op jit(solution)/shard_map/ppermute | solution.py:540
  113.3 4.0 %collective-permute-done.8 = bf16[512,256]{1,0:T(8,128)(2,1)S(1)} collective-permute-done((bf16[512,256]{1,0:T(8,128)(2,1)S(1)}, bf16[512,256]{1,0:T(8,128)(2,1)S(1)}, u32[]{:S(2)}, u32[]{:S(2)}) %collective-permute-start.8) | collective-permute-done | bytes 262176 | tf_op jit(solution)/shard_map/ppermute | solution.py:540
  117.2 1.1 pad_maximum_fusion
  118.6 1.7 collective-permute-start.11
  120.4 1.0 fusion.2
  121.4 1.5 collective-permute-start.2
  122.9 1.8 collective-permute-start
  124.7 19.9 %collective-permute-done.10.refs_1_ = bf16[2,2,512,256]{3,2,1,0:T(8,128)(2,1)S(1)} collective-permute-done((bf16[2,2,512,256]{3,2,1,0:T(8,128)(2,1)}, bf16[2,2,512,256]{3,2,1,0:T(8,128)(2,1)S(1)}, u32[]{:S(2)}, u32[]{:S(2)}) %collective-permute-start.10) | collective-permute-done | bytes 1048608 | tf_op jit(solution)/shard_map/ppermute | solution.py:550
  145.5 2.7 collective-permute-start.1
  148.3 19.1 %collective-permute-done.11.refs_2_ = bf16[2,2,512,256]{3,2,1,0:T(8,128)(2,1)} collective-permute-done((bf16[2,2,512,256]{3,2,1,0:T(8,128)(2,1)}, bf16[2,2,512,256]{3,2,1,0:T(8,128)(2,1)}, u32[]{:S(2)}, u32[]{:S(2)}) %collective-permute-start.11) | collective-permute-done | bytes 1048608 | tf_op jit(solution)/shard_map/ppermute | solution.py:550
  167.4 1.5 collective-permute-start.5
  168.9 1.5 collective-permute-start.3
  171.0 1.0 fusion
  173.5 10.1 %collective-permute-done.5.refs_1_.refs_6_ = bf16[512,512]{1,0:T(8,128)(2,1)S(1)} collective-permute-done((bf16[512,512]{1,0:T(8,128)(2,1)}, bf16[512,512]{1,0:T(8,128)(2,1)S(1)}, u32[]{:S(2)}, u32[]{:S(2)}) %collective-permute-start.5) | collective-permute-done | bytes 524320 | tf_op jit(solution)/shard_map/ppermute | solution.py:560
  183.6 9.2 %collective-permute-done.3.refs_0_.refs_3_ = bf16[512,512]{1,0:T(8,128)(2,1)} collective-permute-done((bf16[512,512]{1,0:T(8,128)(2,1)S(1)}, bf16[512,512]{1,0:T(8,128)(2,1)}, u32[]{:S(2)}, u32[]{:S(2)}) %collective-permute-start.3) | collective-permute-done | bytes 524320 | tf_op jit(solution)/shard_map/ppermute | solution.py:562
  192.8 1.5 collective-permute-start.4
  194.9 5.4 %project.2 = (f32[512,1536]{1,0:T(8,128)}, f32[1,512]{1,0:T(1,128)S(1)}) custom-call(s32[4]{0:T(128)S(1)} %and_select_fusion.places_ref, bf16[1024,512]{1,0:T(8,128)(2,1)S(1)} %bitcast.23, bf16[2,32,4,32,768]{4,3,2,1,0:T(8,128)(2,1)} %bitcast.25), custom_call_target="tpu_custom_call" | custom-call | flops 1610612736 | bytes 4194304 | tf_op jit(solution)/shard_map/project/pallas_call | solution.py:205
  200.3 8.1 %project.3 = (f32[512,1536]{1,0:T(8,128)}, f32[1,512]{1,0:T(1,128)S(1)}) custom-call(s32[4]{0:T(128)S(1)} %and_select_fusion.places_ref, bf16[512,512]{1,0:T(8,128)(2,1)S(1)} %collective-permute-done.2.refs_0_.refs_5_, bf16[512,512]{1,0:T(8,128)(2,1)S(1)} %collective-permute-done.5.refs_1_.refs_6_, ...), custom_call_target="tpu_custom_call" | custom-call | flops 3221225472 | bytes 8388608 | tf_op jit(solution)/shard_map/project/pallas_call | solution.py:205
  208.4 11.3 %attend.1 = (bf16[512,1024]{1,0:T(8,128)(2,1)}, bf16[2,512,256]{2,1,0:T(8,128)(2,1)}) custom-call(s32[4]{0:T(128)S(1)} %and_select_fusion.places_ref, s32[1]{0:T(128)} %dynamic_slice.6.length_ref, bf16[512,512]{1,0:T(8,128)(2,1)} %collective-permute-done.3.refs_0_.refs_3_, bf16[512,512]{1,0:T(8,128)(2,1)} %collective-permute-done.4.refs_1_.refs_4_, ...), custom_call_target="tpu_custom_call" | custom-call | flops 4000000000 | bytes 9000000 | tf_op jit(solution)/shard_map/attend/pallas_call | solution.py:288
  219.7 6.3 %product.3 = (bf16[128,1024]{1,0:T(8,128)(2,1)}, bf16[128,1024]{1,0:T(8,128)(2,1)}, bf16[128,1024]{1,0:T(8,128)(2,1)}, bf16[128,1024]{1,0:T(8,128)(2,1)}, bf16[1...) custom-call(s32[2]{0:T(128)} %pad_add_fusion.1.where_ref, ...), custom_call_target="tpu_custom_call" | custom-call | flops 2147483648 | bytes 5242880 | tf_op jit(solution)/shard_map/product/pallas_call | solution.py:419
  227.5 6.3 %product.2 = (bf16[128,1024]{1,0:T(8,128)(2,1)}, bf16[128,1024]{1,0:T(8,128)(2,1)}, bf16[128,1024]{1,0:T(8,128)(2,1)}, bf16[128,1024]{1,0:T(8,128)(2,1)}, bf16[1...) custom-call(s32[2]{0:T(128)} %pad_add_fusion.1.where_ref, ...), custom_call_target="tpu_custom_call" | custom-call | flops 2147483648 | bytes 5242880 | tf_op jit(solution)/shard_map/product/pallas_call | solution.py:419
  233.9 1.6 collective-permute-start.16
  235.4 1.2 collective-permute-start.13
  236.6 1.1 add_convert_fusion.1
  237.7 2.1 collective-permute-start.27
  239.8 1.1 add_convert_fusion.3
  241.8 2.4 collective-permute-done.16
  244.2 1.0 add_convert_fusion.5
  245.7 4.1 %collective-permute-done.13 = bf16[128,1024]{1,0:T(8,128)(2,1)S(1)} collective-permute-done((bf16[128,1024]{1,0:T(8,128)(2,1)}, bf16[128,1024]{1,0:T(8,128)(2,1)S(1)}, u32[]{:S(2)}, u32[]{:S(2)}) %collective-permute-start.13) | collective-permute-done | bytes 262176 | tf_op jit(solution)/shard_map/ppermute | solution.py:496
  249.8 1.0 add_convert_fusion.7
  251.3 1.0 add_convert_fusion
  252.3 2.8 %collective-permute-start.28 = (bf16[128,1024]{1,0:T(8,128)(2,1)S(1)}, bf16[128,1024]{1,0:T(8,128)(2,1)S(1)}, u32[]{:S(2)}, u32[]{:S(2)}) collective-permute-start(bf16[128,1024]{1,0:T(8,128)(2,1)S(1)} %add_convert_fusion), channel_id=1, source_target_pairs={{0,3},{1,0},{2,1},{3,2},{4,7},{5,4},{6,5},{7,6},{8,11},{9,8},{10,9... | collective-permute-start | bytes 786440 | tf_op jit(solution)/shard_map/ppermute | solution.py:496
  255.6 1.0 add_convert_fusion.4
  256.7 1.8 collective-permute-start.18
  258.5 2.8 %collective-permute-done.14 = bf16[128,1024]{1,0:T(8,128)(2,1)S(1)} collective-permute-done((bf16[128,1024]{1,0:T(8,128)(2,1)S(1)}, bf16[128,1024]{1,0:T(8,128)(2,1)S(1)}, u32[]{:S(2)}, u32[]{:S(2)}) %collective-permute-start.14) | collective-permute-done | bytes 262176 | tf_op jit(solution)/shard_map/ppermute | solution.py:496
  261.3 1.0 add_convert_fusion.6
  262.6 2.0 residual.1.rows_ref
  264.7 1.3 collective-permute-done.18.refs_2_
  266.0 3.9 %collective-permute-done.15.refs_0_ = bf16[128,1024]{1,0:T(8,128)(2,1)S(1)} collective-permute-done((bf16[128,1024]{1,0:T(8,128)(2,1)S(1)}, bf16[128,1024]{1,0:T(8,128)(2,1)S(1)}, u32[]{:S(2)}, u32[]{:S(2)}) %collective-permute-start.15) | collective-permute-done | bytes 262176 | tf_op jit(solution)/shard_map/ppermute | solution.py:496
  270.0 2.0 finish.1
  (73 shorter events, 12.6 us)
Async XLA Ops:
  7.2 187.8 %all-gather.4.cloned.1.call-start = ((), (), s32[]{:S(2)}) async-start(), calls=%async_computation.2 | async-start | bytes 13369344 | tf_op jit(solution)/shard_map/all_gather | solution.py:521
  9.2 12.4 %collective-permute-start.6 = (bf16[1,256,768]{2,1,0:T(8,128)(2,1)S(1)}, bf16[1,256,768]{2,1,0:T(8,128)(2,1)S(1)}, u32[]{:S(2)}, u32[]{:S(2)}) collective-permute-start(bf16[1,256,768]{2,1,0:T(8,128)(2,1)S(1)} %multiply_convert_fusion), channel_id=1, source_target_pairs={{0,4},{4,0},{1,5},{5,1},{2,6},{6,2},{3,7},{7,3},{8,12},{12,8},{9,1... | collective-permute-start | bytes 1179656 | tf_op jit(solution)/shard_map/ppermute | solution.py:34
  43.8 40.5 %copy-start.8 = (bf16[512,256]{1,0:T(8,128)(2,1)S(1)}, bf16[512,256]{1,0:T(8,128)(2,1)}, u32[]{:S(2)}) copy-start(bf16[512,256]{1,0:T(8,128)(2,1)} %param.15) | copy-start | bytes 786436
  43.8 126.6 %copy-start.10 = (s32[32]{0:T(128)S(1)}, s32[32]{0:T(128)}, u32[]{:S(2)}) copy-start(s32[32]{0:T(128)} %param.9) | copy-start | bytes 388
  78.3 42.1 %all-to-all-start.1 = ((bf16[32,32,512]{2,1,0:T(8,128)(2,1)}), bf16[32,32,512]{2,1,0:T(8,128)(2,1)S(1)}, u32[]{:S(2)}, u32[]{:S(2)}) async-start(bf16[32,32,512]{2,1,0:T(8,128)(2,1)} %lookup.1), calls=%async_computation.1 | async-start | bytes 2097152 | tf_op jit(solution)/shard_map/all_to_all | solution.py:542
  84.4 28.9 %collective-permute-start.7 = (bf16[512,256]{1,0:T(8,128)(2,1)S(1)}, bf16[512,256]{1,0:T(8,128)(2,1)S(1)}, u32[]{:S(2)}, u32[]{:S(2)}) collective-permute-start(bf16[512,256]{1,0:T(8,128)(2,1)S(1)} %copy-done.8), channel_id=1, source_target_pairs={{0,4},{4,0},{1,5},{5,1},{2,6},{6,2},{3,7},{7,3},{8,12},{12,8},{9,1... | collective-permute-start | bytes 786440 | tf_op jit(solution)/shard_map/ppermute | solution.py:540
  87.4 29.8 %collective-permute-start.8 = (bf16[512,256]{1,0:T(8,128)(2,1)S(1)}, bf16[512,256]{1,0:T(8,128)(2,1)S(1)}, u32[]{:S(2)}, u32[]{:S(2)}) collective-permute-start(bf16[512,256]{1,0:T(8,128)(2,1)S(1)} %copy-done.8), channel_id=1, source_target_pairs={{0,16},{16,0},{1,17},{17,1},{2,18},{18,2},{3,19},{19,3},{4,20},{20... | collective-permute-start | bytes 786440 | tf_op jit(solution)/shard_map/ppermute | solution.py:540
  88.0 29.2 %collective-permute-start.9 = (bf16[512,256]{1,0:T(8,128)(2,1)S(1)}, bf16[512,256]{1,0:T(8,128)(2,1)S(1)}, u32[]{:S(2)}, u32[]{:S(2)}) collective-permute-start(bf16[512,256]{1,0:T(8,128)(2,1)S(1)} %copy-done.8), channel_id=1, source_target_pairs={{0,20},{4,16},{16,4},{20,0},{1,21},{5,17},{17,5},{21,1},{2,22},{6,... | collective-permute-start | bytes 786440 | tf_op jit(solution)/shard_map/ppermute | solution.py:540
  118.3 26.2 %collective-permute-start.10 = (bf16[2,2,512,256]{3,2,1,0:T(8,128)(2,1)}, bf16[2,2,512,256]{3,2,1,0:T(8,128)(2,1)S(1)}, u32[]{:S(2)}, u32[]{:S(2)}) collective-permute-start(bf16[2,2,512,256]{3,2,1,0:T(8,128)(2,1)} %bitcast.21.refs_0_), channel_id=1, source_target_pairs={{0,32},{32,64},{64,96},{96,0},{1,33},{33,65},{65,97},{97,1},{2,34}... | collective-permute-start | bytes 3145736 | tf_op jit(solution)/shard_map/ppermute | solution.py:550
  118.6 48.7 %collective-permute-start.11 = (bf16[2,2,512,256]{3,2,1,0:T(8,128)(2,1)}, bf16[2,2,512,256]{3,2,1,0:T(8,128)(2,1)}, u32[]{:S(2)}, u32[]{:S(2)}) collective-permute-start(bf16[2,2,512,256]{3,2,1,0:T(8,128)(2,1)} %bitcast.21.refs_0_), channel_id=1, source_target_pairs={{0,96},{32,0},{64,32},{96,64},{1,97},{33,1},{65,33},{97,65},{2,98}... | collective-permute-start | bytes 3145736 | tf_op jit(solution)/shard_map/ppermute | solution.py:550
  120.4 52.6 %collective-permute-start.12 = (bf16[2,2,512,256]{3,2,1,0:T(8,128)(2,1)}, bf16[2,2,512,256]{3,2,1,0:T(8,128)(2,1)}, u32[]{:S(2)}, u32[]{:S(2)}) collective-permute-start(bf16[2,2,512,256]{3,2,1,0:T(8,128)(2,1)} %bitcast.21.refs_0_), channel_id=1, source_target_pairs={{0,64},{32,96},{64,0},{96,32},{1,65},{33,97},{65,1},{97,33},{2,66}... | collective-permute-start | bytes 3145736 | tf_op jit(solution)/shard_map/ppermute | solution.py:550
  121.4 47.5 %collective-permute-start.2 = (bf16[512,512]{1,0:T(8,128)(2,1)}, bf16[512,512]{1,0:T(8,128)(2,1)S(1)}, u32[]{:S(2)}, u32[]{:S(2)}) collective-permute-start(bf16[512,512]{1,0:T(8,128)(2,1)} %bitcast.9), channel_id=1, source_target_pairs={{0,1},{1,2},{2,3},{3,0},{4,5},{5,6},{6,7},{7,4},{8,9},{9,10},{10,1... | collective-permute-start | bytes 1572872 | tf_op jit(solution)/shard_map/ppermute | solution.py:558
  122.9 50.5 %collective-permute-start = (bf16[512,512]{1,0:T(8,128)(2,1)}, bf16[512,512]{1,0:T(8,128)(2,1)S(1)}, u32[]{:S(2)}, u32[]{:S(2)}) collective-permute-start(bf16[512,512]{1,0:T(8,128)(2,1)} %bitcast.9), channel_id=1, source_target_pairs={{0,3},{1,0},{2,1},{3,2},{4,7},{5,4},{6,5},{7,6},{8,11},{9,8},{10,9... | collective-permute-start | bytes 1572872 | tf_op jit(solution)/shard_map/ppermute | solution.py:561
  144.6 1.0 copy-start.9
  145.5 27.4 %collective-permute-start.1 = (bf16[512,512]{1,0:T(8,128)(2,1)}, bf16[512,512]{1,0:T(8,128)(2,1)S(1)}, u32[]{:S(2)}, u32[]{:S(2)}) collective-permute-start(bf16[512,512]{1,0:T(8,128)(2,1)} %bitcast.10), channel_id=1, source_target_pairs={{0,3},{1,0},{2,1},{3,2},{4,7},{5,4},{6,5},{7,6},{8,11},{9,8},{10,9... | collective-permute-start | bytes 1572872 | tf_op jit(solution)/shard_map/ppermute | solution.py:559
  167.4 16.2 %collective-permute-start.5 = (bf16[512,512]{1,0:T(8,128)(2,1)}, bf16[512,512]{1,0:T(8,128)(2,1)S(1)}, u32[]{:S(2)}, u32[]{:S(2)}) collective-permute-start(bf16[512,512]{1,0:T(8,128)(2,1)} %bitcast.10), channel_id=1, source_target_pairs={{0,1},{1,2},{2,3},{3,0},{4,5},{5,6},{6,7},{7,4},{8,9},{9,10},{10,1... | collective-permute-start | bytes 1572872 | tf_op jit(solution)/shard_map/ppermute | solution.py:560
  168.9 23.9 %collective-permute-start.3 = (bf16[512,512]{1,0:T(8,128)(2,1)S(1)}, bf16[512,512]{1,0:T(8,128)(2,1)}, u32[]{:S(2)}, u32[]{:S(2)}) collective-permute-start(bf16[512,512]{1,0:T(8,128)(2,1)S(1)} %collective-permute-done.2.refs_0_.refs_5_), channel_id=1, source_target_pairs={{0,1},{1,2},{2,3},{3,0},{4,5},{5,6},{6,7},{7,4},{8,9},{9,10},{10,1... | collective-permute-start | bytes 1572872 | tf_op jit(solution)/shard_map/ppermute | solution.py:562
  172.9 46.8 %collective-permute-start.19 = (bf16[2,2,512,256]{3,2,1,0:T(8,128)(2,1)}, bf16[2,2,512,256]{3,2,1,0:T(8,128)(2,1)}, u32[]{:S(2)}, u32[]{:S(2)}) collective-permute-start(bf16[2,2,512,256]{3,2,1,0:T(8,128)(2,1)} %bitcast.21.refs_0_), channel_id=1, source_target_pairs={{0,8},{8,0},{1,9},{9,1},{2,10},{10,2},{3,11},{11,3},{4,12},{12,4},... | collective-permute-start | bytes 3145736 | tf_op jit(solution)/shard_map/ppermute | solution.py:553
  172.9 27.4 %copy-start = (bf16[512,512]{1,0:T(8,128)(2,1)}, bf16[512,512]{1,0:T(8,128)(2,1)S(1)}, u32[]{:S(2)}) copy-start(bf16[512,512]{1,0:T(8,128)(2,1)S(1)} %collective-permute-done.1.refs_3_.refs_2_) | copy-start | bytes 1572868
  172.9 46.8 %collective-permute-start.20 = (bf16[2,2,512,256]{3,2,1,0:T(8,128)(2,1)}, bf16[2,2,512,256]{3,2,1,0:T(8,128)(2,1)}, u32[]{:S(2)}, u32[]{:S(2)}) collective-permute-start(bf16[2,2,512,256]{3,2,1,0:T(8,128)(2,1)} %copy-done.9), channel_id=1, source_target_pairs={{0,8},{8,0},{1,9},{9,1},{2,10},{10,2},{3,11},{11,3},{4,12},{12,4},... | collective-permute-start | bytes 3145736 | tf_op jit(solution)/shard_map/ppermute | solution.py:553
  173.4 46.3 %collective-permute-start.21 = (bf16[2,2,512,256]{3,2,1,0:T(8,128)(2,1)}, bf16[2,2,512,256]{3,2,1,0:T(8,128)(2,1)}, u32[]{:S(2)}, u32[]{:S(2)}) collective-permute-start(bf16[2,2,512,256]{3,2,1,0:T(8,128)(2,1)} %collective-permute-done.11.refs_2_), channel_id=1, source_target_pairs={{0,8},{8,0},{1,9},{9,1},{2,10},{10,2},{3,11},{11,3},{4,12},{12,4},... | collective-permute-start | bytes 3145736 | tf_op jit(solution)/shard_map/ppermute | solution.py:553
  183.6 36.1 %collective-permute-start.22 = (bf16[2,2,512,256]{3,2,1,0:T(8,128)(2,1)}, bf16[2,2,512,256]{3,2,1,0:T(8,128)(2,1)}, u32[]{:S(2)}, u32[]{:S(2)}) collective-permute-start(bf16[2,2,512,256]{3,2,1,0:T(8,128)(2,1)} %collective-permute-done.12.refs_3_), channel_id=1, source_target_pairs={{0,8},{8,0},{1,9},{9,1},{2,10},{10,2},{3,11},{11,3},{4,12},{12,4},... | collective-permute-start | bytes 3145736 | tf_op jit(solution)/shard_map/ppermute | solution.py:553
  192.8 15.6 %collective-permute-start.4 = (bf16[512,512]{1,0:T(8,128)(2,1)S(1)}, bf16[512,512]{1,0:T(8,128)(2,1)}, u32[]{:S(2)}, u32[]{:S(2)}) collective-permute-start(bf16[512,512]{1,0:T(8,128)(2,1)S(1)} %collective-permute-done.1.refs_3_.refs_2_), channel_id=1, source_target_pairs={{0,3},{1,0},{2,1},{3,2},{4,7},{5,4},{6,5},{7,6},{8,11},{9,8},{10,9... | collective-permute-start | bytes 1572872 | tf_op jit(solution)/shard_map/ppermute | solution.py:563
  200.3 8.1 %copy-start.2 = (f32[512,128]{1,0:T(8,128)S(1)}, f32[512,128]{1,0:T(8,128)}, u32[]{:S(2)}) copy-start(f32[512,128]{1,0:T(8,128)} %get-tuple-element.79.refs_7_) | copy-start | bytes 786436
  226.1 29.2 %copy-start.7 = (bf16[128,1024]{1,0:T(8,128)(2,1)S(1)}, bf16[128,1024]{1,0:T(8,128)(2,1)}, u32[]{:S(2)}) copy-start(bf16[128,1024]{1,0:T(8,128)(2,1)} %get-tuple-element.61) | copy-start | bytes 786436
  226.1 36.6 %copy-start.1 = (bf16[512,512]{1,0:T(8,128)(2,1)S(1)}, bf16[512,512]{1,0:T(8,128)(2,1)}, u32[]{:S(2)}) copy-start(bf16[512,512]{1,0:T(8,128)(2,1)} %copy-done) | copy-start | bytes 1572868
  226.1 10.5 %collective-permute-start.26 = (bf16[128,1024]{1,0:T(8,128)(2,1)}, bf16[128,1024]{1,0:T(8,128)(2,1)}, u32[]{:S(2)}, u32[]{:S(2)}) collective-permute-start(bf16[128,1024]{1,0:T(8,128)(2,1)} %get-tuple-element.63), channel_id=1, source_target_pairs={{0,3},{1,0},{2,1},{3,2},{4,7},{5,4},{6,5},{7,6},{8,11},{9,8},{10,9... | collective-permute-start | bytes 786440 | tf_op jit(solution)/shard_map/ppermute | solution.py:496
  227.0 43.0 %copy-start.3 = (bf16[128,1024]{1,0:T(8,128)(2,1)S(1)}, bf16[128,1024]{1,0:T(8,128)(2,1)}, u32[]{:S(2)}) copy-start(bf16[128,1024]{1,0:T(8,128)(2,1)} %get-tuple-element.62.refs_5_) | copy-start | bytes 786436
  227.0 43.0 %copy-start.4 = (bf16[128,1024]{1,0:T(8,128)(2,1)S(1)}, bf16[128,1024]{1,0:T(8,128)(2,1)}, u32[]{:S(2)}) copy-start(bf16[128,1024]{1,0:T(8,128)(2,1)} %get-tuple-element.66.refs_7_) | copy-start | bytes 786436
  227.0 12.9 %collective-permute-start.23 = (bf16[128,1024]{1,0:T(8,128)(2,1)}, bf16[128,1024]{1,0:T(8,128)(2,1)}, u32[]{:S(2)}, u32[]{:S(2)}) collective-permute-start(bf16[128,1024]{1,0:T(8,128)(2,1)} %get-tuple-element.59), channel_id=1, source_target_pairs={{0,3},{1,0},{2,1},{3,2},{4,7},{5,4},{6,5},{7,6},{8,11},{9,8},{10,9... | collective-permute-start | bytes 786440 | tf_op jit(solution)/shard_map/ppermute | solution.py:496
  233.8 36.1 %copy-start.5 = (bf16[128,1024]{1,0:T(8,128)(2,1)S(1)}, bf16[128,1024]{1,0:T(8,128)(2,1)}, u32[]{:S(2)}) copy-start(bf16[128,1024]{1,0:T(8,128)(2,1)} %get-tuple-element.54.refs_1_) | copy-start | bytes 786436
  233.9 36.1 %copy-start.6 = (bf16[128,1024]{1,0:T(8,128)(2,1)S(1)}, bf16[128,1024]{1,0:T(8,128)(2,1)}, u32[]{:S(2)}) copy-start(bf16[128,1024]{1,0:T(8,128)(2,1)} %get-tuple-element.58.refs_3_) | copy-start | bytes 786436
  233.9 10.3 %collective-permute-start.16 = (bf16[128,1024]{1,0:T(8,128)(2,1)}, bf16[128,1024]{1,0:T(8,128)(2,1)S(1)}, u32[]{:S(2)}, u32[]{:S(2)}) collective-permute-start(bf16[128,1024]{1,0:T(8,128)(2,1)} %get-tuple-element.55), channel_id=1, source_target_pairs={{0,1},{1,2},{2,3},{3,0},{4,5},{5,6},{6,7},{7,4},{8,9},{9,10},{10,1... | collective-permute-start | bytes 786440 | tf_op jit(solution)/shard_map/ppermute | solution.py:496
  235.4 14.4 %collective-permute-start.13 = (bf16[128,1024]{1,0:T(8,128)(2,1)}, bf16[128,1024]{1,0:T(8,128)(2,1)S(1)}, u32[]{:S(2)}, u32[]{:S(2)}) collective-permute-start(bf16[128,1024]{1,0:T(8,128)(2,1)} %get-tuple-element.51), channel_id=1, source_target_pairs={{0,1},{1,2},{2,3},{3,0},{4,5},{5,6},{6,7},{7,4},{8,9},{9,10},{10,1... | collective-permute-start | bytes 786440 | tf_op jit(solution)/shard_map/ppermute | solution.py:496
  237.7 13.6 %collective-permute-start.27 = (bf16[128,1024]{1,0:T(8,128)(2,1)S(1)}, bf16[128,1024]{1,0:T(8,128)(2,1)S(1)}, u32[]{:S(2)}, u32[]{:S(2)}) collective-permute-start(bf16[128,1024]{1,0:T(8,128)(2,1)S(1)} %add_convert_fusion.1), channel_id=1, source_target_pairs={{0,3},{1,0},{2,1},{3,2},{4,7},{5,4},{6,5},{7,6},{8,11},{9,8},{10,9... | collective-permute-start | bytes 786440 | tf_op jit(solution)/shard_map/ppermute | solution.py:496
  240.9 14.3 %collective-permute-start.24 = (bf16[128,1024]{1,0:T(8,128)(2,1)S(1)}, bf16[128,1024]{1,0:T(8,128)(2,1)S(1)}, u32[]{:S(2)}, u32[]{:S(2)}) collective-permute-start(bf16[128,1024]{1,0:T(8,128)(2,1)S(1)} %add_convert_fusion.3), channel_id=1, source_target_pairs={{0,3},{1,0},{2,1},{3,2},{4,7},{5,4},{6,5},{7,6},{8,11},{9,8},{10,9... | collective-permute-start | bytes 786440 | tf_op jit(solution)/shard_map/ppermute | solution.py:496
  245.2 10.5 %collective-permute-start.17 = (bf16[128,1024]{1,0:T(8,128)(2,1)S(1)}, bf16[128,1024]{1,0:T(8,128)(2,1)S(1)}, u32[]{:S(2)}, u32[]{:S(2)}) collective-permute-start(bf16[128,1024]{1,0:T(8,128)(2,1)S(1)} %add_convert_fusion.5), channel_id=1, source_target_pairs={{0,1},{1,2},{2,3},{3,0},{4,5},{5,6},{6,7},{7,4},{8,9},{9,10},{10,1... | collective-permute-start | bytes 786440 | tf_op jit(solution)/shard_map/ppermute | solution.py:496
  250.8 10.5 %collective-permute-start.14 = (bf16[128,1024]{1,0:T(8,128)(2,1)S(1)}, bf16[128,1024]{1,0:T(8,128)(2,1)S(1)}, u32[]{:S(2)}, u32[]{:S(2)}) collective-permute-start(bf16[128,1024]{1,0:T(8,128)(2,1)S(1)} %add_convert_fusion.7), channel_id=1, source_target_pairs={{0,1},{1,2},{2,3},{3,0},{4,5},{5,6},{6,7},{7,4},{8,9},{9,10},{10,1... | collective-permute-start | bytes 786440 | tf_op jit(solution)/shard_map/ppermute | solution.py:496
  252.3 12.3 %collective-permute-start.28 = (bf16[128,1024]{1,0:T(8,128)(2,1)S(1)}, bf16[128,1024]{1,0:T(8,128)(2,1)S(1)}, u32[]{:S(2)}, u32[]{:S(2)}) collective-permute-start(bf16[128,1024]{1,0:T(8,128)(2,1)S(1)} %add_convert_fusion), channel_id=1, source_target_pairs={{0,3},{1,0},{2,1},{3,2},{4,7},{5,4},{6,5},{7,6},{8,11},{9,8},{10,9... | collective-permute-start | bytes 786440 | tf_op jit(solution)/shard_map/ppermute | solution.py:496
  255.3 9.4 %collective-permute-start.25 = (bf16[128,1024]{1,0:T(8,128)(2,1)S(1)}, bf16[128,1024]{1,0:T(8,128)(2,1)S(1)}, u32[]{:S(2)}, u32[]{:S(2)}) collective-permute-start(bf16[128,1024]{1,0:T(8,128)(2,1)S(1)} %add_convert_fusion.2), channel_id=1, source_target_pairs={{0,3},{1,0},{2,1},{3,2},{4,7},{5,4},{6,5},{7,6},{8,11},{9,8},{10,9... | collective-permute-start | bytes 786440 | tf_op jit(solution)/shard_map/ppermute | solution.py:496
  256.7 9.3 %collective-permute-start.18 = (bf16[128,1024]{1,0:T(8,128)(2,1)S(1)}, bf16[128,1024]{1,0:T(8,128)(2,1)S(1)}, u32[]{:S(2)}, u32[]{:S(2)}) collective-permute-start(bf16[128,1024]{1,0:T(8,128)(2,1)S(1)} %add_convert_fusion.4), channel_id=1, source_target_pairs={{0,1},{1,2},{2,3},{3,0},{4,5},{5,6},{6,7},{7,4},{8,9},{9,10},{10,1... | collective-permute-start | bytes 786440 | tf_op jit(solution)/shard_map/ppermute | solution.py:496
  262.3 7.7 %collective-permute-start.15 = (bf16[128,1024]{1,0:T(8,128)(2,1)S(1)}, bf16[128,1024]{1,0:T(8,128)(2,1)S(1)}, u32[]{:S(2)}, u32[]{:S(2)}) collective-permute-start(bf16[128,1024]{1,0:T(8,128)(2,1)S(1)} %add_convert_fusion.6), channel_id=1, source_target_pairs={{0,1},{1,2},{2,3},{3,0},{4,5},{5,6},{6,7},{7,4},{8,9},{9,10},{10,1... | collective-permute-start | bytes 786440 | tf_op jit(solution)/shard_map/ppermute | solution.py:496
Sparse Core Ops, SparseCore 0:
  22.7 84.1 all-gather.3

commit v7 on v5

--- a/solution.py
+++ b/solution.py
@@ -95,7 +95,7 @@
         lax.fori_loop(0, -(-slab // unroll), prepare, 0)
 
     per_group = row_count // LANES
-    together = 2
+    together = 4
 
     def one_block(step, carry):
         for part in range(together):
@@ -371,23 +371,23 @@
     return [(k, (k + way) % count) for k in range(count)]
 
 
-def product_kernel(where_ref, rows_ref, *refs, pieces, turns, chunks):
+def product_kernel(where_ref, rows_ref, *refs, turns, chunks):
     turned, held, arrived = refs[-3:]
-    out_refs = refs[-3 - len(turns) * chunks : -3]
+    out_refs = refs[-3 - len(turns) : -3]
+    weights = refs[: -3 - len(turns)]
     quarter = out_refs[0].shape[0]
     ring = rows_ref.shape[0] // quarter
-    _, halves, depth, width = refs[0].shape
+    halves, depth, width = weights[0].shape
 
     def incoming(k, half):
-        array, index = pieces[k]
         block = where_ref[1] ^ half
         return pltpu.make_async_copy(
-            refs[array].at[index, half],
+            weights[k].at[half],
             held.at[pl.ds(pl.multiple_of(block * depth, depth), depth), pl.ds(k * width, width)],
             arrived.at[k, half],
         )
 
-    copies = [(k, half) for k in range(len(pieces)) for half in range(halves)]
+    copies = [(k, half) for k in range(len(weights)) for half in range(halves)]
     for copy in copies:
         incoming(*copy).start()
     for at, turn in enumerate(turns):
@@ -395,31 +395,30 @@
         turned[at * quarter : (at + 1) * quarter] = rows_ref[
             pl.ds(pl.multiple_of(block * quarter, quarter), quarter)
         ]
-    each = len(pieces) // chunks
+    each = len(weights) // chunks
     for chunk in range(chunks):
         for copy in copies[chunk * each * halves : (chunk + 1) * each * halves]:
             incoming(*copy).wait()
+        here = slice(chunk * each * width, (chunk + 1) * each * width)
         total = jnp.dot(
-            turned[...],
-            held[:, chunk * each * width : (chunk + 1) * each * width],
-            preferred_element_type=jnp.float32,
+            turned[...], held[:, here], preferred_element_type=jnp.float32
         ).astype(jnp.bfloat16)
         for at in range(len(turns)):
-            out_refs[chunk * len(turns) + at][...] = total[at * quarter : (at + 1) * quarter]
-
-
-def product(where, rows, weights, pieces, turns, chunks):
-    _, halves, depth, width = weights[0].shape
+            out_refs[at][:, here] = total[at * quarter : (at + 1) * quarter]
+
+
+def product(where, rows, weights, turns, chunks=2):
+    halves, depth, width = weights[0].shape
     row_count = rows.shape[0]
-    count = len(pieces)
+    count = len(weights)
     return pl.pallas_call(
-        functools.partial(product_kernel, pieces=pieces, turns=turns, chunks=chunks),
+        functools.partial(product_kernel, turns=turns, chunks=chunks),
         in_specs=[pl.BlockSpec(memory_space=pltpu.SMEM), pl.BlockSpec(memory_space=pltpu.VMEM)]
-        + [pl.BlockSpec(memory_space=pltpu.HBM)] * len(weights),
-        out_specs=tuple([pl.BlockSpec(memory_space=pltpu.VMEM)] * (len(turns) * chunks)),
+        + [pl.BlockSpec(memory_space=pltpu.HBM)] * count,
+        out_specs=tuple([pl.BlockSpec(memory_space=pltpu.VMEM)] * len(turns)),
         out_shape=tuple(
-            [jax.ShapeDtypeStruct((row_count // len(turns), count // chunks * width), jnp.bfloat16)]
-            * (len(turns) * chunks)
+            [jax.ShapeDtypeStruct((row_count // len(turns), count * width), jnp.bfloat16)]
+            * len(turns)
         ),
         scratch_shapes=[
             pltpu.VMEM(rows.shape, jnp.bfloat16),
@@ -441,23 +440,17 @@
 
 def finish_kernel(where_ref, rows_ref, *refs, width):
     hidden_ref = refs[-1]
-    chunks = (len(refs) - 1) // 4
-    each = refs[0].shape[1] // width
     for core in range(2):
-        for chunk in range(chunks):
-            at = 2 * (chunks * core + chunk)
-            for j in range(each):
-                layer, side = divmod(chunk * each + j, 2)
-                z = lax.rem(where_ref[0] + len(LAYERS) - LAYERS[layer], len(LAYERS))
-                column = (z * 2 + (where_ref[1] ^ side)) * 2 + (where_ref[2] ^ core)
-                here = slice(j * width, (j + 1) * width)
-                there = pl.ds(pl.multiple_of(column * width, width), width)
-                total = refs[at][:, here].astype(jnp.float32) + refs[at + 1][:, here].astype(
-                    jnp.float32
-                )
-                hidden_ref[:, there] = (
-                    rows_ref[:, there].astype(jnp.float32) + total
-                ).astype(jnp.bfloat16)
+        terms = refs[3 * core : 3 * core + 3]
+        for j in range(2 * len(LAYERS)):
+            z = lax.rem(where_ref[0] + len(LAYERS) - LAYERS[j // 2], len(LAYERS))
+            column = (z * 2 + (where_ref[1] ^ (j % 2))) * 2 + (where_ref[2] ^ core)
+            here = slice(j * width, (j + 1) * width)
+            there = pl.ds(pl.multiple_of(column * width, width), width)
+            total = sum(term[:, here].astype(jnp.float32) for term in terms)
+            hidden_ref[:, there] = (rows_ref[:, there].astype(jnp.float32) + total).astype(
+                jnp.bfloat16
+            )
 
 
 def finish(where, rows, sums, width):
@@ -475,27 +468,23 @@
     )(where, rows, *sums)
 
 
-CHUNKS = 2
-
-
-def ring_sums(attended, weights):
-    count = lax.axis_size(RING)
-    pieces = [(LAYERS.index(z), side) for z in LAYERS[:3] for side in range(2)]
-    pieces += [(3, 0), (4, 0)]
+def ring_sums(attended, w_mine, w_other):
     where = jnp.stack([lax.axis_index(RING), lax.axis_index("tensor_0")])
-    sums = []
-    for side, way in enumerate((1, -1)):
-        turns = [-way * (step + 1) for step in range(count)]
-        parts = product(where, attended, weights[side], pieces, turns, CHUNKS)
-        for chunk in range(CHUNKS):
-            running, *mine = parts[chunk * count : (chunk + 1) * count]
-            for step in range(1, count):
-                running = lax.ppermute(running, RING, ring_route(way))
-                if step + 1 < count:
-                    running = running.astype(jnp.float32) + mine[step - 1].astype(jnp.float32)
-                    running = running.astype(jnp.bfloat16)
-            sums += [running, mine[-1]]
-    return sums
+    order = [(z, side) for z in LAYERS for side in range(2)]
+    own, first, onward = [], [], []
+    for way, weights in ((1, w_mine), (-1, w_other)):
+        across, against, along, mine = product(
+            where, attended, [weights[name] for name in order], [2, -way, way, 0]
+        )
+        passed = lax.ppermute(across, RING, ring_route(way))
+        first.append(lax.ppermute(against, RING, ring_route(-way)))
+        own.append(mine)
+        onward.append((way, along, passed))
+    last = []
+    for way, along, passed in onward:
+        both = (along.astype(jnp.float32) + passed.astype(jnp.float32)).astype(jnp.bfloat16)
+        last.append(lax.ppermute(both, RING, ring_route(way)))
+    return [term for core in range(2) for term in (own[core], first[core], last[core])]
 
 
 def sublayer(prompt_ids, prompt_lengths, embed_table, norm_gain, w_query, w_key, w_value, w_out):
@@ -536,12 +525,23 @@
         -1, row_count
     )
     pieces_x, _ = lax.optimization_barrier((pieces_x, outgoing))
-    w_mine = [jnp.stack(pieces_x).reshape(2, 2, *w_out.shape)]
+    w_mine = {(0, side): jnp.stack(pieces_x[2 * side : 2 * side + 2]) for side in range(2)}
     layers = lax.axis_size("dp_0")
     ahead = [(z, (z + 1) % layers) for z in range(layers)]
     back = [(z, (z - 1) % layers) for z in range(layers)]
-    for route in (ahead, back):
-        w_mine.append(lax.ppermute(w_mine[0], "dp_0", route))
+    for z, side, before, route in (
+        (1, 0, 0, ahead),
+        (3, 1, 0, back),
+        (1, 1, 0, ahead),
+        (3, 0, 0, back),
+        (2, 0, 1, ahead),
+        (2, 1, 3, back),
+    ):
+        w_mine[z, side] = lax.ppermute(w_mine[before, side], "dp_0", route)
+    w_other = {}
+    for z, side in w_mine:
+        w_other[z, side] = lax.ppermute(w_mine[z, side], "dp_2", [(0, 1), (1, 0)])
+
     places = (place + jnp.arange(ring, dtype=jnp.int32)) % ring
     half = own.shape[0] // 2
     low, high = own[:half], own[half:]
@@ -564,13 +564,6 @@
         ],
         first,
     )
-    z_sides, _ = lax.optimization_barrier((w_mine[1:], second))
-    first_side, last_side = z_sides[0][:1], z_sides[1][1:]
-    w_mine.append(lax.ppermute(first_side, "dp_0", ahead))
-    w_mine.append(lax.ppermute(last_side, "dp_0", back))
-    w_other = []
-    for k in range(len(w_mine)):
-        w_other.append(lax.ppermute(w_mine[k], "dp_2", [(0, 1), (1, 0)]))
     attended, cache = attend(
         places,
         w_in,
@@ -586,7 +579,7 @@
     pieces, _ = lax.optimization_barrier((pieces, attended))
     own_rows = residual(places, pieces, columns, quarter)
 
-    sums = ring_sums(attended, (w_mine, w_other))
+    sums = ring_sums(attended, w_mine, w_other)
     where = jnp.stack([lax.axis_index(name) for name in DP])
     hidden = finish(where, own_rows, sums, w_out.shape[1])
     return hidden, cache[None]

time: 252 us -> 270 us (1.071)
  waiting for transfers between devices: 68.2 us -> 104 us
  other arithmetic: 16.7 us -> 8.79 us
  starting transfers between devices: 49.6 us -> 42.2 us
    ppermute x21 -> x20, waiting for transfers between devices: 15.2 us -> 49.5 us  [the longest x6 22.8 us: sublayer(): w_mine[z, side] = lax.ppermute(w_mine[before, side], 'dp_0', route)]
    ppermute x3, waiting for transfers between devices: 7.77 us -> 31.5 us  [sublayer(): pieces_x.append(lax.ppermute(w_out, axes, route))]
    all_to_all x1, waiting for transfers between devices: 17.7 us -> 0.01 us  [sublayer(): lax.all_to_all(outgoing, PLANE, split_axis=0, concat_axis=0, tiled=True)]
    ppermute x1, waiting for transfers between devices: 10.9 us -> 0.01 us  [sublayer(): high_before = lax.ppermute(high, RING, ring_route(1))]
    ppermute x21 -> x20, starting transfers between devices: 30 us -> 20.1 us  [the longest x6 10.2 us: sublayer(): w_mine[z, side] = lax.ppermute(w_mine[before, side], 'dp_0', route)]
    ppermute x1, waiting for transfers between devices: 0.01 us -> 9.04 us  [sublayer(): low_across = lax.ppermute(low_before, RING, ring_route(1))]
    convert_element_type x8 -> x2, other arithmetic: 8.13 us -> 2.49 us  [ring_sums(): (along.astype(jnp.float32) + passed.astype(jnp.float32)).astype(jnp.bfloa...]
    slice x2 -> x0, local copies, waits for them, and re-layouts: 3.81 us -> none  [sublayer(): first_side, last_side = (z_sides[0][:1], z_sides[1][1:])]
  transfers between devices with their start and end apart: 33 -> 32, of which waited for: 13 -> 14; matrix products, arithmetic and copies ran while one was open for 8% -> 3% of each run, Pallas kernels for 30% -> 25%
where the time goes in v7:
time: 270 us; the launch traced here: 268 us
  waiting for transfers between devices  104 us (39%)
  Pallas kernels  74.8 us (28%)
  starting transfers between devices  42.2 us (16%)
  blocking collectives  18.7 us (7%)
  between operations  14.4 us (5%)
  other arithmetic  8.79 us (3%)
  local copies, waits for them, and re-layouts  5.25 us (2%)
    pallas_call x1, Pallas kernels, lookup(): pl.pallas_call(lookup_kernel, out_shape=jax.ShapeDtypeStruct((group_count...  32.4 us
    ppermute x3, waiting for transfers between devices, sublayer(): pieces_x.append(lax.ppermute(w_out, axes, route))  31.5 us
    ppermute x6, waiting for transfers between devices, sublayer(): w_mine[z, side] = lax.ppermute(w_mine[before, side], 'dp_0', route)  22.8 us
    all_to_all x1, blocking collectives, sublayer(): lax.all_to_all(jnp.broadcast_to(prompt_ids[None], (devices, quarter)), DP...  18.7 us
    pallas_call x2, Pallas kernels, project(): pl.pallas_call(functools.partial(project_kernel, parts=len(parts), carrie...  13.5 us
    pallas_call x2, Pallas kernels, product(): pl.pallas_call(functools.partial(product_kernel, turns=turns, chunks=chun...  13.3 us
    pallas_call x1, Pallas kernels, attend(): pl.pallas_call(functools.partial(attention_kernel, parts=len(parts), mode...  11.4 us
    ppermute x1, waiting for transfers between devices, swapped(): return lax.ppermute(block, axis, route)  11 us
  transfers between devices with their start and end apart: 32, of which 14 were waited for; matrix products, arithmetic and copies ran while one was open for 3% of the time, Pallas kernels for 25%

profile of v7, /device:TPU:6, one launch (start us, length us, event | category | flops | bytes accessed | tf_op | source)
XLA Modules:
  0.0 268.2 jit_solution(740123070260832513)
XLA Ops:
  7.2 0.8 dynamic_slice.7
  8.0 1.2 multiply_convert_fusion
  9.2 1.5 collective-permute-start.6
  10.6 11.0 %collective-permute-done.6 = bf16[1,256,768]{2,1,0:T(8,128)(2,1)S(1)} collective-permute-done((bf16[1,256,768]{2,1,0:T(8,128)(2,1)S(1)}, bf16[1,256,768]{2,1,0:T(8,128)(2,1)S(1)}, u32[]{:S(2)}, u32[]{:S(2)}) %collective-permute-start.6) | collective-permute-done | bytes 393248 | tf_op jit(solution)/shard_map/ppermute | solution.py:34
  21.6 1.0 pad_maximum_fusion
  23.3 18.7 %all_to_all.11 = s32[128,1,128]{2,1,0:T(1,128)S(1)} all-to-all(s32[128,1,128]{2,1,0:T(1,128)S(1)} %broadcast_in_dim.4), channel_id=1, replica_groups=mesh['dp_0'=4,'dp_1'=2,'dp_2'=2,'tensor_0'=2,'tensor_1'=4] {'dp_0','dp_1..., dimensions={0} | all-to-all | bytes 131072 | tf_op jit(solution)/shard_map/all_to_all | solution.py:509
  43.4 32.4 %lookup.1 = bf16[32,32,512]{2,1,0:T(8,128)(2,1)} custom-call(s32[16384]{0:T(1024)} %fusion.2.slots_ref, s32[128,128]{1,0:T(8,128)} %bitcast_or_fusion.lanes_ref, bf16[32,128256]{1,0:T(8,128)(2,1)} %table_ref.1), custom_call_target="tpu_custom_call" | custom-call | flops 30000001024 | bytes 8208384 | tf_op jit(solution)/shard_map/lookup/pallas_call | solution.py:131
  75.8 5.8 %all-to-all-start.1 = ((bf16[32,32,512]{2,1,0:T(8,128)(2,1)}), bf16[32,32,512]{2,1,0:T(8,128)(2,1)S(1)}, u32[]{:S(2)}, u32[]{:S(2)}) async-start(bf16[32,32,512]{2,1,0:T(8,128)(2,1)} %lookup.1), calls=%async_computation.1 | async-start | bytes 2097152 | tf_op jit(solution)/shard_map/all_to_all | solution.py:524
  81.6 1.5 collective-permute-start.7
  83.1 2.6 collective-permute-start.9
  85.8 26.6 %collective-permute-done.7 = bf16[512,256]{1,0:T(8,128)(2,1)S(1)} collective-permute-done((bf16[512,256]{1,0:T(8,128)(2,1)S(1)}, bf16[512,256]{1,0:T(8,128)(2,1)S(1)}, u32[]{:S(2)}, u32[]{:S(2)}) %collective-permute-start.7) | collective-permute-done | bytes 262176 | tf_op jit(solution)/shard_map/ppermute | solution.py:522
  112.4 4.9 %collective-permute-done.8 = bf16[512,256]{1,0:T(8,128)(2,1)S(1)} collective-permute-done((bf16[512,256]{1,0:T(8,128)(2,1)S(1)}, bf16[512,256]{1,0:T(8,128)(2,1)S(1)}, u32[]{:S(2)}, u32[]{:S(2)}) %collective-permute-start.8) | collective-permute-done | bytes 262176 | tf_op jit(solution)/shard_map/ppermute | solution.py:522
  117.5 3.3 %collective-permute-start.13 = (bf16[2,512,256]{2,1,0:T(8,128)(2,1)S(1)}, bf16[2,512,256]{2,1,0:T(8,128)(2,1)}, u32[]{:S(2)}, u32[]{:S(2)}) collective-permute-start(bf16[2,512,256]{2,1,0:T(8,128)(2,1)S(1)} %pad_maximum_fusion.2.refs_1_), channel_id=1, source_target_pairs={{0,96},{32,0},{64,32},{96,64},{1,97},{33,1},{65,33},{97,65},{2,98}... | collective-permute-start | bytes 1572872 | tf_op jit(solution)/shard_map/ppermute | solution.py:540
  120.8 3.2 %collective-permute-start.12 = (bf16[2,512,256]{2,1,0:T(8,128)(2,1)S(1)}, bf16[2,512,256]{2,1,0:T(8,128)(2,1)S(1)}, u32[]{:S(2)}, u32[]{:S(2)}) collective-permute-start(bf16[2,512,256]{2,1,0:T(8,128)(2,1)S(1)} %pad_maximum_fusion.1.refs_0_), channel_id=1, source_target_pairs={{0,96},{32,0},{64,32},{96,64},{1,97},{33,1},{65,33},{97,65},{2,98}... | collective-permute-start | bytes 1572872 | tf_op jit(solution)/shard_map/ppermute | solution.py:540
  124.0 1.1 fusion.4
  125.1 8.4 %collective-permute-done.10.refs_2_ = bf16[2,512,256]{2,1,0:T(8,128)(2,1)} collective-permute-done((bf16[2,512,256]{2,1,0:T(8,128)(2,1)S(1)}, bf16[2,512,256]{2,1,0:T(8,128)(2,1)}, u32[]{:S(2)}, u32[]{:S(2)}) %collective-permute-start.10) | collective-permute-done | bytes 524320 | tf_op jit(solution)/shard_map/ppermute | solution.py:540
  133.5 1.5 collective-permute-start.14
  135.1 9.6 %collective-permute-done.11.refs_3_ = bf16[2,512,256]{2,1,0:T(8,128)(2,1)S(1)} collective-permute-done((bf16[2,512,256]{2,1,0:T(8,128)(2,1)S(1)}, bf16[2,512,256]{2,1,0:T(8,128)(2,1)S(1)}, u32[]{:S(2)}, u32[]{:S(2)}) %collective-permute-start.11) | collective-permute-done | bytes 524320 | tf_op jit(solution)/shard_map/ppermute | solution.py:540
  144.6 2.0 collective-permute-start.15
  146.7 1.6 collective-permute-start.2
  148.2 2.0 collective-permute-start.1
  150.4 4.8 %collective-permute-done.14.refs_6_ = bf16[2,512,256]{2,1,0:T(8,128)(2,1)S(1)} collective-permute-done((bf16[2,512,256]{2,1,0:T(8,128)(2,1)}, bf16[2,512,256]{2,1,0:T(8,128)(2,1)S(1)}, u32[]{:S(2)}, u32[]{:S(2)}) %collective-permute-start.14) | collective-permute-done | bytes 524320 | tf_op jit(solution)/shard_map/ppermute | solution.py:540
  155.2 2.8 %collective-permute-start = (bf16[512,512]{1,0:T(8,128)(2,1)}, bf16[512,512]{1,0:T(8,128)(2,1)S(1)}, u32[]{:S(2)}, u32[]{:S(2)}) collective-permute-start(bf16[512,512]{1,0:T(8,128)(2,1)} %bitcast.8), channel_id=1, source_target_pairs={{0,3},{1,0},{2,1},{3,2},{4,7},{5,4},{6,5},{7,6},{8,11},{9,8},{10,9... | collective-permute-start | bytes 1572872 | tf_op jit(solution)/shard_map/ppermute | solution.py:551
  157.9 0.9 collective-permute-start.5
  158.9 1.0 collective-permute-done.2.refs_0_.refs_5_
  160.4 2.1 collective-permute-done.1.refs_3_.refs_2_
  162.5 2.9 %collective-permute-start.4 = (bf16[512,512]{1,0:T(8,128)(2,1)S(1)}, bf16[512,512]{1,0:T(8,128)(2,1)}, u32[]{:S(2)}, u32[]{:S(2)}) collective-permute-start(bf16[512,512]{1,0:T(8,128)(2,1)S(1)} %collective-permute-done.1.refs_3_.refs_2_), channel_id=1, source_target_pairs={{0,3},{1,0},{2,1},{3,2},{4,7},{5,4},{6,5},{7,6},{8,11},{9,8},{10,9... | collective-permute-start | bytes 1572872 | tf_op jit(solution)/shard_map/ppermute | solution.py:553
  166.6 1.0 fusion
  167.6 0.9 pad_maximum_fusion.3
  168.6 5.4 %project.2 = (f32[512,1536]{1,0:T(8,128)}, f32[1,512]{1,0:T(1,128)S(1)}) custom-call(s32[4]{0:T(128)S(1)} %and_select_fusion.places_ref, bf16[1024,512]{1,0:T(8,128)(2,1)S(1)} %bitcast.27, bf16[2,32,4,32,768]{4,3,2,1,0:T(8,128)(2,1)} %bitcast.29), custom_call_target="tpu_custom_call" | custom-call | flops 1610612736 | bytes 4194304 | tf_op jit(solution)/shard_map/project/pallas_call | solution.py:201
  174.6 9.0 %collective-permute-done.3.refs_0_.refs_3_ = bf16[512,512]{1,0:T(8,128)(2,1)} collective-permute-done((bf16[512,512]{1,0:T(8,128)(2,1)S(1)}, bf16[512,512]{1,0:T(8,128)(2,1)}, u32[]{:S(2)}, u32[]{:S(2)}) %collective-permute-start.3) | collective-permute-done | bytes 524320 | tf_op jit(solution)/shard_map/ppermute | solution.py:552
  184.1 8.1 %project.3 = (f32[512,1536]{1,0:T(8,128)}, f32[1,512]{1,0:T(1,128)S(1)}) custom-call(s32[4]{0:T(128)S(1)} %and_select_fusion.places_ref, bf16[512,512]{1,0:T(8,128)(2,1)S(1)} %collective-permute-done.2.refs_0_.refs_5_, bf16[512,512]{1,0:T(8,128)(2,1)S(1)} %collective-permute-done.5.refs_1_.refs_6_, ...), custom_call_target="tpu_custom_call" | custom-call | flops 3221225472 | bytes 8388608 | tf_op jit(solution)/shard_map/project/pallas_call | solution.py:201
  192.3 11.4 %attend.1 = (bf16[512,1024]{1,0:T(8,128)(2,1)}, bf16[2,512,256]{2,1,0:T(8,128)(2,1)}) custom-call(s32[4]{0:T(128)S(1)} %and_select_fusion.places_ref, s32[1]{0:T(128)} %dynamic_slice.6.length_ref, bf16[512,512]{1,0:T(8,128)(2,1)} %collective-permute-done.3.refs_0_.refs_3_, bf16[512,512]{1,0:T(8,128)(2,1)} %collective-permute-done.4.refs_1_.refs_4_, ...), custom_call_target="tpu_custom_call" | custom-call | flops 4000000000 | bytes 9000000 | tf_op jit(solution)/shard_map/attend/pallas_call | solution.py:284
  203.7 0.8 copy-done.18
  204.9 0.8 copy-done.21
  205.7 6.7 %product.3 = (bf16[128,2048]{1,0:T(8,128)(2,1)}, bf16[128,2048]{1,0:T(8,128)(2,1)}, bf16[128,2048]{1,0:T(8,128)(2,1)}, bf16[128,2048]{1,0:T(8,128)(2,1)}) custom-call(s32[2]{0:T(128)} %pad_add_fusion.1.where_ref, bf16[512,1024]{1,0:T(8,128)(2,1)} %get-tuple-element.31.rows_ref, bf16[2,512,256]{2,1,0:T(8,128)(2,1)} %collective-permute-done.19.refs_0_, ...), custom_call_target="tpu_custom_call" | custom-call | flops 2147483648 | bytes 5242880 | tf_op jit(solution)/shard_map/product/pallas_call | solution.py:414
  212.4 2.1 collective-permute-start.28
  214.5 6.7 %product.2 = (bf16[128,2048]{1,0:T(8,128)(2,1)}, bf16[128,2048]{1,0:T(8,128)(2,1)}, bf16[128,2048]{1,0:T(8,128)(2,1)}, bf16[128,2048]{1,0:T(8,128)(2,1)}) custom-call(s32[2]{0:T(128)} %pad_add_fusion.1.where_ref, bf16[512,1024]{1,0:T(8,128)(2,1)} %get-tuple-element.31.rows_ref, bf16[2,512,256]{2,1,0:T(8,128)(2,1)} %copy-done.5, ...), custom_call_target="tpu_custom_call" | custom-call | flops 2147483648 | bytes 5242880 | tf_op jit(solution)/shard_map/product/pallas_call | solution.py:414
  221.6 3.2 %collective-permute-start.16 = (bf16[128,2048]{1,0:T(8,128)(2,1)}, bf16[128,2048]{1,0:T(8,128)(2,1)S(1)}, u32[]{:S(2)}, u32[]{:S(2)}) collective-permute-start(bf16[128,2048]{1,0:T(8,128)(2,1)} %get-tuple-element.44), channel_id=1, source_target_pairs={{0,3},{1,0},{2,1},{3,2},{4,7},{5,4},{6,5},{7,6},{8,11},{9,8},{10,9... | collective-permute-start | bytes 1572872 | tf_op jit(solution)/shard_map/ppermute | solution.py:480
  224.7 3.1 %collective-permute-done.28 = bf16[128,2048]{1,0:T(8,128)(2,1)} collective-permute-done((bf16[128,2048]{1,0:T(8,128)(2,1)}, bf16[128,2048]{1,0:T(8,128)(2,1)}, u32[]{:S(2)}, u32[]{:S(2)}) %collective-permute-start.28) | collective-permute-done | bytes 524320 | tf_op jit(solution)/shard_map/ppermute | solution.py:479
  227.8 1.3 add_convert_fusion
  229.2 3.1 %collective-permute-start.29 = (bf16[128,2048]{1,0:T(8,128)(2,1)S(1)}, bf16[128,2048]{1,0:T(8,128)(2,1)S(1)}, u32[]{:S(2)}, u32[]{:S(2)}) collective-permute-start(bf16[128,2048]{1,0:T(8,128)(2,1)S(1)} %add_convert_fusion), channel_id=1, source_target_pairs={{0,3},{1,0},{2,1},{3,2},{4,7},{5,4},{6,5},{7,6},{8,11},{9,8},{10,9... | collective-permute-start | bytes 1572872 | tf_op jit(solution)/shard_map/ppermute | solution.py:486
  232.2 5.2 %collective-permute-done.17 = bf16[128,2048]{1,0:T(8,128)(2,1)S(1)} collective-permute-done((bf16[128,2048]{1,0:T(8,128)(2,1)}, bf16[128,2048]{1,0:T(8,128)(2,1)S(1)}, u32[]{:S(2)}, u32[]{:S(2)}) %collective-permute-start.17) | collective-permute-done | bytes 524320 | tf_op jit(solution)/shard_map/ppermute | solution.py:479
  237.4 1.2 add_convert_fusion.1
  238.8 2.0 residual.1.rows_ref
  240.8 7.9 %collective-permute-done.27.refs_4_ = bf16[128,2048]{1,0:T(8,128)(2,1)S(1)} collective-permute-done((bf16[128,2048]{1,0:T(8,128)(2,1)}, bf16[128,2048]{1,0:T(8,128)(2,1)S(1)}, u32[]{:S(2)}, u32[]{:S(2)}) %collective-permute-start.27) | collective-permute-done | bytes 524320 | tf_op jit(solution)/shard_map/ppermute | solution.py:480
  249.3 9.8 %collective-permute-done.18.refs_2_ = bf16[128,2048]{1,0:T(8,128)(2,1)S(1)} collective-permute-done((bf16[128,2048]{1,0:T(8,128)(2,1)S(1)}, bf16[128,2048]{1,0:T(8,128)(2,1)S(1)}, u32[]{:S(2)}, u32[]{:S(2)}) %collective-permute-start.18) | collective-permute-done | bytes 524320 | tf_op jit(solution)/shard_map/ppermute | solution.py:486
  259.2 2.2 finish.1
  (93 shorter events, 7.1 us)
Async XLA Ops:
  7.2 161.4 %all-gather.2.cloned.1.call-start = ((), (), s32[]{:S(2)}) async-start(), calls=%async_computation.2 | async-start | bytes 13369344 | tf_op jit(solution)/shard_map/all_gather | solution.py:507
  9.2 12.4 %collective-permute-start.6 = (bf16[1,256,768]{2,1,0:T(8,128)(2,1)S(1)}, bf16[1,256,768]{2,1,0:T(8,128)(2,1)S(1)}, u32[]{:S(2)}, u32[]{:S(2)}) collective-permute-start(bf16[1,256,768]{2,1,0:T(8,128)(2,1)S(1)} %multiply_convert_fusion), channel_id=1, source_target_pairs={{0,4},{4,0},{1,5},{5,1},{2,6},{6,2},{3,7},{7,3},{8,12},{12,8},{9,1... | collective-permute-start | bytes 1179656 | tf_op jit(solution)/shard_map/ppermute | solution.py:34
  43.4 38.1 %copy-start.7 = (bf16[512,256]{1,0:T(8,128)(2,1)S(1)}, bf16[512,256]{1,0:T(8,128)(2,1)}, u32[]{:S(2)}) copy-start(bf16[512,256]{1,0:T(8,128)(2,1)} %param.15) | copy-start | bytes 786436
  43.4 122.5 %copy-start.22 = (s32[32]{0:T(128)S(1)}, s32[32]{0:T(128)}, u32[]{:S(2)}) copy-start(s32[32]{0:T(128)} %param.9) | copy-start | bytes 388
  75.8 48.2 %all-to-all-start.1 = ((bf16[32,32,512]{2,1,0:T(8,128)(2,1)}), bf16[32,32,512]{2,1,0:T(8,128)(2,1)S(1)}, u32[]{:S(2)}, u32[]{:S(2)}) async-start(bf16[32,32,512]{2,1,0:T(8,128)(2,1)} %lookup.1), calls=%async_computation.1 | async-start | bytes 2097152 | tf_op jit(solution)/shard_map/all_to_all | solution.py:524
  81.6 30.8 %collective-permute-start.7 = (bf16[512,256]{1,0:T(8,128)(2,1)S(1)}, bf16[512,256]{1,0:T(8,128)(2,1)S(1)}, u32[]{:S(2)}, u32[]{:S(2)}) collective-permute-start(bf16[512,256]{1,0:T(8,128)(2,1)S(1)} %copy-done.7), channel_id=1, source_target_pairs={{0,4},{4,0},{1,5},{5,1},{2,6},{6,2},{3,7},{7,3},{8,12},{12,8},{9,1... | collective-permute-start | bytes 786440 | tf_op jit(solution)/shard_map/ppermute | solution.py:522
  83.1 34.1 %collective-permute-start.8 = (bf16[512,256]{1,0:T(8,128)(2,1)S(1)}, bf16[512,256]{1,0:T(8,128)(2,1)S(1)}, u32[]{:S(2)}, u32[]{:S(2)}) collective-permute-start(bf16[512,256]{1,0:T(8,128)(2,1)S(1)} %copy-done.7), channel_id=1, source_target_pairs={{0,16},{16,0},{1,17},{17,1},{2,18},{18,2},{3,19},{19,3},{4,20},{20... | collective-permute-start | bytes 786440 | tf_op jit(solution)/shard_map/ppermute | solution.py:522
  83.1 34.1 %collective-permute-start.9 = (bf16[512,256]{1,0:T(8,128)(2,1)S(1)}, bf16[512,256]{1,0:T(8,128)(2,1)S(1)}, u32[]{:S(2)}, u32[]{:S(2)}) collective-permute-start(bf16[512,256]{1,0:T(8,128)(2,1)S(1)} %copy-done.7), channel_id=1, source_target_pairs={{0,20},{4,16},{16,4},{20,0},{1,21},{5,17},{17,5},{21,1},{2,22},{6,... | collective-permute-start | bytes 786440 | tf_op jit(solution)/shard_map/ppermute | solution.py:522
  117.3 30.9 %copy-start.5 = (bf16[2,512,256]{2,1,0:T(8,128)(2,1)}, bf16[2,512,256]{2,1,0:T(8,128)(2,1)S(1)}, u32[]{:S(2)}) copy-start(bf16[2,512,256]{2,1,0:T(8,128)(2,1)S(1)} %pad_maximum_fusion.1.refs_0_) | copy-start | bytes 1572868
  117.3 16.2 %collective-permute-start.10 = (bf16[2,512,256]{2,1,0:T(8,128)(2,1)S(1)}, bf16[2,512,256]{2,1,0:T(8,128)(2,1)}, u32[]{:S(2)}, u32[]{:S(2)}) collective-permute-start(bf16[2,512,256]{2,1,0:T(8,128)(2,1)S(1)} %pad_maximum_fusion.1.refs_0_), channel_id=1, source_target_pairs={{0,32},{32,64},{64,96},{96,0},{1,33},{33,65},{65,97},{97,1},{2,34}... | collective-permute-start | bytes 1572872 | tf_op jit(solution)/shard_map/ppermute | solution.py:540
  117.5 32.9 %copy-start.6 = (bf16[2,512,256]{2,1,0:T(8,128)(2,1)}, bf16[2,512,256]{2,1,0:T(8,128)(2,1)S(1)}, u32[]{:S(2)}) copy-start(bf16[2,512,256]{2,1,0:T(8,128)(2,1)S(1)} %pad_maximum_fusion.2.refs_1_) | copy-start | bytes 1572868
  117.5 16.0 %collective-permute-start.13 = (bf16[2,512,256]{2,1,0:T(8,128)(2,1)S(1)}, bf16[2,512,256]{2,1,0:T(8,128)(2,1)}, u32[]{:S(2)}, u32[]{:S(2)}) collective-permute-start(bf16[2,512,256]{2,1,0:T(8,128)(2,1)S(1)} %pad_maximum_fusion.2.refs_1_), channel_id=1, source_target_pairs={{0,96},{32,0},{64,32},{96,64},{1,97},{33,1},{65,33},{97,65},{2,98}... | collective-permute-start | bytes 1572872 | tf_op jit(solution)/shard_map/ppermute | solution.py:540
  120.8 23.9 %collective-permute-start.11 = (bf16[2,512,256]{2,1,0:T(8,128)(2,1)S(1)}, bf16[2,512,256]{2,1,0:T(8,128)(2,1)S(1)}, u32[]{:S(2)}, u32[]{:S(2)}) collective-permute-start(bf16[2,512,256]{2,1,0:T(8,128)(2,1)S(1)} %pad_maximum_fusion.2.refs_1_), channel_id=1, source_target_pairs={{0,32},{32,64},{64,96},{96,0},{1,33},{33,65},{65,97},{97,1},{2,34}... | collective-permute-start | bytes 1572872 | tf_op jit(solution)/shard_map/ppermute | solution.py:540
  120.8 25.9 %collective-permute-start.12 = (bf16[2,512,256]{2,1,0:T(8,128)(2,1)S(1)}, bf16[2,512,256]{2,1,0:T(8,128)(2,1)S(1)}, u32[]{:S(2)}, u32[]{:S(2)}) collective-permute-start(bf16[2,512,256]{2,1,0:T(8,128)(2,1)S(1)} %pad_maximum_fusion.1.refs_0_), channel_id=1, source_target_pairs={{0,96},{32,0},{64,32},{96,64},{1,97},{33,1},{65,33},{97,65},{2,98}... | collective-permute-start | bytes 1572872 | tf_op jit(solution)/shard_map/ppermute | solution.py:540
  124.0 24.2 %collective-permute-start.19 = (bf16[2,512,256]{2,1,0:T(8,128)(2,1)S(1)}, bf16[2,512,256]{2,1,0:T(8,128)(2,1)}, u32[]{:S(2)}, u32[]{:S(2)}) collective-permute-start(bf16[2,512,256]{2,1,0:T(8,128)(2,1)S(1)} %pad_maximum_fusion.1.refs_0_), channel_id=1, source_target_pairs={{0,8},{8,0},{1,9},{9,1},{2,10},{10,2},{3,11},{11,3},{4,12},{12,4},... | collective-permute-start | bytes 1572872 | tf_op jit(solution)/shard_map/ppermute | solution.py:543
  133.5 16.7 %collective-permute-start.20 = (bf16[2,512,256]{2,1,0:T(8,128)(2,1)S(1)}, bf16[2,512,256]{2,1,0:T(8,128)(2,1)S(1)}, u32[]{:S(2)}, u32[]{:S(2)}) collective-permute-start(bf16[2,512,256]{2,1,0:T(8,128)(2,1)S(1)} %pad_maximum_fusion.2.refs_1_), channel_id=1, source_target_pairs={{0,8},{8,0},{1,9},{9,1},{2,10},{10,2},{3,11},{11,3},{4,12},{12,4},... | collective-permute-start | bytes 1572872 | tf_op jit(solution)/shard_map/ppermute | solution.py:543
  133.5 21.6 %collective-permute-start.14 = (bf16[2,512,256]{2,1,0:T(8,128)(2,1)}, bf16[2,512,256]{2,1,0:T(8,128)(2,1)S(1)}, u32[]{:S(2)}, u32[]{:S(2)}) collective-permute-start(bf16[2,512,256]{2,1,0:T(8,128)(2,1)} %collective-permute-done.10.refs_2_), channel_id=1, source_target_pairs={{0,32},{32,64},{64,96},{96,0},{1,33},{33,65},{65,97},{97,1},{2,34}... | collective-permute-start | bytes 1572872 | tf_op jit(solution)/shard_map/ppermute | solution.py:540
  144.6 13.3 %collective-permute-start.15 = (bf16[2,512,256]{2,1,0:T(8,128)(2,1)}, bf16[2,512,256]{2,1,0:T(8,128)(2,1)S(1)}, u32[]{:S(2)}, u32[]{:S(2)}) collective-permute-start(bf16[2,512,256]{2,1,0:T(8,128)(2,1)} %collective-permute-done.13.refs_5_), channel_id=1, source_target_pairs={{0,96},{32,0},{64,32},{96,64},{1,97},{33,1},{65,33},{97,65},{2,98}... | collective-permute-start | bytes 1572872 | tf_op jit(solution)/shard_map/ppermute | solution.py:540
  146.7 13.2 %collective-permute-start.2 = (bf16[512,512]{1,0:T(8,128)(2,1)}, bf16[512,512]{1,0:T(8,128)(2,1)S(1)}, u32[]{:S(2)}, u32[]{:S(2)}) collective-permute-start(bf16[512,512]{1,0:T(8,128)(2,1)} %bitcast.8), channel_id=1, source_target_pairs={{0,1},{1,2},{2,3},{3,0},{4,5},{5,6},{6,7},{7,4},{8,9},{9,10},{10,1... | collective-permute-start | bytes 1572872 | tf_op jit(solution)/shard_map/ppermute | solution.py:548
  148.2 14.2 %collective-permute-start.1 = (bf16[512,512]{1,0:T(8,128)(2,1)}, bf16[512,512]{1,0:T(8,128)(2,1)S(1)}, u32[]{:S(2)}, u32[]{:S(2)}) collective-permute-start(bf16[512,512]{1,0:T(8,128)(2,1)} %bitcast.9), channel_id=1, source_target_pairs={{0,3},{1,0},{2,1},{3,2},{4,7},{5,4},{6,5},{7,6},{8,11},{9,8},{10,9... | collective-permute-start | bytes 1572872 | tf_op jit(solution)/shard_map/ppermute | solution.py:549
  150.3 15.1 %copy-start.16 = (bf16[2,512,256]{2,1,0:T(8,128)(2,1)}, bf16[2,512,256]{2,1,0:T(8,128)(2,1)S(1)}, u32[]{:S(2)}) copy-start(bf16[2,512,256]{2,1,0:T(8,128)(2,1)S(1)} %collective-permute-done.20.refs_1_) | copy-start | bytes 1572868
  150.3 23.7 %collective-permute-start.21 = (bf16[2,512,256]{2,1,0:T(8,128)(2,1)}, bf16[2,512,256]{2,1,0:T(8,128)(2,1)}, u32[]{:S(2)}, u32[]{:S(2)}) collective-permute-start(bf16[2,512,256]{2,1,0:T(8,128)(2,1)} %collective-permute-done.10.refs_2_), channel_id=1, source_target_pairs={{0,8},{8,0},{1,9},{9,1},{2,10},{10,2},{3,11},{11,3},{4,12},{12,4},... | collective-permute-start | bytes 1572872 | tf_op jit(solution)/shard_map/ppermute | solution.py:543
  155.2 7.3 %copy-start.12 = (bf16[2,512,256]{2,1,0:T(8,128)(2,1)}, bf16[2,512,256]{2,1,0:T(8,128)(2,1)S(1)}, u32[]{:S(2)}) copy-start(bf16[2,512,256]{2,1,0:T(8,128)(2,1)S(1)} %collective-permute-done.14.refs_6_) | copy-start | bytes 1572868
  155.2 18.8 %collective-permute-start = (bf16[512,512]{1,0:T(8,128)(2,1)}, bf16[512,512]{1,0:T(8,128)(2,1)S(1)}, u32[]{:S(2)}, u32[]{:S(2)}) collective-permute-start(bf16[512,512]{1,0:T(8,128)(2,1)} %bitcast.8), channel_id=1, source_target_pairs={{0,3},{1,0},{2,1},{3,2},{4,7},{5,4},{6,5},{7,6},{8,11},{9,8},{10,9... | collective-permute-start | bytes 1572872 | tf_op jit(solution)/shard_map/ppermute | solution.py:551
  157.9 7.4 %copy-start.14 = (bf16[2,512,256]{2,1,0:T(8,128)(2,1)}, bf16[2,512,256]{2,1,0:T(8,128)(2,1)S(1)}, u32[]{:S(2)}) copy-start(bf16[2,512,256]{2,1,0:T(8,128)(2,1)S(1)} %collective-permute-done.15.refs_7_) | copy-start | bytes 1572868
  157.9 16.5 %collective-permute-start.5 = (bf16[512,512]{1,0:T(8,128)(2,1)}, bf16[512,512]{1,0:T(8,128)(2,1)S(1)}, u32[]{:S(2)}, u32[]{:S(2)}) collective-permute-start(bf16[512,512]{1,0:T(8,128)(2,1)} %bitcast.9), channel_id=1, source_target_pairs={{0,1},{1,2},{2,3},{3,0},{4,5},{5,6},{6,7},{7,4},{8,9},{9,10},{10,1... | collective-permute-start | bytes 1572872 | tf_op jit(solution)/shard_map/ppermute | solution.py:550
  159.8 23.8 %collective-permute-start.3 = (bf16[512,512]{1,0:T(8,128)(2,1)S(1)}, bf16[512,512]{1,0:T(8,128)(2,1)}, u32[]{:S(2)}, u32[]{:S(2)}) collective-permute-start(bf16[512,512]{1,0:T(8,128)(2,1)S(1)} %collective-permute-done.2.refs_0_.refs_5_), channel_id=1, source_target_pairs={{0,1},{1,2},{2,3},{3,0},{4,5},{5,6},{6,7},{7,4},{8,9},{9,10},{10,1... | collective-permute-start | bytes 1572872 | tf_op jit(solution)/shard_map/ppermute | solution.py:552
  162.5 21.7 %copy-start = (bf16[512,512]{1,0:T(8,128)(2,1)}, bf16[512,512]{1,0:T(8,128)(2,1)S(1)}, u32[]{:S(2)}) copy-start(bf16[512,512]{1,0:T(8,128)(2,1)S(1)} %collective-permute-done.1.refs_3_.refs_2_) | copy-start | bytes 1572868
  162.5 21.2 %collective-permute-start.4 = (bf16[512,512]{1,0:T(8,128)(2,1)S(1)}, bf16[512,512]{1,0:T(8,128)(2,1)}, u32[]{:S(2)}, u32[]{:S(2)}) collective-permute-start(bf16[512,512]{1,0:T(8,128)(2,1)S(1)} %collective-permute-done.1.refs_3_.refs_2_), channel_id=1, source_target_pairs={{0,3},{1,0},{2,1},{3,2},{4,7},{5,4},{6,5},{7,6},{8,11},{9,8},{10,9... | collective-permute-start | bytes 1572872 | tf_op jit(solution)/shard_map/ppermute | solution.py:553
  168.5 5.4 %copy-start.9 = (bf16[2,512,256]{2,1,0:T(8,128)(2,1)S(1)}, bf16[2,512,256]{2,1,0:T(8,128)(2,1)}, u32[]{:S(2)}) copy-start(bf16[2,512,256]{2,1,0:T(8,128)(2,1)} %copy-done.8) | copy-start | bytes 1572868
  168.6 5.9 %copy-start.11 = (bf16[2,512,256]{2,1,0:T(8,128)(2,1)S(1)}, bf16[2,512,256]{2,1,0:T(8,128)(2,1)}, u32[]{:S(2)}) copy-start(bf16[2,512,256]{2,1,0:T(8,128)(2,1)} %copy-done.10) | copy-start | bytes 1572868
  168.6 15.1 %copy-start.13 = (bf16[2,512,256]{2,1,0:T(8,128)(2,1)S(1)}, bf16[2,512,256]{2,1,0:T(8,128)(2,1)}, u32[]{:S(2)}) copy-start(bf16[2,512,256]{2,1,0:T(8,128)(2,1)} %copy-done.12) | copy-start | bytes 1572868
  168.6 15.1 %copy-start.15 = (bf16[2,512,256]{2,1,0:T(8,128)(2,1)S(1)}, bf16[2,512,256]{2,1,0:T(8,128)(2,1)}, u32[]{:S(2)}) copy-start(bf16[2,512,256]{2,1,0:T(8,128)(2,1)} %copy-done.14) | copy-start | bytes 1572868
  173.9 29.7 %collective-permute-start.24 = (bf16[2,512,256]{2,1,0:T(8,128)(2,1)}, bf16[2,512,256]{2,1,0:T(8,128)(2,1)S(1)}, u32[]{:S(2)}, u32[]{:S(2)}) collective-permute-start(bf16[2,512,256]{2,1,0:T(8,128)(2,1)} %collective-permute-done.13.refs_5_), channel_id=1, source_target_pairs={{0,8},{8,0},{1,9},{9,1},{2,10},{10,2},{3,11},{11,3},{4,12},{12,4},... | collective-permute-start | bytes 1572872 | tf_op jit(solution)/shard_map/ppermute | solution.py:543
  174.0 29.7 %collective-permute-start.22 = (bf16[2,512,256]{2,1,0:T(8,128)(2,1)S(1)}, bf16[2,512,256]{2,1,0:T(8,128)(2,1)S(1)}, u32[]{:S(2)}, u32[]{:S(2)}) collective-permute-start(bf16[2,512,256]{2,1,0:T(8,128)(2,1)S(1)} %copy-done.9), channel_id=1, source_target_pairs={{0,8},{8,0},{1,9},{9,1},{2,10},{10,2},{3,11},{11,3},{4,12},{12,4},... | collective-permute-start | bytes 1572872 | tf_op jit(solution)/shard_map/ppermute | solution.py:543
  174.5 29.2 %collective-permute-start.23 = (bf16[2,512,256]{2,1,0:T(8,128)(2,1)S(1)}, bf16[2,512,256]{2,1,0:T(8,128)(2,1)S(1)}, u32[]{:S(2)}, u32[]{:S(2)}) collective-permute-start(bf16[2,512,256]{2,1,0:T(8,128)(2,1)S(1)} %copy-done.11), channel_id=1, source_target_pairs={{0,8},{8,0},{1,9},{9,1},{2,10},{10,2},{3,11},{11,3},{4,12},{12,4},... | collective-permute-start | bytes 1572872 | tf_op jit(solution)/shard_map/ppermute | solution.py:543
  183.6 20.1 %collective-permute-start.25 = (bf16[2,512,256]{2,1,0:T(8,128)(2,1)S(1)}, bf16[2,512,256]{2,1,0:T(8,128)(2,1)S(1)}, u32[]{:S(2)}, u32[]{:S(2)}) collective-permute-start(bf16[2,512,256]{2,1,0:T(8,128)(2,1)S(1)} %copy-done.13), channel_id=1, source_target_pairs={{0,8},{8,0},{1,9},{9,1},{2,10},{10,2},{3,11},{11,3},{4,12},{12,4},... | collective-permute-start | bytes 1572872 | tf_op jit(solution)/shard_map/ppermute | solution.py:543
  183.6 20.1 %collective-permute-start.26 = (bf16[2,512,256]{2,1,0:T(8,128)(2,1)S(1)}, bf16[2,512,256]{2,1,0:T(8,128)(2,1)S(1)}, u32[]{:S(2)}, u32[]{:S(2)}) collective-permute-start(bf16[2,512,256]{2,1,0:T(8,128)(2,1)S(1)} %copy-done.15), channel_id=1, source_target_pairs={{0,8},{8,0},{1,9},{9,1},{2,10},{10,2},{3,11},{11,3},{4,12},{12,4},... | collective-permute-start | bytes 1572872 | tf_op jit(solution)/shard_map/ppermute | solution.py:543
  184.1 8.1 %copy-start.2 = (f32[512,128]{1,0:T(8,128)S(1)}, f32[512,128]{1,0:T(8,128)}, u32[]{:S(2)}) copy-start(f32[512,128]{1,0:T(8,128)} %get-tuple-element.60.refs_7_) | copy-start | bytes 786436
  205.7 33.1 %copy-start.1 = (bf16[512,512]{1,0:T(8,128)(2,1)S(1)}, bf16[512,512]{1,0:T(8,128)(2,1)}, u32[]{:S(2)}) copy-start(bf16[512,512]{1,0:T(8,128)(2,1)} %copy-done) | copy-start | bytes 1572868
  212.4 46.8 %copy-start.3 = (bf16[128,2048]{1,0:T(8,128)(2,1)S(1)}, bf16[128,2048]{1,0:T(8,128)(2,1)}, u32[]{:S(2)}) copy-start(bf16[128,2048]{1,0:T(8,128)(2,1)} %get-tuple-element.47.refs_3_) | copy-start | bytes 1572868
  212.4 15.4 %collective-permute-start.28 = (bf16[128,2048]{1,0:T(8,128)(2,1)}, bf16[128,2048]{1,0:T(8,128)(2,1)}, u32[]{:S(2)}, u32[]{:S(2)}) collective-permute-start(bf16[128,2048]{1,0:T(8,128)(2,1)} %get-tuple-element.50), channel_id=1, source_target_pairs={{0,3},{1,0},{2,1},{3,2},{4,7},{5,4},{6,5},{7,6},{8,11},{9,8},{10,9... | collective-permute-start | bytes 1572872 | tf_op jit(solution)/shard_map/ppermute | solution.py:479
  221.1 38.0 %copy-start.4 = (bf16[128,2048]{1,0:T(8,128)(2,1)S(1)}, bf16[128,2048]{1,0:T(8,128)(2,1)}, u32[]{:S(2)}) copy-start(bf16[128,2048]{1,0:T(8,128)(2,1)} %get-tuple-element.43.refs_0_) | copy-start | bytes 1572868
  221.2 16.3 %collective-permute-start.17 = (bf16[128,2048]{1,0:T(8,128)(2,1)}, bf16[128,2048]{1,0:T(8,128)(2,1)S(1)}, u32[]{:S(2)}, u32[]{:S(2)}) collective-permute-start(bf16[128,2048]{1,0:T(8,128)(2,1)} %get-tuple-element.46), channel_id=1, source_target_pairs={{0,1},{1,2},{2,3},{3,0},{4,5},{5,6},{6,7},{7,4},{8,9},{9,10},{10,1... | collective-permute-start | bytes 1572872 | tf_op jit(solution)/shard_map/ppermute | solution.py:479
  221.5 27.2 %collective-permute-start.27 = (bf16[128,2048]{1,0:T(8,128)(2,1)}, bf16[128,2048]{1,0:T(8,128)(2,1)S(1)}, u32[]{:S(2)}, u32[]{:S(2)}) collective-permute-start(bf16[128,2048]{1,0:T(8,128)(2,1)} %get-tuple-element.48), channel_id=1, source_target_pairs={{0,1},{1,2},{2,3},{3,0},{4,5},{5,6},{6,7},{7,4},{8,9},{9,10},{10,1... | collective-permute-start | bytes 1572872 | tf_op jit(solution)/shard_map/ppermute | solution.py:480
  221.6 27.1 %collective-permute-start.16 = (bf16[128,2048]{1,0:T(8,128)(2,1)}, bf16[128,2048]{1,0:T(8,128)(2,1)S(1)}, u32[]{:S(2)}, u32[]{:S(2)}) collective-permute-start(bf16[128,2048]{1,0:T(8,128)(2,1)} %get-tuple-element.44), channel_id=1, source_target_pairs={{0,3},{1,0},{2,1},{3,2},{4,7},{5,4},{6,5},{7,6},{8,11},{9,8},{10,9... | collective-permute-start | bytes 1572872 | tf_op jit(solution)/shard_map/ppermute | solution.py:480
  229.2 20.2 %collective-permute-start.29 = (bf16[128,2048]{1,0:T(8,128)(2,1)S(1)}, bf16[128,2048]{1,0:T(8,128)(2,1)S(1)}, u32[]{:S(2)}, u32[]{:S(2)}) collective-permute-start(bf16[128,2048]{1,0:T(8,128)(2,1)S(1)} %add_convert_fusion), channel_id=1, source_target_pairs={{0,3},{1,0},{2,1},{3,2},{4,7},{5,4},{6,5},{7,6},{8,11},{9,8},{10,9... | collective-permute-start | bytes 1572872 | tf_op jit(solution)/shard_map/ppermute | solution.py:486
  238.6 20.5 %collective-permute-start.18 = (bf16[128,2048]{1,0:T(8,128)(2,1)S(1)}, bf16[128,2048]{1,0:T(8,128)(2,1)S(1)}, u32[]{:S(2)}, u32[]{:S(2)}) collective-permute-start(bf16[128,2048]{1,0:T(8,128)(2,1)S(1)} %add_convert_fusion.1), channel_id=1, source_target_pairs={{0,1},{1,2},{2,3},{3,0},{4,5},{5,6},{6,7},{7,4},{8,9},{9,10},{10,1... | collective-permute-start | bytes 1572872 | tf_op jit(solution)/shard_map/ppermute | solution.py:486
  (7 other events, 9.5 us)
Sparse Core Ops, SparseCore 0:
  22.8 85.9 all-gather.1

commit v8 on v7

--- a/solution.py
+++ b/solution.py
@@ -13,11 +13,11 @@
 KVH = 8
 HD = 128
 TPG = 4
-TENSOR = ("tensor_0", "tensor_1")
-DP_TENSOR = ("dp_0", "dp_1", "dp_2", "tensor_0", "tensor_1")
-DP = ("dp_0", "dp_1", "dp_2")
-RING = "tensor_1"
-PLANE = ("dp_0", "dp_1", "dp_2", "tensor_0")
+AXES = DP_TENSOR = ("dp_0", "dp_1", "dp_2", "tensor_0", "tensor_1")
+CHIP_Z, CHIP_X, CORE, FAR_X, RING = AXES
+TENSOR = (FAR_X, RING)
+DP = (CHIP_Z, CHIP_X, CORE)
+PLANE = (CHIP_Z, CHIP_X, CORE, FAR_X)
 LANES = 128
 
 norm_eps = 1e-05
@@ -146,7 +146,6 @@
         cost_estimate=pl.CostEstimate(
             flops=30_000_000_000, bytes_accessed=embed_table.size * 2, transcendentals=0
         ),
-        name="lookup",
     )(slots, lanes, embed_table)
 
 
@@ -216,7 +215,6 @@
             bytes_accessed=2 * depth * (blocks * width + row_count),
             transcendentals=0,
         ),
-        name="project",
     )(places, *operands)
 
 
@@ -362,7 +360,6 @@
         cost_estimate=pl.CostEstimate(
             flops=1_000_000_000, bytes_accessed=4 * depth * quarter, transcendentals=0
         ),
-        name="residual",
     )(places, *flat)
 
 
@@ -431,7 +428,6 @@
             bytes_accessed=2 * (rows.size + halves * depth * width * count),
             transcendentals=0,
         ),
-        name="product",
     )(where, rows, *weights)
 
 
@@ -464,12 +460,11 @@
         cost_estimate=pl.CostEstimate(
             flops=4 * rows.size, bytes_accessed=8 * rows.size, transcendentals=0
         ),
-        name="finish",
     )(where, rows, *sums)
 
 
 def ring_sums(attended, w_mine, w_other):
-    where = jnp.stack([lax.axis_index(RING), lax.axis_index("tensor_0")])
+    where = jnp.stack([lax.axis_index(RING), lax.axis_index(FAR_X)])
     order = [(z, side) for z in LAYERS for side in range(2)]
     own, first, onward = [], [], []
     for way, weights in ((1, w_mine), (-1, w_other)):
@@ -496,7 +491,7 @@
     group_count = devices // TPG
     place = lax.axis_index(RING)
     ring = lax.axis_size(RING)
-    group_index = lax.axis_index(DP) * lax.axis_size("tensor_0") + lax.axis_index("tensor_0")
+    group_index = lax.axis_index(DP) * lax.axis_size(FAR_X) + lax.axis_index(FAR_X)
     length = lax.dynamic_slice_in_dim(prompt_lengths, group_index, 1, 0)
     cosine, sine = rope_tables(row_count)
 
@@ -515,9 +510,9 @@
     ).reshape(-1)
     pieces_x = [w_out]
     for axes, route in (
-        ("tensor_0", [(0, 1), (1, 0)]),
-        ("dp_1", [(0, 1), (1, 0)]),
-        (("dp_1", "tensor_0"), [(0, 3), (1, 2), (2, 1), (3, 0)]),
+        (FAR_X, [(0, 1), (1, 0)]),
+        (CHIP_X, [(0, 1), (1, 0)]),
+        ((CHIP_X, FAR_X), [(0, 3), (1, 2), (2, 1), (3, 0)]),
     ):
         pieces_x.append(lax.ppermute(w_out, axes, route))
     outgoing = lookup(embed_table, all_ids, group_count)
@@ -526,7 +521,7 @@
     )
     pieces_x, _ = lax.optimization_barrier((pieces_x, outgoing))
     w_mine = {(0, side): jnp.stack(pieces_x[2 * side : 2 * side + 2]) for side in range(2)}
-    layers = lax.axis_size("dp_0")
+    layers = lax.axis_size(CHIP_Z)
     ahead = [(z, (z + 1) % layers) for z in range(layers)]
     back = [(z, (z - 1) % layers) for z in range(layers)]
     for z, side, before, route in (
@@ -537,10 +532,10 @@
         (2, 0, 1, ahead),
         (2, 1, 3, back),
     ):
-        w_mine[z, side] = lax.ppermute(w_mine[before, side], "dp_0", route)
+        w_mine[z, side] = lax.ppermute(w_mine[before, side], CHIP_Z, route)
     w_other = {}
     for z, side in w_mine:
-        w_other[z, side] = lax.ppermute(w_mine[z, side], "dp_2", [(0, 1), (1, 0)])
+        w_other[z, side] = lax.ppermute(w_mine[z, side], CORE, [(0, 1), (1, 0)])
 
     places = (place + jnp.arange(ring, dtype=jnp.int32)) % ring
     half = own.shape[0] // 2
@@ -587,7 +582,7 @@
 
 def solution(mesh):
     split = Mesh(
-        mesh.devices.reshape(4, 2, 2, 2, 4), ("dp_0", "dp_1", "dp_2", "tensor_0", "tensor_1")
+        mesh.devices.reshape(4, 2, 2, 2, 4), AXES
     )
     placed = (
         P(DP_TENSOR),

time: 270 us -> 270 us (level)
  no operation moved by 1% of the time
where the time goes in v8:
time: 270 us; the launch traced here: 268 us
  waiting for transfers between devices  104 us (39%)
  Pallas kernels  74.8 us (28%)
  starting transfers between devices  42.2 us (16%)
  blocking collectives  18.7 us (7%)
  between operations  14.4 us (5%)
  other arithmetic  8.79 us (3%)
  local copies, waits for them, and re-layouts  5.25 us (2%)
    pallas_call x1, Pallas kernels, lookup(): pl.pallas_call(lookup_kernel, out_shape=jax.ShapeDtypeStruct((group_count...  32.4 us
    ppermute x3, waiting for transfers between devices, sublayer(): pieces_x.append(lax.ppermute(w_out, axes, route))  31.5 us
    ppermute x6, waiting for transfers between devices, sublayer(): w_mine[z, side] = lax.ppermute(w_mine[before, side], CHIP_Z, route)  22.8 us
    all_to_all x1, blocking collectives, sublayer(): lax.all_to_all(jnp.broadcast_to(prompt_ids[None], (devices, quarter)), DP...  18.7 us
    pallas_call x2, Pallas kernels, project(): pl.pallas_call(functools.partial(project_kernel, parts=len(parts), carrie...  13.5 us
    pallas_call x2, Pallas kernels, product(): pl.pallas_call(functools.partial(product_kernel, turns=turns, chunks=chun...  13.3 us
    pallas_call x1, Pallas kernels, attend(): pl.pallas_call(functools.partial(attention_kernel, parts=len(parts), mode...  11.4 us
    ppermute x1, waiting for transfers between devices, swapped(): return lax.ppermute(block, axis, route)  11 us
  transfers between devices with their start and end apart: 32, of which 14 were waited for; matrix products, arithmetic and copies ran while one was open for 3% of the time, Pallas kernels for 25%

profile of v8, /device:TPU:6, one launch (start us, length us, event | category | flops | bytes accessed | tf_op | source)
XLA Modules:
  0.0 268.2 jit_solution(740123070260832513)
XLA Ops:
  7.2 0.8 dynamic_slice.7
  8.0 1.2 multiply_convert_fusion
  9.2 1.5 collective-permute-start.6
  10.6 11.0 %collective-permute-done.6 = bf16[1,256,768]{2,1,0:T(8,128)(2,1)S(1)} collective-permute-done((bf16[1,256,768]{2,1,0:T(8,128)(2,1)S(1)}, bf16[1,256,768]{2,1,0:T(8,128)(2,1)S(1)}, u32[]{:S(2)}, u32[]{:S(2)}) %collective-permute-start.6) | collective-permute-done | bytes 393248 | tf_op jit(solution)/shard_map/ppermute | solution.py:34
  21.6 1.0 pad_maximum_fusion
  23.3 18.7 %all_to_all.11 = s32[128,1,128]{2,1,0:T(1,128)S(1)} all-to-all(s32[128,1,128]{2,1,0:T(1,128)S(1)} %broadcast_in_dim.4), channel_id=1, replica_groups=mesh['dp_0'=4,'dp_1'=2,'dp_2'=2,'tensor_0'=2,'tensor_1'=4] {'dp_0','dp_1..., dimensions={0} | all-to-all | bytes 131072 | tf_op jit(solution)/shard_map/all_to_all | solution.py:504
  43.4 32.4 %shard_map.95 = bf16[32,32,512]{2,1,0:T(8,128)(2,1)} custom-call(s32[16384]{0:T(1024)} %fusion.2.slots_ref, s32[128,128]{1,0:T(8,128)} %bitcast_or_fusion.lanes_ref, bf16[32,128256]{1,0:T(8,128)(2,1)} %table_ref.1), custom_call_target="tpu_custom_call" | custom-call | flops 30000001024 | bytes 8208384 | tf_op jit(solution)/shard_map/pallas_call | solution.py:131
  75.8 5.8 %all-to-all-start.1 = ((bf16[32,32,512]{2,1,0:T(8,128)(2,1)}), bf16[32,32,512]{2,1,0:T(8,128)(2,1)S(1)}, u32[]{:S(2)}, u32[]{:S(2)}) async-start(bf16[32,32,512]{2,1,0:T(8,128)(2,1)} %shard_map.95), calls=%async_computation.1 | async-start | bytes 2097152 | tf_op jit(solution)/shard_map/all_to_all | solution.py:519
  81.6 1.5 collective-permute-start.7
  83.1 2.6 collective-permute-start.9
  85.8 26.6 %collective-permute-done.7 = bf16[512,256]{1,0:T(8,128)(2,1)S(1)} collective-permute-done((bf16[512,256]{1,0:T(8,128)(2,1)S(1)}, bf16[512,256]{1,0:T(8,128)(2,1)S(1)}, u32[]{:S(2)}, u32[]{:S(2)}) %collective-permute-start.7) | collective-permute-done | bytes 262176 | tf_op jit(solution)/shard_map/ppermute | solution.py:517
  112.4 4.9 %collective-permute-done.8 = bf16[512,256]{1,0:T(8,128)(2,1)S(1)} collective-permute-done((bf16[512,256]{1,0:T(8,128)(2,1)S(1)}, bf16[512,256]{1,0:T(8,128)(2,1)S(1)}, u32[]{:S(2)}, u32[]{:S(2)}) %collective-permute-start.8) | collective-permute-done | bytes 262176 | tf_op jit(solution)/shard_map/ppermute | solution.py:517
  117.5 3.3 %collective-permute-start.13 = (bf16[2,512,256]{2,1,0:T(8,128)(2,1)S(1)}, bf16[2,512,256]{2,1,0:T(8,128)(2,1)}, u32[]{:S(2)}, u32[]{:S(2)}) collective-permute-start(bf16[2,512,256]{2,1,0:T(8,128)(2,1)S(1)} %pad_maximum_fusion.2.refs_1_), channel_id=1, source_target_pairs={{0,96},{32,0},{64,32},{96,64},{1,97},{33,1},{65,33},{97,65},{2,98}... | collective-permute-start | bytes 1572872 | tf_op jit(solution)/shard_map/ppermute | solution.py:535
  120.8 3.2 %collective-permute-start.12 = (bf16[2,512,256]{2,1,0:T(8,128)(2,1)S(1)}, bf16[2,512,256]{2,1,0:T(8,128)(2,1)S(1)}, u32[]{:S(2)}, u32[]{:S(2)}) collective-permute-start(bf16[2,512,256]{2,1,0:T(8,128)(2,1)S(1)} %pad_maximum_fusion.1.refs_0_), channel_id=1, source_target_pairs={{0,96},{32,0},{64,32},{96,64},{1,97},{33,1},{65,33},{97,65},{2,98}... | collective-permute-start | bytes 1572872 | tf_op jit(solution)/shard_map/ppermute | solution.py:535
  124.0 1.1 fusion.4
  125.1 8.4 %collective-permute-done.10.refs_2_ = bf16[2,512,256]{2,1,0:T(8,128)(2,1)} collective-permute-done((bf16[2,512,256]{2,1,0:T(8,128)(2,1)S(1)}, bf16[2,512,256]{2,1,0:T(8,128)(2,1)}, u32[]{:S(2)}, u32[]{:S(2)}) %collective-permute-start.10) | collective-permute-done | bytes 524320 | tf_op jit(solution)/shard_map/ppermute | solution.py:535
  133.5 1.5 collective-permute-start.14
  135.1 9.6 %collective-permute-done.11.refs_3_ = bf16[2,512,256]{2,1,0:T(8,128)(2,1)S(1)} collective-permute-done((bf16[2,512,256]{2,1,0:T(8,128)(2,1)S(1)}, bf16[2,512,256]{2,1,0:T(8,128)(2,1)S(1)}, u32[]{:S(2)}, u32[]{:S(2)}) %collective-permute-start.11) | collective-permute-done | bytes 524320 | tf_op jit(solution)/shard_map/ppermute | solution.py:535
  144.6 2.0 collective-permute-start.15
  146.7 1.6 collective-permute-start.2
  148.2 2.0 collective-permute-start.1
  150.4 4.8 %collective-permute-done.14.refs_6_ = bf16[2,512,256]{2,1,0:T(8,128)(2,1)S(1)} collective-permute-done((bf16[2,512,256]{2,1,0:T(8,128)(2,1)}, bf16[2,512,256]{2,1,0:T(8,128)(2,1)S(1)}, u32[]{:S(2)}, u32[]{:S(2)}) %collective-permute-start.14) | collective-permute-done | bytes 524320 | tf_op jit(solution)/shard_map/ppermute | solution.py:535
  155.2 2.8 %collective-permute-start = (bf16[512,512]{1,0:T(8,128)(2,1)}, bf16[512,512]{1,0:T(8,128)(2,1)S(1)}, u32[]{:S(2)}, u32[]{:S(2)}) collective-permute-start(bf16[512,512]{1,0:T(8,128)(2,1)} %bitcast.8), channel_id=1, source_target_pairs={{0,3},{1,0},{2,1},{3,2},{4,7},{5,4},{6,5},{7,6},{8,11},{9,8},{10,9... | collective-permute-start | bytes 1572872 | tf_op jit(solution)/shard_map/ppermute | solution.py:546
  157.9 0.9 collective-permute-start.5
  158.9 1.0 collective-permute-done.2.refs_0_.refs_5_
  160.4 2.1 collective-permute-done.1.refs_3_.refs_2_
  162.5 2.9 %collective-permute-start.4 = (bf16[512,512]{1,0:T(8,128)(2,1)S(1)}, bf16[512,512]{1,0:T(8,128)(2,1)}, u32[]{:S(2)}, u32[]{:S(2)}) collective-permute-start(bf16[512,512]{1,0:T(8,128)(2,1)S(1)} %collective-permute-done.1.refs_3_.refs_2_), channel_id=1, source_target_pairs={{0,3},{1,0},{2,1},{3,2},{4,7},{5,4},{6,5},{7,6},{8,11},{9,8},{10,9... | collective-permute-start | bytes 1572872 | tf_op jit(solution)/shard_map/ppermute | solution.py:548
  166.6 1.0 fusion
  167.6 0.9 pad_maximum_fusion.3
  168.6 5.4 %shard_map.96 = (f32[512,1536]{1,0:T(8,128)}, f32[1,512]{1,0:T(1,128)S(1)}) custom-call(s32[4]{0:T(128)S(1)} %and_select_fusion.places_ref, bf16[1024,512]{1,0:T(8,128)(2,1)S(1)} %bitcast.27, bf16[2,32,4,32,768]{4,3,2,1,0:T(8,128)(2,1)} %bitcast.29), custom_call_target="tpu_custom_call" | custom-call | flops 1610612736 | bytes 4194304 | tf_op jit(solution)/shard_map/pallas_call | solution.py:200
  174.6 9.0 %collective-permute-done.3.refs_0_.refs_3_ = bf16[512,512]{1,0:T(8,128)(2,1)} collective-permute-done((bf16[512,512]{1,0:T(8,128)(2,1)S(1)}, bf16[512,512]{1,0:T(8,128)(2,1)}, u32[]{:S(2)}, u32[]{:S(2)}) %collective-permute-start.3) | collective-permute-done | bytes 524320 | tf_op jit(solution)/shard_map/ppermute | solution.py:547
  184.1 8.1 %shard_map.97 = (f32[512,1536]{1,0:T(8,128)}, f32[1,512]{1,0:T(1,128)S(1)}) custom-call(s32[4]{0:T(128)S(1)} %and_select_fusion.places_ref, bf16[512,512]{1,0:T(8,128)(2,1)S(1)} %collective-permute-done.2.refs_0_.refs_5_, bf16[512,512]{1,0:T(8,128)(2,1)S(1)} %collective-permute-done.5.refs_1_.refs_6_, ...), custom_call_target="tpu_custom_call" | custom-call | flops 3221225472 | bytes 8388608 | tf_op jit(solution)/shard_map/pallas_call | solution.py:200
  192.3 11.4 %attend.1 = (bf16[512,1024]{1,0:T(8,128)(2,1)}, bf16[2,512,256]{2,1,0:T(8,128)(2,1)}) custom-call(s32[4]{0:T(128)S(1)} %and_select_fusion.places_ref, s32[1]{0:T(128)} %dynamic_slice.6.length_ref, bf16[512,512]{1,0:T(8,128)(2,1)} %collective-permute-done.3.refs_0_.refs_3_, bf16[512,512]{1,0:T(8,128)(2,1)} %collective-permute-done.4.refs_1_.refs_4_, ...), custom_call_target="tpu_custom_call" | custom-call | flops 4000000000 | bytes 9000000 | tf_op jit(solution)/shard_map/attend/pallas_call | solution.py:282
  203.7 0.8 copy-done.18
  204.9 0.8 copy-done.21
  205.7 6.7 %shard_map.100 = (bf16[128,2048]{1,0:T(8,128)(2,1)}, bf16[128,2048]{1,0:T(8,128)(2,1)}, bf16[128,2048]{1,0:T(8,128)(2,1)}, bf16[128,2048]{1,0:T(8,128)(2,1)}) custom-call(s32[2]{0:T(128)} %pad_add_fusion.1.where_ref, bf16[512,1024]{1,0:T(8,128)(2,1)} %get-tuple-element.31.rows_ref, bf16[2,512,256]{2,1,0:T(8,128)(2,1)} %collective-permute-done.19.refs_0_, ...), custom_call_target="tpu_custom_call" | custom-call | flops 2147483648 | bytes 5242880 | tf_op jit(solution)/shard_map/pallas_call | solution.py:411
  212.4 2.1 collective-permute-start.28
  214.5 6.7 %shard_map.99 = (bf16[128,2048]{1,0:T(8,128)(2,1)}, bf16[128,2048]{1,0:T(8,128)(2,1)}, bf16[128,2048]{1,0:T(8,128)(2,1)}, bf16[128,2048]{1,0:T(8,128)(2,1)}) custom-call(s32[2]{0:T(128)} %pad_add_fusion.1.where_ref, bf16[512,1024]{1,0:T(8,128)(2,1)} %get-tuple-element.31.rows_ref, bf16[2,512,256]{2,1,0:T(8,128)(2,1)} %copy-done.5, ...), custom_call_target="tpu_custom_call" | custom-call | flops 2147483648 | bytes 5242880 | tf_op jit(solution)/shard_map/pallas_call | solution.py:411
  221.6 3.2 %collective-permute-start.16 = (bf16[128,2048]{1,0:T(8,128)(2,1)}, bf16[128,2048]{1,0:T(8,128)(2,1)S(1)}, u32[]{:S(2)}, u32[]{:S(2)}) collective-permute-start(bf16[128,2048]{1,0:T(8,128)(2,1)} %get-tuple-element.44), channel_id=1, source_target_pairs={{0,3},{1,0},{2,1},{3,2},{4,7},{5,4},{6,5},{7,6},{8,11},{9,8},{10,9... | collective-permute-start | bytes 1572872 | tf_op jit(solution)/shard_map/ppermute | solution.py:475
  224.7 3.1 %collective-permute-done.28 = bf16[128,2048]{1,0:T(8,128)(2,1)} collective-permute-done((bf16[128,2048]{1,0:T(8,128)(2,1)}, bf16[128,2048]{1,0:T(8,128)(2,1)}, u32[]{:S(2)}, u32[]{:S(2)}) %collective-permute-start.28) | collective-permute-done | bytes 524320 | tf_op jit(solution)/shard_map/ppermute | solution.py:474
  227.8 1.3 add_convert_fusion
  229.2 3.1 %collective-permute-start.29 = (bf16[128,2048]{1,0:T(8,128)(2,1)S(1)}, bf16[128,2048]{1,0:T(8,128)(2,1)S(1)}, u32[]{:S(2)}, u32[]{:S(2)}) collective-permute-start(bf16[128,2048]{1,0:T(8,128)(2,1)S(1)} %add_convert_fusion), channel_id=1, source_target_pairs={{0,3},{1,0},{2,1},{3,2},{4,7},{5,4},{6,5},{7,6},{8,11},{9,8},{10,9... | collective-permute-start | bytes 1572872 | tf_op jit(solution)/shard_map/ppermute | solution.py:481
  232.2 5.2 %collective-permute-done.17 = bf16[128,2048]{1,0:T(8,128)(2,1)S(1)} collective-permute-done((bf16[128,2048]{1,0:T(8,128)(2,1)}, bf16[128,2048]{1,0:T(8,128)(2,1)S(1)}, u32[]{:S(2)}, u32[]{:S(2)}) %collective-permute-start.17) | collective-permute-done | bytes 524320 | tf_op jit(solution)/shard_map/ppermute | solution.py:474
  237.4 1.2 add_convert_fusion.1
  238.8 2.0 shard_map.98.rows_ref
  240.8 7.9 %collective-permute-done.27.refs_4_ = bf16[128,2048]{1,0:T(8,128)(2,1)S(1)} collective-permute-done((bf16[128,2048]{1,0:T(8,128)(2,1)}, bf16[128,2048]{1,0:T(8,128)(2,1)S(1)}, u32[]{:S(2)}, u32[]{:S(2)}) %collective-permute-start.27) | collective-permute-done | bytes 524320 | tf_op jit(solution)/shard_map/ppermute | solution.py:475
  249.3 9.8 %collective-permute-done.18.refs_2_ = bf16[128,2048]{1,0:T(8,128)(2,1)S(1)} collective-permute-done((bf16[128,2048]{1,0:T(8,128)(2,1)S(1)}, bf16[128,2048]{1,0:T(8,128)(2,1)S(1)}, u32[]{:S(2)}, u32[]{:S(2)}) %collective-permute-start.18) | collective-permute-done | bytes 524320 | tf_op jit(solution)/shard_map/ppermute | solution.py:481
  259.2 2.2 shard_map.101
  (93 shorter events, 7.1 us)
Async XLA Ops:
  7.2 161.4 %all-gather.2.cloned.1.call-start = ((), (), s32[]{:S(2)}) async-start(), calls=%async_computation.2 | async-start | bytes 13369344 | tf_op jit(solution)/shard_map/all_gather | solution.py:502
  9.2 12.4 %collective-permute-start.6 = (bf16[1,256,768]{2,1,0:T(8,128)(2,1)S(1)}, bf16[1,256,768]{2,1,0:T(8,128)(2,1)S(1)}, u32[]{:S(2)}, u32[]{:S(2)}) collective-permute-start(bf16[1,256,768]{2,1,0:T(8,128)(2,1)S(1)} %multiply_convert_fusion), channel_id=1, source_target_pairs={{0,4},{4,0},{1,5},{5,1},{2,6},{6,2},{3,7},{7,3},{8,12},{12,8},{9,1... | collective-permute-start | bytes 1179656 | tf_op jit(solution)/shard_map/ppermute | solution.py:34
  43.4 38.1 %copy-start.7 = (bf16[512,256]{1,0:T(8,128)(2,1)S(1)}, bf16[512,256]{1,0:T(8,128)(2,1)}, u32[]{:S(2)}) copy-start(bf16[512,256]{1,0:T(8,128)(2,1)} %param.15) | copy-start | bytes 786436
  43.4 122.5 %copy-start.22 = (s32[32]{0:T(128)S(1)}, s32[32]{0:T(128)}, u32[]{:S(2)}) copy-start(s32[32]{0:T(128)} %param.9) | copy-start | bytes 388
  75.8 48.2 %all-to-all-start.1 = ((bf16[32,32,512]{2,1,0:T(8,128)(2,1)}), bf16[32,32,512]{2,1,0:T(8,128)(2,1)S(1)}, u32[]{:S(2)}, u32[]{:S(2)}) async-start(bf16[32,32,512]{2,1,0:T(8,128)(2,1)} %shard_map.95), calls=%async_computation.1 | async-start | bytes 2097152 | tf_op jit(solution)/shard_map/all_to_all | solution.py:519
  81.6 30.8 %collective-permute-start.7 = (bf16[512,256]{1,0:T(8,128)(2,1)S(1)}, bf16[512,256]{1,0:T(8,128)(2,1)S(1)}, u32[]{:S(2)}, u32[]{:S(2)}) collective-permute-start(bf16[512,256]{1,0:T(8,128)(2,1)S(1)} %copy-done.7), channel_id=1, source_target_pairs={{0,4},{4,0},{1,5},{5,1},{2,6},{6,2},{3,7},{7,3},{8,12},{12,8},{9,1... | collective-permute-start | bytes 786440 | tf_op jit(solution)/shard_map/ppermute | solution.py:517
  83.1 34.1 %collective-permute-start.8 = (bf16[512,256]{1,0:T(8,128)(2,1)S(1)}, bf16[512,256]{1,0:T(8,128)(2,1)S(1)}, u32[]{:S(2)}, u32[]{:S(2)}) collective-permute-start(bf16[512,256]{1,0:T(8,128)(2,1)S(1)} %copy-done.7), channel_id=1, source_target_pairs={{0,16},{16,0},{1,17},{17,1},{2,18},{18,2},{3,19},{19,3},{4,20},{20... | collective-permute-start | bytes 786440 | tf_op jit(solution)/shard_map/ppermute | solution.py:517
  83.1 34.1 %collective-permute-start.9 = (bf16[512,256]{1,0:T(8,128)(2,1)S(1)}, bf16[512,256]{1,0:T(8,128)(2,1)S(1)}, u32[]{:S(2)}, u32[]{:S(2)}) collective-permute-start(bf16[512,256]{1,0:T(8,128)(2,1)S(1)} %copy-done.7), channel_id=1, source_target_pairs={{0,20},{4,16},{16,4},{20,0},{1,21},{5,17},{17,5},{21,1},{2,22},{6,... | collective-permute-start | bytes 786440 | tf_op jit(solution)/shard_map/ppermute | solution.py:517
  117.3 30.9 %copy-start.5 = (bf16[2,512,256]{2,1,0:T(8,128)(2,1)}, bf16[2,512,256]{2,1,0:T(8,128)(2,1)S(1)}, u32[]{:S(2)}) copy-start(bf16[2,512,256]{2,1,0:T(8,128)(2,1)S(1)} %pad_maximum_fusion.1.refs_0_) | copy-start | bytes 1572868
  117.3 16.2 %collective-permute-start.10 = (bf16[2,512,256]{2,1,0:T(8,128)(2,1)S(1)}, bf16[2,512,256]{2,1,0:T(8,128)(2,1)}, u32[]{:S(2)}, u32[]{:S(2)}) collective-permute-start(bf16[2,512,256]{2,1,0:T(8,128)(2,1)S(1)} %pad_maximum_fusion.1.refs_0_), channel_id=1, source_target_pairs={{0,32},{32,64},{64,96},{96,0},{1,33},{33,65},{65,97},{97,1},{2,34}... | collective-permute-start | bytes 1572872 | tf_op jit(solution)/shard_map/ppermute | solution.py:535
  117.5 32.9 %copy-start.6 = (bf16[2,512,256]{2,1,0:T(8,128)(2,1)}, bf16[2,512,256]{2,1,0:T(8,128)(2,1)S(1)}, u32[]{:S(2)}) copy-start(bf16[2,512,256]{2,1,0:T(8,128)(2,1)S(1)} %pad_maximum_fusion.2.refs_1_) | copy-start | bytes 1572868
  117.5 16.0 %collective-permute-start.13 = (bf16[2,512,256]{2,1,0:T(8,128)(2,1)S(1)}, bf16[2,512,256]{2,1,0:T(8,128)(2,1)}, u32[]{:S(2)}, u32[]{:S(2)}) collective-permute-start(bf16[2,512,256]{2,1,0:T(8,128)(2,1)S(1)} %pad_maximum_fusion.2.refs_1_), channel_id=1, source_target_pairs={{0,96},{32,0},{64,32},{96,64},{1,97},{33,1},{65,33},{97,65},{2,98}... | collective-permute-start | bytes 1572872 | tf_op jit(solution)/shard_map/ppermute | solution.py:535
  120.8 23.9 %collective-permute-start.11 = (bf16[2,512,256]{2,1,0:T(8,128)(2,1)S(1)}, bf16[2,512,256]{2,1,0:T(8,128)(2,1)S(1)}, u32[]{:S(2)}, u32[]{:S(2)}) collective-permute-start(bf16[2,512,256]{2,1,0:T(8,128)(2,1)S(1)} %pad_maximum_fusion.2.refs_1_), channel_id=1, source_target_pairs={{0,32},{32,64},{64,96},{96,0},{1,33},{33,65},{65,97},{97,1},{2,34}... | collective-permute-start | bytes 1572872 | tf_op jit(solution)/shard_map/ppermute | solution.py:535
  120.8 25.9 %collective-permute-start.12 = (bf16[2,512,256]{2,1,0:T(8,128)(2,1)S(1)}, bf16[2,512,256]{2,1,0:T(8,128)(2,1)S(1)}, u32[]{:S(2)}, u32[]{:S(2)}) collective-permute-start(bf16[2,512,256]{2,1,0:T(8,128)(2,1)S(1)} %pad_maximum_fusion.1.refs_0_), channel_id=1, source_target_pairs={{0,96},{32,0},{64,32},{96,64},{1,97},{33,1},{65,33},{97,65},{2,98}... | collective-permute-start | bytes 1572872 | tf_op jit(solution)/shard_map/ppermute | solution.py:535
  124.0 24.2 %collective-permute-start.19 = (bf16[2,512,256]{2,1,0:T(8,128)(2,1)S(1)}, bf16[2,512,256]{2,1,0:T(8,128)(2,1)}, u32[]{:S(2)}, u32[]{:S(2)}) collective-permute-start(bf16[2,512,256]{2,1,0:T(8,128)(2,1)S(1)} %pad_maximum_fusion.1.refs_0_), channel_id=1, source_target_pairs={{0,8},{8,0},{1,9},{9,1},{2,10},{10,2},{3,11},{11,3},{4,12},{12,4},... | collective-permute-start | bytes 1572872 | tf_op jit(solution)/shard_map/ppermute | solution.py:538
  133.5 16.7 %collective-permute-start.20 = (bf16[2,512,256]{2,1,0:T(8,128)(2,1)S(1)}, bf16[2,512,256]{2,1,0:T(8,128)(2,1)S(1)}, u32[]{:S(2)}, u32[]{:S(2)}) collective-permute-start(bf16[2,512,256]{2,1,0:T(8,128)(2,1)S(1)} %pad_maximum_fusion.2.refs_1_), channel_id=1, source_target_pairs={{0,8},{8,0},{1,9},{9,1},{2,10},{10,2},{3,11},{11,3},{4,12},{12,4},... | collective-permute-start | bytes 1572872 | tf_op jit(solution)/shard_map/ppermute | solution.py:538
  133.5 21.6 %collective-permute-start.14 = (bf16[2,512,256]{2,1,0:T(8,128)(2,1)}, bf16[2,512,256]{2,1,0:T(8,128)(2,1)S(1)}, u32[]{:S(2)}, u32[]{:S(2)}) collective-permute-start(bf16[2,512,256]{2,1,0:T(8,128)(2,1)} %collective-permute-done.10.refs_2_), channel_id=1, source_target_pairs={{0,32},{32,64},{64,96},{96,0},{1,33},{33,65},{65,97},{97,1},{2,34}... | collective-permute-start | bytes 1572872 | tf_op jit(solution)/shard_map/ppermute | solution.py:535
  144.6 13.3 %collective-permute-start.15 = (bf16[2,512,256]{2,1,0:T(8,128)(2,1)}, bf16[2,512,256]{2,1,0:T(8,128)(2,1)S(1)}, u32[]{:S(2)}, u32[]{:S(2)}) collective-permute-start(bf16[2,512,256]{2,1,0:T(8,128)(2,1)} %collective-permute-done.13.refs_5_), channel_id=1, source_target_pairs={{0,96},{32,0},{64,32},{96,64},{1,97},{33,1},{65,33},{97,65},{2,98}... | collective-permute-start | bytes 1572872 | tf_op jit(solution)/shard_map/ppermute | solution.py:535
  146.7 13.2 %collective-permute-start.2 = (bf16[512,512]{1,0:T(8,128)(2,1)}, bf16[512,512]{1,0:T(8,128)(2,1)S(1)}, u32[]{:S(2)}, u32[]{:S(2)}) collective-permute-start(bf16[512,512]{1,0:T(8,128)(2,1)} %bitcast.8), channel_id=1, source_target_pairs={{0,1},{1,2},{2,3},{3,0},{4,5},{5,6},{6,7},{7,4},{8,9},{9,10},{10,1... | collective-permute-start | bytes 1572872 | tf_op jit(solution)/shard_map/ppermute | solution.py:543
  148.2 14.2 %collective-permute-start.1 = (bf16[512,512]{1,0:T(8,128)(2,1)}, bf16[512,512]{1,0:T(8,128)(2,1)S(1)}, u32[]{:S(2)}, u32[]{:S(2)}) collective-permute-start(bf16[512,512]{1,0:T(8,128)(2,1)} %bitcast.9), channel_id=1, source_target_pairs={{0,3},{1,0},{2,1},{3,2},{4,7},{5,4},{6,5},{7,6},{8,11},{9,8},{10,9... | collective-permute-start | bytes 1572872 | tf_op jit(solution)/shard_map/ppermute | solution.py:544
  150.3 15.1 %copy-start.16 = (bf16[2,512,256]{2,1,0:T(8,128)(2,1)}, bf16[2,512,256]{2,1,0:T(8,128)(2,1)S(1)}, u32[]{:S(2)}) copy-start(bf16[2,512,256]{2,1,0:T(8,128)(2,1)S(1)} %collective-permute-done.20.refs_1_) | copy-start | bytes 1572868
  150.3 23.7 %collective-permute-start.21 = (bf16[2,512,256]{2,1,0:T(8,128)(2,1)}, bf16[2,512,256]{2,1,0:T(8,128)(2,1)}, u32[]{:S(2)}, u32[]{:S(2)}) collective-permute-start(bf16[2,512,256]{2,1,0:T(8,128)(2,1)} %collective-permute-done.10.refs_2_), channel_id=1, source_target_pairs={{0,8},{8,0},{1,9},{9,1},{2,10},{10,2},{3,11},{11,3},{4,12},{12,4},... | collective-permute-start | bytes 1572872 | tf_op jit(solution)/shard_map/ppermute | solution.py:538
  155.2 7.3 %copy-start.12 = (bf16[2,512,256]{2,1,0:T(8,128)(2,1)}, bf16[2,512,256]{2,1,0:T(8,128)(2,1)S(1)}, u32[]{:S(2)}) copy-start(bf16[2,512,256]{2,1,0:T(8,128)(2,1)S(1)} %collective-permute-done.14.refs_6_) | copy-start | bytes 1572868
  155.2 18.8 %collective-permute-start = (bf16[512,512]{1,0:T(8,128)(2,1)}, bf16[512,512]{1,0:T(8,128)(2,1)S(1)}, u32[]{:S(2)}, u32[]{:S(2)}) collective-permute-start(bf16[512,512]{1,0:T(8,128)(2,1)} %bitcast.8), channel_id=1, source_target_pairs={{0,3},{1,0},{2,1},{3,2},{4,7},{5,4},{6,5},{7,6},{8,11},{9,8},{10,9... | collective-permute-start | bytes 1572872 | tf_op jit(solution)/shard_map/ppermute | solution.py:546
  157.9 7.4 %copy-start.14 = (bf16[2,512,256]{2,1,0:T(8,128)(2,1)}, bf16[2,512,256]{2,1,0:T(8,128)(2,1)S(1)}, u32[]{:S(2)}) copy-start(bf16[2,512,256]{2,1,0:T(8,128)(2,1)S(1)} %collective-permute-done.15.refs_7_) | copy-start | bytes 1572868
  157.9 16.5 %collective-permute-start.5 = (bf16[512,512]{1,0:T(8,128)(2,1)}, bf16[512,512]{1,0:T(8,128)(2,1)S(1)}, u32[]{:S(2)}, u32[]{:S(2)}) collective-permute-start(bf16[512,512]{1,0:T(8,128)(2,1)} %bitcast.9), channel_id=1, source_target_pairs={{0,1},{1,2},{2,3},{3,0},{4,5},{5,6},{6,7},{7,4},{8,9},{9,10},{10,1... | collective-permute-start | bytes 1572872 | tf_op jit(solution)/shard_map/ppermute | solution.py:545
  159.8 23.8 %collective-permute-start.3 = (bf16[512,512]{1,0:T(8,128)(2,1)S(1)}, bf16[512,512]{1,0:T(8,128)(2,1)}, u32[]{:S(2)}, u32[]{:S(2)}) collective-permute-start(bf16[512,512]{1,0:T(8,128)(2,1)S(1)} %collective-permute-done.2.refs_0_.refs_5_), channel_id=1, source_target_pairs={{0,1},{1,2},{2,3},{3,0},{4,5},{5,6},{6,7},{7,4},{8,9},{9,10},{10,1... | collective-permute-start | bytes 1572872 | tf_op jit(solution)/shard_map/ppermute | solution.py:547
  162.5 21.7 %copy-start = (bf16[512,512]{1,0:T(8,128)(2,1)}, bf16[512,512]{1,0:T(8,128)(2,1)S(1)}, u32[]{:S(2)}) copy-start(bf16[512,512]{1,0:T(8,128)(2,1)S(1)} %collective-permute-done.1.refs_3_.refs_2_) | copy-start | bytes 1572868
  162.5 21.2 %collective-permute-start.4 = (bf16[512,512]{1,0:T(8,128)(2,1)S(1)}, bf16[512,512]{1,0:T(8,128)(2,1)}, u32[]{:S(2)}, u32[]{:S(2)}) collective-permute-start(bf16[512,512]{1,0:T(8,128)(2,1)S(1)} %collective-permute-done.1.refs_3_.refs_2_), channel_id=1, source_target_pairs={{0,3},{1,0},{2,1},{3,2},{4,7},{5,4},{6,5},{7,6},{8,11},{9,8},{10,9... | collective-permute-start | bytes 1572872 | tf_op jit(solution)/shard_map/ppermute | solution.py:548
  168.5 5.4 %copy-start.9 = (bf16[2,512,256]{2,1,0:T(8,128)(2,1)S(1)}, bf16[2,512,256]{2,1,0:T(8,128)(2,1)}, u32[]{:S(2)}) copy-start(bf16[2,512,256]{2,1,0:T(8,128)(2,1)} %copy-done.8) | copy-start | bytes 1572868
  168.6 5.9 %copy-start.11 = (bf16[2,512,256]{2,1,0:T(8,128)(2,1)S(1)}, bf16[2,512,256]{2,1,0:T(8,128)(2,1)}, u32[]{:S(2)}) copy-start(bf16[2,512,256]{2,1,0:T(8,128)(2,1)} %copy-done.10) | copy-start | bytes 1572868
  168.6 15.1 %copy-start.13 = (bf16[2,512,256]{2,1,0:T(8,128)(2,1)S(1)}, bf16[2,512,256]{2,1,0:T(8,128)(2,1)}, u32[]{:S(2)}) copy-start(bf16[2,512,256]{2,1,0:T(8,128)(2,1)} %copy-done.12) | copy-start | bytes 1572868
  168.6 15.1 %copy-start.15 = (bf16[2,512,256]{2,1,0:T(8,128)(2,1)S(1)}, bf16[2,512,256]{2,1,0:T(8,128)(2,1)}, u32[]{:S(2)}) copy-start(bf16[2,512,256]{2,1,0:T(8,128)(2,1)} %copy-done.14) | copy-start | bytes 1572868
  173.9 29.7 %collective-permute-start.24 = (bf16[2,512,256]{2,1,0:T(8,128)(2,1)}, bf16[2,512,256]{2,1,0:T(8,128)(2,1)S(1)}, u32[]{:S(2)}, u32[]{:S(2)}) collective-permute-start(bf16[2,512,256]{2,1,0:T(8,128)(2,1)} %collective-permute-done.13.refs_5_), channel_id=1, source_target_pairs={{0,8},{8,0},{1,9},{9,1},{2,10},{10,2},{3,11},{11,3},{4,12},{12,4},... | collective-permute-start | bytes 1572872 | tf_op jit(solution)/shard_map/ppermute | solution.py:538
  174.0 29.7 %collective-permute-start.22 = (bf16[2,512,256]{2,1,0:T(8,128)(2,1)S(1)}, bf16[2,512,256]{2,1,0:T(8,128)(2,1)S(1)}, u32[]{:S(2)}, u32[]{:S(2)}) collective-permute-start(bf16[2,512,256]{2,1,0:T(8,128)(2,1)S(1)} %copy-done.9), channel_id=1, source_target_pairs={{0,8},{8,0},{1,9},{9,1},{2,10},{10,2},{3,11},{11,3},{4,12},{12,4},... | collective-permute-start | bytes 1572872 | tf_op jit(solution)/shard_map/ppermute | solution.py:538
  174.5 29.2 %collective-permute-start.23 = (bf16[2,512,256]{2,1,0:T(8,128)(2,1)S(1)}, bf16[2,512,256]{2,1,0:T(8,128)(2,1)S(1)}, u32[]{:S(2)}, u32[]{:S(2)}) collective-permute-start(bf16[2,512,256]{2,1,0:T(8,128)(2,1)S(1)} %copy-done.11), channel_id=1, source_target_pairs={{0,8},{8,0},{1,9},{9,1},{2,10},{10,2},{3,11},{11,3},{4,12},{12,4},... | collective-permute-start | bytes 1572872 | tf_op jit(solution)/shard_map/ppermute | solution.py:538
  183.6 20.1 %collective-permute-start.25 = (bf16[2,512,256]{2,1,0:T(8,128)(2,1)S(1)}, bf16[2,512,256]{2,1,0:T(8,128)(2,1)S(1)}, u32[]{:S(2)}, u32[]{:S(2)}) collective-permute-start(bf16[2,512,256]{2,1,0:T(8,128)(2,1)S(1)} %copy-done.13), channel_id=1, source_target_pairs={{0,8},{8,0},{1,9},{9,1},{2,10},{10,2},{3,11},{11,3},{4,12},{12,4},... | collective-permute-start | bytes 1572872 | tf_op jit(solution)/shard_map/ppermute | solution.py:538
  183.6 20.1 %collective-permute-start.26 = (bf16[2,512,256]{2,1,0:T(8,128)(2,1)S(1)}, bf16[2,512,256]{2,1,0:T(8,128)(2,1)S(1)}, u32[]{:S(2)}, u32[]{:S(2)}) collective-permute-start(bf16[2,512,256]{2,1,0:T(8,128)(2,1)S(1)} %copy-done.15), channel_id=1, source_target_pairs={{0,8},{8,0},{1,9},{9,1},{2,10},{10,2},{3,11},{11,3},{4,12},{12,4},... | collective-permute-start | bytes 1572872 | tf_op jit(solution)/shard_map/ppermute | solution.py:538
  184.1 8.1 %copy-start.2 = (f32[512,128]{1,0:T(8,128)S(1)}, f32[512,128]{1,0:T(8,128)}, u32[]{:S(2)}) copy-start(f32[512,128]{1,0:T(8,128)} %get-tuple-element.60.refs_7_) | copy-start | bytes 786436
  205.7 33.1 %copy-start.1 = (bf16[512,512]{1,0:T(8,128)(2,1)S(1)}, bf16[512,512]{1,0:T(8,128)(2,1)}, u32[]{:S(2)}) copy-start(bf16[512,512]{1,0:T(8,128)(2,1)} %copy-done) | copy-start | bytes 1572868
  212.4 46.8 %copy-start.3 = (bf16[128,2048]{1,0:T(8,128)(2,1)S(1)}, bf16[128,2048]{1,0:T(8,128)(2,1)}, u32[]{:S(2)}) copy-start(bf16[128,2048]{1,0:T(8,128)(2,1)} %get-tuple-element.47.refs_3_) | copy-start | bytes 1572868
  212.4 15.4 %collective-permute-start.28 = (bf16[128,2048]{1,0:T(8,128)(2,1)}, bf16[128,2048]{1,0:T(8,128)(2,1)}, u32[]{:S(2)}, u32[]{:S(2)}) collective-permute-start(bf16[128,2048]{1,0:T(8,128)(2,1)} %get-tuple-element.50), channel_id=1, source_target_pairs={{0,3},{1,0},{2,1},{3,2},{4,7},{5,4},{6,5},{7,6},{8,11},{9,8},{10,9... | collective-permute-start | bytes 1572872 | tf_op jit(solution)/shard_map/ppermute | solution.py:474
  221.1 38.0 %copy-start.4 = (bf16[128,2048]{1,0:T(8,128)(2,1)S(1)}, bf16[128,2048]{1,0:T(8,128)(2,1)}, u32[]{:S(2)}) copy-start(bf16[128,2048]{1,0:T(8,128)(2,1)} %get-tuple-element.43.refs_0_) | copy-start | bytes 1572868
  221.2 16.3 %collective-permute-start.17 = (bf16[128,2048]{1,0:T(8,128)(2,1)}, bf16[128,2048]{1,0:T(8,128)(2,1)S(1)}, u32[]{:S(2)}, u32[]{:S(2)}) collective-permute-start(bf16[128,2048]{1,0:T(8,128)(2,1)} %get-tuple-element.46), channel_id=1, source_target_pairs={{0,1},{1,2},{2,3},{3,0},{4,5},{5,6},{6,7},{7,4},{8,9},{9,10},{10,1... | collective-permute-start | bytes 1572872 | tf_op jit(solution)/shard_map/ppermute | solution.py:474
  221.5 27.2 %collective-permute-start.27 = (bf16[128,2048]{1,0:T(8,128)(2,1)}, bf16[128,2048]{1,0:T(8,128)(2,1)S(1)}, u32[]{:S(2)}, u32[]{:S(2)}) collective-permute-start(bf16[128,2048]{1,0:T(8,128)(2,1)} %get-tuple-element.48), channel_id=1, source_target_pairs={{0,1},{1,2},{2,3},{3,0},{4,5},{5,6},{6,7},{7,4},{8,9},{9,10},{10,1... | collective-permute-start | bytes 1572872 | tf_op jit(solution)/shard_map/ppermute | solution.py:475
  221.6 27.1 %collective-permute-start.16 = (bf16[128,2048]{1,0:T(8,128)(2,1)}, bf16[128,2048]{1,0:T(8,128)(2,1)S(1)}, u32[]{:S(2)}, u32[]{:S(2)}) collective-permute-start(bf16[128,2048]{1,0:T(8,128)(2,1)} %get-tuple-element.44), channel_id=1, source_target_pairs={{0,3},{1,0},{2,1},{3,2},{4,7},{5,4},{6,5},{7,6},{8,11},{9,8},{10,9... | collective-permute-start | bytes 1572872 | tf_op jit(solution)/shard_map/ppermute | solution.py:475
  229.2 20.2 %collective-permute-start.29 = (bf16[128,2048]{1,0:T(8,128)(2,1)S(1)}, bf16[128,2048]{1,0:T(8,128)(2,1)S(1)}, u32[]{:S(2)}, u32[]{:S(2)}) collective-permute-start(bf16[128,2048]{1,0:T(8,128)(2,1)S(1)} %add_convert_fusion), channel_id=1, source_target_pairs={{0,3},{1,0},{2,1},{3,2},{4,7},{5,4},{6,5},{7,6},{8,11},{9,8},{10,9... | collective-permute-start | bytes 1572872 | tf_op jit(solution)/shard_map/ppermute | solution.py:481
  238.6 20.5 %collective-permute-start.18 = (bf16[128,2048]{1,0:T(8,128)(2,1)S(1)}, bf16[128,2048]{1,0:T(8,128)(2,1)S(1)}, u32[]{:S(2)}, u32[]{:S(2)}) collective-permute-start(bf16[128,2048]{1,0:T(8,128)(2,1)S(1)} %add_convert_fusion.1), channel_id=1, source_target_pairs={{0,1},{1,2},{2,3},{3,0},{4,5},{5,6},{6,7},{7,4},{8,9},{9,10},{10,1... | collective-permute-start | bytes 1572872 | tf_op jit(solution)/shard_map/ppermute | solution.py:481
  (7 other events, 9.5 us)
Sparse Core Ops, SparseCore 0:
  22.8 85.9 all-gather.1

commit v9 on v8

--- a/solution.py
+++ b/solution.py
@@ -406,7 +406,7 @@
 
 def product(where, rows, weights, turns, chunks=2):
     halves, depth, width = weights[0].shape
-    row_count = rows.shape[0]
+    quarter = rows.shape[0] // lax.axis_size(RING)
     count = len(weights)
     return pl.pallas_call(
         functools.partial(product_kernel, turns=turns, chunks=chunks),
@@ -414,17 +414,16 @@
         + [pl.BlockSpec(memory_space=pltpu.HBM)] * count,
         out_specs=tuple([pl.BlockSpec(memory_space=pltpu.VMEM)] * len(turns)),
         out_shape=tuple(
-            [jax.ShapeDtypeStruct((row_count // len(turns), count * width), jnp.bfloat16)]
-            * len(turns)
+            [jax.ShapeDtypeStruct((quarter, count * width), jnp.bfloat16)] * len(turns)
         ),
         scratch_shapes=[
-            pltpu.VMEM(rows.shape, jnp.bfloat16),
+            pltpu.VMEM((len(turns) * quarter, rows.shape[1]), jnp.bfloat16),
             pltpu.VMEM((halves * depth, count * width), jnp.bfloat16),
             pltpu.SemaphoreType.DMA((count, halves)),
         ],
         compiler_params=pltpu.CompilerParams(vmem_limit_bytes=60 * 2**20),
         cost_estimate=pl.CostEstimate(
-            flops=2 * row_count * halves * depth * width * count,
+            flops=2 * len(turns) * quarter * halves * depth * width * count,
             bytes_accessed=2 * (rows.size + halves * depth * width * count),
             transcendentals=0,
         ),
@@ -434,33 +433,48 @@
 LAYERS = (0, 1, 3, 2)
 
 
-def finish_kernel(where_ref, rows_ref, *refs, width):
+def added(where_ref, rows_ref, terms, core, width):
+    for j in range(2 * len(LAYERS)):
+        z = lax.rem(where_ref[0] + len(LAYERS) - LAYERS[j // 2], len(LAYERS))
+        column = (z * 2 + (where_ref[1] ^ (j % 2))) * 2 + (where_ref[2] ^ core)
+        here = slice(j * width, (j + 1) * width)
+        there = pl.ds(pl.multiple_of(column * width, width), width)
+        total = sum(term[:, here].astype(jnp.float32) for term in terms)
+        yield here, there, (rows_ref[:, there].astype(jnp.float32) + total).astype(jnp.bfloat16)
+
+
+def first_half_kernel(where_ref, rows_ref, *refs, width):
+    for here, _, values in added(where_ref, rows_ref, refs[:-1], 0, width):
+        refs[-1][:, here] = values
+
+
+def second_half_kernel(where_ref, rows_ref, first_ref, *refs, width):
     hidden_ref = refs[-1]
-    for core in range(2):
-        terms = refs[3 * core : 3 * core + 3]
-        for j in range(2 * len(LAYERS)):
-            z = lax.rem(where_ref[0] + len(LAYERS) - LAYERS[j // 2], len(LAYERS))
-            column = (z * 2 + (where_ref[1] ^ (j % 2))) * 2 + (where_ref[2] ^ core)
-            here = slice(j * width, (j + 1) * width)
-            there = pl.ds(pl.multiple_of(column * width, width), width)
-            total = sum(term[:, here].astype(jnp.float32) for term in terms)
-            hidden_ref[:, there] = (rows_ref[:, there].astype(jnp.float32) + total).astype(
-                jnp.bfloat16
-            )
-
-
-def finish(where, rows, sums, width):
+    for here, there, values in added(where_ref, rows_ref, refs[:-1], 1, width):
+        hidden_ref[:, there] = values
+        other = pl.ds(pl.multiple_of(there.start + (2 * where_ref[2] - 1) * width, width), width)
+        hidden_ref[:, other] = first_ref[:, here]
+
+
+def add_call(kernel, columns, where, operands, width):
+    shape = (operands[0].shape[0], columns)
     return pl.pallas_call(
-        functools.partial(finish_kernel, width=width),
-        out_shape=jax.ShapeDtypeStruct(rows.shape, jnp.bfloat16),
+        functools.partial(kernel, width=width),
+        out_shape=jax.ShapeDtypeStruct(shape, jnp.bfloat16),
         in_specs=[pl.BlockSpec(memory_space=pltpu.SMEM)]
-        + [pl.BlockSpec(memory_space=pltpu.VMEM)] * (1 + len(sums)),
+        + [pl.BlockSpec(memory_space=pltpu.VMEM)] * len(operands),
         out_specs=pl.BlockSpec(memory_space=pltpu.VMEM),
         compiler_params=pltpu.CompilerParams(vmem_limit_bytes=16 * 2**20),
         cost_estimate=pl.CostEstimate(
-            flops=4 * rows.size, bytes_accessed=8 * rows.size, transcendentals=0
-        ),
-    )(where, rows, *sums)
+            flops=4 * shape[0] * columns, bytes_accessed=8 * shape[0] * columns, transcendentals=0
+        ),
+    )(where, *operands)
+
+
+def finish(where, rows, sums, width):
+    half = sums[0].shape[1]
+    first = add_call(first_half_kernel, half, where, [rows, *sums[:3]], width)
+    return add_call(second_half_kernel, rows.shape[1], where, [rows, first, *sums[3:]], width)
 
 
 def ring_sums(attended, w_mine, w_other):
@@ -468,15 +482,15 @@
     order = [(z, side) for z in LAYERS for side in range(2)]
     own, first, onward = [], [], []
     for way, weights in ((1, w_mine), (-1, w_other)):
-        across, against, along, mine = product(
-            where, attended, [weights[name] for name in order], [2, -way, way, 0]
-        )
+        pieces = [weights[name] for name in order]
+        across, against = product(where, attended, pieces, [2, -way])
         passed = lax.ppermute(across, RING, ring_route(way))
         first.append(lax.ppermute(against, RING, ring_route(-way)))
+        onward.append((way, pieces, passed))
+    last = []
+    for way, pieces, passed in onward:
+        along, mine = product(where, attended, pieces, [way, 0])
         own.append(mine)
-        onward.append((way, along, passed))
-    last = []
-    for way, along, passed in onward:
         both = (along.astype(jnp.float32) + passed.astype(jnp.float32)).astype(jnp.bfloat16)
         last.append(lax.ppermute(both, RING, ring_route(way)))
     return [term for core in range(2) for term in (own[core], first[core], last[core])]

time: 270 us -> 254 us (0.941)
  waiting for transfers between devices: 104 us -> 84.4 us
  blocking collectives: 18.7 us -> 0 us
  starting transfers between devices: 42.2 us -> 53.1 us
  Pallas kernels: 74.8 us -> 83.2 us
    ppermute x3, waiting for transfers between devices: 31.5 us -> 0.01 us  [sublayer(): pieces_x.append(lax.ppermute(w_out, axes, route))]
    ppermute x6, waiting for transfers between devices: 22.8 us -> 43.5 us  [sublayer(): w_mine[z, side] = lax.ppermute(w_mine[before, side], CHIP_Z, route)]
    all_to_all x1 -> x0, blocking collectives: 18.7 us -> none  [sublayer(): lax.all_to_all(jnp.broadcast_to(prompt_ids[None], (devices, quarter)), DP...]
    ppermute x1, waiting for transfers between devices: 2.1 us -> 15 us  [sublayer(): high_after = lax.ppermute(high, RING, ring_route(-1))]
    all_to_all x0 -> x1, starting transfers between devices: none -> 10.5 us  [sublayer(): lax.all_to_all(jnp.broadcast_to(prompt_ids[None], (devices, quarter)), DP...]
    ppermute x1, waiting for transfers between devices: 9.04 us -> 0.01 us  [sublayer(): low_across = lax.ppermute(low_before, RING, ring_route(1))]
    ppermute x2, waiting for transfers between devices: 8.34 us -> 0.01 us  [ring_sums(): passed = lax.ppermute(across, RING, ring_route(way))]
    pallas_call x2 -> x4, Pallas kernels: 13.3 us -> 21.1 us  [product(): pl.pallas_call(functools.partial(product_kernel, turns=turns, chunks=chun...]
  transfers between devices with their start and end apart: 32 -> 33, of which waited for: 14 -> 9; matrix products, arithmetic and copies ran while one was open for 3% -> 5% of each run, Pallas kernels for 25% -> 32%
where the time goes in v9:
time: 254 us; the launch traced here: 252 us
  waiting for transfers between devices  84.4 us (33%)
  Pallas kernels  83.2 us (33%)
  starting transfers between devices  53.1 us (21%)
  between operations  14.4 us (6%)
  other arithmetic  11.1 us (4%)
  local copies, waits for them, and re-layouts  5.34 us (2%)
    ppermute x6, waiting for transfers between devices, sublayer(): w_mine[z, side] = lax.ppermute(w_mine[before, side], CHIP_Z, route)  43.5 us
    pallas_call x1, Pallas kernels, lookup(): pl.pallas_call(lookup_kernel, out_shape=jax.ShapeDtypeStruct((group_count...  32.4 us
    pallas_call x4, Pallas kernels, product(): pl.pallas_call(functools.partial(product_kernel, turns=turns, chunks=chun...  21.1 us
    ppermute x1, waiting for transfers between devices, sublayer(): high_after = lax.ppermute(high, RING, ring_route(-1))  15 us
    pallas_call x2, Pallas kernels, project(): pl.pallas_call(functools.partial(project_kernel, parts=len(parts), carrie...  13.3 us
    pallas_call x1, Pallas kernels, attend(): pl.pallas_call(functools.partial(attention_kernel, parts=len(parts), mode...  11.2 us
    ppermute x6, starting transfers between devices, sublayer(): w_mine[z, side] = lax.ppermute(w_mine[before, side], CHIP_Z, route)  11 us
    ppermute x1, waiting for transfers between devices, swapped(): return lax.ppermute(block, axis, route)  11 us
  transfers between devices with their start and end apart: 33, of which 9 were waited for; matrix products, arithmetic and copies ran while one was open for 5% of the time, Pallas kernels for 32%

profile of v9, /device:TPU:6, one launch (start us, length us, event | category | flops | bytes accessed | tf_op | source)
XLA Modules:
  0.0 251.6 jit_solution(15115803868459486869)
XLA Ops:
  8.0 1.2 multiply_convert_fusion
  9.2 1.5 collective-permute-start.6
  10.6 11.0 %collective-permute-done.6 = bf16[1,256,768]{2,1,0:T(8,128)(2,1)S(1)} collective-permute-done((bf16[1,256,768]{2,1,0:T(8,128)(2,1)S(1)}, bf16[1,256,768]{2,1,0:T(8,128)(2,1)S(1)}, u32[]{:S(2)}, u32[]{:S(2)}) %collective-permute-start.6) | collective-permute-done | bytes 393248 | tf_op jit(solution)/shard_map/ppermute | solution.py:34
  21.6 1.0 pad_maximum_fusion
  22.6 1.3 broadcast_in_dim.4
  24.0 10.5 %all-to-all-start = ((s32[128,1,128]{2,1,0:T(1,128)}), s32[128,1,128]{2,1,0:T(1,128)S(1)}, u32[]{:S(2)}, u32[]{:S(2)}) async-start(s32[128,1,128]{2,1,0:T(1,128)} %broadcast_in_dim.4), calls=%async_computation | async-start | bytes 131072 | tf_op jit(solution)/shard_map/all_to_all | solution.py:518
  34.4 1.5 collective-permute-start.7
  36.4 2.2 collective-permute-start.9
  38.6 4.2 %all-to-all-done = s32[128,1,128]{2,1,0:T(1,128)S(1)} async-done(((s32[128,1,128]{2,1,0:T(1,128)}), s32[128,1,128]{2,1,0:T(1,128)S(1)}, u32[]{:S(2)}, u32[]{:S(2)}) %all-to-all-start) | async-done | bytes 65568 | tf_op jit(solution)/shard_map/all_to_all | solution.py:518
  44.2 32.4 %shard_map.95 = bf16[32,32,512]{2,1,0:T(8,128)(2,1)} custom-call(s32[16384]{0:T(1024)} %fusion.2.slots_ref, s32[128,128]{1,0:T(8,128)} %bitcast_or_fusion.lanes_ref, bf16[32,128256]{1,0:T(8,128)(2,1)} %table_ref.1), custom_call_target="tpu_custom_call" | custom-call | flops 30000001024 | bytes 8208384 | tf_op jit(solution)/shard_map/pallas_call | solution.py:131
  76.5 5.8 %all-to-all-start.1 = ((bf16[32,32,512]{2,1,0:T(8,128)(2,1)}), bf16[32,32,512]{2,1,0:T(8,128)(2,1)S(1)}, u32[]{:S(2)}, u32[]{:S(2)}) async-start(bf16[32,32,512]{2,1,0:T(8,128)(2,1)} %shard_map.95), calls=%async_computation.1 | async-start | bytes 2097152 | tf_op jit(solution)/shard_map/all_to_all | solution.py:533
  82.5 1.6 collective-permute-start.10
  84.1 1.8 collective-permute-start.13
  86.2 2.9 %collective-permute-start.12 = (bf16[2,512,256]{2,1,0:T(8,128)(2,1)S(1)}, bf16[2,512,256]{2,1,0:T(8,128)(2,1)}, u32[]{:S(2)}, u32[]{:S(2)}) collective-permute-start(bf16[2,512,256]{2,1,0:T(8,128)(2,1)S(1)} %pad_maximum_fusion.1.refs_0_), channel_id=1, source_target_pairs={{0,96},{32,0},{64,32},{96,64},{1,97},{33,1},{65,33},{97,65},{2,98}... | collective-permute-start | bytes 1572872 | tf_op jit(solution)/shard_map/ppermute | solution.py:549
  89.1 31.0 %collective-permute-done.10.refs_2_ = bf16[2,512,256]{2,1,0:T(8,128)(2,1)} collective-permute-done((bf16[2,512,256]{2,1,0:T(8,128)(2,1)S(1)}, bf16[2,512,256]{2,1,0:T(8,128)(2,1)}, u32[]{:S(2)}, u32[]{:S(2)}) %collective-permute-start.10) | collective-permute-done | bytes 524320 | tf_op jit(solution)/shard_map/ppermute | solution.py:549
  120.2 1.0 fusion.4
  121.2 2.6 %collective-permute-start.14 = (bf16[2,512,256]{2,1,0:T(8,128)(2,1)}, bf16[2,512,256]{2,1,0:T(8,128)(2,1)}, u32[]{:S(2)}, u32[]{:S(2)}) collective-permute-start(bf16[2,512,256]{2,1,0:T(8,128)(2,1)} %collective-permute-done.10.refs_2_), channel_id=1, source_target_pairs={{0,32},{32,64},{64,96},{96,0},{1,33},{33,65},{65,97},{97,1},{2,34}... | collective-permute-start | bytes 1572872 | tf_op jit(solution)/shard_map/ppermute | solution.py:549
  123.8 11.3 %collective-permute-done.11.refs_3_ = bf16[2,512,256]{2,1,0:T(8,128)(2,1)} collective-permute-done((bf16[2,512,256]{2,1,0:T(8,128)(2,1)S(1)}, bf16[2,512,256]{2,1,0:T(8,128)(2,1)}, u32[]{:S(2)}, u32[]{:S(2)}) %collective-permute-start.11) | collective-permute-done | bytes 524320 | tf_op jit(solution)/shard_map/ppermute | solution.py:549
  135.1 1.5 collective-permute-start.2
  136.6 1.7 collective-permute-start
  138.3 1.6 collective-permute-start.1
  140.5 1.9 fusion
  143.0 2.2 pad_maximum_fusion.3
  145.1 1.2 collective-permute-done.14.refs_6_
  146.3 15.0 %collective-permute-done.1.refs_3_.refs_2_ = bf16[512,512]{1,0:T(8,128)(2,1)S(1)} collective-permute-done((bf16[512,512]{1,0:T(8,128)(2,1)}, bf16[512,512]{1,0:T(8,128)(2,1)S(1)}, u32[]{:S(2)}, u32[]{:S(2)}) %collective-permute-start.1) | collective-permute-done | bytes 524320 | tf_op jit(solution)/shard_map/ppermute | solution.py:558
  161.3 1.8 collective-permute-start.15
  163.1 1.1 collective-permute-start.3
  164.2 2.7 %collective-permute-start.4 = (bf16[512,512]{1,0:T(8,128)(2,1)S(1)}, bf16[512,512]{1,0:T(8,128)(2,1)}, u32[]{:S(2)}, u32[]{:S(2)}) collective-permute-start(bf16[512,512]{1,0:T(8,128)(2,1)S(1)} %collective-permute-done.1.refs_3_.refs_2_), channel_id=1, source_target_pairs={{0,3},{1,0},{2,1},{3,2},{4,7},{5,4},{6,5},{7,6},{8,11},{9,8},{10,9... | collective-permute-start | bytes 1572872 | tf_op jit(solution)/shard_map/ppermute | solution.py:562
  167.5 5.2 %shard_map.96 = (f32[512,1536]{1,0:T(8,128)}, f32[1,512]{1,0:T(1,128)S(1)}) custom-call(s32[4]{0:T(128)S(1)} %and_select_fusion.places_ref, bf16[1024,512]{1,0:T(8,128)(2,1)S(1)} %bitcast.27, bf16[2,32,4,32,768]{4,3,2,1,0:T(8,128)(2,1)} %bitcast.29), custom_call_target="tpu_custom_call" | custom-call | flops 1610612736 | bytes 4194304 | tf_op jit(solution)/shard_map/pallas_call | solution.py:200
  172.7 8.1 %shard_map.97 = (f32[512,1536]{1,0:T(8,128)}, f32[1,512]{1,0:T(1,128)S(1)}) custom-call(s32[4]{0:T(128)S(1)} %and_select_fusion.places_ref, bf16[512,512]{1,0:T(8,128)(2,1)S(1)} %collective-permute-done.2.refs_0_.refs_5_, bf16[512,512]{1,0:T(8,128)(2,1)S(1)} %collective-permute-done.5.refs_1_.refs_6_, ...), custom_call_target="tpu_custom_call" | custom-call | flops 3221225472 | bytes 8388608 | tf_op jit(solution)/shard_map/pallas_call | solution.py:200
  181.9 11.2 %attend.1 = (bf16[512,1024]{1,0:T(8,128)(2,1)}, bf16[2,512,256]{2,1,0:T(8,128)(2,1)}) custom-call(s32[4]{0:T(128)S(1)} %and_select_fusion.places_ref, s32[1]{0:T(128)} %dynamic_slice.6.length_ref, bf16[512,512]{1,0:T(8,128)(2,1)} %collective-permute-done.3.refs_0_.refs_3_, bf16[512,512]{1,0:T(8,128)(2,1)} %collective-permute-done.4.refs_1_.refs_4_, ...), custom_call_target="tpu_custom_call" | custom-call | flops 4000000000 | bytes 9000000 | tf_op jit(solution)/shard_map/attend/pallas_call | solution.py:282
  193.2 5.3 %shard_map.100 = (bf16[128,2048]{1,0:T(8,128)(2,1)}, bf16[128,2048]{1,0:T(8,128)(2,1)}) custom-call(s32[2]{0:T(128)} %pad_add_fusion.1.where_ref, bf16[512,1024]{1,0:T(8,128)(2,1)} %get-tuple-element.31.rows_ref, bf16[2,512,256]{2,1,0:T(8,128)(2,1)} %copy-done.5, bf16[2,512,256]{2,1,0:T(8,128)(2,1)} %copy-done.6, ...), custom_call_target="tpu_custom_call" | custom-call | flops 1073741824 | bytes 5242880 | tf_op jit(solution)/shard_map/pallas_call | solution.py:411
  198.5 0.8 copy-done.7
  199.3 0.8 copy-done.8
  200.1 5.3 %shard_map.103 = (bf16[128,2048]{1,0:T(8,128)(2,1)}, bf16[128,2048]{1,0:T(8,128)(2,1)}) custom-call(s32[2]{0:T(128)} %pad_add_fusion.1.where_ref, bf16[512,1024]{1,0:T(8,128)(2,1)} %get-tuple-element.31.rows_ref, bf16[2,512,256]{2,1,0:T(8,128)(2,1)} %collective-permute-done.19.refs_0_, bf16[2,512,256]{2,1,0:T(8,128)(2,1)} %collective-permute-done.20.refs_1_, ...), custom_call_target="tpu_custom_call" | custom-call | flops 1073741824 | bytes 5242880 | tf_op jit(solution)/shard_map/pallas_call | solution.py:411
  205.4 3.3 %collective-permute-start.28 = (bf16[128,2048]{1,0:T(8,128)(2,1)}, bf16[128,2048]{1,0:T(8,128)(2,1)}, u32[]{:S(2)}, u32[]{:S(2)}) collective-permute-start(bf16[128,2048]{1,0:T(8,128)(2,1)} %get-tuple-element.50), channel_id=1, source_target_pairs={{0,3},{1,0},{2,1},{3,2},{4,7},{5,4},{6,5},{7,6},{8,11},{9,8},{10,9... | collective-permute-start | bytes 1572872 | tf_op jit(solution)/shard_map/ppermute | solution.py:487
  208.7 3.2 %collective-permute-start.16 = (bf16[128,2048]{1,0:T(8,128)(2,1)}, bf16[128,2048]{1,0:T(8,128)(2,1)}, u32[]{:S(2)}, u32[]{:S(2)}) collective-permute-start(bf16[128,2048]{1,0:T(8,128)(2,1)} %get-tuple-element.44), channel_id=1, source_target_pairs={{0,3},{1,0},{2,1},{3,2},{4,7},{5,4},{6,5},{7,6},{8,11},{9,8},{10,9... | collective-permute-start | bytes 1572872 | tf_op jit(solution)/shard_map/ppermute | solution.py:488
  211.9 5.3 %shard_map.102 = (bf16[128,2048]{1,0:T(8,128)(2,1)}, bf16[128,2048]{1,0:T(8,128)(2,1)}) custom-call(s32[2]{0:T(128)} %pad_add_fusion.1.where_ref, bf16[512,1024]{1,0:T(8,128)(2,1)} %get-tuple-element.31.rows_ref, bf16[2,512,256]{2,1,0:T(8,128)(2,1)} %collective-permute-done.19.refs_0_, bf16[2,512,256]{2,1,0:T(8,128)(2,1)} %collective-permute-done.20.refs_1_, ...), custom_call_target="tpu_custom_call" | custom-call | flops 1073741824 | bytes 5242880 | tf_op jit(solution)/shard_map/pallas_call | solution.py:411
  217.2 5.3 %shard_map.99 = (bf16[128,2048]{1,0:T(8,128)(2,1)}, bf16[128,2048]{1,0:T(8,128)(2,1)}) custom-call(s32[2]{0:T(128)} %pad_add_fusion.1.where_ref, bf16[512,1024]{1,0:T(8,128)(2,1)} %get-tuple-element.31.rows_ref, bf16[2,512,256]{2,1,0:T(8,128)(2,1)} %copy-done.5, bf16[2,512,256]{2,1,0:T(8,128)(2,1)} %copy-done.6, ...), custom_call_target="tpu_custom_call" | custom-call | flops 1073741824 | bytes 5242880 | tf_op jit(solution)/shard_map/pallas_call | solution.py:411
  222.5 1.4 add_convert_fusion.1
  224.0 1.4 add_convert_fusion
  225.4 3.3 %collective-permute-start.29 = (bf16[128,2048]{1,0:T(8,128)(2,1)S(1)}, bf16[128,2048]{1,0:T(8,128)(2,1)S(1)}, u32[]{:S(2)}, u32[]{:S(2)}) collective-permute-start(bf16[128,2048]{1,0:T(8,128)(2,1)S(1)} %add_convert_fusion), channel_id=1, source_target_pairs={{0,3},{1,0},{2,1},{3,2},{4,7},{5,4},{6,5},{7,6},{8,11},{9,8},{10,9... | collective-permute-start | bytes 1572872 | tf_op jit(solution)/shard_map/ppermute | solution.py:495
  228.8 2.0 shard_map.98.rows_ref
  230.8 1.8 collective-permute-done.16.refs_1_
  232.6 5.8 %collective-permute-done.18.refs_2_ = bf16[128,2048]{1,0:T(8,128)(2,1)S(1)} collective-permute-done((bf16[128,2048]{1,0:T(8,128)(2,1)S(1)}, bf16[128,2048]{1,0:T(8,128)(2,1)S(1)}, u32[]{:S(2)}, u32[]{:S(2)}) %collective-permute-start.18) | collective-permute-done | bytes 524320 | tf_op jit(solution)/shard_map/ppermute | solution.py:495
  238.3 1.3 shard_map.101.first_ref
  239.7 3.2 %collective-permute-done.29.refs_2_ = bf16[128,2048]{1,0:T(8,128)(2,1)S(1)} collective-permute-done((bf16[128,2048]{1,0:T(8,128)(2,1)S(1)}, bf16[128,2048]{1,0:T(8,128)(2,1)S(1)}, u32[]{:S(2)}, u32[]{:S(2)}) %collective-permute-start.29) | collective-permute-done | bytes 524320 | tf_op jit(solution)/shard_map/ppermute | solution.py:495
  242.9 1.9 shard_map.104
  (73 shorter events, 6.2 us)
Async XLA Ops:
  7.2 160.3 %all-gather.2.cloned.1.call-start = ((), (), s32[]{:S(2)}) async-start(), calls=%async_computation.2 | async-start | bytes 13369344 | tf_op jit(solution)/shard_map/all_gather | solution.py:516
  9.2 12.4 %collective-permute-start.6 = (bf16[1,256,768]{2,1,0:T(8,128)(2,1)S(1)}, bf16[1,256,768]{2,1,0:T(8,128)(2,1)S(1)}, u32[]{:S(2)}, u32[]{:S(2)}) collective-permute-start(bf16[1,256,768]{2,1,0:T(8,128)(2,1)S(1)} %multiply_convert_fusion), channel_id=1, source_target_pairs={{0,4},{4,0},{1,5},{5,1},{2,6},{6,2},{3,7},{7,3},{8,12},{12,8},{9,1... | collective-permute-start | bytes 1179656 | tf_op jit(solution)/shard_map/ppermute | solution.py:34
  24.0 18.8 %all-to-all-start = ((s32[128,1,128]{2,1,0:T(1,128)}), s32[128,1,128]{2,1,0:T(1,128)S(1)}, u32[]{:S(2)}, u32[]{:S(2)}) async-start(s32[128,1,128]{2,1,0:T(1,128)} %broadcast_in_dim.4), calls=%async_computation | async-start | bytes 131072 | tf_op jit(solution)/shard_map/all_to_all | solution.py:518
  34.4 47.9 %collective-permute-start.7 = (bf16[512,256]{1,0:T(8,128)(2,1)}, bf16[512,256]{1,0:T(8,128)(2,1)S(1)}, u32[]{:S(2)}, u32[]{:S(2)}) collective-permute-start(bf16[512,256]{1,0:T(8,128)(2,1)} %param.15), channel_id=1, source_target_pairs={{0,4},{4,0},{1,5},{5,1},{2,6},{6,2},{3,7},{7,3},{8,12},{12,8},{9,1... | collective-permute-start | bytes 786440 | tf_op jit(solution)/shard_map/ppermute | solution.py:531
  36.0 46.4 %collective-permute-start.8 = (bf16[512,256]{1,0:T(8,128)(2,1)}, bf16[512,256]{1,0:T(8,128)(2,1)S(1)}, u32[]{:S(2)}, u32[]{:S(2)}) collective-permute-start(bf16[512,256]{1,0:T(8,128)(2,1)} %param.15), channel_id=1, source_target_pairs={{0,16},{16,0},{1,17},{17,1},{2,18},{18,2},{3,19},{19,3},{4,20},{20... | collective-permute-start | bytes 786440 | tf_op jit(solution)/shard_map/ppermute | solution.py:531
  36.4 45.9 %collective-permute-start.9 = (bf16[512,256]{1,0:T(8,128)(2,1)}, bf16[512,256]{1,0:T(8,128)(2,1)S(1)}, u32[]{:S(2)}, u32[]{:S(2)}) collective-permute-start(bf16[512,256]{1,0:T(8,128)(2,1)} %param.15), channel_id=1, source_target_pairs={{0,20},{4,16},{16,4},{20,0},{1,21},{5,17},{17,5},{21,1},{2,22},{6,... | collective-permute-start | bytes 786440 | tf_op jit(solution)/shard_map/ppermute | solution.py:531
  44.2 38.2 %copy-start.9 = (bf16[512,256]{1,0:T(8,128)(2,1)S(1)}, bf16[512,256]{1,0:T(8,128)(2,1)}, u32[]{:S(2)}) copy-start(bf16[512,256]{1,0:T(8,128)(2,1)} %param.15) | copy-start | bytes 786436
  44.2 98.2 %copy-start.10 = (s32[32]{0:T(128)S(1)}, s32[32]{0:T(128)}, u32[]{:S(2)}) copy-start(s32[32]{0:T(128)} %param.9) | copy-start | bytes 388
  76.5 43.6 %all-to-all-start.1 = ((bf16[32,32,512]{2,1,0:T(8,128)(2,1)}), bf16[32,32,512]{2,1,0:T(8,128)(2,1)S(1)}, u32[]{:S(2)}, u32[]{:S(2)}) async-start(bf16[32,32,512]{2,1,0:T(8,128)(2,1)} %shard_map.95), calls=%async_computation.1 | async-start | bytes 2097152 | tf_op jit(solution)/shard_map/all_to_all | solution.py:533
  82.5 55.9 %copy-start.5 = (bf16[2,512,256]{2,1,0:T(8,128)(2,1)}, bf16[2,512,256]{2,1,0:T(8,128)(2,1)S(1)}, u32[]{:S(2)}) copy-start(bf16[2,512,256]{2,1,0:T(8,128)(2,1)S(1)} %pad_maximum_fusion.1.refs_0_) | copy-start | bytes 1572868
  82.5 37.7 %collective-permute-start.10 = (bf16[2,512,256]{2,1,0:T(8,128)(2,1)S(1)}, bf16[2,512,256]{2,1,0:T(8,128)(2,1)}, u32[]{:S(2)}, u32[]{:S(2)}) collective-permute-start(bf16[2,512,256]{2,1,0:T(8,128)(2,1)S(1)} %pad_maximum_fusion.1.refs_0_), channel_id=1, source_target_pairs={{0,32},{32,64},{64,96},{96,0},{1,33},{33,65},{65,97},{97,1},{2,34}... | collective-permute-start | bytes 1572872 | tf_op jit(solution)/shard_map/ppermute | solution.py:549
  84.1 55.8 %copy-start.6 = (bf16[2,512,256]{2,1,0:T(8,128)(2,1)}, bf16[2,512,256]{2,1,0:T(8,128)(2,1)S(1)}, u32[]{:S(2)}) copy-start(bf16[2,512,256]{2,1,0:T(8,128)(2,1)S(1)} %pad_maximum_fusion.2.refs_1_) | copy-start | bytes 1572868
  84.1 37.1 %collective-permute-start.13 = (bf16[2,512,256]{2,1,0:T(8,128)(2,1)S(1)}, bf16[2,512,256]{2,1,0:T(8,128)(2,1)}, u32[]{:S(2)}, u32[]{:S(2)}) collective-permute-start(bf16[2,512,256]{2,1,0:T(8,128)(2,1)S(1)} %pad_maximum_fusion.2.refs_1_), channel_id=1, source_target_pairs={{0,96},{32,0},{64,32},{96,64},{1,97},{33,1},{65,33},{97,65},{2,98}... | collective-permute-start | bytes 1572872 | tf_op jit(solution)/shard_map/ppermute | solution.py:549
  85.9 49.2 %collective-permute-start.11 = (bf16[2,512,256]{2,1,0:T(8,128)(2,1)S(1)}, bf16[2,512,256]{2,1,0:T(8,128)(2,1)}, u32[]{:S(2)}, u32[]{:S(2)}) collective-permute-start(bf16[2,512,256]{2,1,0:T(8,128)(2,1)S(1)} %pad_maximum_fusion.2.refs_1_), channel_id=1, source_target_pairs={{0,32},{32,64},{64,96},{96,0},{1,33},{33,65},{65,97},{97,1},{2,34}... | collective-permute-start | bytes 1572872 | tf_op jit(solution)/shard_map/ppermute | solution.py:549
  86.2 50.4 %collective-permute-start.12 = (bf16[2,512,256]{2,1,0:T(8,128)(2,1)S(1)}, bf16[2,512,256]{2,1,0:T(8,128)(2,1)}, u32[]{:S(2)}, u32[]{:S(2)}) collective-permute-start(bf16[2,512,256]{2,1,0:T(8,128)(2,1)S(1)} %pad_maximum_fusion.1.refs_0_), channel_id=1, source_target_pairs={{0,96},{32,0},{64,32},{96,64},{1,97},{33,1},{65,33},{97,65},{2,98}... | collective-permute-start | bytes 1572872 | tf_op jit(solution)/shard_map/ppermute | solution.py:549
  89.1 49.2 %collective-permute-start.19 = (bf16[2,512,256]{2,1,0:T(8,128)(2,1)S(1)}, bf16[2,512,256]{2,1,0:T(8,128)(2,1)}, u32[]{:S(2)}, u32[]{:S(2)}) collective-permute-start(bf16[2,512,256]{2,1,0:T(8,128)(2,1)S(1)} %pad_maximum_fusion.1.refs_0_), channel_id=1, source_target_pairs={{0,8},{8,0},{1,9},{9,1},{2,10},{10,2},{3,11},{11,3},{4,12},{12,4},... | collective-permute-start | bytes 1572872 | tf_op jit(solution)/shard_map/ppermute | solution.py:552
  120.2 19.8 %collective-permute-start.20 = (bf16[2,512,256]{2,1,0:T(8,128)(2,1)S(1)}, bf16[2,512,256]{2,1,0:T(8,128)(2,1)}, u32[]{:S(2)}, u32[]{:S(2)}) collective-permute-start(bf16[2,512,256]{2,1,0:T(8,128)(2,1)S(1)} %pad_maximum_fusion.2.refs_1_), channel_id=1, source_target_pairs={{0,8},{8,0},{1,9},{9,1},{2,10},{10,2},{3,11},{11,3},{4,12},{12,4},... | collective-permute-start | bytes 1572872 | tf_op jit(solution)/shard_map/ppermute | solution.py:552
  121.2 25.1 %collective-permute-start.14 = (bf16[2,512,256]{2,1,0:T(8,128)(2,1)}, bf16[2,512,256]{2,1,0:T(8,128)(2,1)}, u32[]{:S(2)}, u32[]{:S(2)}) collective-permute-start(bf16[2,512,256]{2,1,0:T(8,128)(2,1)} %collective-permute-done.10.refs_2_), channel_id=1, source_target_pairs={{0,32},{32,64},{64,96},{96,0},{1,33},{33,65},{65,97},{97,1},{2,34}... | collective-permute-start | bytes 1572872 | tf_op jit(solution)/shard_map/ppermute | solution.py:549
  135.1 27.9 %collective-permute-start.2 = (bf16[512,512]{1,0:T(8,128)(2,1)}, bf16[512,512]{1,0:T(8,128)(2,1)S(1)}, u32[]{:S(2)}, u32[]{:S(2)}) collective-permute-start(bf16[512,512]{1,0:T(8,128)(2,1)} %bitcast.8), channel_id=1, source_target_pairs={{0,1},{1,2},{2,3},{3,0},{4,5},{5,6},{6,7},{7,4},{8,9},{9,10},{10,1... | collective-permute-start | bytes 1572872 | tf_op jit(solution)/shard_map/ppermute | solution.py:557
  136.6 27.6 %collective-permute-start = (bf16[512,512]{1,0:T(8,128)(2,1)}, bf16[512,512]{1,0:T(8,128)(2,1)S(1)}, u32[]{:S(2)}, u32[]{:S(2)}) collective-permute-start(bf16[512,512]{1,0:T(8,128)(2,1)} %bitcast.8), channel_id=1, source_target_pairs={{0,3},{1,0},{2,1},{3,2},{4,7},{5,4},{6,5},{7,6},{8,11},{9,8},{10,9... | collective-permute-start | bytes 1572872 | tf_op jit(solution)/shard_map/ppermute | solution.py:560
  138.3 22.9 %collective-permute-start.1 = (bf16[512,512]{1,0:T(8,128)(2,1)}, bf16[512,512]{1,0:T(8,128)(2,1)S(1)}, u32[]{:S(2)}, u32[]{:S(2)}) collective-permute-start(bf16[512,512]{1,0:T(8,128)(2,1)} %bitcast.9), channel_id=1, source_target_pairs={{0,3},{1,0},{2,1},{3,2},{4,7},{5,4},{6,5},{7,6},{8,11},{9,8},{10,9... | collective-permute-start | bytes 1572872 | tf_op jit(solution)/shard_map/ppermute | solution.py:558
  139.9 32.8 %collective-permute-start.5 = (bf16[512,512]{1,0:T(8,128)(2,1)}, bf16[512,512]{1,0:T(8,128)(2,1)S(1)}, u32[]{:S(2)}, u32[]{:S(2)}) collective-permute-start(bf16[512,512]{1,0:T(8,128)(2,1)} %bitcast.9), channel_id=1, source_target_pairs={{0,1},{1,2},{2,3},{3,0},{4,5},{5,6},{6,7},{7,4},{8,9},{9,10},{10,1... | collective-permute-start | bytes 1572872 | tf_op jit(solution)/shard_map/ppermute | solution.py:559
  146.3 35.0 %collective-permute-start.21 = (bf16[2,512,256]{2,1,0:T(8,128)(2,1)}, bf16[2,512,256]{2,1,0:T(8,128)(2,1)}, u32[]{:S(2)}, u32[]{:S(2)}) collective-permute-start(bf16[2,512,256]{2,1,0:T(8,128)(2,1)} %collective-permute-done.10.refs_2_), channel_id=1, source_target_pairs={{0,8},{8,0},{1,9},{9,1},{2,10},{10,2},{3,11},{11,3},{4,12},{12,4},... | collective-permute-start | bytes 1572872 | tf_op jit(solution)/shard_map/ppermute | solution.py:552
  161.3 11.4 %copy-start = (bf16[512,512]{1,0:T(8,128)(2,1)}, bf16[512,512]{1,0:T(8,128)(2,1)S(1)}, u32[]{:S(2)}) copy-start(bf16[512,512]{1,0:T(8,128)(2,1)S(1)} %collective-permute-done.1.refs_3_.refs_2_) | copy-start | bytes 1572868
  161.3 19.5 %collective-permute-start.15 = (bf16[2,512,256]{2,1,0:T(8,128)(2,1)}, bf16[2,512,256]{2,1,0:T(8,128)(2,1)}, u32[]{:S(2)}, u32[]{:S(2)}) collective-permute-start(bf16[2,512,256]{2,1,0:T(8,128)(2,1)} %collective-permute-done.13.refs_5_), channel_id=1, source_target_pairs={{0,96},{32,0},{64,32},{96,64},{1,97},{33,1},{65,33},{97,65},{2,98}... | collective-permute-start | bytes 1572872 | tf_op jit(solution)/shard_map/ppermute | solution.py:549
  163.1 18.4 %collective-permute-start.3 = (bf16[512,512]{1,0:T(8,128)(2,1)S(1)}, bf16[512,512]{1,0:T(8,128)(2,1)}, u32[]{:S(2)}, u32[]{:S(2)}) collective-permute-start(bf16[512,512]{1,0:T(8,128)(2,1)S(1)} %collective-permute-done.2.refs_0_.refs_5_), channel_id=1, source_target_pairs={{0,1},{1,2},{2,3},{3,0},{4,5},{5,6},{6,7},{7,4},{8,9},{9,10},{10,1... | collective-permute-start | bytes 1572872 | tf_op jit(solution)/shard_map/ppermute | solution.py:561
  164.2 17.6 %collective-permute-start.4 = (bf16[512,512]{1,0:T(8,128)(2,1)S(1)}, bf16[512,512]{1,0:T(8,128)(2,1)}, u32[]{:S(2)}, u32[]{:S(2)}) collective-permute-start(bf16[512,512]{1,0:T(8,128)(2,1)S(1)} %collective-permute-done.1.refs_3_.refs_2_), channel_id=1, source_target_pairs={{0,3},{1,0},{2,1},{3,2},{4,7},{5,4},{6,5},{7,6},{8,11},{9,8},{10,9... | collective-permute-start | bytes 1572872 | tf_op jit(solution)/shard_map/ppermute | solution.py:562
  172.7 25.7 %collective-permute-start.24 = (bf16[2,512,256]{2,1,0:T(8,128)(2,1)}, bf16[2,512,256]{2,1,0:T(8,128)(2,1)S(1)}, u32[]{:S(2)}, u32[]{:S(2)}) collective-permute-start(bf16[2,512,256]{2,1,0:T(8,128)(2,1)} %collective-permute-done.13.refs_5_), channel_id=1, source_target_pairs={{0,8},{8,0},{1,9},{9,1},{2,10},{10,2},{3,11},{11,3},{4,12},{12,4},... | collective-permute-start | bytes 1572872 | tf_op jit(solution)/shard_map/ppermute | solution.py:552
  172.7 9.2 %copy-start.2 = (f32[512,128]{1,0:T(8,128)S(1)}, f32[512,128]{1,0:T(8,128)}, u32[]{:S(2)}) copy-start(f32[512,128]{1,0:T(8,128)} %get-tuple-element.60.refs_7_) | copy-start | bytes 786436
  180.8 18.5 %collective-permute-start.22 = (bf16[2,512,256]{2,1,0:T(8,128)(2,1)}, bf16[2,512,256]{2,1,0:T(8,128)(2,1)}, u32[]{:S(2)}, u32[]{:S(2)}) collective-permute-start(bf16[2,512,256]{2,1,0:T(8,128)(2,1)} %collective-permute-done.11.refs_3_), channel_id=1, source_target_pairs={{0,8},{8,0},{1,9},{9,1},{2,10},{10,2},{3,11},{11,3},{4,12},{12,4},... | collective-permute-start | bytes 1572872 | tf_op jit(solution)/shard_map/ppermute | solution.py:552
  181.3 18.0 %collective-permute-start.23 = (bf16[2,512,256]{2,1,0:T(8,128)(2,1)}, bf16[2,512,256]{2,1,0:T(8,128)(2,1)}, u32[]{:S(2)}, u32[]{:S(2)}) collective-permute-start(bf16[2,512,256]{2,1,0:T(8,128)(2,1)} %collective-permute-done.12.refs_4_), channel_id=1, source_target_pairs={{0,8},{8,0},{1,9},{9,1},{2,10},{10,2},{3,11},{11,3},{4,12},{12,4},... | collective-permute-start | bytes 1572872 | tf_op jit(solution)/shard_map/ppermute | solution.py:552
  181.4 17.9 %collective-permute-start.25 = (bf16[2,512,256]{2,1,0:T(8,128)(2,1)}, bf16[2,512,256]{2,1,0:T(8,128)(2,1)}, u32[]{:S(2)}, u32[]{:S(2)}) collective-permute-start(bf16[2,512,256]{2,1,0:T(8,128)(2,1)} %collective-permute-done.14.refs_6_), channel_id=1, source_target_pairs={{0,8},{8,0},{1,9},{9,1},{2,10},{10,2},{3,11},{11,3},{4,12},{12,4},... | collective-permute-start | bytes 1572872 | tf_op jit(solution)/shard_map/ppermute | solution.py:552
  181.8 17.5 %collective-permute-start.26 = (bf16[2,512,256]{2,1,0:T(8,128)(2,1)}, bf16[2,512,256]{2,1,0:T(8,128)(2,1)S(1)}, u32[]{:S(2)}, u32[]{:S(2)}) collective-permute-start(bf16[2,512,256]{2,1,0:T(8,128)(2,1)} %collective-permute-done.15.refs_7_), channel_id=1, source_target_pairs={{0,8},{8,0},{1,9},{9,1},{2,10},{10,2},{3,11},{11,3},{4,12},{12,4},... | collective-permute-start | bytes 1572872 | tf_op jit(solution)/shard_map/ppermute | solution.py:552
  198.5 0.8 copy-start.7
  199.3 29.5 %copy-start.1 = (bf16[512,512]{1,0:T(8,128)(2,1)S(1)}, bf16[512,512]{1,0:T(8,128)(2,1)}, u32[]{:S(2)}) copy-start(bf16[512,512]{1,0:T(8,128)(2,1)} %copy-done) | copy-start | bytes 1572868
  199.3 23.2 %collective-permute-start.17 = (bf16[128,2048]{1,0:T(8,128)(2,1)}, bf16[128,2048]{1,0:T(8,128)(2,1)}, u32[]{:S(2)}, u32[]{:S(2)}) collective-permute-start(bf16[128,2048]{1,0:T(8,128)(2,1)} %get-tuple-element.46), channel_id=1, source_target_pairs={{0,1},{1,2},{2,3},{3,0},{4,5},{5,6},{6,7},{7,4},{8,9},{9,10},{10,1... | collective-permute-start | bytes 1572872 | tf_op jit(solution)/shard_map/ppermute | solution.py:487
  199.3 0.8 copy-start.8
  205.4 18.6 %collective-permute-start.28 = (bf16[128,2048]{1,0:T(8,128)(2,1)}, bf16[128,2048]{1,0:T(8,128)(2,1)}, u32[]{:S(2)}, u32[]{:S(2)}) collective-permute-start(bf16[128,2048]{1,0:T(8,128)(2,1)} %get-tuple-element.50), channel_id=1, source_target_pairs={{0,3},{1,0},{2,1},{3,2},{4,7},{5,4},{6,5},{7,6},{8,11},{9,8},{10,9... | collective-permute-start | bytes 1572872 | tf_op jit(solution)/shard_map/ppermute | solution.py:487
  208.7 31.0 %collective-permute-start.27 = (bf16[128,2048]{1,0:T(8,128)(2,1)}, bf16[128,2048]{1,0:T(8,128)(2,1)S(1)}, u32[]{:S(2)}, u32[]{:S(2)}) collective-permute-start(bf16[128,2048]{1,0:T(8,128)(2,1)} %get-tuple-element.48), channel_id=1, source_target_pairs={{0,1},{1,2},{2,3},{3,0},{4,5},{5,6},{6,7},{7,4},{8,9},{9,10},{10,1... | collective-permute-start | bytes 1572872 | tf_op jit(solution)/shard_map/ppermute | solution.py:488
  208.7 23.9 %collective-permute-start.16 = (bf16[128,2048]{1,0:T(8,128)(2,1)}, bf16[128,2048]{1,0:T(8,128)(2,1)}, u32[]{:S(2)}, u32[]{:S(2)}) collective-permute-start(bf16[128,2048]{1,0:T(8,128)(2,1)} %get-tuple-element.44), channel_id=1, source_target_pairs={{0,3},{1,0},{2,1},{3,2},{4,7},{5,4},{6,5},{7,6},{8,11},{9,8},{10,9... | collective-permute-start | bytes 1572872 | tf_op jit(solution)/shard_map/ppermute | solution.py:488
  222.5 15.8 %copy-start.4 = (bf16[128,2048]{1,0:T(8,128)(2,1)S(1)}, bf16[128,2048]{1,0:T(8,128)(2,1)}, u32[]{:S(2)}) copy-start(bf16[128,2048]{1,0:T(8,128)(2,1)} %get-tuple-element.43.refs_0_) | copy-start | bytes 1572868
  222.5 20.3 %copy-start.3 = (bf16[128,2048]{1,0:T(8,128)(2,1)S(1)}, bf16[128,2048]{1,0:T(8,128)(2,1)}, u32[]{:S(2)}) copy-start(bf16[128,2048]{1,0:T(8,128)(2,1)} %get-tuple-element.47.refs_0_) | copy-start | bytes 1572868
  223.9 14.4 %collective-permute-start.18 = (bf16[128,2048]{1,0:T(8,128)(2,1)S(1)}, bf16[128,2048]{1,0:T(8,128)(2,1)S(1)}, u32[]{:S(2)}, u32[]{:S(2)}) collective-permute-start(bf16[128,2048]{1,0:T(8,128)(2,1)S(1)} %add_convert_fusion.1), channel_id=1, source_target_pairs={{0,1},{1,2},{2,3},{3,0},{4,5},{5,6},{6,7},{7,4},{8,9},{9,10},{10,1... | collective-permute-start | bytes 1572872 | tf_op jit(solution)/shard_map/ppermute | solution.py:495
  225.4 17.4 %collective-permute-start.29 = (bf16[128,2048]{1,0:T(8,128)(2,1)S(1)}, bf16[128,2048]{1,0:T(8,128)(2,1)S(1)}, u32[]{:S(2)}, u32[]{:S(2)}) collective-permute-start(bf16[128,2048]{1,0:T(8,128)(2,1)S(1)} %add_convert_fusion), channel_id=1, source_target_pairs={{0,3},{1,0},{2,1},{3,2},{4,7},{5,4},{6,5},{7,6},{8,11},{9,8},{10,9... | collective-permute-start | bytes 1572872 | tf_op jit(solution)/shard_map/ppermute | solution.py:495
Sparse Core Ops, SparseCore 0:
  22.8 105.6 all-gather.1

commit v10 on v9

--- a/solution.py
+++ b/solution.py
@@ -71,7 +71,7 @@
     slab = tile_count // slabs
     lane = lax.broadcasted_iota(jnp.int32, (columns, LANES), 1).astype(jnp.int16)
     left = lane < jnp.int16(LANES // 2)
-    unroll = min(56, slab)
+    unroll = min(84, slab)
 
     def incoming(k):
         part = pl.ds(k * slab * LANES, slab * LANES)
@@ -95,7 +95,7 @@
         lax.fori_loop(0, -(-slab // unroll), prepare, 0)
 
     per_group = row_count // LANES
-    together = 4
+    together = 8
 
     def one_block(step, carry):
         for part in range(together):
@@ -561,17 +561,16 @@
     low_across = lax.ppermute(low_before, RING, ring_route(1))
     high_across = lax.ppermute(high_after, RING, ring_route(-1))
 
-    first = project(places, w_in, [(own, 0, 1, 0)])
     second = project(
         places,
         w_in,
         [
+            (own, 0, 1, 0),
             (low_before, ring - 1, 2, 0),
             (high_before, ring - 1, 2, 1),
             (low_after, 1, 2, 0),
             (high_after, 1, 2, 1),
         ],
-        first,
     )
     attended, cache = attend(
         places,

time: 254 us -> 249 us (0.980)
  Pallas kernels: 83.2 us -> 77.8 us
  waiting for transfers between devices: 84.4 us -> 88.7 us
    ppermute x1, waiting for transfers between devices: 15 us -> 6.27 us  [sublayer(): high_after = lax.ppermute(high, RING, ring_route(-1))]
    ppermute x6, waiting for transfers between devices: 43.5 us -> 51.3 us  [sublayer(): w_mine[z, side] = lax.ppermute(w_mine[before, side], CHIP_Z, route)]
    ppermute x1, waiting for transfers between devices: 0.01 us -> 3.43 us  [sublayer(): low_after = lax.ppermute(low, RING, ring_route(-1))]
    pallas_call x2 -> x1, Pallas kernels: 13.3 us -> 9.96 us  [project(): pl.pallas_call(functools.partial(project_kernel, parts=len(parts), carrie...]
    ppermute x1, waiting for transfers between devices: 0.01 us -> 2.94 us  [sublayer(): low_before = lax.ppermute(low, RING, ring_route(1))]
  transfers between devices with their start and end apart: 33 -> 33, of which waited for: 9 -> 12; matrix products, arithmetic and copies ran while one was open for 5% -> 4% of each run, Pallas kernels for 32% -> 31%
where the time goes in v10:
time: 249 us; the launch traced here: 248 us
  waiting for transfers between devices  88.7 us (36%)
  Pallas kernels  77.8 us (31%)
  starting transfers between devices  51.8 us (21%)
  between operations  14.4 us (6%)
  other arithmetic  8.91 us (4%)
  local copies, waits for them, and re-layouts  6.24 us (3%)
    ppermute x6, waiting for transfers between devices, sublayer(): w_mine[z, side] = lax.ppermute(w_mine[before, side], CHIP_Z, route)  51.3 us
    pallas_call x1, Pallas kernels, lookup(): pl.pallas_call(lookup_kernel, out_shape=jax.ShapeDtypeStruct((group_count...  30.2 us
    pallas_call x4, Pallas kernels, product(): pl.pallas_call(functools.partial(product_kernel, turns=turns, chunks=chun...  21.1 us
    pallas_call x1, Pallas kernels, attend(): pl.pallas_call(functools.partial(attention_kernel, parts=len(parts), mode...  11.3 us
    ppermute x1, waiting for transfers between devices, swapped(): return lax.ppermute(block, axis, route)  11 us
    all_to_all x1, starting transfers between devices, sublayer(): lax.all_to_all(jnp.broadcast_to(prompt_ids[None], (devices, quarter)), DP...  10.5 us
    pallas_call x1, Pallas kernels, project(): pl.pallas_call(functools.partial(project_kernel, parts=len(parts), carrie...  9.96 us
    ppermute x6, starting transfers between devices, sublayer(): w_mine[z, side] = lax.ppermute(w_mine[before, side], CHIP_Z, route)  8.64 us
  transfers between devices with their start and end apart: 33, of which 12 were waited for; matrix products, arithmetic and copies ran while one was open for 4% of the time, Pallas kernels for 31%

profile of v10, /device:TPU:6, one launch (start us, length us, event | category | flops | bytes accessed | tf_op | source)
XLA Modules:
  0.0 247.9 jit_solution(3823233543383606841)
XLA Ops:
  8.0 1.2 multiply_convert_fusion
  9.2 1.5 collective-permute-start.6
  10.6 11.0 %collective-permute-done.6 = bf16[1,256,768]{2,1,0:T(8,128)(2,1)S(1)} collective-permute-done((bf16[1,256,768]{2,1,0:T(8,128)(2,1)S(1)}, bf16[1,256,768]{2,1,0:T(8,128)(2,1)S(1)}, u32[]{:S(2)}, u32[]{:S(2)}) %collective-permute-start.6) | collective-permute-done | bytes 393248 | tf_op jit(solution)/shard_map/ppermute | solution.py:34
  21.7 1.0 pad_maximum_fusion
  22.6 1.3 broadcast_in_dim.4
  24.0 10.5 %all-to-all-start = ((s32[128,1,128]{2,1,0:T(1,128)}), s32[128,1,128]{2,1,0:T(1,128)S(1)}, u32[]{:S(2)}, u32[]{:S(2)}) async-start(s32[128,1,128]{2,1,0:T(1,128)} %broadcast_in_dim.4), calls=%async_computation | async-start | bytes 131072 | tf_op jit(solution)/shard_map/all_to_all | solution.py:518
  34.4 1.5 collective-permute-start.7
  36.4 2.2 collective-permute-start.9
  38.6 4.2 %all-to-all-done = s32[128,1,128]{2,1,0:T(1,128)S(1)} async-done(((s32[128,1,128]{2,1,0:T(1,128)}), s32[128,1,128]{2,1,0:T(1,128)S(1)}, u32[]{:S(2)}, u32[]{:S(2)}) %all-to-all-start) | async-done | bytes 65568 | tf_op jit(solution)/shard_map/all_to_all | solution.py:518
  44.2 30.2 %shard_map.95 = bf16[32,32,512]{2,1,0:T(8,128)(2,1)} custom-call(s32[16384]{0:T(1024)} %fusion.2.slots_ref, s32[128,128]{1,0:T(8,128)} %bitcast_or_fusion.lanes_ref, bf16[32,128256]{1,0:T(8,128)(2,1)} %table_ref.1), custom_call_target="tpu_custom_call" | custom-call | flops 30000001024 | bytes 8208384 | tf_op jit(solution)/shard_map/pallas_call | solution.py:131
  74.4 5.8 %all-to-all-start.1 = ((bf16[32,32,512]{2,1,0:T(8,128)(2,1)}), bf16[32,32,512]{2,1,0:T(8,128)(2,1)S(1)}, u32[]{:S(2)}, u32[]{:S(2)}) async-start(bf16[32,32,512]{2,1,0:T(8,128)(2,1)} %shard_map.95), calls=%async_computation.1 | async-start | bytes 2097152 | tf_op jit(solution)/shard_map/all_to_all | solution.py:533
  80.3 1.6 collective-permute-start.10
  82.0 1.6 collective-permute-start.11
  83.6 1.7 collective-permute-start.12
  85.8 32.2 %collective-permute-done.10.refs_2_ = bf16[2,512,256]{2,1,0:T(8,128)(2,1)} collective-permute-done((bf16[2,512,256]{2,1,0:T(8,128)(2,1)S(1)}, bf16[2,512,256]{2,1,0:T(8,128)(2,1)}, u32[]{:S(2)}, u32[]{:S(2)}) %collective-permute-start.10) | collective-permute-done | bytes 524320 | tf_op jit(solution)/shard_map/ppermute | solution.py:549
  118.0 1.1 fusion.4
  119.1 15.8 %collective-permute-done.11.refs_3_ = bf16[2,512,256]{2,1,0:T(8,128)(2,1)} collective-permute-done((bf16[2,512,256]{2,1,0:T(8,128)(2,1)S(1)}, bf16[2,512,256]{2,1,0:T(8,128)(2,1)}, u32[]{:S(2)}, u32[]{:S(2)}) %collective-permute-start.11) | collective-permute-done | bytes 524320 | tf_op jit(solution)/shard_map/ppermute | solution.py:549
  134.9 2.6 %collective-permute-start.14 = (bf16[2,512,256]{2,1,0:T(8,128)(2,1)}, bf16[2,512,256]{2,1,0:T(8,128)(2,1)}, u32[]{:S(2)}, u32[]{:S(2)}) collective-permute-start(bf16[2,512,256]{2,1,0:T(8,128)(2,1)} %collective-permute-done.10.refs_2_), channel_id=1, source_target_pairs={{0,32},{32,64},{64,96},{96,0},{1,33},{33,65},{65,97},{97,1},{2,34}... | collective-permute-start | bytes 1572872 | tf_op jit(solution)/shard_map/ppermute | solution.py:549
  137.5 0.8 copy-done.9
  138.3 2.7 %collective-permute-start = (bf16[512,512]{1,0:T(8,128)(2,1)}, bf16[512,512]{1,0:T(8,128)(2,1)S(1)}, u32[]{:S(2)}, u32[]{:S(2)}) collective-permute-start(bf16[512,512]{1,0:T(8,128)(2,1)} %bitcast.8), channel_id=1, source_target_pairs={{0,3},{1,0},{2,1},{3,2},{4,7},{5,4},{6,5},{7,6},{8,11},{9,8},{10,9... | collective-permute-start | bytes 1572872 | tf_op jit(solution)/shard_map/ppermute | solution.py:560
  141.0 3.2 %collective-permute-start.1 = (bf16[512,512]{1,0:T(8,128)(2,1)}, bf16[512,512]{1,0:T(8,128)(2,1)S(1)}, u32[]{:S(2)}, u32[]{:S(2)}) collective-permute-start(bf16[512,512]{1,0:T(8,128)(2,1)} %bitcast.9), channel_id=1, source_target_pairs={{0,3},{1,0},{2,1},{3,2},{4,7},{5,4},{6,5},{7,6},{8,11},{9,8},{10,9... | collective-permute-start | bytes 1572872 | tf_op jit(solution)/shard_map/ppermute | solution.py:558
  145.0 1.0 fusion
  146.0 0.9 pad_maximum_fusion.3
  146.9 3.3 %collective-permute-done.14.refs_6_ = bf16[2,512,256]{2,1,0:T(8,128)(2,1)} collective-permute-done((bf16[2,512,256]{2,1,0:T(8,128)(2,1)}, bf16[2,512,256]{2,1,0:T(8,128)(2,1)}, u32[]{:S(2)}, u32[]{:S(2)}) %collective-permute-start.14) | collective-permute-done | bytes 524320 | tf_op jit(solution)/shard_map/ppermute | solution.py:549
  150.2 3.4 %collective-permute-done.refs_3_.refs_1_ = bf16[512,512]{1,0:T(8,128)(2,1)S(1)} collective-permute-done((bf16[512,512]{1,0:T(8,128)(2,1)}, bf16[512,512]{1,0:T(8,128)(2,1)S(1)}, u32[]{:S(2)}, u32[]{:S(2)}) %collective-permute-start) | collective-permute-done | bytes 524320 | tf_op jit(solution)/shard_map/ppermute | solution.py:560
  154.3 2.9 %collective-permute-done.2.refs_1_.refs_5_ = bf16[512,512]{1,0:T(8,128)(2,1)S(1)} collective-permute-done((bf16[512,512]{1,0:T(8,128)(2,1)}, bf16[512,512]{1,0:T(8,128)(2,1)S(1)}, u32[]{:S(2)}, u32[]{:S(2)}) %collective-permute-start.2) | collective-permute-done | bytes 524320 | tf_op jit(solution)/shard_map/ppermute | solution.py:557
  157.2 6.3 %collective-permute-done.1.refs_4_.refs_2_ = bf16[512,512]{1,0:T(8,128)(2,1)S(1)} collective-permute-done((bf16[512,512]{1,0:T(8,128)(2,1)}, bf16[512,512]{1,0:T(8,128)(2,1)S(1)}, u32[]{:S(2)}, u32[]{:S(2)}) %collective-permute-start.1) | collective-permute-done | bytes 524320 | tf_op jit(solution)/shard_map/ppermute | solution.py:558
  163.5 3.6 %collective-permute-start.4 = (bf16[512,512]{1,0:T(8,128)(2,1)S(1)}, bf16[512,512]{1,0:T(8,128)(2,1)}, u32[]{:S(2)}, u32[]{:S(2)}) collective-permute-start(bf16[512,512]{1,0:T(8,128)(2,1)S(1)} %collective-permute-done.1.refs_4_.refs_2_), channel_id=1, source_target_pairs={{0,3},{1,0},{2,1},{3,2},{4,7},{5,4},{6,5},{7,6},{8,11},{9,8},{10,9... | collective-permute-start | bytes 1572872 | tf_op jit(solution)/shard_map/ppermute | solution.py:562
  167.7 0.8 collective-permute-done.5.refs_2_.refs_6_
  168.5 10.0 %shard_map.96 = (f32[512,1536]{1,0:T(8,128)}, f32[1,512]{1,0:T(1,128)S(1)}) custom-call(s32[4]{0:T(128)S(1)} %and_select_fusion.places_ref, bf16[1024,512]{1,0:T(8,128)(2,1)} %bitcast.27, bf16[512,512]{1,0:T(8,128)(2,1)S(1)} %collective-permute-done.2.refs_1_.refs_5_, bf16[512,512]{1,0:T(8,128)(2,1)S(1)} %collective-permute-done.5.refs_2_.refs_6_, ...), custom_call_target="tpu_custom_call" | custom-call | flops 4831838208 | bytes 12582912 | tf_op jit(solution)/shard_map/pallas_call | solution.py:200
  179.7 11.3 %attend.1 = (bf16[512,1024]{1,0:T(8,128)(2,1)}, bf16[2,512,256]{2,1,0:T(8,128)(2,1)}) custom-call(s32[4]{0:T(128)S(1)} %and_select_fusion.places_ref, s32[1]{0:T(128)} %dynamic_slice.6.length_ref, bf16[512,512]{1,0:T(8,128)(2,1)} %collective-permute-done.3.refs_0_.refs_3_, bf16[512,512]{1,0:T(8,128)(2,1)} %collective-permute-done.4.refs_1_.refs_4_, ...), custom_call_target="tpu_custom_call" | custom-call | flops 4000000000 | bytes 9000000 | tf_op jit(solution)/shard_map/attend/pallas_call | solution.py:282
  191.0 5.3 %shard_map.99 = (bf16[128,2048]{1,0:T(8,128)(2,1)}, bf16[128,2048]{1,0:T(8,128)(2,1)}) custom-call(s32[2]{0:T(128)} %pad_add_fusion.1.where_ref, bf16[512,1024]{1,0:T(8,128)(2,1)} %get-tuple-element.27.rows_ref, bf16[2,512,256]{2,1,0:T(8,128)(2,1)} %copy-done.7, bf16[2,512,256]{2,1,0:T(8,128)(2,1)} %copy-done.8, ...), custom_call_target="tpu_custom_call" | custom-call | flops 1073741824 | bytes 5242880 | tf_op jit(solution)/shard_map/pallas_call | solution.py:411
  196.4 0.8 copy-done.11
  197.2 3.2 %collective-permute-start.16 = (bf16[128,2048]{1,0:T(8,128)(2,1)}, bf16[128,2048]{1,0:T(8,128)(2,1)}, u32[]{:S(2)}, u32[]{:S(2)}) collective-permute-start(bf16[128,2048]{1,0:T(8,128)(2,1)} %get-tuple-element.40), channel_id=1, source_target_pairs={{0,3},{1,0},{2,1},{3,2},{4,7},{5,4},{6,5},{7,6},{8,11},{9,8},{10,9... | collective-permute-start | bytes 1572872 | tf_op jit(solution)/shard_map/ppermute | solution.py:488
  200.4 0.8 copy-done.12
  201.2 5.2 %shard_map.102 = (bf16[128,2048]{1,0:T(8,128)(2,1)}, bf16[128,2048]{1,0:T(8,128)(2,1)}) custom-call(s32[2]{0:T(128)} %pad_add_fusion.1.where_ref, bf16[512,1024]{1,0:T(8,128)(2,1)} %get-tuple-element.27.rows_ref, bf16[2,512,256]{2,1,0:T(8,128)(2,1)} %collective-permute-done.19.refs_0_, bf16[2,512,256]{2,1,0:T(8,128)(2,1)} %collective-permute-done.20.refs_1_, ...), custom_call_target="tpu_custom_call" | custom-call | flops 1073741824 | bytes 5242880 | tf_op jit(solution)/shard_map/pallas_call | solution.py:411
  206.5 3.2 %collective-permute-start.28 = (bf16[128,2048]{1,0:T(8,128)(2,1)}, bf16[128,2048]{1,0:T(8,128)(2,1)}, u32[]{:S(2)}, u32[]{:S(2)}) collective-permute-start(bf16[128,2048]{1,0:T(8,128)(2,1)} %get-tuple-element.46), channel_id=1, source_target_pairs={{0,3},{1,0},{2,1},{3,2},{4,7},{5,4},{6,5},{7,6},{8,11},{9,8},{10,9... | collective-permute-start | bytes 1572872 | tf_op jit(solution)/shard_map/ppermute | solution.py:487
  209.8 5.3 %shard_map.98 = (bf16[128,2048]{1,0:T(8,128)(2,1)}, bf16[128,2048]{1,0:T(8,128)(2,1)}) custom-call(s32[2]{0:T(128)} %pad_add_fusion.1.where_ref, bf16[512,1024]{1,0:T(8,128)(2,1)} %get-tuple-element.27.rows_ref, bf16[2,512,256]{2,1,0:T(8,128)(2,1)} %copy-done.7, bf16[2,512,256]{2,1,0:T(8,128)(2,1)} %copy-done.8, ...), custom_call_target="tpu_custom_call" | custom-call | flops 1073741824 | bytes 5242880 | tf_op jit(solution)/shard_map/pallas_call | solution.py:411
  215.1 5.3 %shard_map.101 = (bf16[128,2048]{1,0:T(8,128)(2,1)}, bf16[128,2048]{1,0:T(8,128)(2,1)}) custom-call(s32[2]{0:T(128)} %pad_add_fusion.1.where_ref, bf16[512,1024]{1,0:T(8,128)(2,1)} %get-tuple-element.27.rows_ref, bf16[2,512,256]{2,1,0:T(8,128)(2,1)} %collective-permute-done.19.refs_0_, bf16[2,512,256]{2,1,0:T(8,128)(2,1)} %collective-permute-done.20.refs_1_, ...), custom_call_target="tpu_custom_call" | custom-call | flops 1073741824 | bytes 5242880 | tf_op jit(solution)/shard_map/pallas_call | solution.py:411
  220.4 1.4 add_convert_fusion.1
  221.9 1.5 collective-permute-done.28
  223.4 1.4 add_convert_fusion
  224.8 3.8 %collective-permute-start.29 = (bf16[128,2048]{1,0:T(8,128)(2,1)S(1)}, bf16[128,2048]{1,0:T(8,128)(2,1)S(1)}, u32[]{:S(2)}, u32[]{:S(2)}) collective-permute-start(bf16[128,2048]{1,0:T(8,128)(2,1)S(1)} %add_convert_fusion), channel_id=1, source_target_pairs={{0,3},{1,0},{2,1},{3,2},{4,7},{5,4},{6,5},{7,6},{8,11},{9,8},{10,9... | collective-permute-start | bytes 1572872 | tf_op jit(solution)/shard_map/ppermute | solution.py:495
  228.6 2.0 shard_map.97.rows_ref
  230.7 5.5 %collective-permute-done.18.refs_2_ = bf16[128,2048]{1,0:T(8,128)(2,1)S(1)} collective-permute-done((bf16[128,2048]{1,0:T(8,128)(2,1)S(1)}, bf16[128,2048]{1,0:T(8,128)(2,1)S(1)}, u32[]{:S(2)}, u32[]{:S(2)}) %collective-permute-start.18) | collective-permute-done | bytes 524320 | tf_op jit(solution)/shard_map/ppermute | solution.py:495
  236.2 1.3 shard_map.100.first_ref
  237.5 1.6 collective-permute-done.29.refs_2_
  239.2 1.9 shard_map.103
  (80 shorter events, 6.8 us)
Async XLA Ops:
  7.2 161.3 %all-gather.2.cloned.1.call-start = ((), (), s32[]{:S(2)}) async-start(), calls=%async_computation.2 | async-start | bytes 13369344 | tf_op jit(solution)/shard_map/all_gather | solution.py:516
  9.2 12.4 %collective-permute-start.6 = (bf16[1,256,768]{2,1,0:T(8,128)(2,1)S(1)}, bf16[1,256,768]{2,1,0:T(8,128)(2,1)S(1)}, u32[]{:S(2)}, u32[]{:S(2)}) collective-permute-start(bf16[1,256,768]{2,1,0:T(8,128)(2,1)S(1)} %multiply_convert_fusion), channel_id=1, source_target_pairs={{0,4},{4,0},{1,5},{5,1},{2,6},{6,2},{3,7},{7,3},{8,12},{12,8},{9,1... | collective-permute-start | bytes 1179656 | tf_op jit(solution)/shard_map/ppermute | solution.py:34
  24.0 18.8 %all-to-all-start = ((s32[128,1,128]{2,1,0:T(1,128)}), s32[128,1,128]{2,1,0:T(1,128)S(1)}, u32[]{:S(2)}, u32[]{:S(2)}) async-start(s32[128,1,128]{2,1,0:T(1,128)} %broadcast_in_dim.4), calls=%async_computation | async-start | bytes 131072 | tf_op jit(solution)/shard_map/all_to_all | solution.py:518
  34.4 45.8 %collective-permute-start.7 = (bf16[512,256]{1,0:T(8,128)(2,1)}, bf16[512,256]{1,0:T(8,128)(2,1)S(1)}, u32[]{:S(2)}, u32[]{:S(2)}) collective-permute-start(bf16[512,256]{1,0:T(8,128)(2,1)} %param.15), channel_id=1, source_target_pairs={{0,4},{4,0},{1,5},{5,1},{2,6},{6,2},{3,7},{7,3},{8,12},{12,8},{9,1... | collective-permute-start | bytes 786440 | tf_op jit(solution)/shard_map/ppermute | solution.py:531
  36.0 44.3 %collective-permute-start.8 = (bf16[512,256]{1,0:T(8,128)(2,1)}, bf16[512,256]{1,0:T(8,128)(2,1)S(1)}, u32[]{:S(2)}, u32[]{:S(2)}) collective-permute-start(bf16[512,256]{1,0:T(8,128)(2,1)} %param.15), channel_id=1, source_target_pairs={{0,16},{16,0},{1,17},{17,1},{2,18},{18,2},{3,19},{19,3},{4,20},{20... | collective-permute-start | bytes 786440 | tf_op jit(solution)/shard_map/ppermute | solution.py:531
  36.4 43.8 %collective-permute-start.9 = (bf16[512,256]{1,0:T(8,128)(2,1)}, bf16[512,256]{1,0:T(8,128)(2,1)S(1)}, u32[]{:S(2)}, u32[]{:S(2)}) collective-permute-start(bf16[512,256]{1,0:T(8,128)(2,1)} %param.15), channel_id=1, source_target_pairs={{0,20},{4,16},{16,4},{20,0},{1,21},{5,17},{17,5},{21,1},{2,22},{6,... | collective-permute-start | bytes 786440 | tf_op jit(solution)/shard_map/ppermute | solution.py:531
  44.2 36.1 %copy-start.13 = (bf16[512,256]{1,0:T(8,128)(2,1)S(1)}, bf16[512,256]{1,0:T(8,128)(2,1)}, u32[]{:S(2)}) copy-start(bf16[512,256]{1,0:T(8,128)(2,1)} %param.15) | copy-start | bytes 786436
  44.2 100.2 %copy-start.14 = (s32[32]{0:T(128)S(1)}, s32[32]{0:T(128)}, u32[]{:S(2)}) copy-start(s32[32]{0:T(128)} %param.9) | copy-start | bytes 388
  74.4 43.6 %all-to-all-start.1 = ((bf16[32,32,512]{2,1,0:T(8,128)(2,1)}), bf16[32,32,512]{2,1,0:T(8,128)(2,1)S(1)}, u32[]{:S(2)}, u32[]{:S(2)}) async-start(bf16[32,32,512]{2,1,0:T(8,128)(2,1)} %shard_map.95), calls=%async_computation.1 | async-start | bytes 2097152 | tf_op jit(solution)/shard_map/all_to_all | solution.py:533
  80.3 60.7 %copy-start.7 = (bf16[2,512,256]{2,1,0:T(8,128)(2,1)}, bf16[2,512,256]{2,1,0:T(8,128)(2,1)S(1)}, u32[]{:S(2)}) copy-start(bf16[2,512,256]{2,1,0:T(8,128)(2,1)S(1)} %pad_maximum_fusion.1.refs_0_) | copy-start | bytes 1572868
  80.3 37.7 %collective-permute-start.10 = (bf16[2,512,256]{2,1,0:T(8,128)(2,1)S(1)}, bf16[2,512,256]{2,1,0:T(8,128)(2,1)}, u32[]{:S(2)}, u32[]{:S(2)}) collective-permute-start(bf16[2,512,256]{2,1,0:T(8,128)(2,1)S(1)} %pad_maximum_fusion.1.refs_0_), channel_id=1, source_target_pairs={{0,32},{32,64},{64,96},{96,0},{1,33},{33,65},{65,97},{97,1},{2,34}... | collective-permute-start | bytes 1572872 | tf_op jit(solution)/shard_map/ppermute | solution.py:549
  82.0 62.3 %copy-start.8 = (bf16[2,512,256]{2,1,0:T(8,128)(2,1)}, bf16[2,512,256]{2,1,0:T(8,128)(2,1)S(1)}, u32[]{:S(2)}) copy-start(bf16[2,512,256]{2,1,0:T(8,128)(2,1)S(1)} %pad_maximum_fusion.2.refs_1_) | copy-start | bytes 1572868
  82.0 52.9 %collective-permute-start.11 = (bf16[2,512,256]{2,1,0:T(8,128)(2,1)S(1)}, bf16[2,512,256]{2,1,0:T(8,128)(2,1)}, u32[]{:S(2)}, u32[]{:S(2)}) collective-permute-start(bf16[2,512,256]{2,1,0:T(8,128)(2,1)S(1)} %pad_maximum_fusion.2.refs_1_), channel_id=1, source_target_pairs={{0,32},{32,64},{64,96},{96,0},{1,33},{33,65},{65,97},{97,1},{2,34}... | collective-permute-start | bytes 1572872 | tf_op jit(solution)/shard_map/ppermute | solution.py:549
  83.6 53.9 %collective-permute-start.12 = (bf16[2,512,256]{2,1,0:T(8,128)(2,1)S(1)}, bf16[2,512,256]{2,1,0:T(8,128)(2,1)S(1)}, u32[]{:S(2)}, u32[]{:S(2)}) collective-permute-start(bf16[2,512,256]{2,1,0:T(8,128)(2,1)S(1)} %pad_maximum_fusion.1.refs_0_), channel_id=1, source_target_pairs={{0,96},{32,0},{64,32},{96,64},{1,97},{33,1},{65,33},{97,65},{2,98}... | collective-permute-start | bytes 1572872 | tf_op jit(solution)/shard_map/ppermute | solution.py:549
  85.3 55.7 %collective-permute-start.13 = (bf16[2,512,256]{2,1,0:T(8,128)(2,1)S(1)}, bf16[2,512,256]{2,1,0:T(8,128)(2,1)}, u32[]{:S(2)}, u32[]{:S(2)}) collective-permute-start(bf16[2,512,256]{2,1,0:T(8,128)(2,1)S(1)} %pad_maximum_fusion.2.refs_1_), channel_id=1, source_target_pairs={{0,96},{32,0},{64,32},{96,64},{1,97},{33,1},{65,33},{97,65},{2,98}... | collective-permute-start | bytes 1572872 | tf_op jit(solution)/shard_map/ppermute | solution.py:549
  85.8 55.2 %collective-permute-start.19 = (bf16[2,512,256]{2,1,0:T(8,128)(2,1)S(1)}, bf16[2,512,256]{2,1,0:T(8,128)(2,1)}, u32[]{:S(2)}, u32[]{:S(2)}) collective-permute-start(bf16[2,512,256]{2,1,0:T(8,128)(2,1)S(1)} %pad_maximum_fusion.1.refs_0_), channel_id=1, source_target_pairs={{0,8},{8,0},{1,9},{9,1},{2,10},{10,2},{3,11},{11,3},{4,12},{12,4},... | collective-permute-start | bytes 1572872 | tf_op jit(solution)/shard_map/ppermute | solution.py:552
  118.0 26.3 %collective-permute-start.20 = (bf16[2,512,256]{2,1,0:T(8,128)(2,1)S(1)}, bf16[2,512,256]{2,1,0:T(8,128)(2,1)}, u32[]{:S(2)}, u32[]{:S(2)}) collective-permute-start(bf16[2,512,256]{2,1,0:T(8,128)(2,1)S(1)} %pad_maximum_fusion.2.refs_1_), channel_id=1, source_target_pairs={{0,8},{8,0},{1,9},{9,1},{2,10},{10,2},{3,11},{11,3},{4,12},{12,4},... | collective-permute-start | bytes 1572872 | tf_op jit(solution)/shard_map/ppermute | solution.py:552
  118.0 50.5 %copy-start = (bf16[32,32,512]{2,1,0:T(8,128)(2,1)}, bf16[32,32,512]{2,1,0:T(8,128)(2,1)S(1)}, u32[]{:S(2)}) copy-start(bf16[32,32,512]{2,1,0:T(8,128)(2,1)S(1)} %all-to-all-done.1) | copy-start | bytes 3145732
  134.9 15.3 %collective-permute-start.14 = (bf16[2,512,256]{2,1,0:T(8,128)(2,1)}, bf16[2,512,256]{2,1,0:T(8,128)(2,1)}, u32[]{:S(2)}, u32[]{:S(2)}) collective-permute-start(bf16[2,512,256]{2,1,0:T(8,128)(2,1)} %collective-permute-done.10.refs_2_), channel_id=1, source_target_pairs={{0,32},{32,64},{64,96},{96,0},{1,33},{33,65},{65,97},{97,1},{2,34}... | collective-permute-start | bytes 1572872 | tf_op jit(solution)/shard_map/ppermute | solution.py:549
  137.5 0.8 copy-start.9
  138.3 15.3 %collective-permute-start = (bf16[512,512]{1,0:T(8,128)(2,1)}, bf16[512,512]{1,0:T(8,128)(2,1)S(1)}, u32[]{:S(2)}, u32[]{:S(2)}) collective-permute-start(bf16[512,512]{1,0:T(8,128)(2,1)} %bitcast.8), channel_id=1, source_target_pairs={{0,3},{1,0},{2,1},{3,2},{4,7},{5,4},{6,5},{7,6},{8,11},{9,8},{10,9... | collective-permute-start | bytes 1572872 | tf_op jit(solution)/shard_map/ppermute | solution.py:560
  141.0 16.2 %collective-permute-start.2 = (bf16[512,512]{1,0:T(8,128)(2,1)}, bf16[512,512]{1,0:T(8,128)(2,1)S(1)}, u32[]{:S(2)}, u32[]{:S(2)}) collective-permute-start(bf16[512,512]{1,0:T(8,128)(2,1)} %bitcast.8), channel_id=1, source_target_pairs={{0,1},{1,2},{2,3},{3,0},{4,5},{5,6},{6,7},{7,4},{8,9},{9,10},{10,1... | collective-permute-start | bytes 1572872 | tf_op jit(solution)/shard_map/ppermute | solution.py:557
  141.0 22.5 %collective-permute-start.1 = (bf16[512,512]{1,0:T(8,128)(2,1)}, bf16[512,512]{1,0:T(8,128)(2,1)S(1)}, u32[]{:S(2)}, u32[]{:S(2)}) collective-permute-start(bf16[512,512]{1,0:T(8,128)(2,1)} %bitcast.9), channel_id=1, source_target_pairs={{0,3},{1,0},{2,1},{3,2},{4,7},{5,4},{6,5},{7,6},{8,11},{9,8},{10,9... | collective-permute-start | bytes 1572872 | tf_op jit(solution)/shard_map/ppermute | solution.py:558
  144.3 24.2 %collective-permute-start.5 = (bf16[512,512]{1,0:T(8,128)(2,1)}, bf16[512,512]{1,0:T(8,128)(2,1)S(1)}, u32[]{:S(2)}, u32[]{:S(2)}) collective-permute-start(bf16[512,512]{1,0:T(8,128)(2,1)} %bitcast.9), channel_id=1, source_target_pairs={{0,1},{1,2},{2,3},{3,0},{4,5},{5,6},{6,7},{7,4},{8,9},{9,10},{10,1... | collective-permute-start | bytes 1572872 | tf_op jit(solution)/shard_map/ppermute | solution.py:559
  150.2 28.8 %collective-permute-start.21 = (bf16[2,512,256]{2,1,0:T(8,128)(2,1)}, bf16[2,512,256]{2,1,0:T(8,128)(2,1)}, u32[]{:S(2)}, u32[]{:S(2)}) collective-permute-start(bf16[2,512,256]{2,1,0:T(8,128)(2,1)} %collective-permute-done.10.refs_2_), channel_id=1, source_target_pairs={{0,8},{8,0},{1,9},{9,1},{2,10},{10,2},{3,11},{11,3},{4,12},{12,4},... | collective-permute-start | bytes 1572872 | tf_op jit(solution)/shard_map/ppermute | solution.py:552
  153.6 24.8 %collective-permute-start.15 = (bf16[2,512,256]{2,1,0:T(8,128)(2,1)}, bf16[2,512,256]{2,1,0:T(8,128)(2,1)}, u32[]{:S(2)}, u32[]{:S(2)}) collective-permute-start(bf16[2,512,256]{2,1,0:T(8,128)(2,1)} %collective-permute-done.13.refs_5_), channel_id=1, source_target_pairs={{0,96},{32,0},{64,32},{96,64},{1,97},{33,1},{65,33},{97,65},{2,98}... | collective-permute-start | bytes 1572872 | tf_op jit(solution)/shard_map/ppermute | solution.py:549
  157.2 21.9 %collective-permute-start.3 = (bf16[512,512]{1,0:T(8,128)(2,1)S(1)}, bf16[512,512]{1,0:T(8,128)(2,1)}, u32[]{:S(2)}, u32[]{:S(2)}) collective-permute-start(bf16[512,512]{1,0:T(8,128)(2,1)S(1)} %collective-permute-done.2.refs_1_.refs_5_), channel_id=1, source_target_pairs={{0,1},{1,2},{2,3},{3,0},{4,5},{5,6},{6,7},{7,4},{8,9},{9,10},{10,1... | collective-permute-start | bytes 1572872 | tf_op jit(solution)/shard_map/ppermute | solution.py:561
  163.5 5.0 %copy-start.2 = (bf16[512,512]{1,0:T(8,128)(2,1)}, bf16[512,512]{1,0:T(8,128)(2,1)S(1)}, u32[]{:S(2)}) copy-start(bf16[512,512]{1,0:T(8,128)(2,1)S(1)} %collective-permute-done.1.refs_4_.refs_2_) | copy-start | bytes 1572868
  163.5 16.1 %collective-permute-start.4 = (bf16[512,512]{1,0:T(8,128)(2,1)S(1)}, bf16[512,512]{1,0:T(8,128)(2,1)}, u32[]{:S(2)}, u32[]{:S(2)}) collective-permute-start(bf16[512,512]{1,0:T(8,128)(2,1)S(1)} %collective-permute-done.1.refs_4_.refs_2_), channel_id=1, source_target_pairs={{0,3},{1,0},{2,1},{3,2},{4,7},{5,4},{6,5},{7,6},{8,11},{9,8},{10,9... | collective-permute-start | bytes 1572872 | tf_op jit(solution)/shard_map/ppermute | solution.py:562
  168.5 27.8 %collective-permute-start.22 = (bf16[2,512,256]{2,1,0:T(8,128)(2,1)}, bf16[2,512,256]{2,1,0:T(8,128)(2,1)}, u32[]{:S(2)}, u32[]{:S(2)}) collective-permute-start(bf16[2,512,256]{2,1,0:T(8,128)(2,1)} %collective-permute-done.11.refs_3_), channel_id=1, source_target_pairs={{0,8},{8,0},{1,9},{9,1},{2,10},{10,2},{3,11},{11,3},{4,12},{12,4},... | collective-permute-start | bytes 1572872 | tf_op jit(solution)/shard_map/ppermute | solution.py:552
  168.5 10.6 %copy-start.10 = (bf16[2,512,256]{2,1,0:T(8,128)(2,1)S(1)}, bf16[2,512,256]{2,1,0:T(8,128)(2,1)}, u32[]{:S(2)}) copy-start(bf16[2,512,256]{2,1,0:T(8,128)(2,1)} %copy-done.9) | copy-start | bytes 1572868
  168.5 11.2 %copy-start.4 = (f32[512,128]{1,0:T(8,128)S(1)}, f32[512,128]{1,0:T(8,128)}, u32[]{:S(2)}) copy-start(f32[512,128]{1,0:T(8,128)} %get-tuple-element.56.refs_7_) | copy-start | bytes 786436
  178.5 21.9 %collective-permute-start.24 = (bf16[2,512,256]{2,1,0:T(8,128)(2,1)}, bf16[2,512,256]{2,1,0:T(8,128)(2,1)}, u32[]{:S(2)}, u32[]{:S(2)}) collective-permute-start(bf16[2,512,256]{2,1,0:T(8,128)(2,1)} %collective-permute-done.13.refs_5_), channel_id=1, source_target_pairs={{0,8},{8,0},{1,9},{9,1},{2,10},{10,2},{3,11},{11,3},{4,12},{12,4},... | collective-permute-start | bytes 1572872 | tf_op jit(solution)/shard_map/ppermute | solution.py:552
  179.1 17.3 %collective-permute-start.23 = (bf16[2,512,256]{2,1,0:T(8,128)(2,1)S(1)}, bf16[2,512,256]{2,1,0:T(8,128)(2,1)S(1)}, u32[]{:S(2)}, u32[]{:S(2)}) collective-permute-start(bf16[2,512,256]{2,1,0:T(8,128)(2,1)S(1)} %copy-done.10), channel_id=1, source_target_pairs={{0,8},{8,0},{1,9},{9,1},{2,10},{10,2},{3,11},{11,3},{4,12},{12,4},... | collective-permute-start | bytes 1572872 | tf_op jit(solution)/shard_map/ppermute | solution.py:552
  179.2 21.2 %collective-permute-start.25 = (bf16[2,512,256]{2,1,0:T(8,128)(2,1)}, bf16[2,512,256]{2,1,0:T(8,128)(2,1)}, u32[]{:S(2)}, u32[]{:S(2)}) collective-permute-start(bf16[2,512,256]{2,1,0:T(8,128)(2,1)} %collective-permute-done.14.refs_6_), channel_id=1, source_target_pairs={{0,8},{8,0},{1,9},{9,1},{2,10},{10,2},{3,11},{11,3},{4,12},{12,4},... | collective-permute-start | bytes 1572872 | tf_op jit(solution)/shard_map/ppermute | solution.py:552
  179.6 20.8 %collective-permute-start.26 = (bf16[2,512,256]{2,1,0:T(8,128)(2,1)}, bf16[2,512,256]{2,1,0:T(8,128)(2,1)S(1)}, u32[]{:S(2)}, u32[]{:S(2)}) collective-permute-start(bf16[2,512,256]{2,1,0:T(8,128)(2,1)} %collective-permute-done.15.refs_7_), channel_id=1, source_target_pairs={{0,8},{8,0},{1,9},{9,1},{2,10},{10,2},{3,11},{11,3},{4,12},{12,4},... | collective-permute-start | bytes 1572872 | tf_op jit(solution)/shard_map/ppermute | solution.py:552
  196.3 24.1 %collective-permute-start.17 = (bf16[128,2048]{1,0:T(8,128)(2,1)}, bf16[128,2048]{1,0:T(8,128)(2,1)}, u32[]{:S(2)}, u32[]{:S(2)}) collective-permute-start(bf16[128,2048]{1,0:T(8,128)(2,1)} %get-tuple-element.42), channel_id=1, source_target_pairs={{0,1},{1,2},{2,3},{3,0},{4,5},{5,6},{6,7},{7,4},{8,9},{9,10},{10,1... | collective-permute-start | bytes 1572872 | tf_op jit(solution)/shard_map/ppermute | solution.py:487
  196.4 0.8 copy-start.11
  197.2 31.4 %copy-start.1 = (bf16[32,32,512]{2,1,0:T(8,128)(2,1)S(1)}, bf16[32,32,512]{2,1,0:T(8,128)(2,1)}, u32[]{:S(2)}) copy-start(bf16[32,32,512]{2,1,0:T(8,128)(2,1)} %copy-done) | copy-start | bytes 3145732
  197.2 31.4 %copy-start.3 = (bf16[512,512]{1,0:T(8,128)(2,1)S(1)}, bf16[512,512]{1,0:T(8,128)(2,1)}, u32[]{:S(2)}) copy-start(bf16[512,512]{1,0:T(8,128)(2,1)} %copy-done.2) | copy-start | bytes 1572868
  197.2 33.5 %collective-permute-start.16 = (bf16[128,2048]{1,0:T(8,128)(2,1)}, bf16[128,2048]{1,0:T(8,128)(2,1)}, u32[]{:S(2)}, u32[]{:S(2)}) collective-permute-start(bf16[128,2048]{1,0:T(8,128)(2,1)} %get-tuple-element.40), channel_id=1, source_target_pairs={{0,3},{1,0},{2,1},{3,2},{4,7},{5,4},{6,5},{7,6},{8,11},{9,8},{10,9... | collective-permute-start | bytes 1572872 | tf_op jit(solution)/shard_map/ppermute | solution.py:488
  200.4 0.8 copy-start.12
  206.4 31.1 %collective-permute-start.27 = (bf16[128,2048]{1,0:T(8,128)(2,1)}, bf16[128,2048]{1,0:T(8,128)(2,1)S(1)}, u32[]{:S(2)}, u32[]{:S(2)}) collective-permute-start(bf16[128,2048]{1,0:T(8,128)(2,1)} %get-tuple-element.44), channel_id=1, source_target_pairs={{0,1},{1,2},{2,3},{3,0},{4,5},{5,6},{6,7},{7,4},{8,9},{9,10},{10,1... | collective-permute-start | bytes 1572872 | tf_op jit(solution)/shard_map/ppermute | solution.py:488
  206.5 16.9 %collective-permute-start.28 = (bf16[128,2048]{1,0:T(8,128)(2,1)}, bf16[128,2048]{1,0:T(8,128)(2,1)}, u32[]{:S(2)}, u32[]{:S(2)}) collective-permute-start(bf16[128,2048]{1,0:T(8,128)(2,1)} %get-tuple-element.46), channel_id=1, source_target_pairs={{0,3},{1,0},{2,1},{3,2},{4,7},{5,4},{6,5},{7,6},{8,11},{9,8},{10,9... | collective-permute-start | bytes 1572872 | tf_op jit(solution)/shard_map/ppermute | solution.py:487
  220.3 15.8 %copy-start.6 = (bf16[128,2048]{1,0:T(8,128)(2,1)S(1)}, bf16[128,2048]{1,0:T(8,128)(2,1)}, u32[]{:S(2)}) copy-start(bf16[128,2048]{1,0:T(8,128)(2,1)} %get-tuple-element.39.refs_0_) | copy-start | bytes 1572868
  220.3 18.8 %copy-start.5 = (bf16[128,2048]{1,0:T(8,128)(2,1)S(1)}, bf16[128,2048]{1,0:T(8,128)(2,1)}, u32[]{:S(2)}) copy-start(bf16[128,2048]{1,0:T(8,128)(2,1)} %get-tuple-element.43.refs_0_) | copy-start | bytes 1572868
  221.8 14.4 %collective-permute-start.18 = (bf16[128,2048]{1,0:T(8,128)(2,1)S(1)}, bf16[128,2048]{1,0:T(8,128)(2,1)S(1)}, u32[]{:S(2)}, u32[]{:S(2)}) collective-permute-start(bf16[128,2048]{1,0:T(8,128)(2,1)S(1)} %add_convert_fusion.1), channel_id=1, source_target_pairs={{0,1},{1,2},{2,3},{3,0},{4,5},{5,6},{6,7},{7,4},{8,9},{9,10},{10,1... | collective-permute-start | bytes 1572872 | tf_op jit(solution)/shard_map/ppermute | solution.py:495
  224.8 14.4 %collective-permute-start.29 = (bf16[128,2048]{1,0:T(8,128)(2,1)S(1)}, bf16[128,2048]{1,0:T(8,128)(2,1)S(1)}, u32[]{:S(2)}, u32[]{:S(2)}) collective-permute-start(bf16[128,2048]{1,0:T(8,128)(2,1)S(1)} %add_convert_fusion), channel_id=1, source_target_pairs={{0,3},{1,0},{2,1},{3,2},{4,7},{5,4},{6,5},{7,6},{8,11},{9,8},{10,9... | collective-permute-start | bytes 1572872 | tf_op jit(solution)/shard_map/ppermute | solution.py:495
Sparse Core Ops, SparseCore 0:
  22.8 107.8 all-gather.1
